TPU v7x, 32 devices: a whole 2x2x4 slice. The times are simulated.
32 devices in a mesh: rep: 4 (over z), ep: 8 (over y, x, core).
Axes of the slice: x: 2, y: 2, z: 4, core: 2. Of those that a mesh axis runs over, the one named last changes fastest.
Arguments:
- tokens: bfloat16 [32, 256, 2048], P('rep', 'ep'), may hold values from -6 to 6
- cotangent: bfloat16 [32, 256, 2048], P('rep', 'ep'), may hold values from -6 to 6
- gate_weights: bfloat16 [32, 256, 8], P('rep', 'ep'), may hold values from 0.049804688 to 0.25
- expert_ids: int32 [32, 256, 8], P('rep', 'ep'), may hold values from 0 to 15, all different within a row; in each aligned block of 256 rows (0 to 255, 256 to 511, ..., all dimensions but the last counted through in order) at most 144 rows name the same one
- seq_lengths: int32 [32], P(('rep', 'ep')), may hold values from 1 to 256, 5120 in all
- query_weight: bfloat16 [2048, 2048], P('ep'), may hold values from -0.125 to 0.125
- key_weight: bfloat16 [2048, 2048], P('ep'), may hold values from -0.125 to 0.125
- value_weight: bfloat16 [2048, 2048], P('ep'), may hold values from -0.125 to 0.125
- output_weight: bfloat16 [2048, 2048], P('ep'), may hold values from -0.75 to 0.75
- attn_gain: bfloat16 [2048], P('ep'), may hold values from 0.25 to 1.75
- ffn_gain: bfloat16 [2048], P('ep'), may hold values from 0.25 to 1.75
- query_gain: bfloat16 [128], P('ep'), may hold values from 0.25 to 1.75
- key_gain: bfloat16 [128], P('ep'), may hold values from 0.25 to 1.75
- expert_in: bfloat16 [16, 2048, 2048], P('ep'), may hold values from -0.125 to 0.125
- expert_out: bfloat16 [16, 1024, 2048], P('ep'), may hold values from -0.5 to 0.5
Outputs:
- result: bfloat16 [32, 256, 2048], P('rep', 'ep')
- token_grad: bfloat16 [32, 256, 2048], P('rep', 'ep')
- query_weight_grad: float32 [2048, 2048], P('ep')
- key_weight_grad: float32 [2048, 2048], P('ep')
- value_weight_grad: float32 [2048, 2048], P('ep')
- output_weight_grad: float32 [2048, 2048], P('ep')
- attn_gain_grad: float32 [2048], P('ep')
- ffn_gain_grad: float32 [2048], P('ep')
- query_gain_grad: float32 [128], P('ep')
- key_gain_grad: float32 [128], P('ep')
- expert_in_grad: float32 [16, 2048, 2048], P('ep', 'rep')
- expert_out_grad: float32 [16, 1024, 2048], P('ep', 'rep')
Inputs may be any that keep to these rules, and one draw needn't show every extreme that they name: `expert_ids`: each token names 8 different experts; within the 256 token slots of one sequence no expert is named more than 144 times, and some expert of some sequence is named exactly 144 times. `seq_lengths`: some sequence is full, with exactly 256 live tokens; live tokens come first in a sequence.
All inputs are finite; a program needn't handle non-finite values. No bound on the sum of `seq_lengths` on one device may be relied on, other than what follows from the above.
Results may differ from a plain program's by a relative error of at most 0.028.
Values may be sent and summed in bfloat16 or wider, within the bound.
A program may use at most 320 MiB of HBM per device.

v0:
```python
import jax
import jax.numpy as jnp
from jax import lax
from jax.sharding import PartitionSpec as P

HEADS = 16
HEAD_DIM = 128


epsilon = 1e-06
rope_base = 50000.0


def rms_norm(values, gain_vector):
    return (
        values
        * lax.rsqrt(jnp.mean(values * values, axis=-1, keepdims=True) + epsilon)
        * gain_vector
    )


def rotary_tables(length, head_width):
    half_width = head_width // 2
    frequency = rope_base ** (-(jnp.arange(half_width, dtype=jnp.float32) * (2.0 / head_width)))
    angles = jnp.arange(length, dtype=jnp.float32)[:, None] * frequency[None, :]
    angles = jnp.concatenate([angles, angles], axis=-1)
    return (jnp.cos(angles)[:, None, :], jnp.sin(angles)[:, None, :])


def rotate(values, cos_table, sin_table):
    half_width = values.shape[-1] // 2
    turned = jnp.concatenate([-values[..., half_width:], values[..., :half_width]], axis=-1)
    return values * cos_table + turned * sin_table


def slot_index(expert_ids, experts, capacity):
    flat_ids = expert_ids.reshape(-1)
    choose = (flat_ids[:, None] == jnp.arange(experts, dtype=jnp.int32)[None, :]).astype(jnp.int32)
    before = jnp.cumsum(choose, axis=0) - choose
    ranking = jnp.sum(before * choose, axis=1)
    return flat_ids * capacity + ranking


def contract(left_side, right_side, left_dim, right_dim):
    return lax.dot_general(
        left_side,
        right_side,
        (((left_dim,), (right_dim,)), ((), ())),
        preferred_element_type=jnp.float32,
    )


def masked_scores(query_low, key_low, living, score_scale):
    raw_scores = (
        jnp.einsum("qhd,khd->hqk", query_low, key_low, preferred_element_type=jnp.float32)
        * score_scale
    )
    return jnp.where(living[None, None, :] > 0.5, raw_scores, -1000000000.0)


def shards(
    tokens,
    cotangent,
    gate_weights,
    expert_ids,
    seq_lengths,
    query_weight,
    key_weight,
    value_weight,
    output_weight,
    attn_gain,
    ffn_gain,
    query_gain,
    key_gain,
    expert_in,
    expert_out,
):
    ep_count = lax.axis_size("ep")
    dealt_arrays = (
        lax.all_to_all(tokens, "ep", split_axis=0, concat_axis=1, tiled=True),
        lax.all_to_all(cotangent, "ep", split_axis=0, concat_axis=1, tiled=True),
        lax.all_to_all(gate_weights, "ep", split_axis=0, concat_axis=1, tiled=True),
    )
    seq_tokens = dealt_arrays[0][0]
    seq_cot = dealt_arrays[1][0]
    seq_gates = dealt_arrays[2][0]
    seq_ids = lax.all_to_all(expert_ids, "ep", split_axis=0, concat_axis=1, tiled=True)[0]
    length = seq_tokens.shape[0]
    model_width = seq_tokens.shape[1]
    top_count = seq_gates.shape[1]
    local_experts = expert_in.shape[0]
    hidden_size = expert_out.shape[1]
    experts = local_experts * ep_count
    capacity = length * top_count * 9 // (8 * experts)
    score_scale = HEAD_DIM ** (-0.5)
    gathered_weights = (
        lax.all_gather(query_weight, "ep", axis=0, tiled=True),
        lax.all_gather(key_weight, "ep", axis=0, tiled=True),
        lax.all_gather(value_weight, "ep", axis=0, tiled=True),
        lax.all_gather(output_weight, "ep", axis=0, tiled=True),
        lax.all_gather(attn_gain, "ep", axis=0, tiled=True),
        lax.all_gather(ffn_gain, "ep", axis=0, tiled=True),
        lax.all_gather(query_gain, "ep", axis=0, tiled=True),
        lax.all_gather(key_gain, "ep", axis=0, tiled=True),
    )
    w_query = gathered_weights[0]
    w_key = gathered_weights[1]
    w_value = gathered_weights[2]
    w_output = gathered_weights[3]
    gain_attn = gathered_weights[4].astype(jnp.float32)
    gain_ffn = gathered_weights[5].astype(jnp.float32)
    gain_query = gathered_weights[6].astype(jnp.float32)
    gain_key = gathered_weights[7].astype(jnp.float32)
    positions = jnp.arange(length, dtype=jnp.int32)
    living = (positions < seq_lengths[0]).astype(jnp.float32)
    combine_weight = seq_gates.astype(jnp.float32) * living[:, None]
    destination = slot_index(seq_ids, experts, capacity)
    pair_count = length * top_count
    token_of_slot = (
        jnp.zeros((experts * capacity,), jnp.int32)
        .at[destination]
        .set(jnp.arange(pair_count, dtype=jnp.int32) // top_count)
    )
    slot_weight = (
        jnp.zeros((experts * capacity,), jnp.float32)
        .at[destination]
        .set(combine_weight.reshape(-1))
    )
    slot_filled = (
        jnp.zeros((experts * capacity,), jnp.bfloat16)
        .at[destination]
        .set(jnp.ones((pair_count,), jnp.bfloat16))
    )
    cos_table, sin_table = rotary_tables(length, HEAD_DIM)

    def head_piece(inputs_pre, gain_vector):
        return rotate(rms_norm(inputs_pre, gain_vector), cos_table, sin_table)

    residual_in = seq_tokens.astype(jnp.float32)
    normed = rms_norm(residual_in, gain_attn).astype(jnp.bfloat16)
    query_pre = jnp.dot(normed, w_query, preferred_element_type=jnp.float32).reshape(
        length, HEADS, HEAD_DIM
    )
    key_pre = jnp.dot(normed, w_key, preferred_element_type=jnp.float32).reshape(
        length, HEADS, HEAD_DIM
    )
    value_low = (
        jnp.dot(normed, w_value, preferred_element_type=jnp.float32)
        .astype(jnp.bfloat16)
        .reshape(length, HEADS, HEAD_DIM)
    )
    query_rot, query_pull = jax.vjp(head_piece, query_pre, gain_query)
    key_rot, key_pull = jax.vjp(head_piece, key_pre, gain_key)
    query_low = query_rot.astype(jnp.bfloat16)
    key_low = key_rot.astype(jnp.bfloat16)
    scores = masked_scores(query_low, key_low, living, score_scale)
    log_total = jax.nn.logsumexp(scores, axis=-1, keepdims=True)
    attention_low = jnp.exp(scores - log_total).astype(jnp.bfloat16)
    context = jnp.einsum(
        "hqk,khd->qhd", attention_low, value_low, preferred_element_type=jnp.float32
    )
    context = context.astype(jnp.bfloat16).reshape(length, HEADS * HEAD_DIM)
    attended = jnp.dot(context, w_output, preferred_element_type=jnp.float32) * living[:, None]
    middle = residual_in + attended
    mixed_in = rms_norm(middle, gain_ffn).astype(jnp.bfloat16)
    outgoing = (mixed_in[token_of_slot] * slot_filled[:, None]).reshape(
        ep_count, local_experts, capacity, model_width
    )
    arrived = lax.all_to_all(outgoing, "ep", split_axis=0, concat_axis=2, tiled=True)[0]
    gate_up = jnp.einsum("erd,edf->erf", arrived, expert_in, preferred_element_type=jnp.float32)

    def swiglu(paired):
        return jax.nn.silu(paired[..., :hidden_size]) * paired[..., hidden_size:]

    activated, swiglu_pull = jax.vjp(swiglu, gate_up)
    activated_low = activated.astype(jnp.bfloat16)
    produced = jnp.einsum(
        "erf,efd->erd", activated_low, expert_out, preferred_element_type=jnp.float32
    ).astype(jnp.bfloat16)
    returned = lax.all_to_all(
        produced[None], "ep", split_axis=2, concat_axis=0, tiled=True
    ).reshape(experts * capacity, model_width)
    gathered = returned[destination].reshape(length, top_count, model_width).astype(jnp.float32)
    outcome = middle + jnp.sum(combine_weight[:, :, None] * gathered, axis=1)
    upstream = seq_cot.astype(jnp.float32)
    outgoing_grad = (upstream[token_of_slot] * slot_weight[:, None]).astype(jnp.bfloat16)
    outgoing_grad = outgoing_grad.reshape(ep_count, local_experts, capacity, model_width)
    arrived_grad = lax.all_to_all(outgoing_grad, "ep", split_axis=0, concat_axis=2, tiled=True)[0]
    activated_grad = jnp.einsum(
        "erd,efd->erf", arrived_grad, expert_out, preferred_element_type=jnp.float32
    )
    gate_up_grad = swiglu_pull(activated_grad)[0].astype(jnp.bfloat16)
    out_local_grad = jnp.einsum(
        "erf,erd->efd", activated_low, arrived_grad, preferred_element_type=jnp.float32
    )
    in_local_grad = jnp.einsum(
        "erd,erf->edf", arrived, gate_up_grad, preferred_element_type=jnp.float32
    )
    arrived_back = jnp.einsum(
        "erf,edf->erd", gate_up_grad, expert_in, preferred_element_type=jnp.float32
    ).astype(jnp.bfloat16)
    expert_sums = (
        lax.psum_scatter(
            in_local_grad.astype(jnp.bfloat16), "rep", scatter_dimension=1, tiled=True
        ).astype(jnp.float32),
        lax.psum_scatter(
            out_local_grad.astype(jnp.bfloat16), "rep", scatter_dimension=1, tiled=True
        ).astype(jnp.float32),
    )
    returned_grad = lax.all_to_all(
        arrived_back[None], "ep", split_axis=2, concat_axis=0, tiled=True
    ).reshape(experts * capacity, model_width)
    mixed_grad = jnp.sum(
        returned_grad[destination].reshape(length, top_count, model_width).astype(jnp.float32),
        axis=1,
    )
    ffn_values, ffn_pull = jax.vjp(rms_norm, middle, gain_ffn)
    middle_part, ffn_gain_grad = ffn_pull(mixed_grad)
    middle_grad = upstream + middle_part
    attended_grad = (middle_grad * living[:, None]).astype(jnp.bfloat16)
    output_weight_grad = contract(context, attended_grad, 0, 0)
    context_grad = (
        contract(attended_grad, w_output, 1, 1)
        .astype(jnp.bfloat16)
        .reshape(length, HEADS, HEAD_DIM)
    )
    attention_again = jnp.exp(masked_scores(query_low, key_low, living, score_scale) - log_total)
    attention_again_low = attention_again.astype(jnp.bfloat16)
    value_grad = jnp.einsum(
        "hqk,qhd->khd", attention_again_low, context_grad, preferred_element_type=jnp.float32
    )
    value_grad = value_grad.astype(jnp.bfloat16).reshape(length, HEADS * HEAD_DIM)
    prob_grad = jnp.einsum(
        "qhd,khd->hqk", context_grad, value_low, preferred_element_type=jnp.float32
    )
    score_grad = attention_again * (
        prob_grad - jnp.sum(attention_again * prob_grad, axis=-1, keepdims=True)
    )
    score_grad = score_grad.astype(jnp.bfloat16)
    query_rot_grad = (
        jnp.einsum("hqk,khd->qhd", score_grad, key_low, preferred_element_type=jnp.float32)
        * score_scale
    )
    key_rot_grad = (
        jnp.einsum("hqk,qhd->khd", score_grad, query_low, preferred_element_type=jnp.float32)
        * score_scale
    )
    query_grad, query_gain_grad = query_pull(query_rot_grad)
    key_grad, key_gain_grad = key_pull(key_rot_grad)
    query_grad = query_grad.astype(jnp.bfloat16).reshape(length, HEADS * HEAD_DIM)
    key_grad = key_grad.astype(jnp.bfloat16).reshape(length, HEADS * HEAD_DIM)
    normed_grad = (
        contract(query_grad, w_query, 1, 1)
        + contract(key_grad, w_key, 1, 1)
        + contract(value_grad, w_value, 1, 1)
    )
    query_weight_grad = contract(normed, query_grad, 0, 0)
    key_weight_grad = contract(normed, key_grad, 0, 0)
    value_weight_grad = contract(normed, value_grad, 0, 0)
    attn_values, attn_pull = jax.vjp(rms_norm, residual_in, gain_attn)
    input_part, attn_gain_grad = attn_pull(normed_grad)
    input_grad = (middle_grad + input_part).astype(jnp.bfloat16)
    moved_back = (
        lax.all_to_all(
            outcome.astype(jnp.bfloat16)[None], "ep", split_axis=1, concat_axis=0, tiled=True
        ),
        lax.all_to_all(input_grad[None], "ep", split_axis=1, concat_axis=0, tiled=True),
    )
    shares = (
        lax.psum_scatter(
            query_weight_grad.astype(jnp.bfloat16), "ep", scatter_dimension=0, tiled=True
        ).astype(jnp.float32),
        lax.psum_scatter(
            key_weight_grad.astype(jnp.bfloat16), "ep", scatter_dimension=0, tiled=True
        ).astype(jnp.float32),
        lax.psum_scatter(
            value_weight_grad.astype(jnp.bfloat16), "ep", scatter_dimension=0, tiled=True
        ).astype(jnp.float32),
        lax.psum_scatter(
            output_weight_grad.astype(jnp.bfloat16), "ep", scatter_dimension=0, tiled=True
        ).astype(jnp.float32),
        lax.psum_scatter(
            attn_gain_grad.astype(jnp.bfloat16), "ep", scatter_dimension=0, tiled=True
        ).astype(jnp.float32),
        lax.psum_scatter(
            ffn_gain_grad.astype(jnp.bfloat16), "ep", scatter_dimension=0, tiled=True
        ).astype(jnp.float32),
        lax.psum_scatter(
            query_gain_grad.astype(jnp.bfloat16), "ep", scatter_dimension=0, tiled=True
        ).astype(jnp.float32),
        lax.psum_scatter(
            key_gain_grad.astype(jnp.bfloat16), "ep", scatter_dimension=0, tiled=True
        ).astype(jnp.float32),
    )
    shares = (
        lax.psum(shares[0].astype(jnp.bfloat16), "rep").astype(jnp.float32),
        lax.psum(shares[1].astype(jnp.bfloat16), "rep").astype(jnp.float32),
        lax.psum(shares[2].astype(jnp.bfloat16), "rep").astype(jnp.float32),
        lax.psum(shares[3].astype(jnp.bfloat16), "rep").astype(jnp.float32),
        lax.psum(shares[4].astype(jnp.bfloat16), "rep").astype(jnp.float32),
        lax.psum(shares[5].astype(jnp.bfloat16), "rep").astype(jnp.float32),
        lax.psum(shares[6].astype(jnp.bfloat16), "rep").astype(jnp.float32),
        lax.psum(shares[7].astype(jnp.bfloat16), "rep").astype(jnp.float32),
    )
    return (
        moved_back[0],
        moved_back[1],
        shares[0],
        shares[1],
        shares[2],
        shares[3],
        shares[4],
        shares[5],
        shares[6],
        shares[7],
        expert_sums[0],
        expert_sums[1],
    )


def solution(mesh):
    return jax.shard_map(
        shards,
        mesh=mesh,
        in_specs=(
            P("rep", "ep", None),
            P("rep", "ep", None),
            P("rep", "ep", None),
            P("rep", "ep", None),
            P(("rep", "ep")),
            P("ep", None),
            P("ep", None),
            P("ep", None),
            P("ep", None),
            P("ep"),
            P("ep"),
            P("ep"),
            P("ep"),
            P("ep", None, None),
            P("ep", None, None),
        ),
        out_specs=(
            P("rep", "ep", None),
            P("rep", "ep", None),
            P("ep", None),
            P("ep", None),
            P("ep", None),
            P("ep", None),
            P("ep"),
            P("ep"),
            P("ep"),
            P("ep"),
            P("ep", "rep", None),
            P("ep", "rep", None),
        ),
        check_vma=False,
    )
```

profile of v0, /device:TPU:0, one launch (start us, length us, event | category | flops | bytes accessed | tf_op | source)
XLA Modules:
  0.0 1802.4 jit_solution(4447141272363571093)
XLA Ops:
  10.7 5.2 all-to-all-start.1
  24.0 9.7 all-gather
  35.4 13.8 all-reduce.13
  49.2 9.2 all-gather.1
  64.2 4.5 reduce-window.6
  69.8 8.1 all-to-all-done
  82.2 8.1 scatter_custom_fusion
  90.3 14.6 scatter_custom_fusion.1
  105.0 8.1 scatter_custom_fusion.2
  115.5 11.5 gather_fusion.2
  127.0 10.1 multiply_convert_fusion
  137.1 5.1 all-to-all-start.7
  142.9 11.9 copy.101
  154.8 12.5 copy.102
  167.3 6.0 multiply_reduce_fusion.9
  183.2 71.8 %all-gather.7.cloned.1.call-done = bf16[2048,2048]{1,0:T(8,128)(2,1)} async-done(((bf16[256,2048]{1,0:T(8,128)(2,1)}), bf16[2048,2048]{1,0:T(8,128)(2,1)}) %all-gather.7.cloned.1.call-update) | async-done | bytes 8388624 | tf_op jit(solution)/shard_map/all_gather | solution.py:99
  255.0 5.9 fusion.30
  263.1 66.4 %all-gather.13.cloned.1.call-done = bf16[2048,2048]{1,0:T(8,128)(2,1)} async-done(((bf16[256,2048]{1,0:T(8,128)(2,1)}), bf16[2048,2048]{1,0:T(8,128)(2,1)}) %all-gather.13.cloned.1.call-update) | async-done | bytes 8388624 | tf_op jit(solution)/shard_map/all_gather | solution.py:100
  329.5 15.4 multiply_reduce_fusion.7
  346.5 9.8 gather_fusion
  356.3 8.0 broadcast_multiply_fusion
  364.3 5.1 all-to-all-start.3
  369.5 9.2 copy.118
  378.7 96.1 %all-to-all-done.3 = bf16[8,2,144,2048]{3,2,1,0:T(8,128)(2,1)} async-done(((bf16[8,2,144,2048]{3,2,1,0:T(8,128)(2,1)}), bf16[8,2,144,2048]{3,2,1,0:T(8,128)(2,1)}, u32[]{:S(2)}, u32[]{:S(2)}) %all-to-all-start.3) | async-done | bytes 9437216 | tf_op jit(solution)/shard_map/all_to_all | solution.py:169
  474.8 9.2 copy.112
  484.0 27.4 %fusion.66 = f32[2,1152,2048]{2,1,0:T(8,128)} fusion(bf16[2,1152,2048]{2,1,0:T(8,128)(2,1)} %bitcast.188, bf16[2,2048,2048]{2,1,0:T(8,128)(2,1)} %param.28), kind=kOutput, calls=%fused_computation.165 | convolution fusion | flops 19327352832 | bytes 45088768 | tf_op jit(solution)/shard_map/erd,edf->erf/dot_general | solution.py:170
  511.4 27.5 %fusion.31 = (f32[2,1152,1024]{2,1,0:T(8,128)}, f32[2,1152,1024]{2,1,0:T(8,128)}, bf16[2,1152,1024]{2,1,0:T(8,128)(2,1)}) fusion(f32[2,1152,2048]{2,1,0:T(8,128)} %fusion.66, bf16[2,1152,2048]{2,1,0:T(8,128)(2,1)} %bitcast.190, bf16[2,1024,2048]{2,1,0:T(8,128)(2,1)} %param.29), kind=kOutput, calls=%fused_computation.95 | convolution fusion | flops 9696706560 | bytes 60293120 | tf_op jit(solution)/shard_map/erd,efd->erf/dot_general | solution.py:189
  538.8 14.6 fusion.4
  553.5 27.9 %copy.113 = bf16[1,2,1152,2048]{3,1,0,2:T(2,128)(2,1)} copy(bf16[1,2,1152,2048]{3,2,1,0:T(8,128)(2,1)S(1)} %fusion.4) | data formatting | bytes 18874368 | tf_op jit(solution)/shard_map/broadcast_in_dim | solution.py:181
  581.4 5.1 all-to-all-start.4
  586.5 27.6 %fusion.5 = bf16[1,2,1152,2048]{3,2,1,0:T(8,128)(2,1)} fusion(bf16[2,2048,2048]{2,1,0:T(8,128)(2,1)} %param.28, f32[2,1152,1024]{2,1,0:T(8,128)} %get-tuple-element.37, f32[2,1152,1024]{2,1,0:T(8,128)} %get-tuple-element.36), kind=kOutput, calls=%fused_computation.22 | convolution fusion | flops 19341508608 | bytes 45088768 | tf_op jit(solution)/shard_map/erf,edf->erd/dot_general | solution.py:199
  614.1 18.2 %copy.119 = bf16[1,2,1152,2048]{3,1,0,2:T(2,128)(2,1)} copy(bf16[1,2,1152,2048]{3,2,1,0:T(8,128)(2,1)} %fusion.5) | data formatting | bytes 18874368 | tf_op jit(solution)/shard_map/broadcast_in_dim | solution.py:211
  632.3 59.5 %all-to-all-done.4 = bf16[1,2,1152,2048]{3,1,0,2:T(2,128)(2,1)} async-done(((bf16[1,2,1152,2048]{3,1,0,2:T(2,128)(2,1)}), bf16[1,2,1152,2048]{3,1,0,2:T(2,128)(2,1)}, u32[]{:S(2)}, u32[]{:S(2)}) %all-to-all-start.4) | async-done | bytes 9437216 | tf_op jit(solution)/shard_map/all_to_all | solution.py:180
  691.8 5.0 all-to-all-start.8
  697.3 11.7 copy.114
  709.0 93.1 %all-to-all-done.8 = bf16[1,2,1152,2048]{3,1,0,2:T(2,128)(2,1)} async-done(((bf16[1,2,1152,2048]{3,1,0,2:T(2,128)(2,1)}), bf16[1,2,1152,2048]{3,1,0,2:T(2,128)(2,1)}, u32[]{:S(2)}, u32[]{:S(2)}) %all-to-all-start.8) | async-done | bytes 9437216 | tf_op jit(solution)/shard_map/all_to_all | solution.py:210
  802.1 11.8 copy.120
  813.9 21.2 %gather_fusion.1 = bf16[2048,2048]{1,0:T(8,128)(2,1)} fusion(bf16[2304,2048]{1,0:T(8,128)(2,1)} %bitcast.178, s32[2048]{0:T(1024)S(1)} %broadcast_clamp_fusion), kind=kCustom, calls=%fused_computation.1 | custom fusion | bytes 16785408 | tf_op jit(solution)/shard_map/gather | solution.py:183
  835.1 21.4 %gather_fusion.3 = bf16[2048,2048]{1,0:T(8,128)(2,1)} fusion(bf16[2304,2048]{1,0:T(8,128)(2,1)} %bitcast.179, s32[2048]{0:T(1024)S(1)} %broadcast_clamp_fusion), kind=kCustom, calls=%fused_computation.3 | custom fusion | bytes 16785408 | tf_op jit(solution)/shard_map/gather | solution.py:214
  856.5 11.4 convert_reduce_fusion
  870.1 12.9 fusion
  888.5 5.8 convolution_convert_fusion.8
  899.6 5.7 convolution_convert_fusion.4
  906.9 7.7 convolution_convert_fusion.3
  916.5 4.4 multiply_reduce_fusion
  931.9 5.7 convolution_convert_fusion.5
  941.5 5.8 convolution_convert_fusion.6
  947.4 17.9 convolution_convert_fusion.7
  965.3 10.8 reduce-scatter.11.cloned.1.call-done
  976.2 74.9 %reduce-scatter.13.cloned.1.call-done = bf16[256,2048]{1,0:T(8,128)(2,1)} async-done(((bf16[2048,2048]{1,0:T(8,128)(2,1)}), bf16[256,2048]{1,0:T(8,128)(2,1)}) %reduce-scatter.13.cloned.1.call-update) | async-done | bytes 1048592 | tf_op jit(solution)/shard_map/reduce_scatter | solution.py:279
  1051.0 75.0 %reduce-scatter.9.cloned.1.call-done = bf16[256,2048]{1,0:T(8,128)(2,1)} async-done(((bf16[2048,2048]{1,0:T(8,128)(2,1)}), bf16[256,2048]{1,0:T(8,128)(2,1)}) %reduce-scatter.9.cloned.1.call-update) | async-done | bytes 1048592 | tf_op jit(solution)/shard_map/reduce_scatter | solution.py:273
  1126.0 75.6 %reduce-scatter.7.cloned.1.call-done = bf16[256,2048]{1,0:T(8,128)(2,1)} async-done(((bf16[2048,2048]{1,0:T(8,128)(2,1)}), bf16[256,2048]{1,0:T(8,128)(2,1)}) %reduce-scatter.7.cloned.1.call-update) | async-done | bytes 1048592 | tf_op jit(solution)/shard_map/reduce_scatter | solution.py:270
  1201.7 29.4 %convolution_convert_fusion = bf16[2,2048,2048]{2,1,0:T(8,128)(2,1)} fusion(bf16[2,1152,2048]{2,1,0:T(8,128)(2,1)} %bitcast.189, f32[2,1152,1024]{2,1,0:T(8,128)} %get-tuple-element.37, f32[2,1152,1024]{2,1,0:T(8,128)} %get-tuple-element.36), kind=kOutput, calls=%fused_computation.13 | convolution fusion | flops 19345178624 | bytes 45088768 | tf_op jit(solution)/shard_map/erd,erf->edf/dot_general | solution.py:196
  1232.3 5.9 fusion.68
  1238.2 6.0 convolution_add_fusion.1
  1249.9 8.0 reduce.8
  1266.4 6.8 reduce.7
  1274.8 5.4 all-to-all-done.9
  1285.0 21.1 %all-reduce.12 = (bf16[2048]{0:T(1024)(128)(2,1)S(1)}, bf16[2048]{0:T(1024)(128)(2,1)S(1)}, bf16[128]{0:T(256)(128)(2,1)S(1)}, bf16[128]{0:T(256)(128)(2,1)S(1)}) all-reduce(bf16[2048]{0:T(1024)(128)(2,1)S(1)} %get-tuple-element.18, bf16[2048]{0:T(1024)(128)(2,1)S(1)} %get-tuple-element.16, ...), channel_id=6, replica_groups=mesh['rep'=4,'ep'=8] {'ep'}, use_global_device_ids=true, to_apply=%region_28.29.clone | all-reduce | flops 4352 | bytes 17408
  1306.5 12.4 all-reduce.14
  1329.6 19.3 %reduce-scatter.17.cloned.1.call-done = bf16[2,256,2048]{2,1,0:T(8,128)(2,1)} async-done(((bf16[2,1024,2048]{2,1,0:T(8,128)(2,1)}), bf16[2,256,2048]{2,1,0:T(8,128)(2,1)}) %reduce-scatter.17.cloned.1.call-update) | async-done | bytes 2097168 | tf_op jit(solution)/shard_map/reduce_scatter | solution.py:206
  1353.0 153.9 %all-reduce.18.cloned.1.call-done = (bf16[256,2048]{1,0:T(8,128)(2,1)}, bf16[256,2048]{1,0:T(8,128)(2,1)}, bf16[256,2048]{1,0:T(8,128)(2,1)}, bf16[256,2048]{1,0:T(8,128)(2,1)}) async-done(((bf16[256,2048]{1,0:T(8,128)(2,1)}, bf16[256,2048]{1,0:T(8,128)(2,1)}, bf16[256,2048]{1,0:T(8,128)(2,1)}, bf16[256,2048]{1,0:T(8,128)(2,1)}), (bf16[256,2048]{1,0:T(8,128)(2,1)}, bf16[256,2048]{1,0:T(8,128)(2,1)}, ...) | async-done | bytes 4194320 | tf_op jit(solution)/shard_map/psum | solution.py:296
  1515.8 273.0 %reduce-scatter.15.cloned.1.call-done = bf16[2,512,2048]{2,1,0:T(8,128)(2,1)} async-done(((bf16[2,2048,2048]{2,1,0:T(8,128)(2,1)}), bf16[2,512,2048]{2,1,0:T(8,128)(2,1)}) %reduce-scatter.15.cloned.1.call-update) | async-done | bytes 4194320 | tf_op jit(solution)/shard_map/reduce_scatter | solution.py:203
  1788.8 6.7 convert_element_type.294
  (306 shorter events, 115.5 us)
Async XLA Ops:
  7.2 26.5 %copy-start.73 = (u32[32]{0:T(128)S(1)}, u32[32]{0:T(128)}, u32[]{:S(2)}) copy-start(u32[32]{0:T(128)} %constant.91) | copy-start | bytes 388
  7.2 10.7 copy-start.53
  7.2 16.7 copy-start.74
  7.2 27.7 %copy-start.75 = (bf16[16]{0:T(256)(128)(2,1)S(1)}, bf16[16]{0:T(256)(128)(2,1)}, u32[]{:S(2)}) copy-start(bf16[16]{0:T(256)(128)(2,1)} %param.26) | copy-start | bytes 100
  7.2 28.0 %copy-start.76 = (bf16[16]{0:T(256)(128)(2,1)S(1)}, bf16[16]{0:T(256)(128)(2,1)}, u32[]{:S(2)}) copy-start(bf16[16]{0:T(256)(128)(2,1)} %param.27) | copy-start | bytes 100
  7.2 42.0 %copy-start.77 = (bf16[256]{0:T(256)(128)(2,1)S(1)}, bf16[256]{0:T(256)(128)(2,1)}, u32[]{:S(2)}) copy-start(bf16[256]{0:T(256)(128)(2,1)} %param.25) | copy-start | bytes 1540
  7.3 135.6 %all-gather.9.cloned.1.call-start = ((), (), s32[]{:S(2)}) async-start(), calls=%async_computation.17 | async-start | bytes 9437184 | tf_op jit(solution)/shard_map/all_gather | solution.py:97
  8.0 146.8 %all-gather.11.cloned.1.call-start = ((), (), s32[]{:S(2)}) async-start(), calls=%async_computation.18 | async-start | bytes 9437184 | tf_op jit(solution)/shard_map/all_gather | solution.py:98
  8.7 246.3 %all-gather.7.cloned.1.call-start = ((), (), s32[]{:S(2)}) async-start(), calls=%async_computation.16 | async-start | bytes 9437184 | tf_op jit(solution)/shard_map/all_gather | solution.py:99
  9.5 320.0 %all-gather.13.cloned.1.call-start = ((), (), s32[]{:S(2)}) async-start(), calls=%async_computation.19 | async-start | bytes 9437184 | tf_op jit(solution)/shard_map/all_gather | solution.py:100
  10.7 9.8 all-to-all-start.1
  17.9 311.6 %copy-start.59 = (f32[256]{0:T(256)}, f32[256]{0:T(256)S(1)}, u32[]{:S(2)}) copy-start(f32[256]{0:T(256)S(1)} %compare_convert_fusion) | copy-start | bytes 3076
  20.6 38.4 %all-to-all-start.2 = ((s32[8,1,256]{2,1,0:T(1,128)}), s32[8,1,256]{2,1,0:T(1,128)S(1)}, u32[]{:S(2)}, u32[]{:S(2)}) async-start(s32[8,1,256]{2,1,0:T(1,128)} %reshape.509), calls=%async_computation.2 | async-start | bytes 16384 | tf_op jit(solution)/shard_map/all_to_all | solution.py:87
  23.9 237.0 %copy-start.67 = (pred[256]{0:T(512)(128)(4,1)}, pred[256]{0:T(512)(128)(4,1)S(1)}, u32[]{:S(2)}) copy-start(pred[256]{0:T(512)(128)(4,1)S(1)} %broadcast_compare_fusion) | copy-start | bytes 772
  33.6 108.9 %copy-start.45 = (f32[8,1,256]{2,1,0:T(1,128)}, f32[8,1,256]{2,1,0:T(1,128)S(1)}, u32[]{:S(2)}) copy-start(f32[8,1,256]{2,1,0:T(1,128)S(1)} %convert_element_type.303) | copy-start | bytes 24580
  49.2 127.7 %copy-start.69 = (f32[128]{0:T(128)}, f32[128]{0:T(128)S(1)}, u32[]{:S(2)}) copy-start(f32[128]{0:T(128)S(1)} %convert_element_type.242) | copy-start | bytes 1540
  49.2 127.6 %copy-start.71 = (f32[128]{0:T(128)}, f32[128]{0:T(128)S(1)}, u32[]{:S(2)}) copy-start(f32[128]{0:T(128)S(1)} %convert_element_type.244) | copy-start | bytes 1540
  58.5 286.5 %copy-start.47 = (f32[8,1,256]{2,1,0:T(1,128)}, f32[8,1,256]{2,1,0:T(1,128)S(1)}, u32[]{:S(2)}) copy-start(f32[8,1,256]{2,1,0:T(1,128)S(1)} %convert_element_type.304) | copy-start | bytes 24580
  58.8 5.3 copy-start.43
  59.0 18.9 %all-to-all-start = ((bf16[8,32,2048]{2,1,0:T(8,128)(2,1)}), bf16[8,32,2048]{2,1,0:T(8,128)(2,1)S(1)}, u32[]{:S(2)}, u32[]{:S(2)}) async-start(bf16[8,32,2048]{2,1,0:T(8,128)(2,1)} %param.15), calls=%async_computation | async-start | bytes 2097152 | tf_op jit(solution)/shard_map/all_to_all | solution.py:80
  77.9 251.6 %copy-start.3 = (bf16[8,32,2048]{2,1,0:T(8,128)(2,1)}, bf16[8,32,2048]{2,1,0:T(8,128)(2,1)S(1)}, u32[]{:S(2)}) copy-start(bf16[8,32,2048]{2,1,0:T(8,128)(2,1)S(1)} %all-to-all-done) | copy-start | bytes 3145732
  77.9 36.2 %all-to-all-start.6 = ((bf16[8,32,2048]{2,1,0:T(8,128)(2,1)}), bf16[8,32,2048]{2,1,0:T(8,128)(2,1)}, u32[]{:S(2)}, u32[]{:S(2)}) async-start(bf16[8,32,2048]{2,1,0:T(8,128)(2,1)} %param.16), calls=%async_computation.6 | async-start | bytes 2097152 | tf_op jit(solution)/shard_map/all_to_all | solution.py:81
  82.2 22.8 %copy-start.54 = (s32[2048,1]{0,1:T(1,128)}, s32[2048,1]{0,1:T(1,128)S(1)}, u32[]{:S(2)}) copy-start(s32[2048,1]{0,1:T(1,128)S(1)} %compare_select_fusion) | copy-start | bytes 24580
  114.1 28.4 %copy-start.61 = (f32[256]{0:T(256)}, f32[256]{0:T(256)S(1)}, u32[]{:S(2)}) copy-start(f32[256]{0:T(256)S(1)} %rsqrt.45) | copy-start | bytes 3076
  137.1 227.2 %all-to-all-start.7 = ((bf16[8,2,144,2048]{3,2,1,0:T(8,128)(2,1)}), bf16[8,2,144,2048]{3,2,1,0:T(8,128)(2,1)}, u32[]{:S(2)}, u32[]{:S(2)}) async-start(bf16[8,2,144,2048]{3,2,1,0:T(8,128)(2,1)} %multiply_convert_fusion), calls=%async_computation.7 | async-start | bytes 18874368 | tf_op jit(solution)/shard_map/all_to_all | solution.py:188
  142.5 31.3 %copy-start.7 = (bf16[8,32,2048]{2,1,0:T(8,128)(2,1)}, bf16[8,32,2048]{2,1,0:T(8,128)(2,1)S(1)}, u32[]{:S(2)}) copy-start(bf16[8,32,2048]{2,1,0:T(8,128)(2,1)S(1)} %fusion.28) | copy-start | bytes 3145732
  167.2 6.6 copy-start.20
  183.2 77.7 %copy-start.41 = (f32[16,256]{1,0:T(8,128)}, f32[16,256]{1,0:T(8,128)S(1)}, u32[]{:S(2)}) copy-start(f32[16,256]{1,0:T(8,128)S(1)} %log_add_fusion) | copy-start | bytes 49156
  255.0 6.9 copy-start.1
  263.1 81.9 %copy-start.21 = (bf16[16,128,256]{2,1,0:T(8,128)(2,1)}, bf16[16,128,256]{2,1,0:T(8,128)(2,1)S(1)}, u32[]{:S(2)}) copy-start(bf16[16,128,256]{2,1,0:T(8,128)(2,1)S(1)} %convolution_convert_fusion.11) | copy-start | bytes 3145732
  344.9 11.4 copy-start.63
  345.0 11.4 copy-start.56
  364.3 110.4 %all-to-all-start.3 = ((bf16[8,2,144,2048]{3,2,1,0:T(8,128)(2,1)}), bf16[8,2,144,2048]{3,2,1,0:T(8,128)(2,1)}, u32[]{:S(2)}, u32[]{:S(2)}) async-start(bf16[8,2,144,2048]{3,2,1,0:T(8,128)(2,1)} %broadcast_multiply_fusion), calls=%async_computation.3 | async-start | bytes 18874368 | tf_op jit(solution)/shard_map/all_to_all | solution.py:169
  581.4 110.4 %all-to-all-start.4 = ((bf16[1,2,1152,2048]{3,1,0,2:T(2,128)(2,1)}), bf16[1,2,1152,2048]{3,1,0,2:T(2,128)(2,1)}, u32[]{:S(2)}, u32[]{:S(2)}) async-start(bf16[1,2,1152,2048]{3,1,0,2:T(2,128)(2,1)} %copy.113), calls=%async_computation.4 | async-start | bytes 18874368 | tf_op jit(solution)/shard_map/all_to_all | solution.py:180
  632.3 64.7 %copy-start.44 = (bf16[8,8,32]{2,1,0:T(8,128)(2,1)S(1)}, bf16[8,8,32]{2,1,0:T(8,128)(2,1)}, u32[]{:S(2)}) copy-start(bf16[8,8,32]{2,1,0:T(8,128)(2,1)} %copy-done.43) | copy-start | bytes 12292
  632.3 64.8 %copy-start.60 = (f32[256]{0:T(256)S(1)}, f32[256]{0:T(256)}, u32[]{:S(2)}) copy-start(f32[256]{0:T(256)} %copy-done.59) | copy-start | bytes 3076
  632.3 65.0 %copy-start.55 = (s32[2048,1]{0,1:T(1,128)S(1)}, s32[2048,1]{0,1:T(1,128)}, u32[]{:S(2)}) copy-start(s32[2048,1]{0,1:T(1,128)} %copy-done.54) | copy-start | bytes 24580
  691.8 110.3 %all-to-all-start.8 = ((bf16[1,2,1152,2048]{3,1,0,2:T(2,128)(2,1)}), bf16[1,2,1152,2048]{3,1,0,2:T(2,128)(2,1)}, u32[]{:S(2)}, u32[]{:S(2)}) async-start(bf16[1,2,1152,2048]{3,1,0,2:T(2,128)(2,1)} %copy.119), calls=%async_computation.8 | async-start | bytes 18874368 | tf_op jit(solution)/shard_map/all_to_all | solution.py:210
  696.8 279.3 %reduce-scatter.11.cloned.1.call-start = ((), (), s32[]{:S(2)}) async-start(), calls=%async_computation.22 | async-start | bytes 9437184 | tf_op jit(solution)/shard_map/reduce_scatter | solution.py:276
  856.5 11.5 copy-start.6
  856.5 11.4 copy-start.48
  856.5 11.4 copy-start.57
  888.5 6.3 copy-start.42
  888.5 6.3 copy-start.68
  894.3 5.3 copy-start.8
  894.8 10.5 copy-start.23
  905.3 145.7 %reduce-scatter.13.cloned.1.call-start = ((), (), s32[]{:S(2)}) async-start(), calls=%async_computation.23 | async-start | bytes 9437184 | tf_op jit(solution)/shard_map/reduce_scatter | solution.py:279
  914.6 211.4 %reduce-scatter.9.cloned.1.call-start = ((), (), s32[]{:S(2)}) async-start(), calls=%async_computation.21 | async-start | bytes 9437184 | tf_op jit(solution)/shard_map/reduce_scatter | solution.py:273
  937.6 264.0 %reduce-scatter.7.cloned.1.call-start = ((), (), s32[]{:S(2)}) async-start(), calls=%async_computation.20 | async-start | bytes 9437184 | tf_op jit(solution)/shard_map/reduce_scatter | solution.py:270
  947.3 401.6 %reduce-scatter.17.cloned.1.call-start = ((), (), s32[]{:S(2)}) async-start(), calls=%async_computation.25 | async-start | bytes 10485760 | tf_op jit(solution)/shard_map/reduce_scatter | solution.py:206
  965.3 541.7 %all-reduce.18.cloned.1.call-start = ((), (), s32[]{:S(2)}) async-start(), calls=%async_computation.26 | async-start | bytes 8388608 | tf_op jit(solution)/shard_map/psum | solution.py:296
  1201.6 587.2 %reduce-scatter.15.cloned.1.call-start = ((), (), s32[]{:S(2)}) async-start(), calls=%async_computation.24 | async-start | bytes 20971520 | tf_op jit(solution)/shard_map/reduce_scatter | solution.py:203
  1232.3 5.9 copy-start.26
  1232.3 12.0 slice-start
  1238.2 6.1 copy-start.4
  1238.2 6.1 copy-start.32
  1238.2 6.1 copy-start.46
  1238.2 6.1 copy-start.62
  1238.2 6.1 slice-start.1
  1249.4 15.4 copy-start.22
  1260.5 19.6 %all-to-all-start.9 = ((bf16[8,2,32768]{2,1,0:T(2,128)(2,1)}), bf16[8,2,32768]{2,1,0:T(2,128)(2,1)}, u32[]{:S(2)}, u32[]{:S(2)}) async-start(bf16[8,2,32768]{2,1,0:T(2,128)(2,1)} %reshape.515), calls=%async_computation.9 | async-start | bytes 2097152 | tf_op jit(solution)/shard_map/all_to_all | solution.py:267
  1280.2 46.8 %all-to-all-start.5 = ((bf16[8,2,32768]{2,1,0:T(2,128)(2,1)}), bf16[8,2,32768]{2,1,0:T(2,128)(2,1)S(1)}, u32[]{:S(2)}, u32[]{:S(2)}) async-start(bf16[8,2,32768]{2,1,0:T(2,128)(2,1)} %reshape.513), calls=%async_computation.5 | async-start | bytes 2097152 | tf_op jit(solution)/shard_map/all_to_all | solution.py:264
  1506.9 5.7 copy-start.30
  1506.9 7.3 copy-start.29
  (37 other events, 71.9 us)
Sparse Core Ops, SparseCore 0:
  9.9 57.3 all-gather.8
  69.2 65.4 all-gather.10
  136.5 118.4 all-gather.6
  256.7 72.6 all-gather.12
  905.4 70.6 reduce-scatter.10
  979.5 71.5 reduce-scatter.12
  1054.5 71.5 reduce-scatter.8
  1130.1 71.4 reduce-scatter.6
  1204.0 144.8 reduce-scatter.16
  1351.3 155.5 all-reduce.17
  1509.3 279.4 reduce-scatter.14
where the time goes:
time: 1810 us; the launch traced here: 1800 us
  waiting for transfers between devices  1090 us (60%)
  local copies, waits for them, and re-layouts  247 us (14%)
  matrix products  231 us (13%)
  other arithmetic  106 us (6%)
  blocking collectives  66.2 us (4%)
  starting transfers between devices  45.7 us (3%)
  between operations  18.4 us (1%)
    reduce_scatter x1, waiting for transfers between devices, shards(): lax.psum_scatter(in_local_grad.astype(jnp.bfloat16), 'rep', scatter_dimen...  273 us
    psum x1, waiting for transfers between devices, shards(): lax.psum(shares[0].astype(jnp.bfloat16), 'rep').astype(jnp.float32)  154 us
    all_to_all x1, waiting for transfers between devices, shards(): lax.all_to_all(outgoing, 'ep', split_axis=0, concat_axis=2, tiled=True)[0]  96.1 us
    all_to_all x1, waiting for transfers between devices, shards(): lax.all_to_all(arrived_back[None], 'ep', split_axis=2, concat_axis=0, til...  93.1 us
    reduce_scatter x1, waiting for transfers between devices, shards(): lax.psum_scatter(query_weight_grad.astype(jnp.bfloat16), 'ep', scatter_di...  75.6 us
    reduce_scatter x1, waiting for transfers between devices, shards(): lax.psum_scatter(key_weight_grad.astype(jnp.bfloat16), 'ep', scatter_dime...  75 us
    reduce_scatter x1, waiting for transfers between devices, shards(): lax.psum_scatter(output_weight_grad.astype(jnp.bfloat16), 'ep', scatter_d...  74.9 us
    all_gather x1, waiting for transfers between devices, shards(): lax.all_gather(value_weight, 'ep', axis=0, tiled=True)  71.8 us
  transfers between devices with their start and end apart: 21, of which 15 were waited for; matrix products, arithmetic and copies ran while one was open for 20% of the time, Pallas kernels for 0%

commit v1 on v0

v1 whole, which is shorter than its diff:
```python
import jax
import jax.numpy as jnp
from jax import lax
from jax.experimental import pallas as pl
from jax.experimental.pallas import tpu as pltpu
from jax.sharding import PartitionSpec as P

HEAD_DIM = 128
EPS = 1e-06
ROPE_BASE = 50000.0
MESH = pl.DeviceIdType.MESH
F32 = jnp.float32
BF16 = jnp.bfloat16


def sds(shape, dtype):
    return jax.ShapeDtypeStruct(shape, dtype)


VM = pl.BlockSpec(memory_space=pltpu.VMEM)
AN = pl.BlockSpec(memory_space=pl.ANY)


def inverse_rms(v):
    return lax.rsqrt(jnp.mean(v * v, axis=-1, keepdims=True) + EPS)


def rms_back(v, r, ug):
    return r * ug - v * (r * r * r * jnp.mean(ug * v, axis=-1, keepdims=True))


def mix_rows(total, tok, living, gain):
    middle = tok.astype(F32) + living * total
    mixed = middle * inverse_rms(middle) * gain
    return middle, mixed.astype(BF16)


def ffn_back_rows(mixed_grad, middle, cot, living, gain):
    r = inverse_rms(middle)
    middle_grad = cot.astype(F32) + rms_back(middle, r, mixed_grad * gain)
    return middle_grad, (living * middle_grad).astype(BF16), mixed_grad * middle * r


def attn_back_rows(normed_grad, tok, middle_grad, gain):
    v = tok.astype(F32)
    r = inverse_rms(v)
    return (middle_grad + rms_back(v, r, normed_grad * gain)).astype(BF16), normed_grad * v * r


class Place:
    def __init__(self):
        me = lax.axis_index("ep")
        core, x, y = lax.rem(me, 2), lax.rem(me // 2, 2), me // 4
        self.rep = lax.axis_index("rep")
        self.me = me
        self.sb = me + 1 - 2 * core
        self.dx = 2 - 4 * x
        self.dy = 4 - 8 * y
        self.xn = me + self.dx
        self.yn = me + self.dy
        self.dg = me + self.dx + self.dy

    def push(self, src, dst, send, recv, dev):
        return pltpu.make_async_remote_copy(
            src_ref=src, dst_ref=dst, send_sem=send, recv_sem=recv, device_id=(self.rep, dev), device_id_type=MESH
        )

    def peers(self):
        sb, dx, dy = self.sb, self.dx, self.dy
        return (self.xn, self.yn, self.dg, sb, sb + dx, sb + dy, sb + dx + dy)

    def greet(self, peers):
        barrier = pltpu.get_barrier_semaphore()
        for peer in peers:
            pl.semaphore_signal(barrier, inc=1, device_id=(self.rep, peer), device_id_type=MESH)
        pl.semaphore_wait(barrier, len(peers))


class Gather:
    sems = 3

    def __init__(self, at, own, full, ssem, rsem, lsem):
        self.at, self.own, self.full, self.ssem, self.rsem, self.lsem = at, own, full, ssem, rsem, lsem
        self.rows = own.shape[1]

    @staticmethod
    def scratch(seqs):
        return [pltpu.SemaphoreType.DMA((7, seqs)), pltpu.SemaphoreType.DMA((8, seqs)), pltpu.SemaphoreType.DMA((seqs,))]

    def block(self, s, dev):
        return self.full.at[s, pl.ds(pl.multiple_of(dev * self.rows, self.rows), self.rows)]

    def copy(self, s, dev, kind, slot, to, src=None):
        block = self.block(s, dev)
        return self.at.push(block if src is None else src, block, self.ssem.at[kind, s], self.rsem.at[slot, s], to)

    def start(self, s):
        at, own = self.at, self.own.at[s]
        self.copy(s, at.me, 0, 2, at.xn, own).start()
        self.copy(s, at.me, 1, 4, at.yn, own).start()
        self.copy(s, at.me, 2, 1, at.sb, own).start()
        pltpu.make_async_copy(own, self.block(s, at.me), self.lsem.at[s]).start()

    def relay(self, s, by_y):
        at = self.at
        self.copy(s, at.xn, 0, 2, at.xn).wait_recv()
        if by_y:
            self.copy(s, at.xn, 3, 6, at.yn).start()
        self.copy(s, at.xn, 4, 3, at.sb).start()
        self.copy(s, at.yn, 1, 4, at.yn).wait_recv()
        if not by_y:
            self.copy(s, at.yn, 3, 6, at.xn).start()
        self.copy(s, at.yn, 5, 5, at.sb).start()

    def relay_far(self, s):
        at = self.at
        self.copy(s, at.dg, 3, 6, at.yn).wait_recv()
        self.copy(s, at.dg, 6, 7, at.sb).start()

    def finish(self, s):
        at = self.at
        for dev, slot in ((at.sb, 1), (at.sb + at.dx, 3), (at.sb + at.dy, 5), (at.sb + at.dx + at.dy, 7)):
            self.copy(s, dev, 0, slot, at.sb).wait_recv()
        for kind in range(7):
            self.copy(s, at.me, kind, 0, at.sb).wait_send()
        pltpu.make_async_copy(self.own.at[s], self.block(s, at.me), self.lsem.at[s]).wait()


def gather_tail(seqs, gather):
    def relay(i, _):
        gather.relay(2 * i, True)
        gather.relay(2 * i + 1, False)
        return 0

    def far(s, _):
        gather.relay_far(s)
        return 0

    def finish(s, _):
        gather.finish(s)
        return 0

    lax.fori_loop(0, seqs // 2, relay, 0)
    lax.fori_loop(0, seqs, far, 0)
    lax.fori_loop(0, seqs, finish, 0)


class Reduce:
    def __init__(self, at, part, held, x1, y1, x2, y2, hs, hr, d1s, d1r, d2s, d2r):
        self.at, self.part, self.held = at, part, held
        self.x1, self.y1, self.x2, self.y2 = x1, y1, x2, y2
        self.hs, self.hr, self.d1s, self.d1r, self.d2s, self.d2r = hs, hr, d1s, d1r, d2s, d2r
        self.half = part.shape[2] // 2

    @staticmethod
    def scratch(part):
        s, _, t, d = part.shape
        dma = pltpu.SemaphoreType.DMA
        return [
            pltpu.VMEM((s, 4, t, d), BF16),
            pltpu.VMEM((s, t // 2, d), BF16),
            pltpu.VMEM((s, t // 2, d), BF16),
            pltpu.VMEM((s, t, d), BF16),
            pltpu.VMEM((s, t, d), BF16),
            dma((4, s)),
            dma((4, s)),
            dma((2, s)),
            dma((2, s)),
            dma((2, s)),
            dma((2, s)),
        ]

    sems = 11

    def core_copy(self, s, k):
        at = self.at
        dest = (at.sb, at.sb + at.dx, at.sb + at.dy, at.sb + at.dx + at.dy)[k]
        return at.push(self.part.at[s, dest], self.held.at[s, k], self.hs.at[k, s], self.hr.at[k, s], at.sb)

    def first(self, s, k):
        at, h = self.at, self.half
        src = self.held.at[s, 3, pl.ds(k * h, h)]
        return at.push(src, (self.x1, self.y1)[k].at[s], self.d1s.at[k, s], self.d1r.at[k, s], (at.xn, at.yn)[k])

    def second(self, s, k):
        at = self.at
        src = self.held.at[s, 1 + k]
        return at.push(src, (self.x2, self.y2)[k].at[s], self.d2s.at[k, s], self.d2r.at[k, s], (at.xn, at.yn)[k])

    def start(self, s):
        for k in (3, 1, 2, 0):
            self.core_copy(s, k).start()

    def hop1(self, s):
        self.core_copy(s, 3).wait_recv()
        self.held[s, 3] = (self.held[s, 3].astype(F32) + self.part[s, self.at.dg].astype(F32)).astype(BF16)
        self.first(s, 0).start()
        self.first(s, 1).start()

    def hop2(self, s):
        h = self.half
        for k, dest, extra, rows, rest in (
            (0, self.at.xn, self.y1, pl.ds(h, h), pl.ds(0, h)),
            (1, self.at.yn, self.x1, pl.ds(0, h), pl.ds(h, h)),
        ):
            self.core_copy(s, 1 + k).wait_recv()
            self.first(s, 1 - k).wait_recv()
            held, part = self.held.at[s, 1 + k], self.part.at[s, dest]
            held[rows] = (held[rows].astype(F32) + part[rows].astype(F32) + extra[s].astype(F32)).astype(BF16)
            held[rest] = (held[rest].astype(F32) + part[rest].astype(F32)).astype(BF16)
            self.second(s, k).start()

    def total(self, s):
        self.core_copy(s, 0).wait_recv()
        self.second(s, 0).wait_recv()
        self.second(s, 1).wait_recv()
        return (
            self.part[s, self.at.me].astype(F32)
            + self.held[s, 0].astype(F32)
            + self.x2[s].astype(F32)
            + self.y2[s].astype(F32)
        )

    def finish(self, s):
        for k in range(4):
            self.core_copy(s, k).wait_send()
        for k in range(2):
            self.first(s, k).wait_send()
            self.second(s, k).wait_send()


def each(n, *steps):
    def run(s, _):
        for step in steps:
            step(s)
        return 0

    lax.fori_loop(0, n, run, 0)


COMM = dict(has_side_effects=True, vmem_limit_bytes=60 << 20)


def front_kernel(tok, wq, wk, wv, pk, full, weights, packets, tok_v, *sems):
    at = Place()
    gather = Gather(at, tok, full, *sems[:3])
    wsend, wrecv, psend, precv, local = sems[3:]
    seqs = tok.shape[0]
    block, width = wq.shape[0], weights.shape[2]
    at.greet(at.peers())
    each(seqs, gather.start)
    mine = pl.ds(pl.multiple_of(at.me * block, block), block)

    def weight_copy(m, j, dev):
        cols = pl.ds(pl.multiple_of(dev * width, width), width)
        return at.push((wq, wk, wv)[j].at[:, cols], weights.at[j, mine], wsend.at[m, j], wrecv.at[m, j], dev)

    def packet_copy(m, dev):
        return at.push(pk, packets.at[at.me], psend.at[m], precv.at[m], dev)

    own_cols = pl.ds(pl.multiple_of(at.me * width, width), width)
    own = [pltpu.make_async_copy(w.at[:, own_cols], weights.at[j, mine], local.at[j]) for j, w in enumerate((wq, wk, wv))]
    own.append(pltpu.make_async_copy(pk, packets.at[at.me], local.at[3]))
    for copy in own:
        copy.start()
    for m, dev in enumerate(at.peers()):
        packet_copy(m, dev).start()
    for m, dev in enumerate(at.peers()):
        for j in range(3):
            weight_copy(m, j, dev).start()
    gather_tail(seqs, gather)
    for m, dev in enumerate(at.peers()):
        packet_copy(m, dev).wait()
        for j in range(3):
            weight_copy(m, j, dev).wait()
    for copy in own:
        copy.wait()


def front(tokens, wq, wk, wv, packet):
    seqs, rows, width = tokens.shape
    ep = lax.axis_size("ep")
    cols = wq.shape[1] // ep
    if ep != 8:
        full = lax.all_gather(tokens, "ep", axis=1, tiled=True)
        weights = [lax.all_to_all(w, "ep", split_axis=1, concat_axis=0, tiled=True) for w in (wq, wk, wv)]
        return full, jnp.stack(weights), lax.all_gather(packet, "ep", axis=0)
    dma = pltpu.SemaphoreType.DMA
    return pl.pallas_call(
        front_kernel,
        out_shape=(
            sds((seqs, rows * ep, width), BF16),
            sds((3, wq.shape[0] * ep, cols), BF16),
            sds((ep,) + packet.shape, F32),
        ),
        in_specs=[VM] * 5,
        out_specs=(AN, AN, AN),
        scratch_shapes=[pltpu.VMEM((8, 128), F32)]
        + Gather.scratch(seqs)
        + [dma((7, 3)), dma((7, 3)), dma((7,)), dma((7,)), dma((4,))],
        compiler_params=pltpu.CompilerParams(collective_id=1, **COMM),
        name="front",
    )(tokens, wq, wk, wv, packet)


def mix_kernel(part, tok, living, gain, middle, full, own, *scratch):
    at = Place()
    seqs = tok.shape[0]
    reduce = Reduce(at, part, *scratch[: Reduce.sems])
    gather = Gather(at, own, full, *scratch[Reduce.sems :])
    at.greet((at.xn, at.yn, at.sb))
    each(seqs, reduce.start)
    each(seqs, reduce.hop1)
    each(seqs, reduce.hop2)

    def rows(s):
        mid, mixed = mix_rows(reduce.total(s), tok[s], living[s], gain[...])
        middle[s] = mid
        own[s] = mixed
        gather.start(s)

    each(seqs, rows)
    gather_tail(seqs, gather)
    each(seqs, reduce.finish)


def mix(part, tokens, living, gain):
    seqs, rows, width = tokens.shape
    ep = lax.axis_size("ep")
    if ep != 8:
        total = lax.psum_scatter(part, "ep", scatter_dimension=1, tiled=True).astype(F32)
        middle, mixed = mix_rows(total, tokens, living, gain)
        return middle, lax.all_gather(mixed, "ep", axis=1, tiled=True)
    part = part.reshape(seqs, ep, rows, width)
    return pl.pallas_call(
        mix_kernel,
        out_shape=(sds(tokens.shape, F32), sds((seqs, rows * ep, width), BF16)),
        in_specs=[VM] * 4,
        out_specs=(VM, AN),
        scratch_shapes=[pltpu.VMEM(tokens.shape, BF16)] + Reduce.scratch(part) + Gather.scratch(seqs),
        compiler_params=pltpu.CompilerParams(collective_id=2, **COMM),
        name="mix",
    )(part, tokens, living, gain)


def back_kernel(gpart, opart, middle, cot, living, gain, result, mgrad, ggrad, full, own, *scratch):
    at = Place()
    seqs = cot.shape[0]
    n = Reduce.sems
    rg = Reduce(at, gpart, *scratch[:n])
    ro = Reduce(at, opart, *scratch[n : 2 * n])
    gather = Gather(at, own, full, *scratch[2 * n :])
    at.greet((at.xn, at.yn, at.sb))
    each(seqs, rg.start)
    each(seqs, ro.start)
    each(seqs, rg.hop1)
    each(seqs, rg.hop2)
    ggrad[...] = jnp.zeros_like(ggrad)

    def rows(s):
        mg, ag, back = ffn_back_rows(rg.total(s), middle[s], cot[s], living[s], gain[...])
        mgrad[s] = mg
        own[s] = ag
        ggrad[...] += jnp.sum(back, axis=0, keepdims=True)
        gather.start(s)

    each(seqs, rows)
    gather_tail(seqs, gather)
    each(seqs, ro.hop1)
    each(seqs, ro.hop2)

    def out(s):
        result[s] = (middle[s] + ro.total(s)).astype(BF16)

    each(seqs, out)
    each(seqs, rg.finish, ro.finish)


def back(gpart, opart, middle, cot, living, gain):
    seqs, rows, width = cot.shape
    ep = lax.axis_size("ep")
    if ep != 8:
        mixed_grad = lax.psum_scatter(gpart, "ep", scatter_dimension=1, tiled=True).astype(F32)
        moe = lax.psum_scatter(opart, "ep", scatter_dimension=1, tiled=True).astype(F32)
        mg, ag, backs = ffn_back_rows(mixed_grad, middle, cot, living, gain)
        full = lax.all_gather(ag, "ep", axis=1, tiled=True)
        return (middle + moe).astype(BF16), mg, jnp.sum(backs, axis=(0, 1))[None], full
    gpart, opart = (p.reshape(seqs, ep, rows, width) for p in (gpart, opart))
    return pl.pallas_call(
        back_kernel,
        out_shape=(
            sds(cot.shape, BF16),
            sds(cot.shape, F32),
            sds((1, width), F32),
            sds((seqs, rows * ep, width), BF16),
        ),
        in_specs=[VM] * 6,
        out_specs=(VM, VM, VM, AN),
        scratch_shapes=[pltpu.VMEM(cot.shape, BF16)] + 2 * Reduce.scratch(gpart) + Gather.scratch(seqs),
        compiler_params=pltpu.CompilerParams(collective_id=3, **COMM),
        name="back",
    )(gpart, opart, middle, cot, living, gain)


def final_kernel(part, wgrad, tok, mgrad, gain, tgrad, ggrad, wrows, *scratch):
    at = Place()
    seqs = tok.shape[0]
    n = Reduce.sems
    reduce = Reduce(at, part, *scratch[:n])
    wsend, wrecv, local = scratch[n:]
    width = wgrad.shape[2]
    block = wrows.shape[1]
    at.greet(at.peers())
    cols = pl.ds(pl.multiple_of(at.me * width, width), width)

    def weight_copy(m, dev):
        rows = pl.ds(pl.multiple_of(dev * block, block), block)
        return at.push(wgrad.at[:, rows], wrows.at[:, :, cols], wsend.at[m], wrecv.at[m], dev)

    mine = pl.ds(pl.multiple_of(at.me * block, block), block)
    own = pltpu.make_async_copy(wgrad.at[:, mine], wrows.at[:, :, cols], local)
    own.start()
    for m, dev in enumerate(at.peers()):
        weight_copy(m, dev).start()
    each(seqs, reduce.start)
    each(seqs, reduce.hop1)
    each(seqs, reduce.hop2)
    ggrad[...] = jnp.zeros_like(ggrad)

    def rows(s):
        tg, back = attn_back_rows(reduce.total(s), tok[s], mgrad[s], gain[...])
        tgrad[s] = tg
        ggrad[...] += jnp.sum(back, axis=0, keepdims=True)

    each(seqs, rows)
    each(seqs, reduce.finish)
    for m, dev in enumerate(at.peers()):
        weight_copy(m, dev).wait()
    own.wait()


def final(part, wgrad, tokens, mgrad, gain):
    seqs, rows, width = tokens.shape
    ep = lax.axis_size("ep")
    if ep != 8:
        normed_grad = lax.psum_scatter(part, "ep", scatter_dimension=1, tiled=True).astype(F32)
        tg, backs = attn_back_rows(normed_grad, tokens, mgrad, gain)
        wrows = lax.all_to_all(wgrad, "ep", split_axis=1, concat_axis=2, tiled=True)
        return tg, jnp.sum(backs, axis=(0, 1))[None], wrows
    part = part.reshape(seqs, ep, rows, width)
    dma = pltpu.SemaphoreType.DMA
    return pl.pallas_call(
        final_kernel,
        out_shape=(
            sds(tokens.shape, BF16),
            sds((1, width), F32),
            sds((3, wgrad.shape[1] // ep, wgrad.shape[2] * ep), BF16),
        ),
        in_specs=[VM] * 5,
        out_specs=(VM, VM, AN),
        scratch_shapes=Reduce.scratch(part) + [dma((7,)), dma((7,)), dma],
        compiler_params=pltpu.CompilerParams(collective_id=4, **COMM),
        name="final",
    )(part, wgrad, tokens, mgrad, gain)


def dot(a, b, ca, cb):
    return lax.dot_general(a, b, (((ca,), (cb,)), ((), ())), preferred_element_type=F32)


def rope(v, cos, sin_turn):
    return v * cos + pltpu.roll(v, HEAD_DIM // 2, 1) * sin_turn


def probabilities(q, k, length):
    scores = dot(q, k, 1, 1) * HEAD_DIM**-0.5
    column = lax.broadcasted_iota(jnp.int32, scores.shape, 1)
    scores = jnp.where(column < length, scores, -1e9)
    p = jnp.exp(scores - jnp.max(scores, axis=-1, keepdims=True))
    return p * (1.0 / jnp.sum(p, axis=-1, keepdims=True))


def attend_kernel(lens, tok, w, wo, gain, qg, kg, cos, sin, normed, pre, low, ctx, part):
    length = lens[pl.program_id(0)]
    v = tok[0].astype(F32)
    x = (v * inverse_rms(v) * gain[...]).astype(BF16)
    normed[0] = x
    q_pre, k_pre = dot(x, w[0], 1, 0), dot(x, w[1], 1, 0)
    value = dot(x, w[2], 1, 0).astype(BF16)
    pre[0, 0], pre[1, 0] = q_pre, k_pre
    low[2, 0] = value
    for h in range(q_pre.shape[1] // HEAD_DIM):
        cols = slice(h * HEAD_DIM, (h + 1) * HEAD_DIM)
        rot = []
        for i, (u, g) in enumerate(((q_pre[:, cols], qg[...]), (k_pre[:, cols], kg[...]))):
            rot.append(rope(u * inverse_rms(u) * g, cos[...], sin[...]).astype(BF16))
            low[i, 0, :, cols] = rot[i]
        attention = probabilities(rot[0], rot[1], length).astype(BF16)
        ctx[0, :, cols] = dot(attention, value[:, cols], 1, 0).astype(BF16)
    part[0] = dot(ctx[0], wo[...], 1, 0).astype(BF16)


def attend(full, weights, wo, gain, qg, kg, cos, sin, lens):
    seqs, length, width = full.shape
    cols = weights.shape[2]
    row = lambda i, *_: (i, 0, 0)
    row2 = lambda i, *_: (0, i, 0, 0)
    two = lambda i, *_: (0, 0)
    return pl.pallas_call(
        attend_kernel,
        out_shape=(
            sds(full.shape, BF16),
            sds((2, seqs, length, cols), F32),
            sds((3, seqs, length, cols), BF16),
            sds((seqs, length, cols), BF16),
            sds(full.shape, BF16),
        ),
        grid_spec=pltpu.PrefetchScalarGridSpec(
            num_scalar_prefetch=1,
            grid=(seqs,),
            in_specs=[
                pl.BlockSpec((1, length, width), row),
                pl.BlockSpec(weights.shape, lambda i, *_: (0, 0, 0)),
                pl.BlockSpec(wo.shape, two),
                pl.BlockSpec((1, width), two),
                pl.BlockSpec((1, HEAD_DIM), two),
                pl.BlockSpec((1, HEAD_DIM), two),
                pl.BlockSpec((length, HEAD_DIM), two),
                pl.BlockSpec((length, HEAD_DIM), two),
            ],
            out_specs=(
                pl.BlockSpec((1, length, width), row),
                pl.BlockSpec((2, 1, length, cols), row2),
                pl.BlockSpec((3, 1, length, cols), row2),
                pl.BlockSpec((1, length, cols), row),
                pl.BlockSpec((1, length, width), row),
            ),
        ),
        compiler_params=pltpu.CompilerParams(dimension_semantics=("arbitrary",), vmem_limit_bytes=60 << 20),
        cost_estimate=pl.CostEstimate(flops=10**10, bytes_accessed=4 * 10**7, transcendentals=10**6),
        name="attend",
    )(lens, full, weights, wo, gain, qg, kg, cos, sin)


def attend_back_kernel(
    lens, agrad, normed, pre, low, ctx, w, wo, qg, kg, cos, sin, part, wgrad, wograd, gains, wacc, woacc
):
    s = pl.program_id(0)
    length = lens[s]

    @pl.when(s == 0)
    def _():
        wacc[...] = jnp.zeros_like(wacc)
        woacc[...] = jnp.zeros_like(woacc)
        gains[...] = jnp.zeros_like(gains)

    ag = agrad[0]
    woacc[...] += dot(ctx[0], ag, 0, 0)
    cg_all = dot(ag, wo[...], 1, 1).astype(BF16)
    scale = HEAD_DIM**-0.5
    half = HEAD_DIM // 2
    grads = ([], [], [])
    for h in range(cg_all.shape[1] // HEAD_DIM):
        cols = slice(h * HEAD_DIM, (h + 1) * HEAD_DIM)
        q, k, value, cg = low[0, 0, :, cols], low[1, 0, :, cols], low[2, 0, :, cols], cg_all[:, cols]
        attention = probabilities(q, k, length)
        grads[2].append(dot(attention.astype(BF16), cg, 0, 0).astype(BF16))
        pg = dot(cg, value, 1, 1)
        sg = (attention * (pg - jnp.sum(attention * pg, axis=-1, keepdims=True))).astype(BF16)
        for i, (rot_grad, g) in enumerate(((dot(sg, k, 1, 0), qg[...]), (dot(sg, q, 0, 0), kg[...]))):
            wgt = rot_grad * scale
            u = wgt * cos[...] + pltpu.roll(wgt * sin[...], half, 1)
            v = pre[i, 0, :, cols]
            r = inverse_rms(v)
            grads[i].append(rms_back(v, r, u * g).astype(BF16))
            gains[i : i + 1] += jnp.sum(u * v * r, axis=0, keepdims=True)
    total = None
    for i in range(3):
        g = grads[i][0] if len(grads[i]) == 1 else jnp.concatenate(grads[i], axis=1)
        wacc[i] += dot(normed[0], g, 0, 0)
        piece = dot(g, w[i], 1, 1)
        total = piece if total is None else total + piece
    part[0] = total.astype(BF16)

    @pl.when(s == pl.num_programs(0) - 1)
    def _():
        wgrad[...] = wacc[...].astype(BF16)
        wograd[...] = woacc[...].astype(BF16)


def attend_back(agrad, normed, pre, low, ctx, weights, wo, qg, kg, cos, sin, lens):
    seqs, length, width = agrad.shape
    cols = weights.shape[2]
    row = lambda i, *_: (i, 0, 0)
    row2 = lambda i, *_: (0, i, 0, 0)
    two = lambda i, *_: (0, 0)
    three = lambda i, *_: (0, 0, 0)
    return pl.pallas_call(
        attend_back_kernel,
        out_shape=(
            sds(agrad.shape, BF16),
            sds(weights.shape, BF16),
            sds(wo.shape, BF16),
            sds((8, HEAD_DIM), F32),
        ),
        grid_spec=pltpu.PrefetchScalarGridSpec(
            num_scalar_prefetch=1,
            grid=(seqs,),
            in_specs=[
                pl.BlockSpec((1, length, width), row),
                pl.BlockSpec((1, length, width), row),
                pl.BlockSpec((2, 1, length, cols), row2),
                pl.BlockSpec((3, 1, length, cols), row2),
                pl.BlockSpec((1, length, cols), row),
                pl.BlockSpec(weights.shape, three),
                pl.BlockSpec(wo.shape, two),
                pl.BlockSpec((1, HEAD_DIM), two),
                pl.BlockSpec((1, HEAD_DIM), two),
                pl.BlockSpec((length, HEAD_DIM), two),
                pl.BlockSpec((length, HEAD_DIM), two),
            ],
            out_specs=(
                pl.BlockSpec((1, length, width), row),
                pl.BlockSpec(weights.shape, three),
                pl.BlockSpec(wo.shape, two),
                pl.BlockSpec((8, HEAD_DIM), two),
            ),
            scratch_shapes=[pltpu.VMEM(weights.shape, F32), pltpu.VMEM(wo.shape, F32)],
        ),
        compiler_params=pltpu.CompilerParams(dimension_semantics=("arbitrary",), vmem_limit_bytes=60 << 20),
        cost_estimate=pl.CostEstimate(flops=2 * 10**10, bytes_accessed=4 * 10**7, transcendentals=10**6),
        name="attend_back",
    )(lens, agrad, normed, pre, low, ctx, weights, wo, qg, kg, cos, sin)


def shards(
    tokens, cotangent, gate_weights, expert_ids, seq_lengths, query_weight, key_weight, value_weight,
    output_weight, attn_gain, ffn_gain, query_gain, key_gain, expert_in, expert_out,
):
    ep = lax.axis_size("ep")
    me = lax.axis_index("ep")
    seqs, rows, width = tokens.shape
    length = rows * ep
    top = gate_weights.shape[2]
    local = expert_in.shape[0]
    hidden = expert_out.shape[1]
    experts = local * ep
    capacity = length * top * 9 // (8 * experts)

    pairs = jnp.concatenate(
        [expert_ids.astype(F32).transpose(0, 2, 1), gate_weights.astype(F32).transpose(0, 2, 1)], axis=1
    ).reshape(-1, 128)
    gains = jnp.concatenate([attn_gain, ffn_gain]).astype(F32).reshape(-1, 128)
    few = jnp.concatenate([query_gain.astype(F32), key_gain.astype(F32), seq_lengths.astype(F32)])
    few = jnp.pad(few, (0, 128 - few.shape[0]))[None]
    packet = jnp.concatenate([pairs, gains, few], axis=0)
    packet = jnp.pad(packet, ((0, -packet.shape[0] % 8), (0, 0)))

    full, weights, packets = front(tokens, query_weight, key_weight, value_weight, packet)
    cot_full = lax.all_gather(cotangent, "ep", axis=1, tiled=True)

    n = pairs.shape[0]
    g = gains.shape[0] // 2
    gain_attn = packets[:, n : n + g].reshape(1, width)
    gain_ffn = packets[:, n + g : n + 2 * g].reshape(1, width)
    q = query_gain.shape[0]
    gain_query = packets[:, n + 2 * g, :q].reshape(1, HEAD_DIM)
    gain_key = packets[:, n + 2 * g, q : 2 * q].reshape(1, HEAD_DIM)
    lens = packets[:, n + 2 * g, 2 * q].astype(jnp.int32)
    table = packets[:, :n].reshape(ep, seqs, 2 * top, rows).transpose(1, 2, 0, 3).reshape(seqs, 2 * top, length)
    positions = jnp.arange(length, dtype=jnp.int32)
    live = (positions[None] < lens[:, None]).astype(F32)
    living = lax.dynamic_slice_in_dim(live, me * rows, rows, axis=1)[..., None]

    half = HEAD_DIM // 2
    frequency = ROPE_BASE ** (-(jnp.arange(half, dtype=F32) * (2.0 / HEAD_DIM)))
    angles = positions.astype(F32)[:, None] * frequency[None, :]
    cos = jnp.concatenate([jnp.cos(angles)] * 2, axis=-1)
    sin = jnp.concatenate([-jnp.sin(angles), jnp.sin(angles)], axis=-1)

    normed, pre, low, ctx, part = attend(
        full, weights, output_weight, gain_attn, gain_query, gain_key, cos, sin, lens
    )
    middle, mixed = mix(part, tokens, living, gain_ffn)

    mine = (me * local + jnp.arange(local)).astype(F32)
    chosen = (table[None, :, :top] == mine[:, None, None, None]).astype(F32)
    hit = jnp.sum(chosen, axis=2) * live[None]
    weight = jnp.sum(chosen * table[None, :, top:], axis=2) * live[None]
    before = (positions[:, None] < positions[None, :]).astype(BF16)
    rank = jnp.dot(hit.astype(BF16), before, preferred_element_type=F32)
    slot = jnp.where(hit > 0.5, rank, -1.0)
    place = slot[:, :, None, :] == jnp.arange(capacity, dtype=F32)[None, None, :, None]
    pick = place.astype(BF16)
    weighted = jnp.where(place, weight[:, :, None, :], 0.0).astype(BF16)

    def ein(spec, a, b):
        return jnp.einsum(spec, a, b, preferred_element_type=F32)

    slots = seqs * capacity
    arrived = ein("jsrt,std->jsrd", pick, mixed).astype(BF16).reshape(local, slots, width)
    arrived_grad = ein("jsrt,std->jsrd", weighted, cot_full).astype(BF16).reshape(local, slots, width)
    in_grads, out_grads, acts, dgus = [], [], [], []
    token = None
    for j in range(local):
        x, dy = arrived[j], arrived_grad[j]
        if token is not None:
            x, dy, _ = lax.optimization_barrier((x, dy, token))
        gate_up = jnp.dot(x, expert_in[j], preferred_element_type=F32)
        dact = dot(dy, expert_out[j], 1, 1)
        gate, up = gate_up[:, :hidden], gate_up[:, hidden:]
        sig = jax.nn.sigmoid(gate)
        act = (gate * sig * up).astype(BF16)
        dgu = jnp.concatenate(
            [dact * up * sig * (1.0 + gate * (1.0 - sig)), dact * gate * sig], axis=1
        ).astype(BF16)
        out_grad = dot(act, dy, 0, 0).astype(BF16)
        in_grad = dot(x, dgu, 0, 0).astype(BF16)
        out_grad, in_grad, act, dgu = lax.optimization_barrier((out_grad, in_grad, act, dgu))
        token = act
        out_grads.append(lax.psum_scatter(out_grad, "rep", scatter_dimension=0, tiled=True))
        in_grads.append(lax.psum_scatter(in_grad, "rep", scatter_dimension=0, tiled=True))
        acts.append(act)
        dgus.append(dgu)
    out_parts = [jnp.dot(a, expert_out[j], preferred_element_type=F32).astype(BF16) for j, a in enumerate(acts)]
    grad_parts = [dot(d, expert_in[j], 1, 1).astype(BF16) for j, d in enumerate(dgus)]
    stack = lambda parts: jnp.stack(parts).reshape(local, seqs, capacity, width)
    grad_part = ein("jsrt,jsrd->std", pick, stack(grad_parts)).astype(BF16)
    out_part = ein("jsrt,jsrd->std", weighted, stack(out_parts)).astype(BF16)

    result, mgrad, ffn_back, agrad = back(grad_part, out_part, middle, cotangent, living, gain_ffn)
    npart, wgrad, wograd, qk_back = attend_back(
        agrad, normed, pre, low, ctx, weights, output_weight, gain_query, gain_key, cos, sin, lens
    )
    token_grad, attn_back, wrows = final(npart, wgrad, tokens, mgrad, gain_attn)
    sums = lax.psum((wrows, wograd), "rep")
    small = jnp.concatenate([attn_back[0], ffn_back[0], qk_back[0], qk_back[1]])
    small = lax.psum(small, ("rep", "ep"))

    def share(vector):
        return lax.dynamic_slice_in_dim(vector, me * (vector.shape[0] // ep), vector.shape[0] // ep)

    return (
        result,
        token_grad,
        sums[0][0].astype(F32),
        sums[0][1].astype(F32),
        sums[0][2].astype(F32),
        sums[1].astype(F32),
        share(small[:width]),
        share(small[width : 2 * width]),
        share(small[2 * width : 2 * width + HEAD_DIM]),
        share(small[2 * width + HEAD_DIM :]),
        jnp.stack(in_grads).astype(F32),
        jnp.stack(out_grads).astype(F32),
    )


def solution(mesh):
    seq = P("rep", "ep", None)
    row, gain, expert = P("ep", None), P("ep"), P("ep", None, None)
    split = P("ep", "rep", None)

    return jax.shard_map(
        shards,
        mesh=mesh,
        in_specs=(seq, seq, seq, seq, P(("rep", "ep")), row, row, row, row, gain, gain, gain, gain, expert, expert),
        out_specs=(seq, seq, row, row, row, row, gain, gain, gain, gain, split, split),
        check_vma=False,
    )
```

time: 1810 us -> 1330 us (0.73)
  waiting for transfers between devices: 1090 us -> 550 us
  Pallas kernels: 0 us -> 466 us
  local copies, waits for them, and re-layouts: 247 us -> 28.9 us
  other arithmetic: 106 us -> 32 us
  matrix products: 231 us -> 182 us
  starting transfers between devices: 45.7 us -> 0.23 us
  blocking collectives: 66.2 us -> 45.8 us
    pallas_call x0 -> x6, Pallas kernels: none -> 466 us  [the longest x1 122 us: back(): pl.pallas_call(back_kernel, out_shape=(sds(cot.shape, BF16), sds(cot.shap...]
    all_to_all x10 -> x0, waiting for transfers between devices: 264 us -> none  [the longest x1 96.1 us: shards(): lax.all_to_all(outgoing, 'ep', split_axis=0, concat_axis=2, tiled=True)[0]]
    all_gather x4 -> x1, waiting for transfers between devices: 138 us -> 0.01 us  [shards(): cot_full = lax.all_gather(cotangent, 'ep', axis=1, tiled=True)]
    reduce_scatter x6 -> x4, waiting for transfers between devices: 529 us -> 443 us  [the longest x2 291 us: shards(): lax.psum_scatter(in_grad, 'rep', scatter_dimension=0, tiled=True)]
    gather x4 -> x0, local copies, waits for them, and re-layouts: 63.9 us -> none  [the longest x1 21.4 us: shards(): returned_grad[destination].reshape(length, top_count, model_width)]
    psum x1, waiting for transfers between devices: 154 us -> 105 us  [shards(): sums = lax.psum((wrows, wograd), 'rep')]
    dot_general x24 -> x17, matrix products: 231 us -> 182 us  [the longest x8 99.2 us: dot(): lax.dot_general(a, b, (((ca,), (cb,)), ((), ())), preferred_element_type=...]
    broadcast_in_dim x5 -> x2, local copies, waits for them, and re-layouts: 49.4 us -> 0.86 us  [shards(): living = lax.dynamic_slice_in_dim(live, me * rows, rows, axis=1)[..., None]]
  transfers between devices with their start and end apart: 21 -> 6, of which waited for: 15 -> 5; matrix products, arithmetic and copies ran while one was open for 20% -> 4% of each run, Pallas kernels for 0% -> 17%
where the time goes in v1:
time: 1330 us; the launch traced here: 1320 us
  waiting for transfers between devices  550 us (41%)
  Pallas kernels  466 us (35%)
  matrix products  182 us (14%)
  blocking collectives  45.8 us (3%)
  other arithmetic  32 us (2%)
  local copies, waits for them, and re-layouts  28.9 us (2%)
  between operations  15.3 us (1%)
    reduce_scatter x2, waiting for transfers between devices, shards(): lax.psum_scatter(in_grad, 'rep', scatter_dimension=0, tiled=True)  291 us
    reduce_scatter x2, waiting for transfers between devices, shards(): lax.psum_scatter(out_grad, 'rep', scatter_dimension=0, tiled=True)  152 us
    pallas_call x1, Pallas kernels, back(): pl.pallas_call(back_kernel, out_shape=(sds(cot.shape, BF16), sds(cot.shap...  122 us
    pallas_call x1, Pallas kernels, front(): pl.pallas_call(front_kernel, out_shape=(sds((seqs, rows * ep, width), BF1...  114 us
    psum x1, waiting for transfers between devices, shards(): sums = lax.psum((wrows, wograd), 'rep')  105 us
    dot_general x8, matrix products, dot(): lax.dot_general(a, b, (((ca,), (cb,)), ((), ())), preferred_element_type=...  99.2 us
    pallas_call x1, Pallas kernels, mix(): pl.pallas_call(mix_kernel, out_shape=(sds(tokens.shape, F32), sds((seqs,...  80.8 us
    pallas_call x1, Pallas kernels, final(): pl.pallas_call(final_kernel, out_shape=(sds(tokens.shape, BF16), sds((1,...  78.5 us
  transfers between devices with their start and end apart: 6, of which 5 were waited for; matrix products, arithmetic and copies ran while one was open for 4% of the time, Pallas kernels for 17%

profile of v1, /device:TPU:0, one launch (start us, length us, event | category | flops | bytes accessed | tf_op | source)
XLA Modules:
  0.0 1320.8 jit_solution(13900811918196471315)
XLA Ops:
  7.2 0.7 all-gather.2.cloned.1.call-update
  8.6 0.7 convert_element_type.143
  9.3 0.7 convert_element_type.144
  9.9 0.7 convert_bitcast_fusion.2
  10.6 0.8 convert_bitcast_fusion.3
  11.6 0.7 maximum_convert_fusion.2
  12.3 0.6 select_maximum_fusion.pk
  12.9 113.9 %front.1 = (bf16[8,256,2048]{2,1,0:T(8,128)(2,1)}, bf16[3,2048,256]{2,1,0:T(8,128)(2,1)}, f32[8,40,128]{2,1,0:T(8,128)}) custom-call(bf16[8,32,2048]{2,1,0:T(8,128)(2,1)} %tok.5, bf16[256,2048]{1,0:T(8,128)(2,1)} %wq.1, bf16[256,2048]{1,0:T(8,128)(2,1)} %wk.1, bf16[256,2048]{1,0:T(8,128)(2,1)} %wv.1, f32[40,128]{1,0:T(8,128)} %select_maximum_fusion.pk), custom_call_target="tpu_custom_call" | custom-call | tf_op jit(solution)/shard_map/front/pallas_call | solution.py:289
  126.8 0.9 slice.95
  127.7 0.9 slice_reduce_fusion
  128.6 0.6 reshape_squeeze.7.kg
  129.2 0.6 reshape_squeeze.6.qg
  129.8 1.1 convert_reduce_fusion.lens
  131.0 0.8 copy.52.living
  132.9 0.5 fusion.63
  133.5 0.8 pad_maximum_fusion.2
  134.3 1.4 fusion.73
  135.7 25.5 %attend.1 = (bf16[8,256,2048]{2,1,0:T(8,128)(2,1)}, f32[2,8,256,256]{3,2,1,0:T(8,128)}, bf16[3,8,256,256]{3,2,1,0:T(8,128)(2,1)}, bf16[8,256,256]{2,1,0:T(8,128)(2,1)}, bf16[8,256,2048]{2,1,0:T(8,128)(2,1)}) custom-call(s32[8]{0:T(128)} %copy-done.13, bf16[8,256,2048]{2,1,0:T(8,128)(2,1)} %get-tuple-element.44.tok, ...), custom_call_target="tpu_custom_call" | custom-call | flops 10000000000 | bytes 40000000 | tf_op jit(solution)/shard_map/attend/pallas_call | solution.py:509
  161.2 80.8 %mix.1 = (f32[8,32,2048]{2,1,0:T(8,128)}, bf16[8,256,2048]{2,1,0:T(8,128)(2,1)}) custom-call(bf16[8,8,32,2048]{3,2,1,0:T(8,128)(2,1)} %bitcast.134, bf16[8,32,2048]{2,1,0:T(8,128)(2,1)} %tok.5, f32[8,32,1]{2,1,0:T(8,128)} %copy.52.living, f32[1,2048]{1,0:T(1,128)} %bitcast.154), custom_call_target="tpu_custom_call" | custom-call | tf_op jit(solution)/shard_map/mix/pallas_call | solution.py:335
  242.0 8.4 convert_bitcast_fusion.1
  250.4 7.5 fusion.72
  257.9 2.1 copy-done
  260.0 14.7 %fusion.18 = f32[1152,2048]{1,0:T(8,128)} fusion(bf16[1152,2048]{1,0:T(8,128)(2,1)S(1)} %bitcast.145, bf16[2,2048,2048]{2,1,0:T(8,128)(2,1)} %param.28), kind=kOutput, calls=%fused_computation.22 | convolution fusion | flops 9663676416 | bytes 22544384 | tf_op jit(solution)/shard_map/dot_general | solution.py:709
  274.7 6.7 convert_bitcast_fusion
  281.4 5.0 fusion.71
  286.3 13.4 %multiply_convert_fusion.4 = (bf16[1152,1024]{1,0:T(8,128)(2,1)S(1)}, bf16[1152,1024]{1,0:T(8,128)(2,1)S(1)}, bf16[1152,1024]{1,0:T(8,128)(2,1)}) fusion(f32[1152,2048]{1,0:T(8,128)} %fusion.18, bf16[1152,2048]{1,0:T(8,128)(2,1)} %bitcast.147, bf16[2,1024,2048]{2,1,0:T(8,128)(2,1)} %param.29), kind=kOutput, calls=%fused_computation.41 | convolution fusion | flops 4850712576 | bytes 25427968 | tf_op jit(solution)/shard_map/dot_general | solution.py:468
  299.8 1.4 copy-done.3
  301.2 15.7 %convolution_convert_fusion.3 = bf16[2048,2048]{1,0:T(8,128)(2,1)} fusion(bf16[1152,2048]{1,0:T(8,128)(2,1)} %bitcast.146, bf16[1152,1024]{1,0:T(8,128)(2,1)S(1)} %get-tuple-element.83, bf16[1152,1024]{1,0:T(8,128)(2,1)S(1)} %get-tuple-element.82), kind=kOutput, calls=%fused_computation.27 | convolution fusion | flops 9677307904 | bytes 17825792 | tf_op jit(solution)/shard_map/dot_general | solution.py:468
  317.0 4.6 pad_maximum_fusion
  321.6 7.4 convolution_convert_fusion.5
  328.9 9.2 convolution_convert_fusion.1
  338.1 14.7 %fusion.14 = f32[1152,2048]{1,0:T(8,128)} fusion(bf16[1152,2048]{1,0:T(8,128)(2,1)S(1)} %bitcast.137, bf16[2,2048,2048]{2,1,0:T(8,128)(2,1)} %param.28), kind=kOutput, calls=%fused_computation.18 | convolution fusion | flops 9663676416 | bytes 22544384 | tf_op jit(solution)/shard_map/dot_general | solution.py:709
  352.9 10.8 multiply_convert_fusion.1
  363.7 1.5 copy-done.4
  365.2 13.6 %convolution_convert_fusion.2 = bf16[2048,2048]{1,0:T(8,128)(2,1)} fusion(bf16[1152,2048]{1,0:T(8,128)(2,1)S(1)} %bitcast.138, bf16[1152,1024]{1,0:T(8,128)(2,1)S(1)} %get-tuple-element.81, bf16[1152,1024]{1,0:T(8,128)(2,1)S(1)} %get-tuple-element.80), kind=kOutput, calls=%fused_computation.26 | convolution fusion | flops 9677307904 | bytes 17825792 | tf_op jit(solution)/shard_map/dot_general | solution.py:468
  378.8 4.6 pad_maximum_fusion.1
  383.4 15.4 %fusion.20 = bf16[1152,2048]{1,0:T(8,128)(2,1)} fusion(bf16[1152,2048]{1,0:T(8,128)(2,1)} %pad_maximum_fusion, bf16[2,2048,2048]{2,1,0:T(8,128)(2,1)} %param.28), kind=kOutput, calls=%fused_computation.28 | convolution fusion | flops 9666035712 | bytes 17825792 | tf_op jit(solution)/shard_map/dot_general | solution.py:468
  398.9 7.4 convolution_convert_fusion.4
  406.3 15.4 %fusion.23 = bf16[1152,2048]{1,0:T(8,128)(2,1)} fusion(bf16[1152,2048]{1,0:T(8,128)(2,1)} %pad_maximum_fusion.1, bf16[2,2048,2048]{2,1,0:T(8,128)(2,1)} %param.28), kind=kOutput, calls=%fused_computation.29 | convolution fusion | flops 9666035712 | bytes 17825792 | tf_op jit(solution)/shard_map/dot_general | solution.py:468
  421.7 9.2 convolution_convert_fusion
  430.9 11.7 bitcast_convert_fusion.1
  442.6 8.4 bitcast_convert_fusion
  451.1 121.7 %back.1 = (bf16[8,32,2048]{2,1,0:T(8,128)(2,1)}, f32[8,32,2048]{2,1,0:T(8,128)}, f32[1,2048]{1,0:T(1,128)}, bf16[8,256,2048]{2,1,0:T(8,128)(2,1)}) custom-call(bf16[8,8,32,2048]{3,2,1,0:T(8,128)(2,1)} %bitcast.132, bf16[8,8,32,2048]{3,2,1,0:T(8,128)(2,1)} %bitcast.133, f32[8,32,2048]{2,1,0:T(8,128)} %get-tuple-element.54.middle, bf16[8,32,2048]{2,1,0:T(8,128)(2,1)} %cot.1, ...), custom_call_target="tpu_custom_call" | custom-call | tf_op jit(solution)/shard_map/back/pallas_call | solution.py:389
  572.8 45.4 %attend_back.1 = (bf16[8,256,2048]{2,1,0:T(8,128)(2,1)}, bf16[3,2048,256]{2,1,0:T(8,128)(2,1)}, bf16[256,2048]{1,0:T(8,128)(2,1)}, f32[8,128]{1,0:T(8,128)}) custom-call(s32[8]{0:T(128)} %copy-done.13, bf16[8,256,2048]{2,1,0:T(8,128)(2,1)} %get-tuple-element.56.agrad, bf16[8,256,2048]{2,1,0:T(8,128)(2,1)} %get-tuple-element.57.normed, ...), custom_call_target="tpu_custom_call" | custom-call | flops 20000000000 | bytes 40000000 | tf_op jit(solution)/shard_map/attend_back/pallas_call | solution.py:598
  618.2 78.5 %final.1 = (bf16[8,32,2048]{2,1,0:T(8,128)(2,1)}, f32[1,2048]{1,0:T(1,128)}, bf16[3,256,2048]{2,1,0:T(8,128)(2,1)}) custom-call(bf16[8,8,32,2048]{3,2,1,0:T(8,128)(2,1)} %bitcast.131, bf16[3,2048,256]{2,1,0:T(8,128)(2,1)} %get-tuple-element.62.wgrad, bf16[8,32,2048]{2,1,0:T(8,128)(2,1)} %tok.5, f32[8,32,2048]{2,1,0:T(8,128)} %get-tuple-element.63.mgrad, ...), custom_call_target="tpu_custom_call" | custom-call | tf_op jit(solution)/shard_map/final/pallas_call | solution.py:452
  696.8 0.7 reduce-scatter.9.cloned.1.call-update
  698.1 0.5 reduce-scatter.5.cloned.1.call-update
  699.2 0.8 slice_bitcast_fusion.4
  700.0 45.8 %psum.23 = f32[4352]{0:T(1024)S(1)} all-reduce(f32[4352]{0:T(1024)S(1)} %pad_maximum_fusion.5), channel_id=1, replica_groups=mesh['rep'=4,'ep'=8] {'rep','ep'}, use_global_device_ids=true, to_apply=%region_4.5 | all-reduce | flops 4352 | bytes 34816 | tf_op jit(solution)/shard_map/psum | solution.py:738
  745.8 0.6 dynamic_slice.17
  746.4 0.6 dynamic_slice.16
  747.1 0.6 dynamic_slice.19
  747.7 0.6 dynamic_slice.18
  748.3 104.8 %all-reduce.5.cloned.1.call-done = (bf16[3,256,2048]{2,1,0:T(8,128)(2,1)}, bf16[256,2048]{1,0:T(8,128)(2,1)}) async-done(((bf16[3,256,2048]{2,1,0:T(8,128)(2,1)}, bf16[256,2048]{1,0:T(8,128)(2,1)}), (bf16[3,256,2048]{2,1,0:T(8,128)(2,1)}, bf16[256,2048]{1,0:T(8,128)(2,1)})) %all-reduce.5.cloned.1.call-update) | async-done | bytes 4194320 | tf_op jit(solution)/shard_map/psum | solution.py:736
  853.0 2.9 convert_element_type.176
  856.0 2.9 fusion.56
  858.9 72.2 %reduce-scatter.9.cloned.1.call-done = bf16[256,2048]{1,0:T(8,128)(2,1)} async-done(((bf16[1024,2048]{1,0:T(8,128)(2,1)}), bf16[256,2048]{1,0:T(8,128)(2,1)}) %reduce-scatter.9.cloned.1.call-update) | async-done | bytes 1048592 | tf_op jit(solution)/shard_map/reduce_scatter | solution.py:721
  931.1 79.5 %reduce-scatter.11.cloned.1.call-done = bf16[256,2048]{1,0:T(8,128)(2,1)} async-done(((bf16[1024,2048]{1,0:T(8,128)(2,1)}), bf16[256,2048]{1,0:T(8,128)(2,1)}) %reduce-scatter.11.cloned.1.call-update) | async-done | bytes 1048592 | tf_op jit(solution)/shard_map/reduce_scatter | solution.py:721
  1010.6 3.8 maximum_convert_fusion.1
  1014.4 143.6 %reduce-scatter.5.cloned.1.call-done = bf16[512,2048]{1,0:T(8,128)(2,1)} async-done(((bf16[2048,2048]{1,0:T(8,128)(2,1)}), bf16[512,2048]{1,0:T(8,128)(2,1)}) %reduce-scatter.5.cloned.1.call-update) | async-done | bytes 2097168 | tf_op jit(solution)/shard_map/reduce_scatter | solution.py:722
  1158.0 147.5 %reduce-scatter.7.cloned.1.call-done = bf16[512,2048]{1,0:T(8,128)(2,1)} async-done(((bf16[2048,2048]{1,0:T(8,128)(2,1)}), bf16[512,2048]{1,0:T(8,128)(2,1)}) %reduce-scatter.7.cloned.1.call-update) | async-done | bytes 2097168 | tf_op jit(solution)/shard_map/reduce_scatter | solution.py:722
  1305.5 6.3 maximum_convert_fusion
  1311.8 1.0 copy.76
  1312.8 1.0 copy.77
  (86 shorter events, 2.8 us)
Async XLA Ops:
  7.2 267.5 %all-gather.2.cloned.1.call-start = ((), (), s32[]{:S(2)}) async-start(), calls=%async_computation.4 | async-start | bytes 9437184 | tf_op jit(solution)/shard_map/all_gather | solution.py:660
  7.9 845.1 %all-reduce.5.cloned.1.call-start = ((), (), s32[]{:S(2)}) async-start(), calls=%async_computation.9 | async-start | bytes 8388608 | tf_op jit(solution)/shard_map/psum | solution.py:736
  130.9 4.9 copy-start.13
  132.8 141.8 %copy-start.7 = (f32[2,8,256]{2,0,1:T(2,128)}, f32[2,8,256]{2,0,1:T(2,128)S(1)}, u32[]{:S(2)}) copy-start(f32[2,8,256]{2,0,1:T(2,128)S(1)} %copy.51) | copy-start | bytes 49156
  132.9 141.8 %copy-start.9 = (bf16[2,8,256]{2,0,1:T(2,128)(2,1)}, bf16[2,8,256]{2,0,1:T(2,128)(2,1)S(1)}, u32[]{:S(2)}) copy-start(bf16[2,8,256]{2,0,1:T(2,128)(2,1)S(1)} %copy.53) | copy-start | bytes 24580
  257.9 2.1 copy-start
  299.8 1.4 copy-start.3
  316.9 4.6 copy-start.1
  316.9 4.6 copy-start.15
  321.6 7.4 copy-start.16
  321.6 16.5 %slice-start = ((s8[4718592]{0:T(1024)(128)(4,1)}), s8[524288]{0:T(1024)(128)(4,1)S(1)}, s32[]{:S(2)}) async-start(s8[4718592]{0:T(1024)(128)(4,1)} %bitcast.135), calls=%async_computation.10 | async-start | bytes 1048576
  328.9 9.2 slice-start.1
  328.9 23.9 %slice-start.2 = ((s8[4718592]{0:T(1024)(128)(4,1)}), s8[4194304]{0:T(1024)(128)(4,1)S(1)}, s32[]{:S(2)}) async-start(s8[4718592]{0:T(1024)(128)(4,1)} %bitcast.139), calls=%async_computation.12 | async-start | bytes 8388608
  328.9 23.9 %slice-start.6 = ((s8[8388608]{0:T(1024)(128)(4,1)}), s8[4194304]{0:T(1024)(128)(4,1)S(1)}, s32[]{:S(2)}) async-start(s8[8388608]{0:T(1024)(128)(4,1)} %bitcast.162), calls=%async_computation.16 | async-start | bytes 8388608
  338.1 14.7 %slice-start.3 = ((s8[4718592]{0:T(1024)(128)(4,1)}), s8[524288]{0:T(1024)(128)(4,1)S(1)}, s32[]{:S(2)}) async-start(s8[4718592]{0:T(1024)(128)(4,1)} %bitcast.139), calls=%async_computation.13 | async-start | bytes 1048576
  338.1 14.7 %slice-start.7 = ((s8[8388608]{0:T(1024)(128)(4,1)}), s8[4194304]{0:T(1024)(128)(4,1)S(1)}, s32[]{:S(2)}) async-start(s8[8388608]{0:T(1024)(128)(4,1)} %bitcast.162), calls=%async_computation.17 | async-start | bytes 8388608
  363.7 1.5 copy-start.4
  378.8 20.0 %slice-start.4 = ((s8[4718592]{0:T(1024)(128)(4,1)}), s8[4194304]{0:T(1024)(128)(4,1)S(1)}, s32[]{:S(2)}) async-start(s8[4718592]{0:T(1024)(128)(4,1)} %bitcast.142), calls=%async_computation.14 | async-start | bytes 8388608
  383.4 15.4 %slice-start.5 = ((s8[4718592]{0:T(1024)(128)(4,1)}), s8[524288]{0:T(1024)(128)(4,1)S(1)}, s32[]{:S(2)}) async-start(s8[4718592]{0:T(1024)(128)(4,1)} %bitcast.142), calls=%async_computation.15 | async-start | bytes 1048576
  383.4 15.4 %copy-start.14 = (bf16[1152,1024]{1,0:T(8,128)(2,1)S(1)}, bf16[1152,1024]{1,0:T(8,128)(2,1)}, u32[]{:S(2)}) copy-start(bf16[1152,1024]{1,0:T(8,128)(2,1)} %get-tuple-element.53) | copy-start | bytes 7077892
  398.9 43.7 %slice-start.8 = ((s8[4718592]{0:T(1024)(128)(4,1)}), s8[524288]{0:T(1024)(128)(4,1)S(1)}, s32[]{:S(2)}) async-start(s8[4718592]{0:T(1024)(128)(4,1)} %bitcast.164), calls=%async_computation.18 | async-start | bytes 1048576
  406.3 36.4 %slice-start.9 = ((s8[4718592]{0:T(1024)(128)(4,1)}), s8[4194304]{0:T(1024)(128)(4,1)S(1)}, s32[]{:S(2)}) async-start(s8[4718592]{0:T(1024)(128)(4,1)} %bitcast.164), calls=%async_computation.19 | async-start | bytes 8388608
  421.7 9.2 copy-start.8
  430.9 11.7 copy-start.10
  696.7 234.4 %reduce-scatter.9.cloned.1.call-start = ((), (), s32[]{:S(2)}) async-start(), calls=%async_computation.7 | async-start | bytes 5242880 | tf_op jit(solution)/shard_map/reduce_scatter | solution.py:721
  697.5 313.2 %reduce-scatter.11.cloned.1.call-start = ((), (), s32[]{:S(2)}) async-start(), calls=%async_computation.8 | async-start | bytes 5242880 | tf_op jit(solution)/shard_map/reduce_scatter | solution.py:721
  698.0 460.0 %reduce-scatter.5.cloned.1.call-start = ((), (), s32[]{:S(2)}) async-start(), calls=%async_computation.5 | async-start | bytes 10485760 | tf_op jit(solution)/shard_map/reduce_scatter | solution.py:722
  698.6 1.4 copy-start.11
  698.6 1.4 copy-start.12
  698.6 606.8 %reduce-scatter.7.cloned.1.call-start = ((), (), s32[]{:S(2)}) async-start(), calls=%async_computation.6 | async-start | bytes 10485760 | tf_op jit(solution)/shard_map/reduce_scatter | solution.py:722
  853.0 2.9 copy-start.2
  1305.5 6.3 copy-start.5
  1305.5 7.3 copy-start.6
Sparse Core Ops, SparseCore 0:
  9.9 108.5 all-gather.1
  696.8 156.1 all-reduce.4
  855.3 75.7 reduce-scatter.8
  933.3 77.2 reduce-scatter.10
  1012.8 145.1 reduce-scatter.4
  1160.2 145.2 reduce-scatter.6

commit v2 on v1

--- a/solution.py
+++ b/solution.py
@@ -1,3 +1,5 @@
+import functools
+
 import jax
 import jax.numpy as jnp
 from jax import lax
@@ -402,12 +404,12 @@
     )(gpart, opart, middle, cot, living, gain)
 
 
-def final_kernel(part, wgrad, tok, mgrad, gain, tgrad, ggrad, wrows, *scratch):
+def final_kernel(part, wgrad, tok, mgrad, gain, others, tgrad, small, wrows, ggrad, parcel, landed, *scratch):
     at = Place()
     seqs = tok.shape[0]
     n = Reduce.sems
     reduce = Reduce(at, part, *scratch[:n])
-    wsend, wrecv, local = scratch[n:]
+    wsend, wrecv, local, gsend, grecv = scratch[n:]
     width = wgrad.shape[2]
     block = wrows.shape[1]
     at.greet(at.peers())
@@ -433,35 +435,258 @@
         ggrad[...] += jnp.sum(back, axis=0, keepdims=True)
 
     each(seqs, rows)
+
+    parcel[...] = jnp.zeros_like(parcel)
+    devices = parcel.shape[0]
+    rows_of = ggrad.shape[1] // (128 * devices)
+    for dev in range(devices):
+        for k in range(rows_of):
+            lanes = pl.ds((dev * rows_of + k) * 128, 128)
+            parcel[dev, k : k + 1] = ggrad[:, lanes]
+            parcel[dev, rows_of + k : rows_of + k + 1] = others[0:1, lanes]
+        parcel[dev, 2 * rows_of : 2 * rows_of + 2] = others[1:3, 0:128]
+
+    def parcel_copy(m, dev):
+        return at.push(parcel.at[dev], landed.at[m], gsend.at[m], grecv.at[m], dev)
+
+    for m, dev in enumerate(at.peers()):
+        parcel_copy(m, dev).start()
+    total = parcel[at.me]
+    for m, dev in enumerate(at.peers()):
+        parcel_copy(m, dev).wait_recv()
+        total = total + landed[m]
+    small[...] = total
     each(seqs, reduce.finish)
     for m, dev in enumerate(at.peers()):
         weight_copy(m, dev).wait()
+        parcel_copy(m, dev).wait_send()
     own.wait()
 
 
-def final(part, wgrad, tokens, mgrad, gain):
+def final(part, wgrad, tokens, mgrad, gain, ffn_back, qk_back):
     seqs, rows, width = tokens.shape
     ep = lax.axis_size("ep")
     if ep != 8:
         normed_grad = lax.psum_scatter(part, "ep", scatter_dimension=1, tiled=True).astype(F32)
         tg, backs = attn_back_rows(normed_grad, tokens, mgrad, gain)
         wrows = lax.all_to_all(wgrad, "ep", split_axis=1, concat_axis=2, tiled=True)
-        return tg, jnp.sum(backs, axis=(0, 1))[None], wrows
+        share = width // ep
+        small = jnp.concatenate([jnp.sum(backs, axis=(0, 1)), ffn_back[0], qk_back[0], qk_back[1]])
+        small = lax.psum(small, "ep")
+        mine = lax.axis_index("ep") * share
+        cut = [lax.dynamic_slice_in_dim(small, k * width + mine, share).reshape(-1, 128) for k in range(2)]
+        small = jnp.concatenate(cut + [small[2 * width :].reshape(2, HEAD_DIM)], axis=0)
+        return tg, jnp.pad(small, ((0, 8 - small.shape[0]), (0, 0))), wrows
+    others = jnp.concatenate([ffn_back, jnp.pad(qk_back[:2], ((0, 0), (0, width - HEAD_DIM)))], axis=0)
     part = part.reshape(seqs, ep, rows, width)
     dma = pltpu.SemaphoreType.DMA
     return pl.pallas_call(
         final_kernel,
         out_shape=(
             sds(tokens.shape, BF16),
-            sds((1, width), F32),
+            sds((8, 128), F32),
             sds((3, wgrad.shape[1] // ep, wgrad.shape[2] * ep), BF16),
         ),
-        in_specs=[VM] * 5,
+        in_specs=[VM] * 6,
         out_specs=(VM, VM, AN),
-        scratch_shapes=Reduce.scratch(part) + [dma((7,)), dma((7,)), dma],
+        scratch_shapes=[pltpu.VMEM((1, width), F32), pltpu.VMEM((ep, 8, 128), F32), pltpu.VMEM((7, 8, 128), F32)]
+        + Reduce.scratch(part)
+        + [dma((7,)), dma((7,)), dma, dma((7,)), dma((7,))],
         compiler_params=pltpu.CompilerParams(collective_id=4, **COMM),
         name="final",
-    )(part, wgrad, tokens, mgrad, gain)
+    )(part, wgrad, tokens, mgrad, gain, others)
+
+
+def line_kernel(own, small, out, small_out, right, left, landed, rs, rr, ls, lr, gs, gr, hs, hr, ss, sr):
+    z = lax.axis_index("rep")
+    ep = lax.axis_index("ep")
+    count = 4
+    halves = own.shape[2]
+    chunks = own.shape[0] * halves
+
+    def part(ref, c, q):
+        return ref.at[c // halves, q, lax.rem(c, halves)]
+
+    def push(src, dst, send, recv, dev):
+        return pltpu.make_async_remote_copy(
+            src_ref=src, dst_ref=dst, send_sem=send, recv_sem=recv, device_id=(dev, ep), device_id_type=MESH
+        )
+
+    barrier = pltpu.get_barrier_semaphore()
+    others = [lax.rem(z + k, count) for k in range(1, count)]
+    for dev in others:
+        pl.semaphore_signal(barrier, inc=1, device_id=(dev, ep), device_id_type=MESH)
+    pl.semaphore_wait(barrier, count - 1)
+
+    def small_copy(k):
+        return push(small, landed.at[k], ss.at[k], sr.at[k], others[k])
+
+    for k in range(count - 1):
+        small_copy(k).start()
+
+    def to_right(c, q):
+        return push(part(right, c, q), part(right, c, q), rs.at[c, q], rr.at[c, q], z + 1)
+
+    def to_left(c, q):
+        return push(part(left, c, q), part(left, c, q), ls.at[c, q], lr.at[c, q], z - 1)
+
+    def give_right(c, q):
+        return push(part(out, c, q), part(out, c, q), gs.at[c, q], gr.at[c, q], z + 1)
+
+    def give_left(c, q):
+        return push(part(out, c, q), part(out, c, q), hs.at[c, q], hr.at[c, q], z - 1)
+
+    def load(ref, c, q):
+        return part(ref, c, q)[...].astype(F32)
+
+    def add(held, c, q, first):
+        @pl.when(first)
+        def _():
+            part(held, c, q)[...] = part(own, c, q)[...]
+
+        @pl.when(jnp.logical_not(first))
+        def _():
+            part(held, c, q)[...] = (load(held, c, q) + load(own, c, q)).astype(BF16)
+
+    def walk(c):
+        for step in range(count - 1):
+            q = count - 1 - step
+
+            @pl.when(z < q)
+            def _():
+                @pl.when(z > 0)
+                def _():
+                    to_right(c, q).wait_recv()
+
+                add(right, c, q, z == 0)
+                to_right(c, q).start()
+
+            @pl.when(z > step)
+            def _():
+                @pl.when(z < count - 1)
+                def _():
+                    to_left(c, step).wait_recv()
+
+                add(left, c, step, z == count - 1)
+                to_left(c, step).start()
+
+
+    def total(c):
+        @pl.when(z > 0)
+        def _():
+            to_right(c, z).wait_recv()
+
+        @pl.when(z < count - 1)
+        def _():
+            to_left(c, z).wait_recv()
+
+        @pl.when(z == 0)
+        def _():
+            part(out, c, z)[...] = (load(own, c, z) + load(left, c, z)).astype(BF16)
+
+        @pl.when(z == count - 1)
+        def _():
+            part(out, c, z)[...] = (load(own, c, z) + load(right, c, z)).astype(BF16)
+
+        @pl.when(jnp.logical_and(z > 0, z < count - 1))
+        def _():
+            part(out, c, z)[...] = (load(own, c, z) + load(left, c, z) + load(right, c, z)).astype(BF16)
+
+        @pl.when(z < count - 1)
+        def _():
+            give_right(c, z).start()
+
+        @pl.when(z > 0)
+        def _():
+            give_left(c, z).start()
+
+
+    def spread(c):
+        for d in range(1, count):
+
+            @pl.when(z >= d)
+            def _():
+                give_right(c, z - d).wait_recv()
+
+                @pl.when(z < count - 1)
+                def _():
+                    give_right(c, z - d).start()
+
+            @pl.when(z + d < count)
+            def _():
+                give_left(c, z + d).wait_recv()
+
+                @pl.when(z > 0)
+                def _():
+                    give_left(c, z + d).start()
+
+    def run(c, _):
+        @pl.when(c < chunks)
+        def _():
+            walk(c)
+
+        @pl.when(jnp.logical_and(c >= 1, c < chunks + 1))
+        def _():
+            total(c - 1)
+
+        @pl.when(c >= 2)
+        def _():
+            spread(c - 2)
+
+        return 0
+
+    lax.fori_loop(0, chunks + 2, run, 0)
+
+    def finish(c):
+        for q in range(count):
+
+            @pl.when(z < q)
+            def _():
+                to_right(c, q).wait_send()
+
+            @pl.when(z > q)
+            def _():
+                to_left(c, q).wait_send()
+
+            @pl.when(jnp.logical_and(q <= z, z < count - 1))
+            def _():
+                give_right(c, q).wait_send()
+
+            @pl.when(jnp.logical_and(q >= z, z > 0))
+            def _():
+                give_left(c, q).wait_send()
+
+    each(chunks, finish)
+    total_small = small[...]
+    for k in range(count - 1):
+        small_copy(k).wait()
+        total_small = total_small + landed[k]
+    small_out[...] = total_small
+
+
+def line_sum(big, small):
+    if lax.axis_size("rep") != 4 or lax.axis_size("ep") != 8:
+        return lax.psum(big, "rep"), lax.psum(small, "rep")
+    count, rows, cols = big.shape
+    own = big.reshape(count, 4, 2, rows // 8, cols)
+    chunks = 2 * count
+    dma = pltpu.SemaphoreType.DMA
+    out, small = pl.pallas_call(
+        line_kernel,
+        out_shape=(sds(own.shape, BF16), sds(small.shape, F32)),
+        in_specs=[VM, VM],
+        out_specs=(VM, VM),
+        scratch_shapes=[
+            pltpu.VMEM(own.shape, BF16),
+            pltpu.VMEM(own.shape, BF16),
+            pltpu.VMEM((3,) + small.shape, F32),
+        ]
+        + [dma((chunks, 4))] * 8
+        + [dma((3,))] * 2,
+        compiler_params=pltpu.CompilerParams(collective_id=5, has_side_effects=True, vmem_limit_bytes=40 << 20),
+        name="line_sum",
+    )(own, small)
+    return out.reshape(big.shape), small
 
 
 def dot(a, b, ca, cb):
@@ -633,33 +858,289 @@
     )(lens, agrad, normed, pre, low, ctx, weights, wo, qg, kg, cos, sin)
 
 
+BLOCK = 256
+
+
+def pack_rows(seqs, capacity):
+    return -(-seqs * capacity // BLOCK) * BLOCK + BLOCK
+
+
+def expert_kernel(
+    capacity, top, j, number, lens, mixed, cot, table, w_in, w_out, slots, starts, act, dgu, out_grad, in_grad,
+    x, dy, wi, wo, acts, dgus, acc, stage, wsem, ssem, rsem,
+):
+    s = pl.program_id(0)
+    seqs = pl.num_programs(0)
+    length, width = mixed.shape[1:]
+    hidden = wo.shape[0]
+    loads = [pltpu.make_async_copy(w_in.at[j], wi, wsem.at[0]), pltpu.make_async_copy(w_out.at[j], wo, wsem.at[1])]
+
+    @pl.when(s == 0)
+    def _():
+        for copy in loads:
+            copy.start()
+        starts[0] = 0
+
+    tab = table[0].astype(F32)
+    lane = lax.broadcasted_iota(jnp.int32, tab.shape, 1)
+    row = lax.broadcasted_iota(jnp.int32, tab.shape, 0)
+    chosen = jnp.logical_and(jnp.logical_and(tab == number[0].astype(F32), lane < top), row < lens[s])
+    chosen = jnp.where(chosen, 1.0, 0.0)
+    hit = jnp.sum(chosen, axis=1, keepdims=True)
+    weight = jnp.sum(chosen * pltpu.roll(tab, 128 - top, 1), axis=1, keepdims=True)
+    later = lax.broadcasted_iota(jnp.int32, (length, length), 0)
+    earlier = lax.broadcasted_iota(jnp.int32, (length, length), 1)
+    before = jnp.where(earlier < later, 1.0, 0.0).astype(BF16)
+    rank = dot(before, jnp.broadcast_to(hit, (length, 128)).astype(BF16), 1, 0)
+    slot = jnp.where(hit > 0.5, rank, -1.0)
+    slots[0] = jnp.where(lane < 64, slot, weight)
+    column = lax.broadcasted_iota(jnp.int32, (length, capacity), 1).astype(F32)
+    place = slot[:, 0:1] == column
+    start = pl.multiple_of(starts[s], 16)
+    span = pl.ds(start, capacity)
+    x[span] = dot(jnp.where(place, 1.0, 0.0).astype(BF16), mixed[0], 0, 0).astype(BF16)
+    dy[span] = dot(jnp.where(place, weight, 0.0).astype(BF16), cot[0], 0, 0).astype(BF16)
+    count = jnp.sum(hit).astype(jnp.int32)
+    starts[s + 1] = start + (count + 15) // 16 * 16
+
+    @pl.when(s == seqs - 1)
+    def _():
+        total = starts[seqs]
+        tail = pl.ds(pl.multiple_of(start + capacity, 16), BLOCK)
+        x[tail] = jnp.zeros((BLOCK, width), BF16)
+        dy[tail] = jnp.zeros((BLOCK, width), BF16)
+        blocks = (total + BLOCK - 1) // BLOCK
+        for copy in loads:
+            copy.wait()
+        part = min(hidden, 512)
+
+        def forward(b, _):
+            rows = pl.ds(pl.multiple_of(b * BLOCK, BLOCK), BLOCK)
+            for h in range(hidden // part):
+                gcols, ucols = pl.ds(h * part, part), pl.ds(hidden + h * part, part)
+                gate = dot(x[rows], wi[:, gcols], 1, 0)
+                up = dot(x[rows], wi[:, ucols], 1, 0)
+                dact = dot(dy[rows], wo[gcols], 1, 1)
+                sig = 1.0 / (1.0 + jnp.exp(-gate))
+                silu = gate * sig
+                acts[rows, gcols] = (silu * up).astype(BF16)
+                dgus[rows, gcols] = (dact * up * sig * (1.0 + gate * (1.0 - sig))).astype(BF16)
+                dgus[rows, ucols] = (dact * silu).astype(BF16)
+            return 0
+
+        lax.fori_loop(0, blocks, forward, 0)
+        saves = [pltpu.make_async_copy(acts, act, rsem.at[0]), pltpu.make_async_copy(dgus, dgu, rsem.at[1])]
+        for copy in saves:
+            copy.start()
+
+        tr, tc = acc.shape
+
+        def grads(left, right, result, first):
+            down, across = result.shape[0] // tr, result.shape[1] // tc
+
+            def tile(t, _):
+                rt, ct = t // across, lax.rem(t, across)
+                left_cols = pl.ds(pl.multiple_of(rt * tr, tr), tr)
+                right_cols = pl.ds(pl.multiple_of(ct * tc, tc), tc)
+
+                def step(b, _):
+                    rows = pl.ds(pl.multiple_of(b * BLOCK, BLOCK), BLOCK)
+                    piece = dot(left[rows, left_cols], right[rows, right_cols], 0, 0)
+
+                    @pl.when(b == 0)
+                    def _():
+                        acc[...] = piece
+
+                    @pl.when(b > 0)
+                    def _():
+                        acc[...] += piece
+
+                    return 0
+
+                @pl.when(blocks == 0)
+                def _():
+                    acc[...] = jnp.zeros_like(acc)
+
+                lax.fori_loop(0, blocks, step, 0)
+                k = lax.rem(t, 2)
+                out = pltpu.make_async_copy(stage.at[k], result.at[left_cols, right_cols], ssem.at[k])
+
+                @pl.when(jnp.logical_or(t >= 2, not first))
+                def _():
+                    out.wait()
+
+                stage[k] = acc[...].astype(BF16)
+                out.start()
+                return 0
+
+            lax.fori_loop(0, down * across, tile, 0)
+
+        grads(acts, dy, out_grad, True)
+        grads(x, dgus, in_grad, False)
+        for k in range(2):
+            pltpu.make_async_copy(stage.at[k], in_grad.at[pl.ds(0, tr), pl.ds(0, tc)], ssem.at[k]).wait()
+        for copy in saves:
+            copy.wait()
+
+
+def expert_pass(j, number, lens, mixed, cot, w_in, w_out, capacity, top):
+    seqs, length, width = mixed.shape
+    hidden = w_out.shape[1]
+    rows = pack_rows(seqs, capacity)
+    dma = pltpu.SemaphoreType.DMA
+    kernel = functools.partial(expert_kernel, capacity, top, j)
+    seq = lambda i, *_: (i, 0, 0)
+    return pl.pallas_call(
+        kernel,
+        out_shape=(
+            sds((seqs, length, 128), F32),
+            sds((seqs + 1,), jnp.int32),
+            sds((rows, hidden), BF16),
+            sds((rows, 2 * hidden), BF16),
+            sds((hidden, width), BF16),
+            sds((width, 2 * hidden), BF16),
+        ),
+        grid_spec=pltpu.PrefetchScalarGridSpec(
+            num_scalar_prefetch=2,
+            grid=(seqs,),
+            in_specs=[
+                pl.BlockSpec((1, length, width), seq),
+                pl.BlockSpec((1, length, width), seq),
+                pl.BlockSpec((1, length, 128), lambda i, *_: (i, 0, width // 128)),
+                AN,
+                AN,
+            ],
+            out_specs=(
+                pl.BlockSpec((1, length, 128), seq),
+                pl.BlockSpec(memory_space=pltpu.SMEM),
+                AN,
+                AN,
+                AN,
+                AN,
+            ),
+            scratch_shapes=[
+                pltpu.VMEM((rows, width), BF16),
+                pltpu.VMEM((rows, width), BF16),
+                pltpu.VMEM(w_in.shape[1:], BF16),
+                pltpu.VMEM(w_out.shape[1:], BF16),
+                pltpu.VMEM((rows, hidden), BF16),
+                pltpu.VMEM((rows, 2 * hidden), BF16),
+                pltpu.VMEM((min(hidden, 512), min(width, 1024)), F32),
+                pltpu.VMEM((2, min(hidden, 512), min(width, 1024)), BF16),
+                dma((2,)),
+                dma((2,)),
+                dma((2,)),
+            ],
+        ),
+        compiler_params=pltpu.CompilerParams(dimension_semantics=("arbitrary",), vmem_limit_bytes=60 << 20),
+        cost_estimate=pl.CostEstimate(flops=25 * 10**9, bytes_accessed=6 * 10**7, transcendentals=10**6),
+        name="expert_pass",
+    )(number, lens, mixed, cot, cot, w_in, w_out)
+
+
+def tail_kernel(starts, act, dgu, w_in, w_out, produced, dx):
+    @pl.when(pl.program_id(0) * BLOCK < starts[starts.shape[0] - 1])
+    def _():
+        produced[...] = dot(act[...], w_out[...], 1, 0).astype(BF16)
+        dx[...] = dot(dgu[...], w_in[...], 1, 1).astype(BF16)
+
+
+def expert_tail(j, starts, act, dgu, w_in, w_out):
+    rows, hidden = act.shape
+    width = w_in.shape[1]
+    last = starts.shape[0] - 1
+    block = lambda i, st: (jnp.maximum(jnp.minimum(i, (st[last] + BLOCK - 1) // BLOCK - 1), 0), 0)
+    return pl.pallas_call(
+        tail_kernel,
+        out_shape=(sds((rows, width), BF16), sds((rows, width), BF16)),
+        grid_spec=pltpu.PrefetchScalarGridSpec(
+            num_scalar_prefetch=1,
+            grid=(rows // BLOCK - 1,),
+            in_specs=[
+                pl.BlockSpec((BLOCK, hidden), block),
+                pl.BlockSpec((BLOCK, 2 * hidden), block),
+                pl.BlockSpec((None,) + w_in.shape[1:], lambda i, *_: (j, 0, 0)),
+                pl.BlockSpec((None,) + w_out.shape[1:], lambda i, *_: (j, 0, 0)),
+            ],
+            out_specs=(pl.BlockSpec((BLOCK, width), block), pl.BlockSpec((BLOCK, width), block)),
+        ),
+        compiler_params=pltpu.CompilerParams(dimension_semantics=("arbitrary",), vmem_limit_bytes=60 << 20),
+        cost_estimate=pl.CostEstimate(flops=12 * 10**9, bytes_accessed=3 * 10**7, transcendentals=0),
+        name="expert_tail",
+    )(starts, act, dgu, w_in, w_out)
+
+
+def combine_kernel(capacity, local, *refs):
+    s = pl.program_id(0)
+    starts = refs[:local]
+    slots = refs[local : 2 * local]
+    produced = refs[2 * local : 3 * local]
+    dx = refs[3 * local : 4 * local]
+    out_part, grad_part = refs[4 * local :]
+    out_sum, grad_sum = None, None
+    for j in range(local):
+        length = slots[j].shape[1]
+        column = lax.broadcasted_iota(jnp.int32, (length, capacity), 1).astype(F32)
+        place = slots[j][0, :, 0:1] == column
+        span = pl.ds(pl.multiple_of(starts[j][s], 16), capacity)
+        held = lax.broadcasted_iota(jnp.int32, (capacity, 1), 0) < starts[j][s + 1] - starts[j][s]
+        rows = jnp.where(held, produced[j][span], 0.0).astype(BF16)
+        grads = jnp.where(held, dx[j][span], 0.0).astype(BF16)
+        out = dot(jnp.where(place, slots[j][0, :, 64:65], 0.0).astype(BF16), rows, 1, 0)
+        grad = dot(jnp.where(place, 1.0, 0.0).astype(BF16), grads, 1, 0)
+        out_sum = out if out_sum is None else out_sum + out
+        grad_sum = grad if grad_sum is None else grad_sum + grad
+    out_part[0] = out_sum.astype(BF16)
+    grad_part[0] = grad_sum.astype(BF16)
+
+
+def combine(starts, slots, produced, dx, capacity):
+    local = len(starts)
+    seqs, length, _ = slots[0].shape
+    width = produced[0].shape[1]
+    seq = lambda i, *_: (i, 0, 0)
+    two = lambda i, *_: (0, 0)
+    rows = pl.BlockSpec(produced[0].shape, two)
+    return pl.pallas_call(
+        functools.partial(combine_kernel, capacity, local),
+        out_shape=(sds((seqs, length, width), BF16), sds((seqs, length, width), BF16)),
+        grid_spec=pltpu.PrefetchScalarGridSpec(
+            num_scalar_prefetch=local,
+            grid=(seqs,),
+            in_specs=[pl.BlockSpec((1, length, 128), seq)] * local + [rows] * (2 * local),
+            out_specs=(pl.BlockSpec((1, length, width), seq), pl.BlockSpec((1, length, width), seq)),
+        ),
+        compiler_params=pltpu.CompilerParams(dimension_semantics=("arbitrary",), vmem_limit_bytes=60 << 20),
+        cost_estimate=pl.CostEstimate(flops=3 * 10**9, bytes_accessed=4 * 10**7, transcendentals=0),
+        name="combine",
+    )(*starts, *slots, *produced, *dx)
+
+
 def shards(
     tokens, cotangent, gate_weights, expert_ids, seq_lengths, query_weight, key_weight, value_weight,
     output_weight, attn_gain, ffn_gain, query_gain, key_gain, expert_in, expert_out,
 ):
     ep = lax.axis_size("ep")
     me = lax.axis_index("ep")
-    seqs, rows, width = tokens.shape
+    _, rows, width = tokens.shape
     length = rows * ep
     top = gate_weights.shape[2]
     local = expert_in.shape[0]
-    hidden = expert_out.shape[1]
     experts = local * ep
-    capacity = length * top * 9 // (8 * experts)
-
-    pairs = jnp.concatenate(
-        [expert_ids.astype(F32).transpose(0, 2, 1), gate_weights.astype(F32).transpose(0, 2, 1)], axis=1
-    ).reshape(-1, 128)
+    capacity = -(-(length * top * 9 // (8 * experts)) // 16) * 16
+
     gains = jnp.concatenate([attn_gain, ffn_gain]).astype(F32).reshape(-1, 128)
     few = jnp.concatenate([query_gain.astype(F32), key_gain.astype(F32), seq_lengths.astype(F32)])
     few = jnp.pad(few, (0, 128 - few.shape[0]))[None]
-    packet = jnp.concatenate([pairs, gains, few], axis=0)
+    packet = jnp.concatenate([gains, few], axis=0)
     packet = jnp.pad(packet, ((0, -packet.shape[0] % 8), (0, 0)))
 
     full, weights, packets = front(tokens, query_weight, key_weight, value_weight, packet)
-    cot_full = lax.all_gather(cotangent, "ep", axis=1, tiled=True)
-
-    n = pairs.shape[0]
+    routes = jnp.concatenate([expert_ids.astype(BF16), gate_weights], axis=-1)
+    routes = jnp.pad(routes, ((0, 0), (0, 0), (0, 128 - 2 * top)))
+    cot_full = lax.all_gather(jnp.concatenate([cotangent, routes], axis=-1), "ep", axis=1, tiled=True)
+
+    n = 0
     g = gains.shape[0] // 2
     gain_attn = packets[:, n : n + g].reshape(1, width)
     gain_ffn = packets[:, n + g : n + 2 * g].reshape(1, width)
@@ -667,7 +1148,6 @@
     gain_query = packets[:, n + 2 * g, :q].reshape(1, HEAD_DIM)
     gain_key = packets[:, n + 2 * g, q : 2 * q].reshape(1, HEAD_DIM)
     lens = packets[:, n + 2 * g, 2 * q].astype(jnp.int32)
-    table = packets[:, :n].reshape(ep, seqs, 2 * top, rows).transpose(1, 2, 0, 3).reshape(seqs, 2 * top, length)
     positions = jnp.arange(length, dtype=jnp.int32)
     live = (positions[None] < lens[:, None]).astype(F32)
     living = lax.dynamic_slice_in_dim(live, me * rows, rows, axis=1)[..., None]
@@ -683,74 +1163,46 @@
     )
     middle, mixed = mix(part, tokens, living, gain_ffn)
 
-    mine = (me * local + jnp.arange(local)).astype(F32)
-    chosen = (table[None, :, :top] == mine[:, None, None, None]).astype(F32)
-    hit = jnp.sum(chosen, axis=2) * live[None]
-    weight = jnp.sum(chosen * table[None, :, top:], axis=2) * live[None]
-    before = (positions[:, None] < positions[None, :]).astype(BF16)
-    rank = jnp.dot(hit.astype(BF16), before, preferred_element_type=F32)
-    slot = jnp.where(hit > 0.5, rank, -1.0)
-    place = slot[:, :, None, :] == jnp.arange(capacity, dtype=F32)[None, None, :, None]
-    pick = place.astype(BF16)
-    weighted = jnp.where(place, weight[:, :, None, :], 0.0).astype(BF16)
-
-    def ein(spec, a, b):
-        return jnp.einsum(spec, a, b, preferred_element_type=F32)
-
-    slots = seqs * capacity
-    arrived = ein("jsrt,std->jsrd", pick, mixed).astype(BF16).reshape(local, slots, width)
-    arrived_grad = ein("jsrt,std->jsrd", weighted, cot_full).astype(BF16).reshape(local, slots, width)
-    in_grads, out_grads, acts, dgus = [], [], [], []
-    token = None
+    in_grads, out_grads, passes = [], [], []
     for j in range(local):
-        x, dy = arrived[j], arrived_grad[j]
-        if token is not None:
-            x, dy, _ = lax.optimization_barrier((x, dy, token))
-        gate_up = jnp.dot(x, expert_in[j], preferred_element_type=F32)
-        dact = dot(dy, expert_out[j], 1, 1)
-        gate, up = gate_up[:, :hidden], gate_up[:, hidden:]
-        sig = jax.nn.sigmoid(gate)
-        act = (gate * sig * up).astype(BF16)
-        dgu = jnp.concatenate(
-            [dact * up * sig * (1.0 + gate * (1.0 - sig)), dact * gate * sig], axis=1
-        ).astype(BF16)
-        out_grad = dot(act, dy, 0, 0).astype(BF16)
-        in_grad = dot(x, dgu, 0, 0).astype(BF16)
-        out_grad, in_grad, act, dgu = lax.optimization_barrier((out_grad, in_grad, act, dgu))
-        token = act
+        number = (me * local + j).astype(jnp.int32)[None]
+        if passes:
+            number, _ = lax.optimization_barrier((number, passes[-1][1]))
+        slots, starts, act, dgu, out_grad, in_grad = expert_pass(
+            j, number, lens, mixed, cot_full, expert_in, expert_out, capacity, top
+        )
+        passes.append((slots, starts, act, dgu))
         out_grads.append(lax.psum_scatter(out_grad, "rep", scatter_dimension=0, tiled=True))
         in_grads.append(lax.psum_scatter(in_grad, "rep", scatter_dimension=0, tiled=True))
-        acts.append(act)
-        dgus.append(dgu)
-    out_parts = [jnp.dot(a, expert_out[j], preferred_element_type=F32).astype(BF16) for j, a in enumerate(acts)]
-    grad_parts = [dot(d, expert_in[j], 1, 1).astype(BF16) for j, d in enumerate(dgus)]
-    stack = lambda parts: jnp.stack(parts).reshape(local, seqs, capacity, width)
-    grad_part = ein("jsrt,jsrd->std", pick, stack(grad_parts)).astype(BF16)
-    out_part = ein("jsrt,jsrd->std", weighted, stack(out_parts)).astype(BF16)
-
+    tails = [
+        expert_tail(j, starts, act, dgu, expert_in, expert_out)
+        for j, (slots, starts, act, dgu) in enumerate(passes)
+    ]
+    out_part, grad_part = combine(
+        [p[1] for p in passes], [p[0] for p in passes], [t[0] for t in tails], [t[1] for t in tails], capacity
+    )
     result, mgrad, ffn_back, agrad = back(grad_part, out_part, middle, cotangent, living, gain_ffn)
     npart, wgrad, wograd, qk_back = attend_back(
         agrad, normed, pre, low, ctx, weights, output_weight, gain_query, gain_key, cos, sin, lens
     )
-    token_grad, attn_back, wrows = final(npart, wgrad, tokens, mgrad, gain_attn)
-    sums = lax.psum((wrows, wograd), "rep")
-    small = jnp.concatenate([attn_back[0], ffn_back[0], qk_back[0], qk_back[1]])
-    small = lax.psum(small, ("rep", "ep"))
-
-    def share(vector):
-        return lax.dynamic_slice_in_dim(vector, me * (vector.shape[0] // ep), vector.shape[0] // ep)
+    token_grad, small, wrows = final(npart, wgrad, tokens, mgrad, gain_attn, ffn_back, qk_back)
+    sums, small = line_sum(jnp.concatenate([wrows, wograd[None]], axis=0), small)
+    share = g
+
+    def head_share(vector):
+        return lax.dynamic_slice_in_dim(vector, me * (HEAD_DIM // ep), HEAD_DIM // ep)
 
     return (
         result,
         token_grad,
-        sums[0][0].astype(F32),
-        sums[0][1].astype(F32),
-        sums[0][2].astype(F32),
+        sums[0].astype(F32),
         sums[1].astype(F32),
-        share(small[:width]),
-        share(small[width : 2 * width]),
-        share(small[2 * width : 2 * width + HEAD_DIM]),
-        share(small[2 * width + HEAD_DIM :]),
+        sums[2].astype(F32),
+        sums[3].astype(F32),
+        small[:share].reshape(-1),
+        small[share : 2 * share].reshape(-1),
+        head_share(small[2 * share]),
+        head_share(small[2 * share + 1]),
         jnp.stack(in_grads).astype(F32),
         jnp.stack(out_grads).astype(F32),
     )

time: 1330 us -> 953 us (0.72)
  waiting for transfers between devices: 550 us -> 1.13 us
  Pallas kernels: 466 us -> 898 us
  matrix products: 182 us -> 0 us
  blocking collectives: 45.8 us -> 0 us
  local copies, waits for them, and re-layouts: 28.9 us -> 10.1 us
    pallas_call x1 -> x7, Pallas kernels: 78.5 us -> 509 us  [the longest x1 264 us: line_sum(): pl.pallas_call(line_kernel, out_shape=(sds(own.shape, BF16), sds(small.sh...]
    reduce_scatter x2, waiting for transfers between devices: 291 us -> 0.01 us  [shards(): lax.psum_scatter(in_grad, 'rep', scatter_dimension=0, tiled=True)]
    dot_general x17 -> x0, matrix products: 182 us -> none  [the longest x8 99.2 us: dot(): lax.dot_general(a, b, (((ca,), (cb,)), ((), ())), preferred_element_type=...]
    reduce_scatter x2, waiting for transfers between devices: 152 us -> 0.01 us  [shards(): lax.psum_scatter(out_grad, 'rep', scatter_dimension=0, tiled=True)]
    psum x1 -> x0, waiting for transfers between devices: 105 us -> none  [shards(): sums = lax.psum((wrows, wograd), 'rep')]
    psum x1 -> x0, blocking collectives: 45.8 us -> none  [shards(): small = lax.psum(small, ('rep', 'ep'))]
  transfers between devices with their start and end apart: 6 -> 5, of which waited for: 5 -> 0; matrix products, arithmetic and copies ran while one was open for 4% -> 3% of each run, Pallas kernels for 17% -> 89%
where the time goes in v2:
time: 953 us; the launch traced here: 952 us
  Pallas kernels  898 us (94%)
  other arithmetic  28 us (3%)
  between operations  14.6 us (2%)
  local copies, waits for them, and re-layouts  10.1 us (1%)
    pallas_call x1, Pallas kernels, line_sum(): pl.pallas_call(line_kernel, out_shape=(sds(own.shape, BF16), sds(small.sh...  264 us
    pallas_call x1, Pallas kernels, back(): pl.pallas_call(back_kernel, out_shape=(sds(cot.shape, BF16), sds(cot.shap...  122 us
    pallas_call x1, Pallas kernels, front(): pl.pallas_call(front_kernel, out_shape=(sds((seqs, rows * ep, width), BF1...  115 us
    pallas_call x2, Pallas kernels, expert_pass(): pl.pallas_call(kernel, out_shape=(sds((seqs, length, 128), F32), sds((seq...  106 us
    pallas_call x1, Pallas kernels, final(): pl.pallas_call(final_kernel, out_shape=(sds(tokens.shape, BF16), sds((8,...  81.8 us
    pallas_call x1, Pallas kernels, mix(): pl.pallas_call(mix_kernel, out_shape=(sds(tokens.shape, F32), sds((seqs,...  80.7 us
    pallas_call x1, Pallas kernels, attend_back(): pl.pallas_call(attend_back_kernel, out_shape=(sds(agrad.shape, BF16), sds...  45.7 us
    pallas_call x2, Pallas kernels, expert_tail(): pl.pallas_call(tail_kernel, out_shape=(sds((rows, width), BF16), sds((row...  35.5 us
  transfers between devices with their start and end apart: 5, of which 0 were waited for; matrix products, arithmetic and copies ran while one was open for 3% of the time, Pallas kernels for 89%

profile of v2, /device:TPU:0, one launch (start us, length us, event | category | flops | bytes accessed | tf_op | source)
XLA Modules:
  0.0 952.1 jit_solution(1706824475008766483)
XLA Ops:
  7.2 0.0 all-gather.2.cloned.1.call-start
  7.2 0.8 convert_element_type.83
  8.0 0.1 copy.34
  8.1 0.8 copy.35
  8.9 0.1 fusion.2
  9.0 2.3 pad_maximum_fusion.1
  11.3 0.0 all-gather.2.cloned.1.call-update
  11.3 0.0 reduce-scatter.9.cloned.1.call-start
  12.0 0.7 convert_element_type.76
  12.7 0.7 convert_element_type.77
  13.4 0.1 fusion.4
  13.4 0.7 maximum_convert_fusion.2
  14.1 0.6 select_maximum_fusion.1.pk
  14.7 114.6 %front.1 = (bf16[8,256,2048]{2,1,0:T(8,128)(2,1)}, bf16[3,2048,256]{2,1,0:T(8,128)(2,1)}, f32[8,8,128]{2,1,0:T(8,128)}) custom-call(bf16[8,32,2048]{2,1,0:T(8,128)(2,1)} %tok.5, bf16[256,2048]{1,0:T(8,128)(2,1)} %wq.1, bf16[256,2048]{1,0:T(8,128)(2,1)} %wk.1, bf16[256,2048]{1,0:T(8,128)(2,1)} %wv.1, f32[8,128]{1,0:T(8,128)} %select_maximum_fusion.1.pk), custom_call_target="tpu_custom_call" | custom-call | tf_op jit(solution)/shard_map/front/pallas_call | solution.py:291
  129.3 0.9 slice_reduce_fusion
  130.2 0.6 reshape_squeeze.7.kg
  130.8 0.6 reshape_squeeze.6.qg
  131.4 1.1 convert_reduce_fusion.lens
  132.5 0.0 copy-start.5
  132.5 0.1 convert_bitcast_fusion
  132.6 0.8 copy.33.living
  133.4 0.5 fusion.3
  133.9 0.8 pad_maximum_fusion.2
  134.8 1.4 fusion.6
  136.2 0.0 copy-done.5
  136.2 25.5 %attend.1 = (bf16[8,256,2048]{2,1,0:T(8,128)(2,1)}, f32[2,8,256,256]{3,2,1,0:T(8,128)}, bf16[3,8,256,256]{3,2,1,0:T(8,128)(2,1)}, bf16[8,256,256]{2,1,0:T(8,128)(2,1)}, bf16[8,256,2048]{2,1,0:T(8,128)(2,1)}) custom-call(s32[8]{0:T(128)} %copy-done.5, bf16[8,256,2048]{2,1,0:T(8,128)(2,1)} %get-tuple-element.55.tok, ...), custom_call_target="tpu_custom_call" | custom-call | flops 10000000000 | bytes 40000000 | tf_op jit(solution)/shard_map/attend/pallas_call | solution.py:734
  161.7 80.7 %mix.1 = (f32[8,32,2048]{2,1,0:T(8,128)}, bf16[8,256,2048]{2,1,0:T(8,128)(2,1)}) custom-call(bf16[8,8,32,2048]{3,2,1,0:T(8,128)(2,1)} %bitcast.43, bf16[8,32,2048]{2,1,0:T(8,128)(2,1)} %tok.5, f32[8,32,1]{2,1,0:T(8,128)} %copy.33.living, f32[1,2048]{1,0:T(1,128)} %bitcast.50), custom_call_target="tpu_custom_call" | custom-call | tf_op jit(solution)/shard_map/mix/pallas_call | solution.py:337
  242.4 0.0 all-gather.2.cloned.1.call-done.cot.table
  242.4 52.9 %expert_pass.2 = (f32[8,256,128]{2,1,0:T(8,128)}, s32[9]{0:T(128)}, bf16[1536,1024]{1,0:T(8,128)(2,1)}, bf16[1536,2048]{1,0:T(8,128)(2,1)}, bf16[1024,2048]{1,0:T(8,128)(2,1)}, /*index=5*/bf16[2048,2048]{1,0:T(8,128)(2,1)}) custom-call(s32[1]{0:T(128)} %bitcast.number, s32[8]{0:T(128)} %copy-done.5, bf16[8,256,2048]{2,1,0:T(8,128)(2,1)} %get-tuple-element.58.mixed, ...), custom_call_target="tpu_custom_call" | custom-call | flops 24999999488 | bytes 60000000 | tf_op jit(solution)/shard_map/expert_pass/pallas_call | solution.py:993
  295.4 0.0 reduce-scatter.9.cloned.1.call-update
  295.4 0.2 reduce-scatter.11.cloned.1.call-start
  295.6 53.2 %expert_pass.3 = (f32[8,256,128]{2,1,0:T(8,128)}, s32[9]{0:T(128)}, bf16[1536,1024]{1,0:T(8,128)(2,1)}, bf16[1536,2048]{1,0:T(8,128)(2,1)}, bf16[1024,2048]{1,0:T(8,128)(2,1)}, /*index=5*/bf16[2048,2048]{1,0:T(8,128)(2,1)}) custom-call(s32[1]{0:T(128)} %bitcast.8.number, s32[8]{0:T(128)} %copy-done.5, bf16[8,256,2048]{2,1,0:T(8,128)(2,1)} %get-tuple-element.58.mixed, ...), custom_call_target="tpu_custom_call" | custom-call | flops 24999999488 | bytes 60000000 | tf_op jit(solution)/shard_map/expert_pass/pallas_call | solution.py:993
  348.8 0.0 reduce-scatter.11.cloned.1.call-update
  348.8 0.0 reduce-scatter.5.cloned.1.call-start
  348.9 0.5 reduce-scatter.5.cloned.1.call-update
  349.4 0.0 reduce-scatter.7.cloned.1.call-start
  349.5 0.5 reduce-scatter.7.cloned.1.call-update
  350.0 17.8 %expert_tail.2 = (bf16[1536,2048]{1,0:T(8,128)(2,1)}, bf16[1536,2048]{1,0:T(8,128)(2,1)}) custom-call(s32[9]{0:T(128)} %get-tuple-element.59.starts.refs_0_, bf16[1536,1024]{1,0:T(8,128)(2,1)} %get-tuple-element.64.act, bf16[1536,2048]{1,0:T(8,128)(2,1)} %get-tuple-element.65.dgu, bf16[2,2048,2048]{2,1,0:T(8,128)(2,1)} %w_in.7, bf16[2,1024,2048]{2,1,0:T(8,128)(2,1)} %w_out.7), custom_call_target="tpu_custom_call" | custom-call | flops 12000000000 | bytes 30000000 | tf_op jit(solution)/shard_map/expert_tail/pallas_call | solution.py:1053
  367.8 17.7 %expert_tail.3 = (bf16[1536,2048]{1,0:T(8,128)(2,1)}, bf16[1536,2048]{1,0:T(8,128)(2,1)}) custom-call(s32[9]{0:T(128)} %get-tuple-element.61.starts.refs_1_, bf16[1536,1024]{1,0:T(8,128)(2,1)} %get-tuple-element.67.act, bf16[1536,2048]{1,0:T(8,128)(2,1)} %get-tuple-element.68.dgu, bf16[2,2048,2048]{2,1,0:T(8,128)(2,1)} %w_in.7, bf16[2,1024,2048]{2,1,0:T(8,128)(2,1)} %w_out.7), custom_call_target="tpu_custom_call" | custom-call | flops 12000000000 | bytes 30000000 | tf_op jit(solution)/shard_map/expert_tail/pallas_call | solution.py:1053
  385.5 21.6 %combine.1 = (bf16[8,256,2048]{2,1,0:T(8,128)(2,1)}, bf16[8,256,2048]{2,1,0:T(8,128)(2,1)}) custom-call(s32[9]{0:T(128)} %get-tuple-element.59.starts.refs_0_, s32[9]{0:T(128)} %get-tuple-element.61.starts.refs_1_, f32[8,256,128]{2,1,0:T(8,128)} %get-tuple-element.62.refs_2_, f32[8,256,128]{2,1,0:T(8,128)} %get-tuple-element.63.refs_3_, ...), custom_call_target="tpu_custom_call" | custom-call | flops 3000000000 | bytes 40000000 | tf_op jit(solution)/shard_map/combine/pallas_call | solution.py:1104
  407.1 121.9 %back.1 = (bf16[8,32,2048]{2,1,0:T(8,128)(2,1)}, f32[8,32,2048]{2,1,0:T(8,128)}, f32[1,2048]{1,0:T(1,128)}, bf16[8,256,2048]{2,1,0:T(8,128)(2,1)}) custom-call(bf16[8,8,32,2048]{3,2,1,0:T(8,128)(2,1)} %bitcast.42, bf16[8,8,32,2048]{3,2,1,0:T(8,128)(2,1)} %bitcast.41, f32[8,32,2048]{2,1,0:T(8,128)} %get-tuple-element.74.middle, bf16[8,32,2048]{2,1,0:T(8,128)(2,1)} %cot.1, ...), custom_call_target="tpu_custom_call" | custom-call | tf_op jit(solution)/shard_map/back/pallas_call | solution.py:391
  529.0 0.0 copy-start.4
  529.0 45.7 %attend_back.1 = (bf16[8,256,2048]{2,1,0:T(8,128)(2,1)}, bf16[3,2048,256]{2,1,0:T(8,128)(2,1)}, bf16[256,2048]{1,0:T(8,128)(2,1)}, f32[8,128]{1,0:T(8,128)}) custom-call(s32[8]{0:T(128)} %copy-done.5, bf16[8,256,2048]{2,1,0:T(8,128)(2,1)} %get-tuple-element.76.agrad, bf16[8,256,2048]{2,1,0:T(8,128)(2,1)} %get-tuple-element.77.normed, ...), custom_call_target="tpu_custom_call" | custom-call | flops 20000000000 | bytes 40000000 | tf_op jit(solution)/shard_map/attend_back/pallas_call | solution.py:823
  574.7 0.7 slice.51
  575.4 0.0 copy-done.4
  575.4 0.6 select_maximum_fusion.others
  576.0 81.8 %final.1 = (bf16[8,32,2048]{2,1,0:T(8,128)(2,1)}, f32[8,128]{1,0:T(8,128)}, bf16[3,256,2048]{2,1,0:T(8,128)(2,1)}) custom-call(bf16[8,8,32,2048]{3,2,1,0:T(8,128)(2,1)} %bitcast.40, bf16[3,2048,256]{2,1,0:T(8,128)(2,1)} %get-tuple-element.82.wgrad, bf16[8,32,2048]{2,1,0:T(8,128)(2,1)} %tok.5, f32[8,32,2048]{2,1,0:T(8,128)} %get-tuple-element.83.mgrad, ...), custom_call_target="tpu_custom_call" | custom-call | tf_op jit(solution)/shard_map/final/pallas_call | solution.py:483
  657.8 0.0 copy-done.3
  657.8 0.0 copy-start
  657.8 2.3 pad_maximum_fusion.own
  660.2 0.0 copy-done
  660.2 264.5 %line_sum.1 = (bf16[4,4,2,32,2048]{4,3,2,1,0:T(8,128)(2,1)S(1)}, f32[8,128]{1,0:T(8,128)S(1)}) custom-call(bf16[4,4,2,32,2048]{4,3,2,1,0:T(8,128)(2,1)S(1)} %pad_maximum_fusion.own, f32[8,128]{1,0:T(8,128)S(1)} %copy-done), custom_call_target="tpu_custom_call" | custom-call | tf_op jit(solution)/shard_map/line_sum/pallas_call | solution.py:674
  924.7 0.6 dynamic-slice_bitcast_fusion
  925.3 0.6 dynamic-slice_bitcast_fusion.1
  925.8 0.6 slice_bitcast_fusion
  926.4 0.5 fusion.5
  926.9 1.6 bitcast_convert_fusion
  928.6 1.6 bitcast_convert_fusion.1
  930.2 1.6 bitcast_convert_fusion.2
  931.8 1.6 bitcast_convert_fusion.3
  933.5 3.8 maximum_convert_fusion.1
  937.3 6.3 maximum_convert_fusion
  943.6 1.0 copy.40
  944.6 1.0 copy.41
  (12 shorter events, 0.0 us)
Async XLA Ops:
  7.2 235.3 %all-gather.2.cloned.1.call-start = ((), (), s32[]{:S(2)}) async-start(), calls=%async_computation.4 | async-start | bytes 10027008 | tf_op jit(solution)/shard_map/all_gather | solution.py:1141
  11.3 922.1 %reduce-scatter.9.cloned.1.call-start = ((), (), s32[]{:S(2)}) async-start(), calls=%async_computation.7 | async-start | bytes 5242880 | tf_op jit(solution)/shard_map/reduce_scatter | solution.py:1175
  132.5 3.7 copy-start.5
  295.4 638.1 %reduce-scatter.11.cloned.1.call-start = ((), (), s32[]{:S(2)}) async-start(), calls=%async_computation.8 | async-start | bytes 5242880 | tf_op jit(solution)/shard_map/reduce_scatter | solution.py:1175
  348.8 588.4 %reduce-scatter.5.cloned.1.call-start = ((), (), s32[]{:S(2)}) async-start(), calls=%async_computation.5 | async-start | bytes 10485760 | tf_op jit(solution)/shard_map/reduce_scatter | solution.py:1176
  349.4 587.9 %reduce-scatter.7.cloned.1.call-start = ((), (), s32[]{:S(2)}) async-start(), calls=%async_computation.6 | async-start | bytes 10485760 | tf_op jit(solution)/shard_map/reduce_scatter | solution.py:1176
  529.0 46.4 %copy-start.4 = (f32[1,2048]{1,0:T(1,128)S(1)}, f32[1,2048]{1,0:T(1,128)}, u32[]{:S(2)}) copy-start(f32[1,2048]{1,0:T(1,128)} %get-tuple-element.84) | copy-start | bytes 24580
  576.0 81.8 %copy-start.3 = (bf16[256,2048]{1,0:T(8,128)(2,1)S(1)}, bf16[256,2048]{1,0:T(8,128)(2,1)}, u32[]{:S(2)}) copy-start(bf16[256,2048]{1,0:T(8,128)(2,1)} %get-tuple-element.88) | copy-start | bytes 3145732
  657.8 2.4 copy-start
  937.3 6.3 copy-start.1
  937.3 7.3 copy-start.2
Sparse Core Ops, SparseCore 0:
  11.5 112.1 all-gather.1
  295.5 86.8 reduce-scatter.8
  384.7 77.2 reduce-scatter.10
  464.2 145.1 reduce-scatter.4
  611.6 176.7 reduce-scatter.6

commit v3 on v2

--- a/solution.py
+++ b/solution.py
@@ -497,15 +497,10 @@
     )(part, wgrad, tokens, mgrad, gain, others)
 
 
-def line_kernel(own, small, out, small_out, right, left, landed, rs, rr, ls, lr, gs, gr, hs, hr, ss, sr):
+def line_kernel(own, small, out, small_out, held, met, landed, os, or_, ps, pr, qs, qr, fs, fr, ss, sr):
     z = lax.axis_index("rep")
     ep = lax.axis_index("ep")
-    count = 4
-    halves = own.shape[2]
-    chunks = own.shape[0] * halves
-
-    def part(ref, c, q):
-        return ref.at[c // halves, q, lax.rem(c, halves)]
+    chunks = own.shape[0]
 
     def push(src, dst, send, recv, dev):
         return pltpu.make_async_remote_copy(
@@ -513,163 +508,98 @@
         )
 
     barrier = pltpu.get_barrier_semaphore()
-    others = [lax.rem(z + k, count) for k in range(1, count)]
+    others = [lax.rem(z + k, 4) for k in range(1, 4)]
     for dev in others:
         pl.semaphore_signal(barrier, inc=1, device_id=(dev, ep), device_id_type=MESH)
-    pl.semaphore_wait(barrier, count - 1)
+    pl.semaphore_wait(barrier, 3)
+    inner = jnp.logical_and(z > 0, z < 3)
+    middle, partner, outer = 1 + z // 3, 3 - z, 3 * (z - 1)
+
+    def inward(c):
+        return push(own.at[c], held.at[c], os.at[c], or_.at[c], middle)
+
+    def across(c):
+        return push(held.at[c], met.at[c], ps.at[c], pr.at[c], partner)
+
+    def share(c):
+        return push(out.at[c], out.at[c], qs.at[c], qr.at[c], partner)
+
+    def outward(c):
+        return push(out.at[c], out.at[c], fs.at[c], fr.at[c], outer)
 
     def small_copy(k):
         return push(small, landed.at[k], ss.at[k], sr.at[k], others[k])
 
-    for k in range(count - 1):
+    for k in range(3):
         small_copy(k).start()
 
-    def to_right(c, q):
-        return push(part(right, c, q), part(right, c, q), rs.at[c, q], rr.at[c, q], z + 1)
-
-    def to_left(c, q):
-        return push(part(left, c, q), part(left, c, q), ls.at[c, q], lr.at[c, q], z - 1)
-
-    def give_right(c, q):
-        return push(part(out, c, q), part(out, c, q), gs.at[c, q], gr.at[c, q], z + 1)
-
-    def give_left(c, q):
-        return push(part(out, c, q), part(out, c, q), hs.at[c, q], hr.at[c, q], z - 1)
-
-    def load(ref, c, q):
-        return part(ref, c, q)[...].astype(F32)
-
-    def add(held, c, q, first):
-        @pl.when(first)
-        def _():
-            part(held, c, q)[...] = part(own, c, q)[...]
-
-        @pl.when(jnp.logical_not(first))
-        def _():
-            part(held, c, q)[...] = (load(held, c, q) + load(own, c, q)).astype(BF16)
-
-    def walk(c):
-        for step in range(count - 1):
-            q = count - 1 - step
-
-            @pl.when(z < q)
+    @pl.when(jnp.logical_not(inner))
+    def _():
+        each(chunks, lambda c: inward(c).start())
+        each(chunks, lambda c: outward(c).wait_recv())
+        each(chunks, lambda c: inward(c).wait_send())
+
+    def mine(c):
+        return 1 + lax.rem(c, 2) == z
+
+    @pl.when(inner)
+    def _():
+        def run(c, _):
+            @pl.when(c < chunks)
             def _():
-                @pl.when(z > 0)
+                inward(c).wait_recv()
+                held[c] = (held[c].astype(F32) + own[c].astype(F32)).astype(BF16)
+
+                @pl.when(jnp.logical_not(mine(c)))
                 def _():
-                    to_right(c, q).wait_recv()
-
-                add(right, c, q, z == 0)
-                to_right(c, q).start()
-
-            @pl.when(z > step)
+                    across(c).start()
+
+            b = c - 1
+
+            @pl.when(jnp.logical_and(jnp.logical_and(c >= 1, c < chunks + 1), mine(c + 1)))
             def _():
-                @pl.when(z < count - 1)
-                def _():
-                    to_left(c, step).wait_recv()
-
-                add(left, c, step, z == count - 1)
-                to_left(c, step).start()
-
-
-    def total(c):
-        @pl.when(z > 0)
-        def _():
-            to_right(c, z).wait_recv()
-
-        @pl.when(z < count - 1)
-        def _():
-            to_left(c, z).wait_recv()
-
-        @pl.when(z == 0)
-        def _():
-            part(out, c, z)[...] = (load(own, c, z) + load(left, c, z)).astype(BF16)
-
-        @pl.when(z == count - 1)
-        def _():
-            part(out, c, z)[...] = (load(own, c, z) + load(right, c, z)).astype(BF16)
-
-        @pl.when(jnp.logical_and(z > 0, z < count - 1))
-        def _():
-            part(out, c, z)[...] = (load(own, c, z) + load(left, c, z) + load(right, c, z)).astype(BF16)
-
-        @pl.when(z < count - 1)
-        def _():
-            give_right(c, z).start()
-
-        @pl.when(z > 0)
-        def _():
-            give_left(c, z).start()
-
-
-    def spread(c):
-        for d in range(1, count):
-
-            @pl.when(z >= d)
+                across(b).wait_recv()
+                out[b] = (held[b].astype(F32) + met[b].astype(F32)).astype(BF16)
+                share(b).start()
+                outward(b).start()
+
+            a = c - 2
+
+            @pl.when(jnp.logical_and(c >= 2, jnp.logical_not(mine(c))))
             def _():
-                give_right(c, z - d).wait_recv()
-
-                @pl.when(z < count - 1)
-                def _():
-                    give_right(c, z - d).start()
-
-            @pl.when(z + d < count)
+                share(a).wait_recv()
+                outward(a).start()
+
+            return 0
+
+        lax.fori_loop(0, chunks + 2, run, 0)
+
+        def finish(c):
+            outward(c).wait_send()
+
+            @pl.when(mine(c))
             def _():
-                give_left(c, z + d).wait_recv()
-
-                @pl.when(z > 0)
-                def _():
-                    give_left(c, z + d).start()
-
-    def run(c, _):
-        @pl.when(c < chunks)
-        def _():
-            walk(c)
-
-        @pl.when(jnp.logical_and(c >= 1, c < chunks + 1))
-        def _():
-            total(c - 1)
-
-        @pl.when(c >= 2)
-        def _():
-            spread(c - 2)
-
-        return 0
-
-    lax.fori_loop(0, chunks + 2, run, 0)
-
-    def finish(c):
-        for q in range(count):
-
-            @pl.when(z < q)
+                share(c).wait_send()
+
+            @pl.when(jnp.logical_not(mine(c)))
             def _():
-                to_right(c, q).wait_send()
-
-            @pl.when(z > q)
-            def _():
-                to_left(c, q).wait_send()
-
-            @pl.when(jnp.logical_and(q <= z, z < count - 1))
-            def _():
-                give_right(c, q).wait_send()
-
-            @pl.when(jnp.logical_and(q >= z, z > 0))
-            def _():
-                give_left(c, q).wait_send()
-
-    each(chunks, finish)
-    total_small = small[...]
-    for k in range(count - 1):
+                across(c).wait_send()
+
+        each(chunks, finish)
+
+    total = small[...]
+    for k in range(3):
         small_copy(k).wait()
-        total_small = total_small + landed[k]
-    small_out[...] = total_small
+        total = total + landed[k]
+    small_out[...] = total
 
 
 def line_sum(big, small):
     if lax.axis_size("rep") != 4 or lax.axis_size("ep") != 8:
         return lax.psum(big, "rep"), lax.psum(small, "rep")
     count, rows, cols = big.shape
-    own = big.reshape(count, 4, 2, rows // 8, cols)
-    chunks = 2 * count
+    chunks = 16
+    own = big.reshape(chunks, count * rows // chunks, cols)
     dma = pltpu.SemaphoreType.DMA
     out, small = pl.pallas_call(
         line_kernel,
@@ -681,7 +611,7 @@
             pltpu.VMEM(own.shape, BF16),
             pltpu.VMEM((3,) + small.shape, F32),
         ]
-        + [dma((chunks, 4))] * 8
+        + [dma((chunks,))] * 8
         + [dma((3,))] * 2,
         compiler_params=pltpu.CompilerParams(collective_id=5, has_side_effects=True, vmem_limit_bytes=40 << 20),
         name="line_sum",
@@ -859,6 +789,7 @@
 
 
 BLOCK = 256
+TILE = (512, 2048)
 
 
 def pack_rows(seqs, capacity):
@@ -885,22 +816,25 @@
     lane = lax.broadcasted_iota(jnp.int32, tab.shape, 1)
     row = lax.broadcasted_iota(jnp.int32, tab.shape, 0)
     chosen = jnp.logical_and(jnp.logical_and(tab == number[0].astype(F32), lane < top), row < lens[s])
-    chosen = jnp.where(chosen, 1.0, 0.0)
-    hit = jnp.sum(chosen, axis=1, keepdims=True)
-    weight = jnp.sum(chosen * pltpu.roll(tab, 128 - top, 1), axis=1, keepdims=True)
-    later = lax.broadcasted_iota(jnp.int32, (length, length), 0)
-    earlier = lax.broadcasted_iota(jnp.int32, (length, length), 1)
+    gates = jnp.where(chosen, pltpu.roll(tab, 128 - top, 1), 0.0).astype(BF16)
+    chosen = jnp.where(chosen, 1.0, 0.0).astype(BF16)
+    ones = jnp.ones((8, 128), BF16)
+    hit = dot(ones, chosen, 1, 1)
+    weight = dot(ones, gates, 1, 1)
+    earlier = lax.broadcasted_iota(jnp.int32, (length, length), 0)
+    later = lax.broadcasted_iota(jnp.int32, (length, length), 1)
     before = jnp.where(earlier < later, 1.0, 0.0).astype(BF16)
-    rank = dot(before, jnp.broadcast_to(hit, (length, 128)).astype(BF16), 1, 0)
+    rank = dot(hit.astype(BF16), before, 1, 0)
     slot = jnp.where(hit > 0.5, rank, -1.0)
-    slots[0] = jnp.where(lane < 64, slot, weight)
-    column = lax.broadcasted_iota(jnp.int32, (length, capacity), 1).astype(F32)
-    place = slot[:, 0:1] == column
+    slots[0, 0:8] = slot
+    slots[0, 8:16] = weight
+    column = lax.broadcasted_iota(jnp.int32, (capacity, length), 0).astype(F32)
+    place = column == slot[0:1]
     start = pl.multiple_of(starts[s], 16)
     span = pl.ds(start, capacity)
-    x[span] = dot(jnp.where(place, 1.0, 0.0).astype(BF16), mixed[0], 0, 0).astype(BF16)
-    dy[span] = dot(jnp.where(place, weight, 0.0).astype(BF16), cot[0], 0, 0).astype(BF16)
-    count = jnp.sum(hit).astype(jnp.int32)
+    x[span] = dot(jnp.where(place, 1.0, 0.0).astype(BF16), mixed[0], 1, 0).astype(BF16)
+    dy[span] = dot(jnp.where(place, weight[0:1], 0.0).astype(BF16), cot[0], 1, 0).astype(BF16)
+    count = jnp.sum(hit[0:1]).astype(jnp.int32)
     starts[s + 1] = start + (count + 15) // 16 * 16
 
     @pl.when(s == seqs - 1)
@@ -993,7 +927,7 @@
     return pl.pallas_call(
         kernel,
         out_shape=(
-            sds((seqs, length, 128), F32),
+            sds((seqs, 16, length), F32),
             sds((seqs + 1,), jnp.int32),
             sds((rows, hidden), BF16),
             sds((rows, 2 * hidden), BF16),
@@ -1011,7 +945,7 @@
                 AN,
             ],
             out_specs=(
-                pl.BlockSpec((1, length, 128), seq),
+                pl.BlockSpec((1, 16, length), seq),
                 pl.BlockSpec(memory_space=pltpu.SMEM),
                 AN,
                 AN,
@@ -1025,8 +959,8 @@
                 pltpu.VMEM(w_out.shape[1:], BF16),
                 pltpu.VMEM((rows, hidden), BF16),
                 pltpu.VMEM((rows, 2 * hidden), BF16),
-                pltpu.VMEM((min(hidden, 512), min(width, 1024)), F32),
-                pltpu.VMEM((2, min(hidden, 512), min(width, 1024)), BF16),
+                pltpu.VMEM(TILE, F32),
+                pltpu.VMEM((2,) + TILE, BF16),
                 dma((2,)),
                 dma((2,)),
                 dma((2,)),
@@ -1079,15 +1013,15 @@
     out_part, grad_part = refs[4 * local :]
     out_sum, grad_sum = None, None
     for j in range(local):
-        length = slots[j].shape[1]
-        column = lax.broadcasted_iota(jnp.int32, (length, capacity), 1).astype(F32)
-        place = slots[j][0, :, 0:1] == column
+        length = slots[j].shape[2]
+        column = lax.broadcasted_iota(jnp.int32, (capacity, length), 0).astype(F32)
+        place = column == slots[j][0, 0:1]
         span = pl.ds(pl.multiple_of(starts[j][s], 16), capacity)
         held = lax.broadcasted_iota(jnp.int32, (capacity, 1), 0) < starts[j][s + 1] - starts[j][s]
         rows = jnp.where(held, produced[j][span], 0.0).astype(BF16)
         grads = jnp.where(held, dx[j][span], 0.0).astype(BF16)
-        out = dot(jnp.where(place, slots[j][0, :, 64:65], 0.0).astype(BF16), rows, 1, 0)
-        grad = dot(jnp.where(place, 1.0, 0.0).astype(BF16), grads, 1, 0)
+        out = dot(jnp.where(place, slots[j][0, 8:9], 0.0).astype(BF16), rows, 0, 0)
+        grad = dot(jnp.where(place, 1.0, 0.0).astype(BF16), grads, 0, 0)
         out_sum = out if out_sum is None else out_sum + out
         grad_sum = grad if grad_sum is None else grad_sum + grad
     out_part[0] = out_sum.astype(BF16)
@@ -1096,7 +1030,7 @@
 
 def combine(starts, slots, produced, dx, capacity):
     local = len(starts)
-    seqs, length, _ = slots[0].shape
+    seqs, _, length = slots[0].shape
     width = produced[0].shape[1]
     seq = lambda i, *_: (i, 0, 0)
     two = lambda i, *_: (0, 0)
@@ -1107,7 +1041,7 @@
         grid_spec=pltpu.PrefetchScalarGridSpec(
             num_scalar_prefetch=local,
             grid=(seqs,),
-            in_specs=[pl.BlockSpec((1, length, 128), seq)] * local + [rows] * (2 * local),
+            in_specs=[pl.BlockSpec((1, 16, length), seq)] * local + [rows] * (2 * local),
             out_specs=(pl.BlockSpec((1, length, width), seq), pl.BlockSpec((1, length, width), seq)),
         ),
         compiler_params=pltpu.CompilerParams(dimension_semantics=("arbitrary",), vmem_limit_bytes=60 << 20),

time: 953 us -> 895 us (0.939)
  Pallas kernels: 898 us -> 836 us
    pallas_call x1, Pallas kernels: 264 us -> 211 us  [line_sum(): pl.pallas_call(line_kernel, out_shape=(sds(own.shape, BF16), sds(small.sh...]
  transfers between devices with their start and end apart: 5 -> 5, of which waited for: 0 -> 0; matrix products, arithmetic and copies ran while one was open for 3% -> 3% of each run, Pallas kernels for 89% -> 88%
where the time goes in v3:
time: 895 us; the launch traced here: 890 us
  Pallas kernels  836 us (93%)
  other arithmetic  27.9 us (3%)
  between operations  14.8 us (2%)
  local copies, waits for them, and re-layouts  10.1 us (1%)
    pallas_call x1, Pallas kernels, line_sum(): pl.pallas_call(line_kernel, out_shape=(sds(own.shape, BF16), sds(small.sh...  211 us
    pallas_call x1, Pallas kernels, back(): pl.pallas_call(back_kernel, out_shape=(sds(cot.shape, BF16), sds(cot.shap...  122 us
    pallas_call x1, Pallas kernels, front(): pl.pallas_call(front_kernel, out_shape=(sds((seqs, rows * ep, width), BF1...  115 us
    pallas_call x2, Pallas kernels, expert_pass(): pl.pallas_call(kernel, out_shape=(sds((seqs, 16, length), F32), sds((seqs...  97.8 us
    pallas_call x1, Pallas kernels, final(): pl.pallas_call(final_kernel, out_shape=(sds(tokens.shape, BF16), sds((8,...  81.9 us
    pallas_call x1, Pallas kernels, mix(): pl.pallas_call(mix_kernel, out_shape=(sds(tokens.shape, F32), sds((seqs,...  80.7 us
    pallas_call x1, Pallas kernels, attend_back(): pl.pallas_call(attend_back_kernel, out_shape=(sds(agrad.shape, BF16), sds...  45.6 us
    pallas_call x2, Pallas kernels, expert_tail(): pl.pallas_call(tail_kernel, out_shape=(sds((rows, width), BF16), sds((row...  35.6 us
  transfers between devices with their start and end apart: 5, of which 0 were waited for; matrix products, arithmetic and copies ran while one was open for 3% of the time, Pallas kernels for 88%

profile of v3, /device:TPU:0, one launch (start us, length us, event | category | flops | bytes accessed | tf_op | source)
XLA Modules:
  0.0 889.8 jit_solution(6927761623332565773)
XLA Ops:
  7.2 0.0 all-gather.2.cloned.1.call-start
  7.2 0.8 convert_element_type.83
  8.0 0.1 copy.34
  8.1 0.8 copy.35
  8.9 0.1 fusion.2
  9.0 2.3 pad_maximum_fusion.1
  11.3 0.0 all-gather.2.cloned.1.call-update
  11.3 0.0 reduce-scatter.9.cloned.1.call-start
  12.0 0.7 convert_element_type.76
  12.7 0.7 convert_element_type.77
  13.4 0.1 fusion.4
  13.4 0.7 maximum_convert_fusion.2
  14.1 0.6 select_maximum_fusion.1.pk
  14.7 114.6 %front.1 = (bf16[8,256,2048]{2,1,0:T(8,128)(2,1)}, bf16[3,2048,256]{2,1,0:T(8,128)(2,1)}, f32[8,8,128]{2,1,0:T(8,128)}) custom-call(bf16[8,32,2048]{2,1,0:T(8,128)(2,1)} %tok.5, bf16[256,2048]{1,0:T(8,128)(2,1)} %wq.1, bf16[256,2048]{1,0:T(8,128)(2,1)} %wk.1, bf16[256,2048]{1,0:T(8,128)(2,1)} %wv.1, f32[8,128]{1,0:T(8,128)} %select_maximum_fusion.1.pk), custom_call_target="tpu_custom_call" | custom-call | tf_op jit(solution)/shard_map/front/pallas_call | solution.py:291
  129.3 0.9 slice_reduce_fusion
  130.2 0.6 reshape_squeeze.7.kg
  130.8 0.6 reshape_squeeze.6.qg
  131.4 1.1 convert_reduce_fusion.lens
  132.5 0.0 copy-start.5
  132.5 0.1 convert_bitcast_fusion
  132.6 0.8 copy.33.living
  133.4 0.5 fusion.3
  133.9 0.8 pad_maximum_fusion.2
  134.8 1.4 fusion.6
  136.2 0.0 copy-done.5
  136.2 25.5 %attend.1 = (bf16[8,256,2048]{2,1,0:T(8,128)(2,1)}, f32[2,8,256,256]{3,2,1,0:T(8,128)}, bf16[3,8,256,256]{3,2,1,0:T(8,128)(2,1)}, bf16[8,256,256]{2,1,0:T(8,128)(2,1)}, bf16[8,256,2048]{2,1,0:T(8,128)(2,1)}) custom-call(s32[8]{0:T(128)} %copy-done.5, bf16[8,256,2048]{2,1,0:T(8,128)(2,1)} %get-tuple-element.55.tok, ...), custom_call_target="tpu_custom_call" | custom-call | flops 10000000000 | bytes 40000000 | tf_op jit(solution)/shard_map/attend/pallas_call | solution.py:664
  161.7 80.7 %mix.1 = (f32[8,32,2048]{2,1,0:T(8,128)}, bf16[8,256,2048]{2,1,0:T(8,128)(2,1)}) custom-call(bf16[8,8,32,2048]{3,2,1,0:T(8,128)(2,1)} %bitcast.44, bf16[8,32,2048]{2,1,0:T(8,128)(2,1)} %tok.5, f32[8,32,1]{2,1,0:T(8,128)} %copy.33.living, f32[1,2048]{1,0:T(1,128)} %bitcast.50), custom_call_target="tpu_custom_call" | custom-call | tf_op jit(solution)/shard_map/mix/pallas_call | solution.py:337
  242.4 0.0 all-gather.2.cloned.1.call-done.cot.table
  242.5 48.8 %expert_pass.2 = (f32[8,16,256]{2,1,0:T(8,128)}, s32[9]{0:T(128)}, bf16[1536,1024]{1,0:T(8,128)(2,1)}, bf16[1536,2048]{1,0:T(8,128)(2,1)}, bf16[1024,2048]{1,0:T(8,128)(2,1)}, /*index=5*/bf16[2048,2048]{1,0:T(8,128)(2,1)}) custom-call(s32[1]{0:T(128)} %bitcast.number, s32[8]{0:T(128)} %copy-done.5, bf16[8,256,2048]{2,1,0:T(8,128)(2,1)} %get-tuple-element.58.mixed, ...), custom_call_target="tpu_custom_call" | custom-call | flops 24999999488 | bytes 60000000 | tf_op jit(solution)/shard_map/expert_pass/pallas_call | solution.py:927
  291.2 0.0 reduce-scatter.9.cloned.1.call-update
  291.3 0.0 reduce-scatter.11.cloned.1.call-start
  291.3 49.0 %expert_pass.3 = (f32[8,16,256]{2,1,0:T(8,128)}, s32[9]{0:T(128)}, bf16[1536,1024]{1,0:T(8,128)(2,1)}, bf16[1536,2048]{1,0:T(8,128)(2,1)}, bf16[1024,2048]{1,0:T(8,128)(2,1)}, /*index=5*/bf16[2048,2048]{1,0:T(8,128)(2,1)}) custom-call(s32[1]{0:T(128)} %bitcast.8.number, s32[8]{0:T(128)} %copy-done.5, bf16[8,256,2048]{2,1,0:T(8,128)(2,1)} %get-tuple-element.58.mixed, ...), custom_call_target="tpu_custom_call" | custom-call | flops 24999999488 | bytes 60000000 | tf_op jit(solution)/shard_map/expert_pass/pallas_call | solution.py:927
  340.3 0.0 reduce-scatter.11.cloned.1.call-update
  340.4 0.0 reduce-scatter.5.cloned.1.call-start
  340.4 0.5 reduce-scatter.5.cloned.1.call-update
  340.9 0.0 reduce-scatter.7.cloned.1.call-start
  341.0 0.5 reduce-scatter.7.cloned.1.call-update
  341.5 17.9 %expert_tail.2 = (bf16[1536,2048]{1,0:T(8,128)(2,1)}, bf16[1536,2048]{1,0:T(8,128)(2,1)}) custom-call(s32[9]{0:T(128)} %get-tuple-element.59.starts.refs_0_, bf16[1536,1024]{1,0:T(8,128)(2,1)} %get-tuple-element.64.act, bf16[1536,2048]{1,0:T(8,128)(2,1)} %get-tuple-element.65.dgu, bf16[2,2048,2048]{2,1,0:T(8,128)(2,1)} %w_in.7, bf16[2,1024,2048]{2,1,0:T(8,128)(2,1)} %w_out.7), custom_call_target="tpu_custom_call" | custom-call | flops 12000000000 | bytes 30000000 | tf_op jit(solution)/shard_map/expert_tail/pallas_call | solution.py:987
  359.4 17.7 %expert_tail.3 = (bf16[1536,2048]{1,0:T(8,128)(2,1)}, bf16[1536,2048]{1,0:T(8,128)(2,1)}) custom-call(s32[9]{0:T(128)} %get-tuple-element.61.starts.refs_1_, bf16[1536,1024]{1,0:T(8,128)(2,1)} %get-tuple-element.67.act, bf16[1536,2048]{1,0:T(8,128)(2,1)} %get-tuple-element.68.dgu, bf16[2,2048,2048]{2,1,0:T(8,128)(2,1)} %w_in.7, bf16[2,1024,2048]{2,1,0:T(8,128)(2,1)} %w_out.7), custom_call_target="tpu_custom_call" | custom-call | flops 12000000000 | bytes 30000000 | tf_op jit(solution)/shard_map/expert_tail/pallas_call | solution.py:987
  377.1 20.8 %combine.1 = (bf16[8,256,2048]{2,1,0:T(8,128)(2,1)}, bf16[8,256,2048]{2,1,0:T(8,128)(2,1)}) custom-call(s32[9]{0:T(128)} %get-tuple-element.59.starts.refs_0_, s32[9]{0:T(128)} %get-tuple-element.61.starts.refs_1_, f32[8,16,256]{2,1,0:T(8,128)} %get-tuple-element.62.refs_2_, f32[8,16,256]{2,1,0:T(8,128)} %get-tuple-element.63.refs_3_, ...), custom_call_target="tpu_custom_call" | custom-call | flops 3000000000 | bytes 40000000 | tf_op jit(solution)/shard_map/combine/pallas_call | solution.py:1038
  397.9 121.7 %back.1 = (bf16[8,32,2048]{2,1,0:T(8,128)(2,1)}, f32[8,32,2048]{2,1,0:T(8,128)}, f32[1,2048]{1,0:T(1,128)}, bf16[8,256,2048]{2,1,0:T(8,128)(2,1)}) custom-call(bf16[8,8,32,2048]{3,2,1,0:T(8,128)(2,1)} %bitcast.43, bf16[8,8,32,2048]{3,2,1,0:T(8,128)(2,1)} %bitcast.42, f32[8,32,2048]{2,1,0:T(8,128)} %get-tuple-element.74.middle, bf16[8,32,2048]{2,1,0:T(8,128)(2,1)} %cot.1, ...), custom_call_target="tpu_custom_call" | custom-call | tf_op jit(solution)/shard_map/back/pallas_call | solution.py:391
  519.5 0.0 copy-start.4
  519.5 45.6 %attend_back.1 = (bf16[8,256,2048]{2,1,0:T(8,128)(2,1)}, bf16[3,2048,256]{2,1,0:T(8,128)(2,1)}, bf16[256,2048]{1,0:T(8,128)(2,1)}, f32[8,128]{1,0:T(8,128)}) custom-call(s32[8]{0:T(128)} %copy-done.5, bf16[8,256,2048]{2,1,0:T(8,128)(2,1)} %get-tuple-element.76.agrad, bf16[8,256,2048]{2,1,0:T(8,128)(2,1)} %get-tuple-element.77.normed, ...), custom_call_target="tpu_custom_call" | custom-call | flops 20000000000 | bytes 40000000 | tf_op jit(solution)/shard_map/attend_back/pallas_call | solution.py:753
  565.2 0.7 slice.51
  565.9 0.0 copy-done.4
  565.9 0.6 select_maximum_fusion.others
  566.5 81.9 %final.1 = (bf16[8,32,2048]{2,1,0:T(8,128)(2,1)}, f32[8,128]{1,0:T(8,128)}, bf16[3,256,2048]{2,1,0:T(8,128)(2,1)}) custom-call(bf16[8,8,32,2048]{3,2,1,0:T(8,128)(2,1)} %bitcast.41, bf16[3,2048,256]{2,1,0:T(8,128)(2,1)} %get-tuple-element.82.wgrad, bf16[8,32,2048]{2,1,0:T(8,128)(2,1)} %tok.5, f32[8,32,2048]{2,1,0:T(8,128)} %get-tuple-element.83.mgrad, ...), custom_call_target="tpu_custom_call" | custom-call | tf_op jit(solution)/shard_map/final/pallas_call | solution.py:483
  648.4 0.0 copy-done.3
  648.5 0.0 copy-start
  648.5 2.3 pad_maximum_fusion
  650.7 0.0 copy-done
  650.7 211.4 %line_sum.1 = (bf16[16,64,2048]{2,1,0:T(8,128)(2,1)S(1)}, f32[8,128]{1,0:T(8,128)S(1)}) custom-call(bf16[16,64,2048]{2,1,0:T(8,128)(2,1)S(1)} %bitcast.40, f32[8,128]{1,0:T(8,128)S(1)} %copy-done), custom_call_target="tpu_custom_call" | custom-call | tf_op jit(solution)/shard_map/line_sum/pallas_call | solution.py:604
  862.2 0.6 dynamic-slice_bitcast_fusion
  862.8 0.6 dynamic-slice_bitcast_fusion.1
  863.4 0.6 slice_bitcast_fusion
  863.9 0.5 fusion.5
  864.4 1.6 bitcast_convert_fusion
  866.1 1.6 bitcast_convert_fusion.1
  867.7 1.6 bitcast_convert_fusion.2
  869.3 1.6 bitcast_convert_fusion.3
  871.0 3.8 maximum_convert_fusion.1
  874.8 6.3 maximum_convert_fusion
  881.1 1.0 copy.40
  882.1 1.0 copy.41
  (12 shorter events, 0.0 us)
Async XLA Ops:
  7.2 235.3 %all-gather.2.cloned.1.call-start = ((), (), s32[]{:S(2)}) async-start(), calls=%async_computation.4 | async-start | bytes 10027008 | tf_op jit(solution)/shard_map/all_gather | solution.py:1075
  11.3 859.6 %reduce-scatter.9.cloned.1.call-start = ((), (), s32[]{:S(2)}) async-start(), calls=%async_computation.7 | async-start | bytes 5242880 | tf_op jit(solution)/shard_map/reduce_scatter | solution.py:1109
  132.5 3.7 copy-start.5
  291.3 579.7 %reduce-scatter.11.cloned.1.call-start = ((), (), s32[]{:S(2)}) async-start(), calls=%async_computation.8 | async-start | bytes 5242880 | tf_op jit(solution)/shard_map/reduce_scatter | solution.py:1109
  340.4 534.5 %reduce-scatter.5.cloned.1.call-start = ((), (), s32[]{:S(2)}) async-start(), calls=%async_computation.5 | async-start | bytes 10485760 | tf_op jit(solution)/shard_map/reduce_scatter | solution.py:1110
  340.9 533.9 %reduce-scatter.7.cloned.1.call-start = ((), (), s32[]{:S(2)}) async-start(), calls=%async_computation.6 | async-start | bytes 10485760 | tf_op jit(solution)/shard_map/reduce_scatter | solution.py:1110
  519.5 46.4 %copy-start.4 = (f32[1,2048]{1,0:T(1,128)S(1)}, f32[1,2048]{1,0:T(1,128)}, u32[]{:S(2)}) copy-start(f32[1,2048]{1,0:T(1,128)} %get-tuple-element.84) | copy-start | bytes 24580
  566.5 81.9 %copy-start.3 = (bf16[256,2048]{1,0:T(8,128)(2,1)S(1)}, bf16[256,2048]{1,0:T(8,128)(2,1)}, u32[]{:S(2)}) copy-start(bf16[256,2048]{1,0:T(8,128)(2,1)} %get-tuple-element.88) | copy-start | bytes 3145732
  648.5 2.3 copy-start
  874.8 6.3 copy-start.1
  874.8 7.3 copy-start.2
Sparse Core Ops, SparseCore 0:
  11.5 112.1 all-gather.1
  291.4 85.6 reduce-scatter.8
  379.3 77.3 reduce-scatter.10
  458.9 145.1 reduce-scatter.4
  606.3 209.7 reduce-scatter.6

commit v4 on v3

--- a/solution.py
+++ b/solution.py
@@ -345,16 +345,14 @@
     )(part, tokens, living, gain)
 
 
-def back_kernel(gpart, opart, middle, cot, living, gain, result, mgrad, ggrad, full, own, *scratch):
+def back_kernel(gpart, middle, cot, living, gain, mgrad, ggrad, full, own, *scratch):
     at = Place()
     seqs = cot.shape[0]
     n = Reduce.sems
     rg = Reduce(at, gpart, *scratch[:n])
-    ro = Reduce(at, opart, *scratch[n : 2 * n])
-    gather = Gather(at, own, full, *scratch[2 * n :])
+    gather = Gather(at, own, full, *scratch[n:])
     at.greet((at.xn, at.yn, at.sb))
     each(seqs, rg.start)
-    each(seqs, ro.start)
     each(seqs, rg.hop1)
     each(seqs, rg.hop2)
     ggrad[...] = jnp.zeros_like(ggrad)
@@ -368,40 +366,31 @@
 
     each(seqs, rows)
     gather_tail(seqs, gather)
-    each(seqs, ro.hop1)
-    each(seqs, ro.hop2)
-
-    def out(s):
-        result[s] = (middle[s] + ro.total(s)).astype(BF16)
-
-    each(seqs, out)
-    each(seqs, rg.finish, ro.finish)
-
-
-def back(gpart, opart, middle, cot, living, gain):
+    each(seqs, rg.finish)
+
+
+def back(gpart, middle, cot, living, gain):
     seqs, rows, width = cot.shape
     ep = lax.axis_size("ep")
     if ep != 8:
         mixed_grad = lax.psum_scatter(gpart, "ep", scatter_dimension=1, tiled=True).astype(F32)
-        moe = lax.psum_scatter(opart, "ep", scatter_dimension=1, tiled=True).astype(F32)
         mg, ag, backs = ffn_back_rows(mixed_grad, middle, cot, living, gain)
         full = lax.all_gather(ag, "ep", axis=1, tiled=True)
-        return (middle + moe).astype(BF16), mg, jnp.sum(backs, axis=(0, 1))[None], full
-    gpart, opart = (p.reshape(seqs, ep, rows, width) for p in (gpart, opart))
+        return mg, jnp.sum(backs, axis=(0, 1))[None], full
+    gpart = gpart.reshape(seqs, ep, rows, width)
     return pl.pallas_call(
         back_kernel,
         out_shape=(
-            sds(cot.shape, BF16),
             sds(cot.shape, F32),
             sds((1, width), F32),
             sds((seqs, rows * ep, width), BF16),
         ),
-        in_specs=[VM] * 6,
-        out_specs=(VM, VM, VM, AN),
-        scratch_shapes=[pltpu.VMEM(cot.shape, BF16)] + 2 * Reduce.scratch(gpart) + Gather.scratch(seqs),
+        in_specs=[VM] * 5,
+        out_specs=(VM, VM, AN),
+        scratch_shapes=[pltpu.VMEM(cot.shape, BF16)] + Reduce.scratch(gpart) + Gather.scratch(seqs),
         compiler_params=pltpu.CompilerParams(collective_id=3, **COMM),
         name="back",
-    )(gpart, opart, middle, cot, living, gain)
+    )(gpart, middle, cot, living, gain)
 
 
 def final_kernel(part, wgrad, tok, mgrad, gain, others, tgrad, small, wrows, ggrad, parcel, landed, *scratch):
@@ -497,7 +486,12 @@
     )(part, wgrad, tokens, mgrad, gain, others)
 
 
-def line_kernel(own, small, out, small_out, held, met, landed, os, or_, ps, pr, qs, qr, fs, fr, ss, sr):
+def line_kernel(
+    own, small, opart, mid_rows, out, small_out, result, held, met, landed, os, or_, ps, pr, qs, qr, fs, fr, ss, sr, *scratch
+):
+    at = Place()
+    reduce = Reduce(at, opart, *scratch)
+    seqs = opart.shape[0]
     z = lax.axis_index("rep")
     ep = lax.axis_index("ep")
     chunks = own.shape[0]
@@ -511,7 +505,9 @@
     others = [lax.rem(z + k, 4) for k in range(1, 4)]
     for dev in others:
         pl.semaphore_signal(barrier, inc=1, device_id=(dev, ep), device_id_type=MESH)
-    pl.semaphore_wait(barrier, 3)
+    for dev in (at.xn, at.yn, at.sb):
+        pl.semaphore_signal(barrier, inc=1, device_id=(z, dev), device_id_type=MESH)
+    pl.semaphore_wait(barrier, 6)
     inner = jnp.logical_and(z > 0, z < 3)
     middle, partner, outer = 1 + z // 3, 3 - z, 3 * (z - 1)
 
@@ -529,6 +525,9 @@
 
     def small_copy(k):
         return push(small, landed.at[k], ss.at[k], sr.at[k], others[k])
+
+    def out_rows(s):
+        result[s] = (mid_rows[s] + reduce.total(s)).astype(BF16)
 
     for k in range(3):
         small_copy(k).start()
@@ -536,6 +535,10 @@
     @pl.when(jnp.logical_not(inner))
     def _():
         each(chunks, lambda c: inward(c).start())
+        each(seqs, reduce.start)
+        each(seqs, reduce.hop1)
+        each(seqs, reduce.hop2)
+        each(seqs, out_rows)
         each(chunks, lambda c: outward(c).wait_recv())
         each(chunks, lambda c: inward(c).wait_send())
 
@@ -544,7 +547,16 @@
 
     @pl.when(inner)
     def _():
+        each(seqs, reduce.start)
+        half = seqs // 2
+
         def run(c, _):
+            for step, lag in ((reduce.hop1, 0), (reduce.hop2, half), (out_rows, 2 * half)):
+
+                @pl.when(jnp.logical_and(c >= lag, c < seqs + lag))
+                def _():
+                    step(c - lag)
+
             @pl.when(c < chunks)
             def _():
                 inward(c).wait_recv()
@@ -587,6 +599,7 @@
 
         each(chunks, finish)
 
+    each(seqs, reduce.finish)
     total = small[...]
     for k in range(3):
         small_copy(k).wait()
@@ -594,29 +607,34 @@
     small_out[...] = total
 
 
-def line_sum(big, small):
+def line_sum(big, small, opart, middle):
     if lax.axis_size("rep") != 4 or lax.axis_size("ep") != 8:
-        return lax.psum(big, "rep"), lax.psum(small, "rep")
+        moe = lax.psum_scatter(opart, "ep", scatter_dimension=1, tiled=True).astype(F32)
+        return lax.psum(big, "rep"), lax.psum(small, "rep"), (middle + moe).astype(BF16)
+    seqs, tokens, width = middle.shape
+    opart = opart.reshape(seqs, 8, tokens, width)
+    assert 2 * seqs <= 18
     count, rows, cols = big.shape
     chunks = 16
     own = big.reshape(chunks, count * rows // chunks, cols)
     dma = pltpu.SemaphoreType.DMA
-    out, small = pl.pallas_call(
+    out, small, result = pl.pallas_call(
         line_kernel,
-        out_shape=(sds(own.shape, BF16), sds(small.shape, F32)),
-        in_specs=[VM, VM],
-        out_specs=(VM, VM),
+        out_shape=(sds(own.shape, BF16), sds(small.shape, F32), sds(middle.shape, BF16)),
+        in_specs=[VM] * 4,
+        out_specs=(VM, VM, VM),
         scratch_shapes=[
             pltpu.VMEM(own.shape, BF16),
             pltpu.VMEM(own.shape, BF16),
             pltpu.VMEM((3,) + small.shape, F32),
         ]
         + [dma((chunks,))] * 8
-        + [dma((3,))] * 2,
-        compiler_params=pltpu.CompilerParams(collective_id=5, has_side_effects=True, vmem_limit_bytes=40 << 20),
+        + [dma((3,))] * 2
+        + Reduce.scratch(opart),
+        compiler_params=pltpu.CompilerParams(collective_id=5, **COMM),
         name="line_sum",
-    )(own, small)
-    return out.reshape(big.shape), small
+    )(own, small, opart, middle)
+    return out.reshape(big.shape), small, result
 
 
 def dot(a, b, ca, cb):
@@ -789,33 +807,18 @@
 
 
 BLOCK = 256
-TILE = (512, 2048)
 
 
 def pack_rows(seqs, capacity):
     return -(-seqs * capacity // BLOCK) * BLOCK + BLOCK
 
 
-def expert_kernel(
-    capacity, top, j, number, lens, mixed, cot, table, w_in, w_out, slots, starts, act, dgu, out_grad, in_grad,
-    x, dy, wi, wo, acts, dgus, acc, stage, wsem, ssem, rsem,
-):
-    s = pl.program_id(0)
-    seqs = pl.num_programs(0)
-    length, width = mixed.shape[1:]
-    hidden = wo.shape[0]
-    loads = [pltpu.make_async_copy(w_in.at[j], wi, wsem.at[0]), pltpu.make_async_copy(w_out.at[j], wo, wsem.at[1])]
-
-    @pl.when(s == 0)
-    def _():
-        for copy in loads:
-            copy.start()
-        starts[0] = 0
-
-    tab = table[0].astype(F32)
+def packed_slots(number, table, length_live, top):
+    tab = table.astype(F32)
+    length = tab.shape[0]
     lane = lax.broadcasted_iota(jnp.int32, tab.shape, 1)
     row = lax.broadcasted_iota(jnp.int32, tab.shape, 0)
-    chosen = jnp.logical_and(jnp.logical_and(tab == number[0].astype(F32), lane < top), row < lens[s])
+    chosen = jnp.logical_and(jnp.logical_and(tab == number, lane < top), row < length_live)
     gates = jnp.where(chosen, pltpu.roll(tab, 128 - top, 1), 0.0).astype(BF16)
     chosen = jnp.where(chosen, 1.0, 0.0).astype(BF16)
     ones = jnp.ones((8, 128), BF16)
@@ -823,116 +826,152 @@
     weight = dot(ones, gates, 1, 1)
     earlier = lax.broadcasted_iota(jnp.int32, (length, length), 0)
     later = lax.broadcasted_iota(jnp.int32, (length, length), 1)
-    before = jnp.where(earlier < later, 1.0, 0.0).astype(BF16)
-    rank = dot(hit.astype(BF16), before, 1, 0)
-    slot = jnp.where(hit > 0.5, rank, -1.0)
-    slots[0, 0:8] = slot
-    slots[0, 8:16] = weight
-    column = lax.broadcasted_iota(jnp.int32, (capacity, length), 0).astype(F32)
-    place = column == slot[0:1]
-    start = pl.multiple_of(starts[s], 16)
-    span = pl.ds(start, capacity)
-    x[span] = dot(jnp.where(place, 1.0, 0.0).astype(BF16), mixed[0], 1, 0).astype(BF16)
-    dy[span] = dot(jnp.where(place, weight[0:1], 0.0).astype(BF16), cot[0], 1, 0).astype(BF16)
-    count = jnp.sum(hit[0:1]).astype(jnp.int32)
-    starts[s + 1] = start + (count + 15) // 16 * 16
+    rank = dot(hit.astype(BF16), jnp.where(earlier < later, 1.0, 0.0).astype(BF16), 1, 0)
+    return jnp.where(hit > 0.5, rank, -1.0), weight, jnp.sum(hit[0:1]).astype(jnp.int32)
+
+
+def forward_blocks(blocks, x, dy, wi, wo, acts, dgus):
+    hidden = wo.shape[0]
+    part = min(hidden, 512)
+
+    def forward(b, _):
+        rows = pl.ds(pl.multiple_of(b * BLOCK, BLOCK), BLOCK)
+        for h in range(hidden // part):
+            gcols, ucols = pl.ds(h * part, part), pl.ds(hidden + h * part, part)
+            gate = dot(x[rows], wi[:, gcols], 1, 0)
+            up = dot(x[rows], wi[:, ucols], 1, 0)
+            dact = dot(dy[rows], wo[gcols], 1, 1)
+            sig = 1.0 / (1.0 + jnp.exp(-gate))
+            silu = gate * sig
+            acts[rows, gcols] = (silu * up).astype(BF16)
+            dgus[rows, gcols] = (dact * up * sig * (1.0 + gate * (1.0 - sig))).astype(BF16)
+            dgus[rows, ucols] = (dact * silu).astype(BF16)
+        return 0
+
+    lax.fori_loop(0, blocks, forward, 0)
+
+
+def gradient_tiles(blocks, left, right, result, acc, stage, ssem, busy):
+    tr, tc = acc.shape
+    down, across = result.shape[0] // tr, result.shape[1] // tc
+
+    def tile(t, _):
+        rt, ct = t // across, lax.rem(t, across)
+        left_cols = pl.ds(pl.multiple_of(rt * tr, tr), tr)
+        right_cols = pl.ds(pl.multiple_of(ct * tc, tc), tc)
+
+        def step(b, _):
+            rows = pl.ds(pl.multiple_of(b * BLOCK, BLOCK), BLOCK)
+            piece = dot(left[rows, left_cols], right[rows, right_cols], 0, 0)
+
+            @pl.when(b == 0)
+            def _():
+                acc[...] = piece
+
+            @pl.when(b > 0)
+            def _():
+                acc[...] += piece
+
+            return 0
+
+        @pl.when(blocks == 0)
+        def _():
+            acc[...] = jnp.zeros_like(acc)
+
+        lax.fori_loop(0, blocks, step, 0)
+        k = lax.rem(t, 2)
+        out = pltpu.make_async_copy(stage.at[k], result.at[left_cols, right_cols], ssem.at[k])
+
+        @pl.when(jnp.logical_or(t >= 2, busy))
+        def _():
+            out.wait()
+
+        stage[k] = acc[...].astype(BF16)
+        out.start()
+        return 0
+
+    lax.fori_loop(0, down * across, tile, 0)
+
+
+def drain_tiles(result, acc, stage, ssem):
+    tr, tc = acc.shape
+    for k in range(2):
+        pltpu.make_async_copy(stage.at[k], result.at[pl.ds(0, tr), pl.ds(0, tc)], ssem.at[k]).wait()
+
+
+def first_kernel(
+    capacity, top, number, lens, mixed, cot, table, w_in, w_out,
+    slots0, slots1, starts, act, dgu, x_all, dy_all, out_grad,
+    x, dy, wi, wo, acts, dgus, acc, stage, wsem, ssem, rsem,
+):
+    s = pl.program_id(0)
+    seqs = pl.num_programs(0)
+    width = mixed.shape[2]
+    loads = [pltpu.make_async_copy(w_in.at[0], wi, wsem.at[0]), pltpu.make_async_copy(w_out.at[0], wo, wsem.at[1])]
+
+    @pl.when(s == 0)
+    def _():
+        for copy in loads:
+            copy.start()
+        starts[0, 0] = 0
+        starts[1, 0] = 0
+
+    spread, gate_spread, spans = [], [], []
+    for j, slots in enumerate((slots0, slots1)):
+        slot, weight, count = packed_slots((number[0] + j).astype(F32), table[0], lens[s], top)
+        slots[0, 0:8] = slot
+        slots[0, 8:16] = weight
+        place = lax.broadcasted_iota(jnp.int32, (capacity, slot.shape[1]), 0).astype(F32) == slot[0:1]
+        spread.append(jnp.where(place, 1.0, 0.0).astype(BF16))
+        gate_spread.append(jnp.where(place, weight[0:1], 0.0).astype(BF16))
+        start = pl.multiple_of(starts[j, s], 16)
+        spans.append(pl.ds(start, capacity))
+        starts[j, s + 1] = start + (count + 15) // 16 * 16
+    for target, source, weights in ((x, mixed, spread), (dy, cot, gate_spread)):
+        packed = dot(jnp.concatenate(weights, axis=0), source[0], 1, 0).astype(BF16)
+        for j in range(2):
+            target[j, spans[j]] = packed[j * capacity : (j + 1) * capacity]
 
     @pl.when(s == seqs - 1)
     def _():
-        total = starts[seqs]
-        tail = pl.ds(pl.multiple_of(start + capacity, 16), BLOCK)
-        x[tail] = jnp.zeros((BLOCK, width), BF16)
-        dy[tail] = jnp.zeros((BLOCK, width), BF16)
-        blocks = (total + BLOCK - 1) // BLOCK
+        for j in range(2):
+            tail = pl.ds(pl.multiple_of(starts[j, s] + capacity, 16), BLOCK)
+            x[j, tail] = jnp.zeros((BLOCK, width), BF16)
+            dy[j, tail] = jnp.zeros((BLOCK, width), BF16)
+        saves = [pltpu.make_async_copy(x, x_all, rsem.at[0]), pltpu.make_async_copy(dy.at[1], dy_all, rsem.at[1])]
+        for copy in saves:
+            copy.start()
+        blocks = (starts[0, seqs] + BLOCK - 1) // BLOCK
         for copy in loads:
             copy.wait()
-        part = min(hidden, 512)
-
-        def forward(b, _):
-            rows = pl.ds(pl.multiple_of(b * BLOCK, BLOCK), BLOCK)
-            for h in range(hidden // part):
-                gcols, ucols = pl.ds(h * part, part), pl.ds(hidden + h * part, part)
-                gate = dot(x[rows], wi[:, gcols], 1, 0)
-                up = dot(x[rows], wi[:, ucols], 1, 0)
-                dact = dot(dy[rows], wo[gcols], 1, 1)
-                sig = 1.0 / (1.0 + jnp.exp(-gate))
-                silu = gate * sig
-                acts[rows, gcols] = (silu * up).astype(BF16)
-                dgus[rows, gcols] = (dact * up * sig * (1.0 + gate * (1.0 - sig))).astype(BF16)
-                dgus[rows, ucols] = (dact * silu).astype(BF16)
-            return 0
-
-        lax.fori_loop(0, blocks, forward, 0)
-        saves = [pltpu.make_async_copy(acts, act, rsem.at[0]), pltpu.make_async_copy(dgus, dgu, rsem.at[1])]
-        for copy in saves:
+        forward_blocks(blocks, x.at[0], dy.at[0], wi, wo, acts, dgus)
+        saves += [pltpu.make_async_copy(acts, act, rsem.at[2]), pltpu.make_async_copy(dgus, dgu, rsem.at[3])]
+        for copy in saves[2:]:
             copy.start()
-
-        tr, tc = acc.shape
-
-        def grads(left, right, result, first):
-            down, across = result.shape[0] // tr, result.shape[1] // tc
-
-            def tile(t, _):
-                rt, ct = t // across, lax.rem(t, across)
-                left_cols = pl.ds(pl.multiple_of(rt * tr, tr), tr)
-                right_cols = pl.ds(pl.multiple_of(ct * tc, tc), tc)
-
-                def step(b, _):
-                    rows = pl.ds(pl.multiple_of(b * BLOCK, BLOCK), BLOCK)
-                    piece = dot(left[rows, left_cols], right[rows, right_cols], 0, 0)
-
-                    @pl.when(b == 0)
-                    def _():
-                        acc[...] = piece
-
-                    @pl.when(b > 0)
-                    def _():
-                        acc[...] += piece
-
-                    return 0
-
-                @pl.when(blocks == 0)
-                def _():
-                    acc[...] = jnp.zeros_like(acc)
-
-                lax.fori_loop(0, blocks, step, 0)
-                k = lax.rem(t, 2)
-                out = pltpu.make_async_copy(stage.at[k], result.at[left_cols, right_cols], ssem.at[k])
-
-                @pl.when(jnp.logical_or(t >= 2, not first))
-                def _():
-                    out.wait()
-
-                stage[k] = acc[...].astype(BF16)
-                out.start()
-                return 0
-
-            lax.fori_loop(0, down * across, tile, 0)
-
-        grads(acts, dy, out_grad, True)
-        grads(x, dgus, in_grad, False)
-        for k in range(2):
-            pltpu.make_async_copy(stage.at[k], in_grad.at[pl.ds(0, tr), pl.ds(0, tc)], ssem.at[k]).wait()
+        gradient_tiles(blocks, acts, dy.at[0], out_grad, acc, stage, ssem, False)
+        drain_tiles(out_grad, acc, stage, ssem)
         for copy in saves:
             copy.wait()
 
 
-def expert_pass(j, number, lens, mixed, cot, w_in, w_out, capacity, top):
+def expert_first(number, lens, mixed, cot, w_in, w_out, capacity, top):
     seqs, length, width = mixed.shape
     hidden = w_out.shape[1]
     rows = pack_rows(seqs, capacity)
     dma = pltpu.SemaphoreType.DMA
-    kernel = functools.partial(expert_kernel, capacity, top, j)
     seq = lambda i, *_: (i, 0, 0)
+    slot_spec = pl.BlockSpec((1, 16, length), seq)
     return pl.pallas_call(
-        kernel,
+        functools.partial(first_kernel, capacity, top),
         out_shape=(
             sds((seqs, 16, length), F32),
-            sds((seqs + 1,), jnp.int32),
+            sds((seqs, 16, length), F32),
+            sds((2, seqs + 1), jnp.int32),
             sds((rows, hidden), BF16),
             sds((rows, 2 * hidden), BF16),
+            sds((2, rows, width), BF16),
+            sds((rows, width), BF16),
             sds((hidden, width), BF16),
-            sds((width, 2 * hidden), BF16),
         ),
         grid_spec=pltpu.PrefetchScalarGridSpec(
             num_scalar_prefetch=2,
@@ -944,14 +983,124 @@
                 AN,
                 AN,
             ],
-            out_specs=(
-                pl.BlockSpec((1, 16, length), seq),
-                pl.BlockSpec(memory_space=pltpu.SMEM),
-                AN,
-                AN,
-                AN,
-                AN,
-            ),
+            out_specs=(slot_spec, slot_spec, pl.BlockSpec(memory_space=pltpu.SMEM), AN, AN, AN, AN, AN),
+            scratch_shapes=[
+                pltpu.VMEM((2, rows, width), BF16),
+                pltpu.VMEM((2, rows, width), BF16),
+                pltpu.VMEM(w_in.shape[1:], BF16),
+                pltpu.VMEM(w_out.shape[1:], BF16),
+                pltpu.VMEM((rows, hidden), BF16),
+                pltpu.VMEM((rows, 2 * hidden), BF16),
+                pltpu.VMEM((512, 1024), F32),
+                pltpu.VMEM((2, 512, 1024), BF16),
+                dma((2,)),
+                dma((2,)),
+                dma((4,)),
+            ],
+        ),
+        compiler_params=pltpu.CompilerParams(dimension_semantics=("arbitrary",), vmem_limit_bytes=62 << 20),
+        cost_estimate=pl.CostEstimate(flops=2 * 10**10, bytes_accessed=6 * 10**7, transcendentals=10**6),
+        name="expert_first",
+    )(number, lens, mixed, cot, cot, w_in, w_out)
+
+
+def in_grad_kernel(starts, x_all, dgu, in_grad, x, dgus, acc, stage, lsem, ssem):
+    blocks = (starts[0, starts.shape[1] - 1] + BLOCK - 1) // BLOCK
+
+    def load(b):
+        rows = pl.ds(pl.multiple_of(b * BLOCK, BLOCK), BLOCK)
+        return (
+            pltpu.make_async_copy(x_all.at[0, rows], x.at[rows], lsem.at[0, b]),
+            pltpu.make_async_copy(dgu.at[rows], dgus.at[rows], lsem.at[1, b]),
+        )
+
+    def run(b, action):
+        for copy in load(b):
+            getattr(copy, action)()
+        return 0
+
+    lax.fori_loop(0, blocks, lambda b, _: run(b, "start"), 0)
+    lax.fori_loop(0, blocks, lambda b, _: run(b, "wait"), 0)
+    gradient_tiles(blocks, x, dgus, in_grad, acc, stage, ssem, False)
+    drain_tiles(in_grad, acc, stage, ssem)
+
+
+def first_in_grad(starts, x_all, dgu):
+    rows, width = x_all.shape[1:]
+    dma = pltpu.SemaphoreType.DMA
+    return pl.pallas_call(
+        in_grad_kernel,
+        out_shape=sds((width, dgu.shape[1]), BF16),
+        grid_spec=pltpu.PrefetchScalarGridSpec(
+            num_scalar_prefetch=1,
+            grid=(1,),
+            in_specs=[AN, AN],
+            out_specs=AN,
+            scratch_shapes=[
+                pltpu.VMEM((rows, width), BF16),
+                pltpu.VMEM(dgu.shape, BF16),
+                pltpu.VMEM((512, 2048), F32),
+                pltpu.VMEM((2, 512, 2048), BF16),
+                dma((2, rows // BLOCK)),
+                dma((2,)),
+            ],
+        ),
+        compiler_params=pltpu.CompilerParams(dimension_semantics=("arbitrary",), vmem_limit_bytes=60 << 20),
+        cost_estimate=pl.CostEstimate(flops=10**10, bytes_accessed=2 * 10**7, transcendentals=0),
+        name="first_in_grad",
+    )(starts, x_all, dgu)
+
+
+def second_kernel(
+    starts, x_all, dy_all, w_in, w_out, act, dgu, out_grad, in_grad,
+    x, dy, wi, wo, acts, dgus, acc, stage, wsem, lsem, ssem, rsem,
+):
+    blocks = (starts[1, starts.shape[1] - 1] + BLOCK - 1) // BLOCK
+    loads = [pltpu.make_async_copy(w_in.at[1], wi, wsem.at[0]), pltpu.make_async_copy(w_out.at[1], wo, wsem.at[1])]
+
+    def load(b, action):
+        rows = pl.ds(pl.multiple_of(b * BLOCK, BLOCK), BLOCK)
+        for copy in (
+            pltpu.make_async_copy(x_all.at[1, rows], x.at[rows], lsem.at[0, b]),
+            pltpu.make_async_copy(dy_all.at[rows], dy.at[rows], lsem.at[1, b]),
+        ):
+            getattr(copy, action)()
+        return 0
+
+    for copy in loads:
+        copy.start()
+    lax.fori_loop(0, blocks, lambda b, _: load(b, "start"), 0)
+    for copy in loads:
+        copy.wait()
+    lax.fori_loop(0, blocks, lambda b, _: load(b, "wait"), 0)
+    forward_blocks(blocks, x, dy, wi, wo, acts, dgus)
+    saves = [pltpu.make_async_copy(acts, act, rsem.at[0]), pltpu.make_async_copy(dgus, dgu, rsem.at[1])]
+    for copy in saves:
+        copy.start()
+    gradient_tiles(blocks, x, dgus, in_grad, acc, stage, ssem, False)
+    gradient_tiles(blocks, acts, dy, out_grad, acc, stage, ssem, True)
+    drain_tiles(out_grad, acc, stage, ssem)
+    for copy in saves:
+        copy.wait()
+
+
+def expert_second(starts, x_all, dy_all, w_in, w_out):
+    rows, width = dy_all.shape
+    hidden = w_out.shape[1]
+    dma = pltpu.SemaphoreType.DMA
+    return pl.pallas_call(
+        second_kernel,
+        out_shape=(
+            sds((rows, hidden), BF16),
+            sds((rows, 2 * hidden), BF16),
+            sds((hidden, width), BF16),
+            sds((width, 2 * hidden), BF16),
+        ),
+        grid_spec=pltpu.PrefetchScalarGridSpec(
+            num_scalar_prefetch=1,
+            grid=(1,),
+            in_specs=[AN] * 4,
+            out_specs=(AN, AN, AN, AN),
             scratch_shapes=[
                 pltpu.VMEM((rows, width), BF16),
                 pltpu.VMEM((rows, width), BF16),
@@ -959,21 +1108,22 @@
                 pltpu.VMEM(w_out.shape[1:], BF16),
                 pltpu.VMEM((rows, hidden), BF16),
                 pltpu.VMEM((rows, 2 * hidden), BF16),
-                pltpu.VMEM(TILE, F32),
-                pltpu.VMEM((2,) + TILE, BF16),
+                pltpu.VMEM((512, 2048), F32),
+                pltpu.VMEM((2, 512, 2048), BF16),
                 dma((2,)),
+                dma((2, rows // BLOCK)),
                 dma((2,)),
                 dma((2,)),
             ],
         ),
         compiler_params=pltpu.CompilerParams(dimension_semantics=("arbitrary",), vmem_limit_bytes=60 << 20),
         cost_estimate=pl.CostEstimate(flops=25 * 10**9, bytes_accessed=6 * 10**7, transcendentals=10**6),
-        name="expert_pass",
-    )(number, lens, mixed, cot, cot, w_in, w_out)
-
-
-def tail_kernel(starts, act, dgu, w_in, w_out, produced, dx):
-    @pl.when(pl.program_id(0) * BLOCK < starts[starts.shape[0] - 1])
+        name="expert_second",
+    )(starts, x_all, dy_all, w_in, w_out)
+
+
+def tail_kernel(j, starts, act, dgu, w_in, w_out, produced, dx):
+    @pl.when(pl.program_id(0) * BLOCK < starts[j, starts.shape[1] - 1])
     def _():
         produced[...] = dot(act[...], w_out[...], 1, 0).astype(BF16)
         dx[...] = dot(dgu[...], w_in[...], 1, 1).astype(BF16)
@@ -982,10 +1132,10 @@
 def expert_tail(j, starts, act, dgu, w_in, w_out):
     rows, hidden = act.shape
     width = w_in.shape[1]
-    last = starts.shape[0] - 1
-    block = lambda i, st: (jnp.maximum(jnp.minimum(i, (st[last] + BLOCK - 1) // BLOCK - 1), 0), 0)
+    last = starts.shape[1] - 1
+    block = lambda i, st: (jnp.maximum(jnp.minimum(i, (st[j, last] + BLOCK - 1) // BLOCK - 1), 0), 0)
     return pl.pallas_call(
-        tail_kernel,
+        functools.partial(tail_kernel, j),
         out_shape=(sds((rows, width), BF16), sds((rows, width), BF16)),
         grid_spec=pltpu.PrefetchScalarGridSpec(
             num_scalar_prefetch=1,
@@ -1006,18 +1156,18 @@
 
 def combine_kernel(capacity, local, *refs):
     s = pl.program_id(0)
-    starts = refs[:local]
-    slots = refs[local : 2 * local]
-    produced = refs[2 * local : 3 * local]
-    dx = refs[3 * local : 4 * local]
-    out_part, grad_part = refs[4 * local :]
+    starts = refs[0]
+    slots = refs[1 : 1 + local]
+    produced = refs[1 + local : 1 + 2 * local]
+    dx = refs[1 + 2 * local : 1 + 3 * local]
+    out_part, grad_part = refs[1 + 3 * local :]
     out_sum, grad_sum = None, None
     for j in range(local):
         length = slots[j].shape[2]
         column = lax.broadcasted_iota(jnp.int32, (capacity, length), 0).astype(F32)
         place = column == slots[j][0, 0:1]
-        span = pl.ds(pl.multiple_of(starts[j][s], 16), capacity)
-        held = lax.broadcasted_iota(jnp.int32, (capacity, 1), 0) < starts[j][s + 1] - starts[j][s]
+        span = pl.ds(pl.multiple_of(starts[j, s], 16), capacity)
+        held = lax.broadcasted_iota(jnp.int32, (capacity, 1), 0) < starts[j, s + 1] - starts[j, s]
         rows = jnp.where(held, produced[j][span], 0.0).astype(BF16)
         grads = jnp.where(held, dx[j][span], 0.0).astype(BF16)
         out = dot(jnp.where(place, slots[j][0, 8:9], 0.0).astype(BF16), rows, 0, 0)
@@ -1029,7 +1179,7 @@
 
 
 def combine(starts, slots, produced, dx, capacity):
-    local = len(starts)
+    local = len(slots)
     seqs, _, length = slots[0].shape
     width = produced[0].shape[1]
     seq = lambda i, *_: (i, 0, 0)
@@ -1039,7 +1189,7 @@
         functools.partial(combine_kernel, capacity, local),
         out_shape=(sds((seqs, length, width), BF16), sds((seqs, length, width), BF16)),
         grid_spec=pltpu.PrefetchScalarGridSpec(
-            num_scalar_prefetch=local,
+            num_scalar_prefetch=1,
             grid=(seqs,),
             in_specs=[pl.BlockSpec((1, 16, length), seq)] * local + [rows] * (2 * local),
             out_specs=(pl.BlockSpec((1, length, width), seq), pl.BlockSpec((1, length, width), seq)),
@@ -1047,7 +1197,7 @@
         compiler_params=pltpu.CompilerParams(dimension_semantics=("arbitrary",), vmem_limit_bytes=60 << 20),
         cost_estimate=pl.CostEstimate(flops=3 * 10**9, bytes_accessed=4 * 10**7, transcendentals=0),
         name="combine",
-    )(*starts, *slots, *produced, *dx)
+    )(starts, *slots, *produced, *dx)
 
 
 def shards(
@@ -1072,7 +1222,8 @@
     full, weights, packets = front(tokens, query_weight, key_weight, value_weight, packet)
     routes = jnp.concatenate([expert_ids.astype(BF16), gate_weights], axis=-1)
     routes = jnp.pad(routes, ((0, 0), (0, 0), (0, 128 - 2 * top)))
-    cot_full = lax.all_gather(jnp.concatenate([cotangent, routes], axis=-1), "ep", axis=1, tiled=True)
+    routed, packets = lax.optimization_barrier((jnp.concatenate([cotangent, routes], axis=-1), packets))
+    cot_full = lax.all_gather(routed, "ep", axis=1, tiled=True)
 
     n = 0
     g = gains.shape[0] // 2
@@ -1097,30 +1248,31 @@
     )
     middle, mixed = mix(part, tokens, living, gain_ffn)
 
-    in_grads, out_grads, passes = [], [], []
-    for j in range(local):
-        number = (me * local + j).astype(jnp.int32)[None]
-        if passes:
-            number, _ = lax.optimization_barrier((number, passes[-1][1]))
-        slots, starts, act, dgu, out_grad, in_grad = expert_pass(
-            j, number, lens, mixed, cot_full, expert_in, expert_out, capacity, top
-        )
-        passes.append((slots, starts, act, dgu))
-        out_grads.append(lax.psum_scatter(out_grad, "rep", scatter_dimension=0, tiled=True))
-        in_grads.append(lax.psum_scatter(in_grad, "rep", scatter_dimension=0, tiled=True))
-    tails = [
-        expert_tail(j, starts, act, dgu, expert_in, expert_out)
-        for j, (slots, starts, act, dgu) in enumerate(passes)
-    ]
-    out_part, grad_part = combine(
-        [p[1] for p in passes], [p[0] for p in passes], [t[0] for t in tails], [t[1] for t in tails], capacity
+    number = (me * local).astype(jnp.int32)[None]
+    slots0, slots1, starts, act0, dgu0, x_all, dy_all, out_grad0 = expert_first(
+        number, lens, mixed, cot_full, expert_in, expert_out, capacity, top
     )
-    result, mgrad, ffn_back, agrad = back(grad_part, out_part, middle, cotangent, living, gain_ffn)
+
+    def over_rep(value):
+        return lax.psum_scatter(value, "rep", scatter_dimension=0, tiled=True)
+
+    out0 = over_rep(out_grad0)
+    in_grad0 = first_in_grad(starts, x_all, dgu0)
+    in0 = over_rep(in_grad0)
+    x_all, _ = lax.optimization_barrier((x_all, in_grad0))
+    act1, dgu1, out_grad1, in_grad1 = expert_second(starts, x_all, dy_all, expert_in, expert_out)
+    in1 = over_rep(in_grad1)
+    out1 = over_rep(out_grad1)
+    produced0, dx0 = expert_tail(0, starts, act0, dgu0, expert_in, expert_out)
+    produced1, dx1 = expert_tail(1, starts, act1, dgu1, expert_in, expert_out)
+    out_part, grad_part = combine(starts, (slots0, slots1), (produced0, produced1), (dx0, dx1), capacity)
+
+    mgrad, ffn_back, agrad = back(grad_part, middle, cotangent, living, gain_ffn)
     npart, wgrad, wograd, qk_back = attend_back(
         agrad, normed, pre, low, ctx, weights, output_weight, gain_query, gain_key, cos, sin, lens
     )
     token_grad, small, wrows = final(npart, wgrad, tokens, mgrad, gain_attn, ffn_back, qk_back)
-    sums, small = line_sum(jnp.concatenate([wrows, wograd[None]], axis=0), small)
+    sums, small, result = line_sum(jnp.concatenate([wrows, wograd[None]], axis=0), small, out_part, middle)
     share = g
 
     def head_share(vector):
@@ -1137,8 +1289,8 @@
         small[share : 2 * share].reshape(-1),
         head_share(small[2 * share]),
         head_share(small[2 * share + 1]),
-        jnp.stack(in_grads).astype(F32),
-        jnp.stack(out_grads).astype(F32),
+        jnp.stack([in0, in1]).astype(F32),
+        jnp.stack([out0, out1]).astype(F32),
     )
 
 

time: 895 us -> 869 us (0.971)
  Pallas kernels: 836 us -> 800 us
    pallas_call x5 -> x6, Pallas kernels: 255 us -> 215 us  [the longest x1 81.4 us: back(): pl.pallas_call(back_kernel, out_shape=(sds(cot.shape, F32), sds((1, width...]
    pallas_call x1, Pallas kernels: 115 us -> 78.8 us  [front(): pl.pallas_call(front_kernel, out_shape=(sds((seqs, rows * ep, width), BF1...]
    pallas_call x1, Pallas kernels: 211 us -> 237 us  [line_sum(): pl.pallas_call(line_kernel, out_shape=(sds(own.shape, BF16), sds(small.sh...]
    pallas_call x1, Pallas kernels: 80.7 us -> 94.6 us  [mix(): pl.pallas_call(mix_kernel, out_shape=(sds(tokens.shape, F32), sds((seqs,...]
  transfers between devices with their start and end apart: 5 -> 5, of which waited for: 0 -> 0; matrix products, arithmetic and copies ran while one was open for 3% -> 3% of each run, Pallas kernels for 88% -> 79%
where the time goes in v4:
time: 869 us; the launch traced here: 860 us
  Pallas kernels  800 us (92%)
  other arithmetic  29.9 us (3%)
  between operations  14.8 us (2%)
  local copies, waits for them, and re-layouts  14 us (2%)
    pallas_call x1, Pallas kernels, line_sum(): pl.pallas_call(line_kernel, out_shape=(sds(own.shape, BF16), sds(small.sh...  237 us
    pallas_call x1, Pallas kernels, mix(): pl.pallas_call(mix_kernel, out_shape=(sds(tokens.shape, F32), sds((seqs,...  94.6 us
    pallas_call x1, Pallas kernels, final(): pl.pallas_call(final_kernel, out_shape=(sds(tokens.shape, BF16), sds((8,...  82.6 us
    pallas_call x1, Pallas kernels, back(): pl.pallas_call(back_kernel, out_shape=(sds(cot.shape, F32), sds((1, width...  81.4 us
    pallas_call x1, Pallas kernels, front(): pl.pallas_call(front_kernel, out_shape=(sds((seqs, rows * ep, width), BF1...  78.8 us
    pallas_call x1, Pallas kernels, attend_back(): pl.pallas_call(attend_back_kernel, out_shape=(sds(agrad.shape, BF16), sds...  45.4 us
    pallas_call x1, Pallas kernels, expert_second(): pl.pallas_call(second_kernel, out_shape=(sds((rows, hidden), BF16), sds((...  40.7 us
    pallas_call x1, Pallas kernels, expert_first(): pl.pallas_call(functools.partial(first_kernel, capacity, top), out_shape=...  37.6 us
  transfers between devices with their start and end apart: 5, of which 0 were waited for; matrix products, arithmetic and copies ran while one was open for 3% of the time, Pallas kernels for 79%

profile of v4, /device:TPU:0, one launch (start us, length us, event | category | flops | bytes accessed | tf_op | source)
XLA Modules:
  0.0 859.9 jit_solution(5478170118874346387)
XLA Ops:
  7.2 0.0 all-gather.2.cloned.1.call-start
  7.9 0.7 convert_element_type.77
  8.5 0.7 convert_element_type.78
  9.2 0.8 convert_element_type.75
  9.9 0.1 copy.33
  10.1 0.8 copy.34
  10.9 0.7 maximum_convert_fusion.2
  11.6 0.1 fusion.4
  11.6 0.6 select_maximum_fusion.1.pk
  12.2 0.1 fusion.2
  12.3 2.3 pad_maximum_fusion.1
  14.6 78.8 %front.1 = (bf16[8,256,2048]{2,1,0:T(8,128)(2,1)}, bf16[3,2048,256]{2,1,0:T(8,128)(2,1)}, f32[8,8,128]{2,1,0:T(8,128)}) custom-call(bf16[8,32,2048]{2,1,0:T(8,128)(2,1)} %tok.5, bf16[256,2048]{1,0:T(8,128)(2,1)} %wq.1, bf16[256,2048]{1,0:T(8,128)(2,1)} %wk.1, bf16[256,2048]{1,0:T(8,128)(2,1)} %wv.1, f32[8,128]{1,0:T(8,128)} %select_maximum_fusion.1.pk), custom_call_target="tpu_custom_call" | custom-call | tf_op jit(solution)/shard_map/front/pallas_call | solution.py:291
  93.4 0.0 all-gather.2.cloned.1.call-update
  93.4 0.0 reduce-scatter.9.cloned.1.call-start
  93.5 0.9 slice_reduce_fusion
  94.4 0.7 reshape_squeeze.7.kg
  95.1 0.6 reshape_squeeze.6.qg
  95.7 1.1 convert_reduce_fusion.lens
  96.7 0.0 copy-start.4
  96.8 0.1 convert_bitcast_fusion
  96.8 0.8 copy.35.living
  97.6 0.5 fusion.3
  98.2 0.8 pad_maximum_fusion.2
  99.0 1.4 fusion.6
  100.5 0.0 copy-done.4
  100.5 26.1 %attend.1 = (bf16[8,256,2048]{2,1,0:T(8,128)(2,1)}, f32[2,8,256,256]{3,2,1,0:T(8,128)}, bf16[3,8,256,256]{3,2,1,0:T(8,128)(2,1)}, bf16[8,256,256]{2,1,0:T(8,128)(2,1)}, bf16[8,256,2048]{2,1,0:T(8,128)(2,1)}) custom-call(s32[8]{0:T(128)} %copy-done.4, bf16[8,256,2048]{2,1,0:T(8,128)(2,1)} %get-tuple-element.58.tok, ...), custom_call_target="tpu_custom_call" | custom-call | flops 10000000000 | bytes 40000000 | tf_op jit(solution)/shard_map/attend/pallas_call | solution.py:682
  126.5 94.6 %mix.1 = (f32[8,32,2048]{2,1,0:T(8,128)}, bf16[8,256,2048]{2,1,0:T(8,128)(2,1)}) custom-call(bf16[8,8,32,2048]{3,2,1,0:T(8,128)(2,1)} %bitcast.43, bf16[8,32,2048]{2,1,0:T(8,128)(2,1)} %tok.5, f32[8,32,1]{2,1,0:T(8,128)} %copy.35.living, f32[1,2048]{1,0:T(1,128)} %bitcast.49), custom_call_target="tpu_custom_call" | custom-call | tf_op jit(solution)/shard_map/mix/pallas_call | solution.py:337
  221.1 0.0 all-gather.2.cloned.1.call-done.cot.table
  221.2 37.6 %expert_first.1 = (f32[8,16,256]{2,1,0:T(8,128)}, f32[8,16,256]{2,1,0:T(8,128)}, s32[2,9]{1,0:T(2,128)}, bf16[1536,1024]{1,0:T(8,128)(2,1)}, bf16[1536,2048]{1,0...) custom-call(s32[1]{0:T(128)} %bitcast.3.number, ...), custom_call_target="tpu_custom_call" | custom-call | flops 20000000000 | bytes 60000000 | tf_op jit(solution)/shard_map/expert_first/pallas_call | solution.py:964
  258.7 0.0 reduce-scatter.9.cloned.1.call-update
  258.7 0.0 reduce-scatter.11.cloned.1.call-start
  258.8 19.6 %first_in_grad.1 = bf16[2048,2048]{1,0:T(8,128)(2,1)} custom-call(s32[2,9]{1,0:T(2,128)} %get-tuple-element.63.starts.refs_0_, bf16[2,1536,2048]{2,1,0:T(8,128)(2,1)} %get-tuple-element.70.x_all, bf16[1536,2048]{1,0:T(8,128)(2,1)} %get-tuple-element.67.dgu), custom_call_target="tpu_custom_call" | custom-call | flops 10000000000 | bytes 20000000 | tf_op jit(solution)/shard_map/first_in_grad/pallas_call | solution.py:1031
  278.4 40.7 %expert_second.1 = (bf16[1536,1024]{1,0:T(8,128)(2,1)}, bf16[1536,2048]{1,0:T(8,128)(2,1)}, bf16[1024,2048]{1,0:T(8,128)(2,1)}, bf16[2048,2048]{1,0:T(8,128)(2,1)}) custom-call(s32[2,9]{1,0:T(2,128)} %get-tuple-element.63.starts.refs_0_, bf16[2,1536,2048]{2,1,0:T(8,128)(2,1)} %get-tuple-element.70.x_all, bf16[1536,2048]{1,0:T(8,128)(2,1)} %get-tuple-element.71.dy_all, ...), custom_call_target="tpu_custom_call" | custom-call | flops 24999999488 | bytes 60000000 | tf_op jit(solution)/shard_map/expert_second/pallas_call | solution.py:1091
  319.1 0.0 reduce-scatter.11.cloned.1.call-update
  319.1 0.0 reduce-scatter.5.cloned.1.call-start
  319.2 0.5 reduce-scatter.5.cloned.1.call-update
  319.7 0.2 reduce-scatter.7.cloned.1.call-start
  319.9 0.4 reduce-scatter.7.cloned.1.call-update
  320.3 17.8 %expert_tail.2 = (bf16[1536,2048]{1,0:T(8,128)(2,1)}, bf16[1536,2048]{1,0:T(8,128)(2,1)}) custom-call(s32[2,9]{1,0:T(2,128)} %get-tuple-element.63.starts.refs_0_, bf16[1536,1024]{1,0:T(8,128)(2,1)} %get-tuple-element.66.act, bf16[1536,2048]{1,0:T(8,128)(2,1)} %get-tuple-element.67.dgu, bf16[2,2048,2048]{2,1,0:T(8,128)(2,1)} %w_in.7, ...), custom_call_target="tpu_custom_call" | custom-call | flops 12000000000 | bytes 30000000 | tf_op jit(solution)/shard_map/expert_tail/pallas_call | solution.py:1137
  338.1 17.9 %expert_tail.3 = (bf16[1536,2048]{1,0:T(8,128)(2,1)}, bf16[1536,2048]{1,0:T(8,128)(2,1)}) custom-call(s32[2,9]{1,0:T(2,128)} %get-tuple-element.63.starts.refs_0_, bf16[1536,1024]{1,0:T(8,128)(2,1)} %get-tuple-element.72.act, bf16[1536,2048]{1,0:T(8,128)(2,1)} %get-tuple-element.73.dgu, bf16[2,2048,2048]{2,1,0:T(8,128)(2,1)} %w_in.7, ...), custom_call_target="tpu_custom_call" | custom-call | flops 12000000000 | bytes 30000000 | tf_op jit(solution)/shard_map/expert_tail/pallas_call | solution.py:1137
  355.9 20.8 %combine.1 = (bf16[8,256,2048]{2,1,0:T(8,128)(2,1)}, bf16[8,256,2048]{2,1,0:T(8,128)(2,1)}) custom-call(s32[2,9]{1,0:T(2,128)} %get-tuple-element.63.starts.refs_0_, f32[8,16,256]{2,1,0:T(8,128)} %get-tuple-element.64.refs_1_, f32[8,16,256]{2,1,0:T(8,128)} %get-tuple-element.65.refs_2_, bf16[1536,2048]{1,0:T(8,128)(2,1)} %get-tuple-element.68.refs_3_, ...), custom_call_target="tpu_custom_call" | custom-call | flops 3000000000 | bytes 40000000 | tf_op jit(solution)/shard_map/combine/pallas_call | solution.py:1188
  376.8 81.4 %back.1 = (f32[8,32,2048]{2,1,0:T(8,128)}, f32[1,2048]{1,0:T(1,128)}, bf16[8,256,2048]{2,1,0:T(8,128)(2,1)}) custom-call(bf16[8,8,32,2048]{3,2,1,0:T(8,128)(2,1)} %bitcast.40, f32[8,32,2048]{2,1,0:T(8,128)} %get-tuple-element.78.middle.mid_rows, bf16[8,32,2048]{2,1,0:T(8,128)(2,1)} %cot.1, f32[8,32,1]{2,1,0:T(8,128)} %copy.35.living, f32[1,2048]{1,0:T(1,128)} %bitcast.50), custom_call_target="tpu_custom_call" | custom-call | tf_op jit(solution)/shard_map/back/pallas_call | solution.py:381
  458.2 0.0 copy-start.3
  458.2 45.4 %attend_back.1 = (bf16[8,256,2048]{2,1,0:T(8,128)(2,1)}, bf16[3,2048,256]{2,1,0:T(8,128)(2,1)}, bf16[256,2048]{1,0:T(8,128)(2,1)}, f32[8,128]{1,0:T(8,128)}) custom-call(s32[8]{0:T(128)} %copy-done.4, bf16[8,256,2048]{2,1,0:T(8,128)(2,1)} %get-tuple-element.79.agrad, bf16[8,256,2048]{2,1,0:T(8,128)(2,1)} %get-tuple-element.80.normed, ...), custom_call_target="tpu_custom_call" | custom-call | flops 20000000000 | bytes 40000000 | tf_op jit(solution)/shard_map/attend_back/pallas_call | solution.py:771
  503.6 0.7 slice.51
  504.3 0.0 copy-done.3
  504.3 0.6 select_maximum_fusion.others
  504.9 82.6 %final.1 = (bf16[8,32,2048]{2,1,0:T(8,128)(2,1)}, f32[8,128]{1,0:T(8,128)}, bf16[3,256,2048]{2,1,0:T(8,128)(2,1)}) custom-call(bf16[8,8,32,2048]{3,2,1,0:T(8,128)(2,1)} %bitcast.42, bf16[3,2048,256]{2,1,0:T(8,128)(2,1)} %get-tuple-element.85.wgrad, bf16[8,32,2048]{2,1,0:T(8,128)(2,1)} %tok.5, f32[8,32,2048]{2,1,0:T(8,128)} %get-tuple-element.86.mgrad, ...), custom_call_target="tpu_custom_call" | custom-call | tf_op jit(solution)/shard_map/final/pallas_call | solution.py:472
  587.6 0.0 copy-done.2
  587.6 4.3 pad_maximum_fusion
  591.8 236.6 %line_sum.1 = (bf16[16,64,2048]{2,1,0:T(8,128)(2,1)}, f32[8,128]{1,0:T(8,128)}, bf16[8,32,2048]{2,1,0:T(8,128)(2,1)}) custom-call(bf16[16,64,2048]{2,1,0:T(8,128)(2,1)} %bitcast.39, f32[8,128]{1,0:T(8,128)} %get-tuple-element.91.small, bf16[8,8,32,2048]{3,2,1,0:T(8,128)(2,1)} %bitcast.41, f32[8,32,2048]{2,1,0:T(8,128)} %get-tuple-element.78.middle.mid_rows), custom_call_target="tpu_custom_call" | custom-call | tf_op jit(solution)/shard_map/line_sum/pallas_call | solution.py:621
  828.5 0.8 fusion.7
  829.3 0.6 dynamic-slice_bitcast_fusion
  829.8 0.6 dynamic-slice_bitcast_fusion.1
  830.4 1.3 slice_bitcast_fusion
  831.7 2.7 fusion.5
  834.5 1.6 bitcast_convert_fusion
  836.1 1.6 bitcast_convert_fusion.1
  837.8 1.6 bitcast_convert_fusion.2
  839.4 1.6 bitcast_convert_fusion.3
  841.0 3.8 maximum_convert_fusion.1
  844.9 6.3 maximum_convert_fusion
  851.2 1.0 copy.40
  852.2 1.0 copy.41
  (11 shorter events, 0.0 us)
Async XLA Ops:
  7.2 214.0 %all-gather.2.cloned.1.call-start = ((), (), s32[]{:S(2)}) async-start(), calls=%async_computation.4 | async-start | bytes 10027008 | tf_op jit(solution)/shard_map/all_gather | solution.py:1226
  93.4 747.6 %reduce-scatter.9.cloned.1.call-start = ((), (), s32[]{:S(2)}) async-start(), calls=%async_computation.7 | async-start | bytes 5242880 | tf_op jit(solution)/shard_map/reduce_scatter | solution.py:1257
  96.7 3.7 copy-start.4
  258.7 582.3 %reduce-scatter.11.cloned.1.call-start = ((), (), s32[]{:S(2)}) async-start(), calls=%async_computation.8 | async-start | bytes 5242880 | tf_op jit(solution)/shard_map/reduce_scatter | solution.py:1257
  319.1 525.8 %reduce-scatter.5.cloned.1.call-start = ((), (), s32[]{:S(2)}) async-start(), calls=%async_computation.5 | async-start | bytes 10485760 | tf_op jit(solution)/shard_map/reduce_scatter | solution.py:1257
  319.7 525.2 %reduce-scatter.7.cloned.1.call-start = ((), (), s32[]{:S(2)}) async-start(), calls=%async_computation.6 | async-start | bytes 10485760 | tf_op jit(solution)/shard_map/reduce_scatter | solution.py:1257
  458.2 46.1 %copy-start.3 = (f32[1,2048]{1,0:T(1,128)S(1)}, f32[1,2048]{1,0:T(1,128)}, u32[]{:S(2)}) copy-start(f32[1,2048]{1,0:T(1,128)} %get-tuple-element.87) | copy-start | bytes 24580
  504.9 82.7 %copy-start.2 = (bf16[256,2048]{1,0:T(8,128)(2,1)S(1)}, bf16[256,2048]{1,0:T(8,128)(2,1)}, u32[]{:S(2)}) copy-start(bf16[256,2048]{1,0:T(8,128)(2,1)} %get-tuple-element.90) | copy-start | bytes 3145732
  844.9 6.3 copy-start.1
  844.9 7.3 copy-start
Sparse Core Ops, SparseCore 0:
  93.6 70.9 all-gather.1
  258.9 81.2 reduce-scatter.8
  342.5 77.2 reduce-scatter.10
  422.0 145.1 reduce-scatter.4
  569.4 227.0 reduce-scatter.6

commit v5 on v4

--- a/solution.py
+++ b/solution.py
@@ -2,6 +2,7 @@
 
 import jax
 import jax.numpy as jnp
+import numpy as np
 from jax import lax
 from jax.experimental import pallas as pl
 from jax.experimental.pallas import tpu as pltpu
@@ -47,6 +48,16 @@
     v = tok.astype(F32)
     r = inverse_rms(v)
     return (middle_grad + rms_back(v, r, normed_grad * gain)).astype(BF16), normed_grad * v * r
+
+
+def seq_len(small, s):
+    lane = lax.broadcasted_iota(jnp.int32, (1, 128), 1)
+    return jnp.sum(jnp.where(lane == s, small[2:3, :], 0.0), axis=1, keepdims=True)
+
+
+def live_rows(small, s, me, rows):
+    place = (lax.broadcasted_iota(jnp.int32, (rows, 1), 0) + me * rows).astype(F32)
+    return jnp.where(place < seq_len(small, s), 1.0, 0.0)
 
 
 class Place:
@@ -243,69 +254,196 @@
 COMM = dict(has_side_effects=True, vmem_limit_bytes=60 << 20)
 
 
-def front_kernel(tok, wq, wk, wv, pk, full, weights, packets, tok_v, *sems):
+def front_kernel(
+    tok, cot, ids, gates, wq, wk, wv, pk, full, weights, routed, gains, small,
+    packets, gsend, grecv, glocal, wsend, wrecv, psend, precv, rsend, rrecv, lsend, lrecv, local,
+):
     at = Place()
-    gather = Gather(at, tok, full, *sems[:3])
-    wsend, wrecv, psend, precv, local = sems[3:]
-    seqs = tok.shape[0]
-    block, width = wq.shape[0], weights.shape[2]
-    at.greet(at.peers())
-    each(seqs, gather.start)
-    mine = pl.ds(pl.multiple_of(at.me * block, block), block)
-
-    def weight_copy(m, j, dev):
-        cols = pl.ds(pl.multiple_of(dev * width, width), width)
-        return at.push((wq, wk, wv)[j].at[:, cols], weights.at[j, mine], wsend.at[m, j], wrecv.at[m, j], dev)
+    z = at.rep
+    gather = Gather(at, tok, full, gsend, grecv, glocal)
+    seqs, _, width = tok.shape
+    top = ids.shape[1]
+    block, cols = wq.shape[0], weights.shape[2]
+    quarter = block // 4
+    peers = at.peers()
+    barrier = pltpu.get_barrier_semaphore()
+    line = [lax.rem(z + k, 4) for k in range(1, 4)]
+    for dev in line:
+        pl.semaphore_signal(barrier, inc=1, device_id=(dev, at.me), device_id_type=MESH)
+    for dev in peers:
+        pl.semaphore_signal(barrier, inc=1, device_id=(z, dev), device_id_type=MESH)
+    pl.semaphore_wait(barrier, 10)
 
     def packet_copy(m, dev):
         return at.push(pk, packets.at[at.me], psend.at[m], precv.at[m], dev)
 
-    own_cols = pl.ds(pl.multiple_of(at.me * width, width), width)
+    def weight_copy(m, j, dev):
+        theirs = pl.ds(pl.multiple_of(dev * cols, cols), cols)
+        src = (wq, wk, wv)[j].at[pl.ds(pl.multiple_of(z * quarter, quarter), quarter), theirs]
+        dst = weights.at[j, pl.ds(pl.multiple_of(at.me * block + z * quarter, quarter), quarter)]
+        return at.push(src, dst, wsend.at[m, j], wrecv.at[m, j], dev)
+
+    def weight_landed(m, j, dev):
+        dst = weights.at[j, pl.ds(pl.multiple_of(dev * block + z * quarter, quarter), quarter)]
+        return at.push(dst, dst, wsend.at[m, j], wrecv.at[m, j], dev)
+
+    def walk(m, q, right):
+        part = weights.at[:, pl.ds(pl.multiple_of(peers[m] * block + q * quarter, quarter), quarter)]
+        send, recv, dev = (rsend, rrecv, z + 1) if right else (lsend, lrecv, z - 1)
+        return pltpu.make_async_remote_copy(
+            src_ref=part, dst_ref=part, send_sem=send.at[m, q], recv_sem=recv.at[m, q],
+            device_id=(dev, at.me), device_id_type=MESH,
+        )
+
+    for m, dev in enumerate(peers):
+        packet_copy(m, dev).start()
+        for j in range(3):
+            weight_copy(m, j, dev).start()
+    each(seqs, gather.start)
+    own_cols = pl.ds(pl.multiple_of(at.me * cols, cols), cols)
+    mine = pl.ds(pl.multiple_of(at.me * block, block), block)
     own = [pltpu.make_async_copy(w.at[:, own_cols], weights.at[j, mine], local.at[j]) for j, w in enumerate((wq, wk, wv))]
-    own.append(pltpu.make_async_copy(pk, packets.at[at.me], local.at[3]))
     for copy in own:
         copy.start()
-    for m, dev in enumerate(at.peers()):
-        packet_copy(m, dev).start()
-    for m, dev in enumerate(at.peers()):
+
+    place = lax.broadcasted_iota(jnp.int32, (top, 128), 0)
+    lane = lax.broadcasted_iota(jnp.int32, (top, 128), 1)
+    first = jnp.where(lane == place, 1.0, 0.0).astype(BF16)
+    second = jnp.where(lane == place + top, 1.0, 0.0).astype(BF16)
+
+    def join(s):
+        routed[s, :, 0:width] = cot[s]
+        table = dot(ids[s].astype(F32).astype(BF16), first, 0, 0) + dot(gates[s], second, 0, 0)
+        routed[s, :, width : width + 128] = table.astype(BF16)
+
+    each(seqs, join)
+
+    for m, dev in enumerate(peers):
         for j in range(3):
-            weight_copy(m, j, dev).start()
-    gather_tail(seqs, gather)
-    for m, dev in enumerate(at.peers()):
-        packet_copy(m, dev).wait()
+            weight_landed(m, j, dev).wait_recv()
+
+        @pl.when(z < 3)
+        def _():
+            walk(m, z, True).start()
+
+        @pl.when(z > 0)
+        def _():
+            walk(m, z, False).start()
+
+    def pass_on(d):
+        @pl.when(z - d >= 0)
+        def _():
+            for m in range(7):
+                walk(m, z - d, True).wait_recv()
+
+                @pl.when(z < 3)
+                def _():
+                    walk(m, z - d, True).start()
+
+        @pl.when(z + d <= 3)
+        def _():
+            for m in range(7):
+                walk(m, z + d, False).wait_recv()
+
+                @pl.when(z > 0)
+                def _():
+                    walk(m, z + d, False).start()
+
+    def relay(i, _):
+        gather.relay(2 * i, True)
+        gather.relay(2 * i + 1, False)
+        return 0
+
+    pairs = seqs // 2
+    lax.fori_loop(0, pairs // 2, relay, 0)
+    pass_on(1)
+    lax.fori_loop(pairs // 2, pairs, relay, 0)
+    pass_on(2)
+    each(seqs, gather.relay_far)
+    for m, dev in enumerate(peers):
+        packet_copy(m, dev).wait_recv()
+    packets[at.me] = pk[...]
+    devices = packets.shape[0]
+    share = width // (128 * devices)
+    heads = HEAD_DIM // devices
+    gains[...] = jnp.zeros_like(gains)
+    small[...] = jnp.zeros_like(small)
+    for o in range(devices):
+        for k in range(share):
+            lanes = pl.ds((o * share + k) * 128, 128)
+            gains[0:1, lanes] = packets[o, k : k + 1]
+            gains[1:2, lanes] = packets[o, share + k : share + k + 1]
+        base = 2 * share
+        small[0:1] += pltpu.roll(packets[o, base : base + 1], o * heads, 1)
+        small[1:2] += pltpu.roll(packets[o, base + 1 : base + 2], o * heads, 1)
+        small[2:3] += pltpu.roll(packets[o, base + 2 : base + 3], o, 1)
+    each(seqs, gather.finish)
+    pass_on(3)
+
+    def sent(q, going, right):
+        @pl.when(going)
+        def _():
+            for m in range(7):
+                walk(m, q, right).wait_send()
+
+    for q in range(4):
+        sent(q, jnp.logical_and(q <= z, z < 3), True)
+        sent(q, jnp.logical_and(q >= z, z > 0), False)
+    for m, dev in enumerate(peers):
+        packet_copy(m, dev).wait_send()
         for j in range(3):
-            weight_copy(m, j, dev).wait()
+            weight_copy(m, j, dev).wait_send()
     for copy in own:
         copy.wait()
 
 
-def front(tokens, wq, wk, wv, packet):
+def front(tokens, cotangent, ids, gates, wq, wk, wv, packet):
     seqs, rows, width = tokens.shape
     ep = lax.axis_size("ep")
     cols = wq.shape[1] // ep
-    if ep != 8:
+    top = ids.shape[1]
+    if ep != 8 or lax.axis_size("rep") != 4:
         full = lax.all_gather(tokens, "ep", axis=1, tiled=True)
         weights = [lax.all_to_all(w, "ep", split_axis=1, concat_axis=0, tiled=True) for w in (wq, wk, wv)]
-        return full, jnp.stack(weights), lax.all_gather(packet, "ep", axis=0)
+        routes = jnp.concatenate([ids.astype(BF16), gates], axis=1).transpose(0, 2, 1)
+        routes = jnp.pad(routes, ((0, 0), (0, 0), (0, 128 - 2 * top)))
+        packets = lax.all_gather(packet, "ep", axis=0)
+        share, heads = width // (128 * ep), HEAD_DIM // ep
+        gains = jnp.stack([packets[:, :share].reshape(width), packets[:, share : 2 * share].reshape(width)])
+        lens = jnp.pad(packets[:, 2 * share + 2, 0], (0, 128 - ep))
+        few = [packets[:, 2 * share + k, :heads].reshape(HEAD_DIM) for k in range(2)] + [lens]
+        return (
+            full, jnp.stack(weights), jnp.concatenate([cotangent, routes], axis=-1),
+            jnp.pad(gains, ((0, 6), (0, 0))), jnp.pad(jnp.stack(few), ((0, 5), (0, 0))),
+        )
     dma = pltpu.SemaphoreType.DMA
     return pl.pallas_call(
         front_kernel,
         out_shape=(
             sds((seqs, rows * ep, width), BF16),
             sds((3, wq.shape[0] * ep, cols), BF16),
-            sds((ep,) + packet.shape, F32),
+            sds((seqs, rows, width + 128), BF16),
+            sds((8, width), F32),
+            sds((8, 128), F32),
         ),
-        in_specs=[VM] * 5,
-        out_specs=(AN, AN, AN),
-        scratch_shapes=[pltpu.VMEM((8, 128), F32)]
+        in_specs=[VM] * 8,
+        out_specs=(AN, AN, VM, VM, VM),
+        scratch_shapes=[pltpu.VMEM((ep,) + packet.shape, F32)]
         + Gather.scratch(seqs)
-        + [dma((7, 3)), dma((7, 3)), dma((7,)), dma((7,)), dma((4,))],
+        + [dma((7, 3)), dma((7, 3)), dma((7,)), dma((7,))]
+        + [dma((7, 4))] * 4
+        + [dma((3,))],
         compiler_params=pltpu.CompilerParams(collective_id=1, **COMM),
         name="front",
-    )(tokens, wq, wk, wv, packet)
-
-
-def mix_kernel(part, tok, living, gain, middle, full, own, *scratch):
+    )(tokens, cotangent, ids, gates, wq, wk, wv, packet)
+
+
+def plain_living(small, seqs, rows):
+    place = (jnp.arange(rows) + lax.axis_index("ep") * rows).astype(F32)
+    return (place[None] < small[2, :seqs, None]).astype(F32)[..., None]
+
+
+def mix_kernel(part, tok, small, gains, middle, full, own, *scratch):
     at = Place()
     seqs = tok.shape[0]
     reduce = Reduce(at, part, *scratch[: Reduce.sems])
@@ -316,7 +454,8 @@
     each(seqs, reduce.hop2)
 
     def rows(s):
-        mid, mixed = mix_rows(reduce.total(s), tok[s], living[s], gain[...])
+        living = live_rows(small, s, at.me, tok.shape[1])
+        mid, mixed = mix_rows(reduce.total(s), tok[s], living, gains[1:2])
         middle[s] = mid
         own[s] = mixed
         gather.start(s)
@@ -326,12 +465,12 @@
     each(seqs, reduce.finish)
 
 
-def mix(part, tokens, living, gain):
+def mix(part, tokens, small, gains):
     seqs, rows, width = tokens.shape
     ep = lax.axis_size("ep")
     if ep != 8:
         total = lax.psum_scatter(part, "ep", scatter_dimension=1, tiled=True).astype(F32)
-        middle, mixed = mix_rows(total, tokens, living, gain)
+        middle, mixed = mix_rows(total, tokens, plain_living(small, seqs, rows), gains[1])
         return middle, lax.all_gather(mixed, "ep", axis=1, tiled=True)
     part = part.reshape(seqs, ep, rows, width)
     return pl.pallas_call(
@@ -342,10 +481,10 @@
         scratch_shapes=[pltpu.VMEM(tokens.shape, BF16)] + Reduce.scratch(part) + Gather.scratch(seqs),
         compiler_params=pltpu.CompilerParams(collective_id=2, **COMM),
         name="mix",
-    )(part, tokens, living, gain)
-
-
-def back_kernel(gpart, middle, cot, living, gain, mgrad, ggrad, full, own, *scratch):
+    )(part, tokens, small, gains)
+
+
+def back_kernel(gpart, middle, cot, small, gains, mgrad, ggrad, full, own, *scratch):
     at = Place()
     seqs = cot.shape[0]
     n = Reduce.sems
@@ -358,7 +497,8 @@
     ggrad[...] = jnp.zeros_like(ggrad)
 
     def rows(s):
-        mg, ag, back = ffn_back_rows(rg.total(s), middle[s], cot[s], living[s], gain[...])
+        living = live_rows(small, s, at.me, cot.shape[1])
+        mg, ag, back = ffn_back_rows(rg.total(s), middle[s], cot[s], living, gains[1:2])
         mgrad[s] = mg
         own[s] = ag
         ggrad[...] += jnp.sum(back, axis=0, keepdims=True)
@@ -369,12 +509,12 @@
     each(seqs, rg.finish)
 
 
-def back(gpart, middle, cot, living, gain):
+def back(gpart, middle, cot, small, gains):
     seqs, rows, width = cot.shape
     ep = lax.axis_size("ep")
     if ep != 8:
         mixed_grad = lax.psum_scatter(gpart, "ep", scatter_dimension=1, tiled=True).astype(F32)
-        mg, ag, backs = ffn_back_rows(mixed_grad, middle, cot, living, gain)
+        mg, ag, backs = ffn_back_rows(mixed_grad, middle, cot, plain_living(small, seqs, rows), gains[1])
         full = lax.all_gather(ag, "ep", axis=1, tiled=True)
         return mg, jnp.sum(backs, axis=(0, 1))[None], full
     gpart = gpart.reshape(seqs, ep, rows, width)
@@ -390,10 +530,10 @@
         scratch_shapes=[pltpu.VMEM(cot.shape, BF16)] + Reduce.scratch(gpart) + Gather.scratch(seqs),
         compiler_params=pltpu.CompilerParams(collective_id=3, **COMM),
         name="back",
-    )(gpart, middle, cot, living, gain)
-
-
-def final_kernel(part, wgrad, tok, mgrad, gain, others, tgrad, small, wrows, ggrad, parcel, landed, *scratch):
+    )(gpart, middle, cot, small, gains)
+
+
+def final_kernel(part, wgrad, tok, mgrad, gains, others, tgrad, small, wrows, ggrad, parcel, landed, *scratch):
     at = Place()
     seqs = tok.shape[0]
     n = Reduce.sems
@@ -419,7 +559,7 @@
     ggrad[...] = jnp.zeros_like(ggrad)
 
     def rows(s):
-        tg, back = attn_back_rows(reduce.total(s), tok[s], mgrad[s], gain[...])
+        tg, back = attn_back_rows(reduce.total(s), tok[s], mgrad[s], gains[0:1])
         tgrad[s] = tg
         ggrad[...] += jnp.sum(back, axis=0, keepdims=True)
 
@@ -452,12 +592,12 @@
     own.wait()
 
 
-def final(part, wgrad, tokens, mgrad, gain, ffn_back, qk_back):
+def final(part, wgrad, tokens, mgrad, gains, ffn_back, qk_back):
     seqs, rows, width = tokens.shape
     ep = lax.axis_size("ep")
     if ep != 8:
         normed_grad = lax.psum_scatter(part, "ep", scatter_dimension=1, tiled=True).astype(F32)
-        tg, backs = attn_back_rows(normed_grad, tokens, mgrad, gain)
+        tg, backs = attn_back_rows(normed_grad, tokens, mgrad, gains[0])
         wrows = lax.all_to_all(wgrad, "ep", split_axis=1, concat_axis=2, tiled=True)
         share = width // ep
         small = jnp.concatenate([jnp.sum(backs, axis=(0, 1)), ffn_back[0], qk_back[0], qk_back[1]])
@@ -483,7 +623,7 @@
         + [dma((7,)), dma((7,)), dma, dma((7,)), dma((7,))],
         compiler_params=pltpu.CompilerParams(collective_id=4, **COMM),
         name="final",
-    )(part, wgrad, tokens, mgrad, gain, others)
+    )(part, wgrad, tokens, mgrad, gains, others)
 
 
 def line_kernel(
@@ -647,16 +787,16 @@
 
 def probabilities(q, k, length):
     scores = dot(q, k, 1, 1) * HEAD_DIM**-0.5
-    column = lax.broadcasted_iota(jnp.int32, scores.shape, 1)
+    column = lax.broadcasted_iota(jnp.int32, (1, scores.shape[1]), 1).astype(F32)
     scores = jnp.where(column < length, scores, -1e9)
     p = jnp.exp(scores - jnp.max(scores, axis=-1, keepdims=True))
     return p * (1.0 / jnp.sum(p, axis=-1, keepdims=True))
 
 
-def attend_kernel(lens, tok, w, wo, gain, qg, kg, cos, sin, normed, pre, low, ctx, part):
-    length = lens[pl.program_id(0)]
+def attend_kernel(tok, w, wo, gains, small, cos, sin, normed, pre, low, ctx, part):
+    length = seq_len(small, pl.program_id(0))
     v = tok[0].astype(F32)
-    x = (v * inverse_rms(v) * gain[...]).astype(BF16)
+    x = (v * inverse_rms(v) * gains[0:1]).astype(BF16)
     normed[0] = x
     q_pre, k_pre = dot(x, w[0], 1, 0), dot(x, w[1], 1, 0)
     value = dot(x, w[2], 1, 0).astype(BF16)
@@ -665,7 +805,7 @@
     for h in range(q_pre.shape[1] // HEAD_DIM):
         cols = slice(h * HEAD_DIM, (h + 1) * HEAD_DIM)
         rot = []
-        for i, (u, g) in enumerate(((q_pre[:, cols], qg[...]), (k_pre[:, cols], kg[...]))):
+        for i, (u, g) in enumerate(((q_pre[:, cols], small[0:1]), (k_pre[:, cols], small[1:2]))):
             rot.append(rope(u * inverse_rms(u) * g, cos[...], sin[...]).astype(BF16))
             low[i, 0, :, cols] = rot[i]
         attention = probabilities(rot[0], rot[1], length).astype(BF16)
@@ -673,7 +813,7 @@
     part[0] = dot(ctx[0], wo[...], 1, 0).astype(BF16)
 
 
-def attend(full, weights, wo, gain, qg, kg, cos, sin, lens):
+def attend(full, weights, wo, gains, small, cos, sin):
     seqs, length, width = full.shape
     cols = weights.shape[2]
     row = lambda i, *_: (i, 0, 0)
@@ -689,15 +829,14 @@
             sds(full.shape, BF16),
         ),
         grid_spec=pltpu.PrefetchScalarGridSpec(
-            num_scalar_prefetch=1,
+            num_scalar_prefetch=0,
             grid=(seqs,),
             in_specs=[
                 pl.BlockSpec((1, length, width), row),
                 pl.BlockSpec(weights.shape, lambda i, *_: (0, 0, 0)),
                 pl.BlockSpec(wo.shape, two),
-                pl.BlockSpec((1, width), two),
-                pl.BlockSpec((1, HEAD_DIM), two),
-                pl.BlockSpec((1, HEAD_DIM), two),
+                pl.BlockSpec((8, width), two),
+                pl.BlockSpec((8, 128), two),
                 pl.BlockSpec((length, HEAD_DIM), two),
                 pl.BlockSpec((length, HEAD_DIM), two),
             ],
@@ -712,14 +851,14 @@
         compiler_params=pltpu.CompilerParams(dimension_semantics=("arbitrary",), vmem_limit_bytes=60 << 20),
         cost_estimate=pl.CostEstimate(flops=10**10, bytes_accessed=4 * 10**7, transcendentals=10**6),
         name="attend",
-    )(lens, full, weights, wo, gain, qg, kg, cos, sin)
+    )(full, weights, wo, gains, small, cos, sin)
 
 
 def attend_back_kernel(
-    lens, agrad, normed, pre, low, ctx, w, wo, qg, kg, cos, sin, part, wgrad, wograd, gains, wacc, woacc
+    agrad, normed, pre, low, ctx, w, wo, small, cos, sin, part, wgrad, wograd, gains, wacc, woacc
 ):
     s = pl.program_id(0)
-    length = lens[s]
+    length = seq_len(small, s)
 
     @pl.when(s == 0)
     def _():
@@ -740,7 +879,7 @@
         grads[2].append(dot(attention.astype(BF16), cg, 0, 0).astype(BF16))
         pg = dot(cg, value, 1, 1)
         sg = (attention * (pg - jnp.sum(attention * pg, axis=-1, keepdims=True))).astype(BF16)
-        for i, (rot_grad, g) in enumerate(((dot(sg, k, 1, 0), qg[...]), (dot(sg, q, 0, 0), kg[...]))):
+        for i, (rot_grad, g) in enumerate(((dot(sg, k, 1, 0), small[0:1]), (dot(sg, q, 0, 0), small[1:2]))):
             wgt = rot_grad * scale
             u = wgt * cos[...] + pltpu.roll(wgt * sin[...], half, 1)
             v = pre[i, 0, :, cols]
@@ -761,7 +900,7 @@
         wograd[...] = woacc[...].astype(BF16)
 
 
-def attend_back(agrad, normed, pre, low, ctx, weights, wo, qg, kg, cos, sin, lens):
+def attend_back(agrad, normed, pre, low, ctx, weights, wo, small, cos, sin):
     seqs, length, width = agrad.shape
     cols = weights.shape[2]
     row = lambda i, *_: (i, 0, 0)
@@ -777,7 +916,7 @@
             sds((8, HEAD_DIM), F32),
         ),
         grid_spec=pltpu.PrefetchScalarGridSpec(
-            num_scalar_prefetch=1,
+            num_scalar_prefetch=0,
             grid=(seqs,),
             in_specs=[
                 pl.BlockSpec((1, length, width), row),
@@ -787,8 +926,7 @@
                 pl.BlockSpec((1, length, cols), row),
                 pl.BlockSpec(weights.shape, three),
                 pl.BlockSpec(wo.shape, two),
-                pl.BlockSpec((1, HEAD_DIM), two),
-                pl.BlockSpec((1, HEAD_DIM), two),
+                pl.BlockSpec((8, 128), two),
                 pl.BlockSpec((length, HEAD_DIM), two),
                 pl.BlockSpec((length, HEAD_DIM), two),
             ],
@@ -803,21 +941,21 @@
         compiler_params=pltpu.CompilerParams(dimension_semantics=("arbitrary",), vmem_limit_bytes=60 << 20),
         cost_estimate=pl.CostEstimate(flops=2 * 10**10, bytes_accessed=4 * 10**7, transcendentals=10**6),
         name="attend_back",
-    )(lens, agrad, normed, pre, low, ctx, weights, wo, qg, kg, cos, sin)
+    )(agrad, normed, pre, low, ctx, weights, wo, small, cos, sin)
 
 
 BLOCK = 256
 
 
 def pack_rows(seqs, capacity):
-    return -(-seqs * capacity // BLOCK) * BLOCK + BLOCK
+    return -(-seqs * capacity // BLOCK) * BLOCK
 
 
 def packed_slots(number, table, length_live, top):
     tab = table.astype(F32)
     length = tab.shape[0]
     lane = lax.broadcasted_iota(jnp.int32, tab.shape, 1)
-    row = lax.broadcasted_iota(jnp.int32, tab.shape, 0)
+    row = lax.broadcasted_iota(jnp.int32, (length, 1), 0).astype(F32)
     chosen = jnp.logical_and(jnp.logical_and(tab == number, lane < top), row < length_live)
     gates = jnp.where(chosen, pltpu.roll(tab, 128 - top, 1), 0.0).astype(BF16)
     chosen = jnp.where(chosen, 1.0, 0.0).astype(BF16)
@@ -900,44 +1038,65 @@
 
 
 def first_kernel(
-    capacity, top, number, lens, mixed, cot, table, w_in, w_out,
+    capacity, top, number, mixed, cot, table, small, w_in, w_out,
     slots0, slots1, starts, act, dgu, x_all, dy_all, out_grad,
     x, dy, wi, wo, acts, dgus, acc, stage, wsem, ssem, rsem,
 ):
-    s = pl.program_id(0)
-    seqs = pl.num_programs(0)
+    step = pl.program_id(0)
+    steps = pl.num_programs(0)
+    together = mixed.shape[0]
+    seqs = steps * together
     width = mixed.shape[2]
     loads = [pltpu.make_async_copy(w_in.at[0], wi, wsem.at[0]), pltpu.make_async_copy(w_out.at[0], wo, wsem.at[1])]
 
-    @pl.when(s == 0)
+    @pl.when(step == 0)
     def _():
         for copy in loads:
             copy.start()
         starts[0, 0] = 0
         starts[1, 0] = 0
 
-    spread, gate_spread, spans = [], [], []
-    for j, slots in enumerate((slots0, slots1)):
-        slot, weight, count = packed_slots((number[0] + j).astype(F32), table[0], lens[s], top)
-        slots[0, 0:8] = slot
-        slots[0, 8:16] = weight
-        place = lax.broadcasted_iota(jnp.int32, (capacity, slot.shape[1]), 0).astype(F32) == slot[0:1]
-        spread.append(jnp.where(place, 1.0, 0.0).astype(BF16))
-        gate_spread.append(jnp.where(place, weight[0:1], 0.0).astype(BF16))
-        start = pl.multiple_of(starts[j, s], 16)
-        spans.append(pl.ds(start, capacity))
-        starts[j, s + 1] = start + (count + 15) // 16 * 16
-    for target, source, weights in ((x, mixed, spread), (dy, cot, gate_spread)):
-        packed = dot(jnp.concatenate(weights, axis=0), source[0], 1, 0).astype(BF16)
+    packed = []
+    for k in range(together):
+        spread, gate_spread, counts = [], [], []
+        for j, slots in enumerate((slots0, slots1)):
+            slot, weight, count = packed_slots(
+                (number[0] + j).astype(F32), table[k], seq_len(small, step * together + k), top
+            )
+            slots[k, 0:8] = slot
+            slots[k, 8:16] = weight
+            place = lax.broadcasted_iota(jnp.int32, (capacity, slot.shape[1]), 0).astype(F32) == slot[0:1]
+            spread.append(jnp.where(place, 1.0, 0.0).astype(BF16))
+            gate_spread.append(jnp.where(place, weight[0:1], 0.0).astype(BF16))
+            counts.append(count)
+        packed.append(
+            (
+                counts,
+                dot(jnp.concatenate(spread, axis=0), mixed[k], 1, 0).astype(BF16),
+                dot(jnp.concatenate(gate_spread, axis=0), cot[k], 1, 0).astype(BF16),
+            )
+        )
+    for k, (counts, x_rows, dy_rows) in enumerate(packed):
+        s = step * together + k
         for j in range(2):
-            target[j, spans[j]] = packed[j * capacity : (j + 1) * capacity]
-
-    @pl.when(s == seqs - 1)
+            start = pl.multiple_of(starts[j, s], 16)
+            x[j, pl.ds(start, capacity)] = x_rows[j * capacity : (j + 1) * capacity]
+            dy[j, pl.ds(start, capacity)] = dy_rows[j * capacity : (j + 1) * capacity]
+            starts[j, s + 1] = start + (counts[j] + 15) // 16 * 16
+
+    @pl.when(step == steps - 1)
     def _():
         for j in range(2):
-            tail = pl.ds(pl.multiple_of(starts[j, s] + capacity, 16), BLOCK)
-            x[j, tail] = jnp.zeros((BLOCK, width), BF16)
-            dy[j, tail] = jnp.zeros((BLOCK, width), BF16)
+            past = (starts[j, seqs - 1] + capacity) // 16
+            end = (starts[j, seqs] + BLOCK - 1) // BLOCK * (BLOCK // 16)
+
+            def clear(i, _):
+                rows = pl.ds(pl.multiple_of(i * 16, 16), 16)
+                x[j, rows] = jnp.zeros((16, width), BF16)
+                dy[j, rows] = jnp.zeros((16, width), BF16)
+                return 0
+
+            lax.fori_loop(past, end, clear, 0)
         saves = [pltpu.make_async_copy(x, x_all, rsem.at[0]), pltpu.make_async_copy(dy.at[1], dy_all, rsem.at[1])]
         for copy in saves:
             copy.start()
@@ -954,13 +1113,14 @@
             copy.wait()
 
 
-def expert_first(number, lens, mixed, cot, w_in, w_out, capacity, top):
+def expert_first(number, mixed, cot, small, w_in, w_out, capacity, top):
     seqs, length, width = mixed.shape
     hidden = w_out.shape[1]
     rows = pack_rows(seqs, capacity)
     dma = pltpu.SemaphoreType.DMA
     seq = lambda i, *_: (i, 0, 0)
-    slot_spec = pl.BlockSpec((1, 16, length), seq)
+    together = 2
+    slot_spec = pl.BlockSpec((together, 16, length), seq)
     return pl.pallas_call(
         functools.partial(first_kernel, capacity, top),
         out_shape=(
@@ -974,12 +1134,13 @@
             sds((hidden, width), BF16),
         ),
         grid_spec=pltpu.PrefetchScalarGridSpec(
-            num_scalar_prefetch=2,
-            grid=(seqs,),
+            num_scalar_prefetch=1,
+            grid=(seqs // together,),
             in_specs=[
-                pl.BlockSpec((1, length, width), seq),
-                pl.BlockSpec((1, length, width), seq),
-                pl.BlockSpec((1, length, 128), lambda i, *_: (i, 0, width // 128)),
+                pl.BlockSpec((together, length, width), seq),
+                pl.BlockSpec((together, length, width), seq),
+                pl.BlockSpec((together, length, 128), lambda i, *_: (i, 0, width // 128)),
+                pl.BlockSpec((8, 128), lambda i, *_: (0, 0)),
                 AN,
                 AN,
             ],
@@ -991,17 +1152,17 @@
                 pltpu.VMEM(w_out.shape[1:], BF16),
                 pltpu.VMEM((rows, hidden), BF16),
                 pltpu.VMEM((rows, 2 * hidden), BF16),
-                pltpu.VMEM((512, 1024), F32),
-                pltpu.VMEM((2, 512, 1024), BF16),
+                pltpu.VMEM((256, 1024), F32),
+                pltpu.VMEM((2, 256, 1024), BF16),
                 dma((2,)),
                 dma((2,)),
                 dma((4,)),
             ],
         ),
-        compiler_params=pltpu.CompilerParams(dimension_semantics=("arbitrary",), vmem_limit_bytes=62 << 20),
+        compiler_params=pltpu.CompilerParams(dimension_semantics=("arbitrary",), vmem_limit_bytes=63 << 20),
         cost_estimate=pl.CostEstimate(flops=2 * 10**10, bytes_accessed=6 * 10**7, transcendentals=10**6),
         name="expert_first",
-    )(number, lens, mixed, cot, cot, w_in, w_out)
+    )(number, mixed, cot, cot, small, w_in, w_out)
 
 
 def in_grad_kernel(starts, x_all, dgu, in_grad, x, dgus, acc, stage, lsem, ssem):
@@ -1139,7 +1300,7 @@
         out_shape=(sds((rows, width), BF16), sds((rows, width), BF16)),
         grid_spec=pltpu.PrefetchScalarGridSpec(
             num_scalar_prefetch=1,
-            grid=(rows // BLOCK - 1,),
+            grid=(rows // BLOCK,),
             in_specs=[
                 pl.BlockSpec((BLOCK, hidden), block),
                 pl.BlockSpec((BLOCK, 2 * hidden), block),
@@ -1206,7 +1367,7 @@
 ):
     ep = lax.axis_size("ep")
     me = lax.axis_index("ep")
-    _, rows, width = tokens.shape
+    _, rows, _ = tokens.shape
     length = rows * ep
     top = gate_weights.shape[2]
     local = expert_in.shape[0]
@@ -1214,43 +1375,30 @@
     capacity = -(-(length * top * 9 // (8 * experts)) // 16) * 16
 
     gains = jnp.concatenate([attn_gain, ffn_gain]).astype(F32).reshape(-1, 128)
-    few = jnp.concatenate([query_gain.astype(F32), key_gain.astype(F32), seq_lengths.astype(F32)])
-    few = jnp.pad(few, (0, 128 - few.shape[0]))[None]
+    few = [query_gain.astype(F32), key_gain.astype(F32), seq_lengths.astype(F32)]
+    few = jnp.stack([jnp.pad(v, (0, 128 - v.shape[0])) for v in few])
     packet = jnp.concatenate([gains, few], axis=0)
     packet = jnp.pad(packet, ((0, -packet.shape[0] % 8), (0, 0)))
-
-    full, weights, packets = front(tokens, query_weight, key_weight, value_weight, packet)
-    routes = jnp.concatenate([expert_ids.astype(BF16), gate_weights], axis=-1)
-    routes = jnp.pad(routes, ((0, 0), (0, 0), (0, 128 - 2 * top)))
-    routed, packets = lax.optimization_barrier((jnp.concatenate([cotangent, routes], axis=-1), packets))
+    share = gains.shape[0] // 2
+
+    full, weights, routed, gains, small_in = front(
+        tokens, cotangent, expert_ids.transpose(0, 2, 1), gate_weights.transpose(0, 2, 1),
+        query_weight, key_weight, value_weight, packet,
+    )
     cot_full = lax.all_gather(routed, "ep", axis=1, tiled=True)
 
-    n = 0
-    g = gains.shape[0] // 2
-    gain_attn = packets[:, n : n + g].reshape(1, width)
-    gain_ffn = packets[:, n + g : n + 2 * g].reshape(1, width)
-    q = query_gain.shape[0]
-    gain_query = packets[:, n + 2 * g, :q].reshape(1, HEAD_DIM)
-    gain_key = packets[:, n + 2 * g, q : 2 * q].reshape(1, HEAD_DIM)
-    lens = packets[:, n + 2 * g, 2 * q].astype(jnp.int32)
-    positions = jnp.arange(length, dtype=jnp.int32)
-    live = (positions[None] < lens[:, None]).astype(F32)
-    living = lax.dynamic_slice_in_dim(live, me * rows, rows, axis=1)[..., None]
-
     half = HEAD_DIM // 2
-    frequency = ROPE_BASE ** (-(jnp.arange(half, dtype=F32) * (2.0 / HEAD_DIM)))
-    angles = positions.astype(F32)[:, None] * frequency[None, :]
-    cos = jnp.concatenate([jnp.cos(angles)] * 2, axis=-1)
-    sin = jnp.concatenate([-jnp.sin(angles), jnp.sin(angles)], axis=-1)
-
-    normed, pre, low, ctx, part = attend(
-        full, weights, output_weight, gain_attn, gain_query, gain_key, cos, sin, lens
-    )
-    middle, mixed = mix(part, tokens, living, gain_ffn)
+    frequency = ROPE_BASE ** (-(np.arange(half, dtype=np.float32) * np.float32(2.0 / HEAD_DIM)))
+    angles = np.arange(length, dtype=np.float32)[:, None] * frequency.astype(np.float32)[None, :]
+    cos = jnp.asarray(np.concatenate([np.cos(angles)] * 2, axis=-1), F32)
+    sin = jnp.asarray(np.concatenate([-np.sin(angles), np.sin(angles)], axis=-1), F32)
+
+    normed, pre, low, ctx, part = attend(full, weights, output_weight, gains, small_in, cos, sin)
+    middle, mixed = mix(part, tokens, small_in, gains)
 
     number = (me * local).astype(jnp.int32)[None]
     slots0, slots1, starts, act0, dgu0, x_all, dy_all, out_grad0 = expert_first(
-        number, lens, mixed, cot_full, expert_in, expert_out, capacity, top
+        number, mixed, cot_full, small_in, expert_in, expert_out, capacity, top
     )
 
     def over_rep(value):
@@ -1267,13 +1415,20 @@
     produced1, dx1 = expert_tail(1, starts, act1, dgu1, expert_in, expert_out)
     out_part, grad_part = combine(starts, (slots0, slots1), (produced0, produced1), (dx0, dx1), capacity)
 
-    mgrad, ffn_back, agrad = back(grad_part, middle, cotangent, living, gain_ffn)
+    mgrad, ffn_back, agrad = back(grad_part, middle, cotangent, small_in, gains)
     npart, wgrad, wograd, qk_back = attend_back(
-        agrad, normed, pre, low, ctx, weights, output_weight, gain_query, gain_key, cos, sin, lens
+        agrad, normed, pre, low, ctx, weights, output_weight, small_in, cos, sin
     )
-    token_grad, small, wrows = final(npart, wgrad, tokens, mgrad, gain_attn, ffn_back, qk_back)
-    sums, small, result = line_sum(jnp.concatenate([wrows, wograd[None]], axis=0), small, out_part, middle)
-    share = g
+    token_grad, small, wrows = final(npart, wgrad, tokens, mgrad, gains, ffn_back, qk_back)
+    big = jnp.concatenate([wrows, wograd[None]], axis=0)
+
+    def widen(into, value, j):
+        return lax.dynamic_update_slice(into, value.astype(F32)[None], (j, 0, 0))
+
+    in_all = widen(jnp.zeros((local,) + in0.shape, F32), in0, 0)
+    out_all = widen(jnp.zeros((local,) + out0.shape, F32), out0, 0)
+    big, in_all, out_all = lax.optimization_barrier((big, in_all, out_all))
+    sums, small, result = line_sum(big, small, out_part, middle)
 
     def head_share(vector):
         return lax.dynamic_slice_in_dim(vector, me * (HEAD_DIM // ep), HEAD_DIM // ep)
@@ -1289,8 +1444,8 @@
         small[share : 2 * share].reshape(-1),
         head_share(small[2 * share]),
         head_share(small[2 * share + 1]),
-        jnp.stack([in0, in1]).astype(F32),
-        jnp.stack([out0, out1]).astype(F32),
+        widen(in_all, in1, 1),
+        widen(out_all, out1, 1),
     )
 
 

time: 869 us -> 846 us (0.974)
  Pallas kernels: 800 us -> 783 us
    dynamic_update_slice x0 -> x4, other arithmetic: none -> 16.9 us  [widen(): return lax.dynamic_update_slice(into, value.astype(F32)[None], (j, 0, 0))]
    pallas_call x1, Pallas kernels: 78.8 us -> 63.6 us  [front(): pl.pallas_call(front_kernel, out_shape=(sds((seqs, rows * ep, width), BF1...]
    convert_element_type x7 -> x0, other arithmetic: 13.3 us -> none  [the longest x1 6.31 us: shards(): jnp.stack([in0, in1]).astype(F32)]
  transfers between devices with their start and end apart: 5 -> 5, of which waited for: 0 -> 0; matrix products, arithmetic and copies ran while one was open for 3% -> 4% of each run, Pallas kernels for 79% -> 81%
where the time goes in v5:
time: 846 us; the launch traced here: 837 us
  Pallas kernels  783 us (93%)
  other arithmetic  30.2 us (4%)
  between operations  14.8 us (2%)
  local copies, waits for them, and re-layouts  8.65 us (1%)
    pallas_call x1, Pallas kernels, line_sum(): pl.pallas_call(line_kernel, out_shape=(sds(own.shape, BF16), sds(small.sh...  231 us
    pallas_call x1, Pallas kernels, mix(): pl.pallas_call(mix_kernel, out_shape=(sds(tokens.shape, F32), sds((seqs,...  102 us
    pallas_call x1, Pallas kernels, final(): pl.pallas_call(final_kernel, out_shape=(sds(tokens.shape, BF16), sds((8,...  82.4 us
    pallas_call x1, Pallas kernels, back(): pl.pallas_call(back_kernel, out_shape=(sds(cot.shape, F32), sds((1, width...  81.3 us
    pallas_call x1, Pallas kernels, front(): pl.pallas_call(front_kernel, out_shape=(sds((seqs, rows * ep, width), BF1...  63.6 us
    pallas_call x1, Pallas kernels, attend_back(): pl.pallas_call(attend_back_kernel, out_shape=(sds(agrad.shape, BF16), sds...  45.3 us
    pallas_call x1, Pallas kernels, expert_second(): pl.pallas_call(second_kernel, out_shape=(sds((rows, hidden), BF16), sds((...  40.7 us
    pallas_call x1, Pallas kernels, expert_first(): pl.pallas_call(functools.partial(first_kernel, capacity, top), out_shape=...  37.8 us
  transfers between devices with their start and end apart: 5, of which 0 were waited for; matrix products, arithmetic and copies ran while one was open for 4% of the time, Pallas kernels for 81%

profile of v5, /device:TPU:0, one launch (start us, length us, event | category | flops | bytes accessed | tf_op | source)
XLA Modules:
  0.0 837.5 jit_solution(6593209519705211575)
XLA Ops:
  7.2 0.0 all-gather.2.cloned.1.call-start
  7.9 0.7 bitcast_convert_fusion.4
  8.6 0.7 maximum_convert_fusion
  9.2 0.6 select_maximum_fusion.1.pk
  9.8 63.6 %front.1 = (bf16[8,256,2048]{2,1,0:T(8,128)(2,1)}, bf16[3,2048,256]{2,1,0:T(8,128)(2,1)}, bf16[8,32,2176]{2,1,0:T(8,128)(2,1)}, f32[8,2048]{1,0:T(8,128)}, f32[8,128]{1,0:T(8,128)}) custom-call(bf16[8,32,2048]{2,1,0:T(8,128)(2,1)} %tok.5, bf16[8,32,2048]{2,1,0:T(8,128)(2,1)} %cot.3, s32[8,8,32]{2,1,0:T(8,128)} %bitcast.55, bf16[8,8,32]{2,1,0:T(8,128)(2,1)} %bitcast.56, ...), custom_call_target="tpu_custom_call" | custom-call | tf_op jit(solution)/shard_map/front/pallas_call | solution.py:420
  73.5 0.0 all-gather.2.cloned.1.call-update
  73.5 0.0 reduce-scatter.7.cloned.1.call-start
  73.5 24.8 %attend.1 = (bf16[8,256,2048]{2,1,0:T(8,128)(2,1)}, f32[2,8,256,256]{3,2,1,0:T(8,128)}, bf16[3,8,256,256]{3,2,1,0:T(8,128)(2,1)}, bf16[8,256,256]{2,1,0:T(8,128)(2,1)}, bf16[8,256,2048]{2,1,0:T(8,128)(2,1)}) custom-call(bf16[8,256,2048]{2,1,0:T(8,128)(2,1)} %get-tuple-element.59.tok, bf16[3,2048,256]{2,1,0:T(8,128)(2,1)} %get-tuple-element.60.w, ...), custom_call_target="tpu_custom_call" | custom-call | flops 10000000000 | bytes 40000000 | tf_op jit(solution)/shard_map/attend/pallas_call | solution.py:822
  98.4 101.7 %mix.1 = (f32[8,32,2048]{2,1,0:T(8,128)}, bf16[8,256,2048]{2,1,0:T(8,128)(2,1)}) custom-call(bf16[8,8,32,2048]{3,2,1,0:T(8,128)(2,1)} %bitcast.51, bf16[8,32,2048]{2,1,0:T(8,128)(2,1)} %tok.5, f32[8,128]{1,0:T(8,128)} %get-tuple-element.62.small, f32[8,2048]{1,0:T(8,128)} %get-tuple-element.61.gains), custom_call_target="tpu_custom_call" | custom-call | tf_op jit(solution)/shard_map/mix/pallas_call | solution.py:476
  200.1 0.0 all-gather.2.cloned.1.call-done.cot.table
  200.1 37.8 %expert_first.1 = (f32[8,16,256]{2,1,0:T(8,128)}, f32[8,16,256]{2,1,0:T(8,128)}, s32[2,9]{1,0:T(2,128)}, bf16[1280,1024]{1,0:T(8,128)(2,1)}, bf16[1280,2048]{1,0...) custom-call(s32[1]{0:T(128)} %bitcast.number, ...), custom_call_target="tpu_custom_call" | custom-call | flops 20000000000 | bytes 60000000 | tf_op jit(solution)/shard_map/expert_first/pallas_call | solution.py:1124
  238.0 0.0 reduce-scatter.7.cloned.1.call-update
  238.0 0.0 reduce-scatter.5.cloned.1.call-start
  238.0 19.5 %first_in_grad.1 = bf16[2048,2048]{1,0:T(8,128)(2,1)} custom-call(s32[2,9]{1,0:T(2,128)} %get-tuple-element.66.starts.refs_0_, bf16[2,1280,2048]{2,1,0:T(8,128)(2,1)} %get-tuple-element.73.x_all, bf16[1280,2048]{1,0:T(8,128)(2,1)} %get-tuple-element.70.dgu), custom_call_target="tpu_custom_call" | custom-call | flops 10000000000 | bytes 20000000 | tf_op jit(solution)/shard_map/first_in_grad/pallas_call | solution.py:1192
  257.5 0.0 reduce-scatter.5.cloned.1.call-update
  257.6 0.0 reduce-scatter.11.cloned.1.call-start
  257.6 40.7 %expert_second.1 = (bf16[1280,1024]{1,0:T(8,128)(2,1)}, bf16[1280,2048]{1,0:T(8,128)(2,1)}, bf16[1024,2048]{1,0:T(8,128)(2,1)}, bf16[2048,2048]{1,0:T(8,128)(2,1)}) custom-call(s32[2,9]{1,0:T(2,128)} %get-tuple-element.66.starts.refs_0_, bf16[2,1280,2048]{2,1,0:T(8,128)(2,1)} %get-tuple-element.73.x_all, bf16[1280,2048]{1,0:T(8,128)(2,1)} %get-tuple-element.74.dy_all, ...), custom_call_target="tpu_custom_call" | custom-call | flops 24999999488 | bytes 60000000 | tf_op jit(solution)/shard_map/expert_second/pallas_call | solution.py:1252
  298.3 0.0 reduce-scatter.11.cloned.1.call-update
  298.3 0.2 reduce-scatter.9.cloned.1.call-start
  298.5 0.4 reduce-scatter.9.cloned.1.call-update
  298.9 17.8 %expert_tail.2 = (bf16[1280,2048]{1,0:T(8,128)(2,1)}, bf16[1280,2048]{1,0:T(8,128)(2,1)}) custom-call(s32[2,9]{1,0:T(2,128)} %get-tuple-element.66.starts.refs_0_, bf16[1280,1024]{1,0:T(8,128)(2,1)} %get-tuple-element.69.act, bf16[1280,2048]{1,0:T(8,128)(2,1)} %get-tuple-element.70.dgu, bf16[2,2048,2048]{2,1,0:T(8,128)(2,1)} %w_in.7, ...), custom_call_target="tpu_custom_call" | custom-call | flops 12000000000 | bytes 30000000 | tf_op jit(solution)/shard_map/expert_tail/pallas_call | solution.py:1298
  316.7 17.8 %expert_tail.3 = (bf16[1280,2048]{1,0:T(8,128)(2,1)}, bf16[1280,2048]{1,0:T(8,128)(2,1)}) custom-call(s32[2,9]{1,0:T(2,128)} %get-tuple-element.66.starts.refs_0_, bf16[1280,1024]{1,0:T(8,128)(2,1)} %get-tuple-element.75.act, bf16[1280,2048]{1,0:T(8,128)(2,1)} %get-tuple-element.76.dgu, bf16[2,2048,2048]{2,1,0:T(8,128)(2,1)} %w_in.7, ...), custom_call_target="tpu_custom_call" | custom-call | flops 12000000000 | bytes 30000000 | tf_op jit(solution)/shard_map/expert_tail/pallas_call | solution.py:1298
  334.5 19.6 %combine.1 = (bf16[8,256,2048]{2,1,0:T(8,128)(2,1)}, bf16[8,256,2048]{2,1,0:T(8,128)(2,1)}) custom-call(s32[2,9]{1,0:T(2,128)} %get-tuple-element.66.starts.refs_0_, f32[8,16,256]{2,1,0:T(8,128)} %get-tuple-element.67.refs_1_, f32[8,16,256]{2,1,0:T(8,128)} %get-tuple-element.68.refs_2_, bf16[1280,2048]{1,0:T(8,128)(2,1)} %get-tuple-element.71.refs_3_, ...), custom_call_target="tpu_custom_call" | custom-call | flops 3000000000 | bytes 40000000 | tf_op jit(solution)/shard_map/combine/pallas_call | solution.py:1349
  354.1 81.3 %back.1 = (f32[8,32,2048]{2,1,0:T(8,128)}, f32[1,2048]{1,0:T(1,128)}, bf16[8,256,2048]{2,1,0:T(8,128)(2,1)}) custom-call(bf16[8,8,32,2048]{3,2,1,0:T(8,128)(2,1)} %bitcast.50, f32[8,32,2048]{2,1,0:T(8,128)} %get-tuple-element.81.middle.mid_rows, bf16[8,32,2048]{2,1,0:T(8,128)(2,1)} %cot.3, f32[8,128]{1,0:T(8,128)} %get-tuple-element.62.small, ...), custom_call_target="tpu_custom_call" | custom-call | tf_op jit(solution)/shard_map/back/pallas_call | solution.py:521
  435.3 0.0 copy-start.3
  435.3 45.3 %attend_back.1 = (bf16[8,256,2048]{2,1,0:T(8,128)(2,1)}, bf16[3,2048,256]{2,1,0:T(8,128)(2,1)}, bf16[256,2048]{1,0:T(8,128)(2,1)}, f32[8,128]{1,0:T(8,128)}) custom-call(bf16[8,256,2048]{2,1,0:T(8,128)(2,1)} %get-tuple-element.82.agrad, bf16[8,256,2048]{2,1,0:T(8,128)(2,1)} %get-tuple-element.83.normed, f32[2,8,256,256]{3,2,1,0:T(8,128)} %get-tuple-element.84.pre, ...), custom_call_target="tpu_custom_call" | custom-call | flops 20000000000 | bytes 40000000 | tf_op jit(solution)/shard_map/attend_back/pallas_call | solution.py:910
  480.7 0.7 slice.31
  481.4 0.0 copy-done.3
  481.4 0.6 select_maximum_fusion.others
  482.0 0.0 copy-start.2
  482.0 82.4 %final.1 = (bf16[8,32,2048]{2,1,0:T(8,128)(2,1)}, f32[8,128]{1,0:T(8,128)}, bf16[3,256,2048]{2,1,0:T(8,128)(2,1)}) custom-call(bf16[8,8,32,2048]{3,2,1,0:T(8,128)(2,1)} %bitcast.48, bf16[3,2048,256]{2,1,0:T(8,128)(2,1)} %get-tuple-element.88.wgrad, bf16[8,32,2048]{2,1,0:T(8,128)(2,1)} %tok.5, f32[8,32,2048]{2,1,0:T(8,128)} %get-tuple-element.89.mgrad, ...), custom_call_target="tpu_custom_call" | custom-call | tf_op jit(solution)/shard_map/final/pallas_call | solution.py:612
  564.4 0.0 copy-done.2
  564.4 4.2 pad_maximum_fusion
  568.7 0.0 reduce-scatter.7.cloned.1.call-done
  568.7 3.7 pad_convert_fusion.1
  572.4 0.0 reduce-scatter.5.cloned.1.call-done
  572.4 6.1 pad_convert_fusion
  578.5 230.7 %line_sum.1 = (bf16[16,64,2048]{2,1,0:T(8,128)(2,1)}, f32[8,128]{1,0:T(8,128)}, bf16[8,32,2048]{2,1,0:T(8,128)(2,1)}) custom-call(bf16[16,64,2048]{2,1,0:T(8,128)(2,1)} %bitcast.47, f32[8,128]{1,0:T(8,128)} %get-tuple-element.96.small, bf16[8,8,32,2048]{3,2,1,0:T(8,128)(2,1)} %bitcast.49, f32[8,32,2048]{2,1,0:T(8,128)} %get-tuple-element.81.middle.mid_rows), custom_call_target="tpu_custom_call" | custom-call | tf_op jit(solution)/shard_map/line_sum/pallas_call | solution.py:761
  809.1 0.8 fusion.3
  809.9 0.6 fusion.1
  810.5 0.6 fusion
  811.1 1.3 slice_bitcast_fusion
  812.4 2.7 fusion.2
  815.1 1.6 bitcast_convert_fusion
  816.8 1.6 bitcast_convert_fusion.1
  818.4 1.6 bitcast_convert_fusion.2
  820.0 1.6 bitcast_convert_fusion.3
  821.7 0.0 copy-start.1
  821.7 0.0 reduce-scatter.11.cloned.1.call-done
  821.7 2.9 convert_dynamic-update-slice_fusion.1
  824.6 0.0 copy-start
  824.6 0.0 reduce-scatter.9.cloned.1.call-done
  824.6 4.2 convert_dynamic-update-slice_fusion
  828.8 0.0 copy-done.1
  828.8 1.0 copy.34
  829.8 0.0 copy-done
  829.8 1.0 copy.35
  (1 shorter events, 0.0 us)
Async XLA Ops:
  7.2 192.9 %all-gather.2.cloned.1.call-start = ((), (), s32[]{:S(2)}) async-start(), calls=%async_computation.4 | async-start | bytes 10027008 | tf_op jit(solution)/shard_map/all_gather | solution.py:1388
  73.5 495.2 %reduce-scatter.7.cloned.1.call-start = ((), (), s32[]{:S(2)}) async-start(), calls=%async_computation.6 | async-start | bytes 5242880 | tf_op jit(solution)/shard_map/reduce_scatter | solution.py:1405
  238.0 334.4 %reduce-scatter.5.cloned.1.call-start = ((), (), s32[]{:S(2)}) async-start(), calls=%async_computation.5 | async-start | bytes 10485760 | tf_op jit(solution)/shard_map/reduce_scatter | solution.py:1405
  257.6 564.1 %reduce-scatter.11.cloned.1.call-start = ((), (), s32[]{:S(2)}) async-start(), calls=%async_computation.8 | async-start | bytes 5242880 | tf_op jit(solution)/shard_map/reduce_scatter | solution.py:1405
  298.3 526.3 %reduce-scatter.9.cloned.1.call-start = ((), (), s32[]{:S(2)}) async-start(), calls=%async_computation.7 | async-start | bytes 10485760 | tf_op jit(solution)/shard_map/reduce_scatter | solution.py:1405
  435.3 46.0 %copy-start.3 = (f32[1,2048]{1,0:T(1,128)S(1)}, f32[1,2048]{1,0:T(1,128)}, u32[]{:S(2)}) copy-start(f32[1,2048]{1,0:T(1,128)} %get-tuple-element.90) | copy-start | bytes 24580
  482.0 82.4 %copy-start.2 = (bf16[256,2048]{1,0:T(8,128)(2,1)S(1)}, bf16[256,2048]{1,0:T(8,128)(2,1)}, u32[]{:S(2)}) copy-start(bf16[256,2048]{1,0:T(8,128)(2,1)} %get-tuple-element.93) | copy-start | bytes 3145732
  821.7 7.1 copy-start.1
  824.6 5.2 copy-start
Sparse Core Ops, SparseCore 0:
  73.6 76.3 all-gather.1
  238.1 82.2 reduce-scatter.6
  322.8 145.1 reduce-scatter.4
  470.1 77.4 reduce-scatter.10
  549.7 219.3 reduce-scatter.8

commit v6 on v5

--- a/solution.py
+++ b/solution.py
@@ -159,10 +159,10 @@
 
 
 class Reduce:
-    def __init__(self, at, part, held, x1, y1, x2, y2, hs, hr, d1s, d1r, d2s, d2r):
-        self.at, self.part, self.held = at, part, held
+    def __init__(self, at, part, held, mine, x1, y1, x2, y2, ms, hs, hr, d1s, d1r, d2s, d2r):
+        self.at, self.part, self.held, self.mine = at, part, held, mine
         self.x1, self.y1, self.x2, self.y2 = x1, y1, x2, y2
-        self.hs, self.hr, self.d1s, self.d1r, self.d2s, self.d2r = hs, hr, d1s, d1r, d2s, d2r
+        self.ms, self.hs, self.hr, self.d1s, self.d1r, self.d2s, self.d2r = ms, hs, hr, d1s, d1r, d2s, d2r
         self.half = part.shape[2] // 2
 
     @staticmethod
@@ -170,6 +170,7 @@
         s, _, t, d = part.shape
         dma = pltpu.SemaphoreType.DMA
         return [
+            pltpu.VMEM((s, 4, t, d), BF16),
             pltpu.VMEM((s, 4, t, d), BF16),
             pltpu.VMEM((s, t // 2, d), BF16),
             pltpu.VMEM((s, t // 2, d), BF16),
@@ -177,19 +178,25 @@
             pltpu.VMEM((s, t, d), BF16),
             dma((4, s)),
             dma((4, s)),
+            dma((4, s)),
             dma((2, s)),
             dma((2, s)),
             dma((2, s)),
             dma((2, s)),
         ]
 
-    sems = 11
+    sems = 13
 
     def core_copy(self, s, k):
         at = self.at
         dest = (at.sb, at.sb + at.dx, at.sb + at.dy, at.sb + at.dx + at.dy)[k]
         return at.push(self.part.at[s, dest], self.held.at[s, k], self.hs.at[k, s], self.hr.at[k, s], at.sb)
 
+    def load(self, s, k):
+        at = self.at
+        dest = (at.me, at.xn, at.yn, at.dg)[k]
+        return pltpu.make_async_copy(self.part.at[s, dest], self.mine.at[s, k], self.ms.at[k, s])
+
     def first(self, s, k):
         at, h = self.at, self.half
         src = self.held.at[s, 3, pl.ds(k * h, h)]
@@ -203,32 +210,36 @@
     def start(self, s):
         for k in (3, 1, 2, 0):
             self.core_copy(s, k).start()
+            self.load(s, k).start()
 
     def hop1(self, s):
         self.core_copy(s, 3).wait_recv()
-        self.held[s, 3] = (self.held[s, 3].astype(F32) + self.part[s, self.at.dg].astype(F32)).astype(BF16)
+        self.load(s, 3).wait()
+        self.held[s, 3] = (self.held[s, 3].astype(F32) + self.mine[s, 3].astype(F32)).astype(BF16)
         self.first(s, 0).start()
         self.first(s, 1).start()
 
     def hop2(self, s):
         h = self.half
-        for k, dest, extra, rows, rest in (
-            (0, self.at.xn, self.y1, pl.ds(h, h), pl.ds(0, h)),
-            (1, self.at.yn, self.x1, pl.ds(0, h), pl.ds(h, h)),
+        for k, extra, rows, rest in (
+            (0, self.y1, pl.ds(h, h), pl.ds(0, h)),
+            (1, self.x1, pl.ds(0, h), pl.ds(h, h)),
         ):
             self.core_copy(s, 1 + k).wait_recv()
+            self.load(s, 1 + k).wait()
             self.first(s, 1 - k).wait_recv()
-            held, part = self.held.at[s, 1 + k], self.part.at[s, dest]
-            held[rows] = (held[rows].astype(F32) + part[rows].astype(F32) + extra[s].astype(F32)).astype(BF16)
-            held[rest] = (held[rest].astype(F32) + part[rest].astype(F32)).astype(BF16)
+            held, mine = self.held.at[s, 1 + k], self.mine.at[s, 1 + k]
+            held[rows] = (held[rows].astype(F32) + mine[rows].astype(F32) + extra[s].astype(F32)).astype(BF16)
+            held[rest] = (held[rest].astype(F32) + mine[rest].astype(F32)).astype(BF16)
             self.second(s, k).start()
 
     def total(self, s):
         self.core_copy(s, 0).wait_recv()
+        self.load(s, 0).wait()
         self.second(s, 0).wait_recv()
         self.second(s, 1).wait_recv()
         return (
-            self.part[s, self.at.me].astype(F32)
+            self.mine[s, 0].astype(F32)
             + self.held[s, 0].astype(F32)
             + self.x2[s].astype(F32)
             + self.y2[s].astype(F32)
@@ -476,7 +487,7 @@
     return pl.pallas_call(
         mix_kernel,
         out_shape=(sds(tokens.shape, F32), sds((seqs, rows * ep, width), BF16)),
-        in_specs=[VM] * 4,
+        in_specs=[AN] + [VM] * 3,
         out_specs=(VM, AN),
         scratch_shapes=[pltpu.VMEM(tokens.shape, BF16)] + Reduce.scratch(part) + Gather.scratch(seqs),
         compiler_params=pltpu.CompilerParams(collective_id=2, **COMM),
@@ -525,7 +536,7 @@
             sds((1, width), F32),
             sds((seqs, rows * ep, width), BF16),
         ),
-        in_specs=[VM] * 5,
+        in_specs=[AN] + [VM] * 4,
         out_specs=(VM, VM, AN),
         scratch_shapes=[pltpu.VMEM(cot.shape, BF16)] + Reduce.scratch(gpart) + Gather.scratch(seqs),
         compiler_params=pltpu.CompilerParams(collective_id=3, **COMM),
@@ -533,37 +544,139 @@
     )(gpart, middle, cot, small, gains)
 
 
-def final_kernel(part, wgrad, tok, mgrad, gains, others, tgrad, small, wrows, ggrad, parcel, landed, *scratch):
+def finish_kernel(
+    wgrad, wograd, npart, opart, tok, middle, mgrad, gains, others,
+    out, small_out, result, tgrad,
+    own, held, met, ggrad, parcel, landed, spare,
+    wsend, wrecv, local, gsend, grecv, os, or_, ps, pr, qs, qr, fs, fr, ss, sr, *scratch,
+):
     at = Place()
+    z, me = at.rep, at.me
+    n = Reduce.sems
+    normed_sum = Reduce(at, npart, *scratch[:n])
+    result_sum = Reduce(at, opart, *scratch[n:])
     seqs = tok.shape[0]
-    n = Reduce.sems
-    reduce = Reduce(at, part, *scratch[:n])
-    wsend, wrecv, local, gsend, grecv = scratch[n:]
-    width = wgrad.shape[2]
-    block = wrows.shape[1]
-    at.greet(at.peers())
-    cols = pl.ds(pl.multiple_of(at.me * width, width), width)
-
-    def weight_copy(m, dev):
-        rows = pl.ds(pl.multiple_of(dev * block, block), block)
-        return at.push(wgrad.at[:, rows], wrows.at[:, :, cols], wsend.at[m], wrecv.at[m], dev)
-
-    mine = pl.ds(pl.multiple_of(at.me * block, block), block)
-    own = pltpu.make_async_copy(wgrad.at[:, mine], wrows.at[:, :, cols], local)
-    own.start()
-    for m, dev in enumerate(at.peers()):
-        weight_copy(m, dev).start()
-    each(seqs, reduce.start)
-    each(seqs, reduce.hop1)
-    each(seqs, reduce.hop2)
+    parts, pieces = own.shape[:2]
+    chunks = parts * pieces
+    width = wgrad.shape[3]
+    peers = at.peers()
+    barrier = pltpu.get_barrier_semaphore()
+    line = [lax.rem(z + k, 4) for k in range(1, 4)]
+    for dev in line:
+        pl.semaphore_signal(barrier, inc=1, device_id=(dev, me), device_id_type=MESH)
+    for dev in peers:
+        pl.semaphore_signal(barrier, inc=1, device_id=(z, dev), device_id_type=MESH)
+    pl.semaphore_wait(barrier, 10)
+    inner = jnp.logical_and(z > 0, z < 3)
+    outer_end, partner, outer = 1 + z // 3, 3 - z, 3 * (z - 1)
+    cols = pl.ds(pl.multiple_of(me * width, width), width)
+
+    def column_copy(m, j, dev):
+        rows = pl.ds(pl.multiple_of(dev * pieces, pieces), pieces)
+        return at.push(wgrad.at[j, rows], own.at[1 + j, :, :, cols], wsend.at[m, j], wrecv.at[m, j], dev)
+
+    mine_rows = pl.ds(pl.multiple_of(me * pieces, pieces), pieces)
+    locals_ = [pltpu.make_async_copy(wgrad.at[j, mine_rows], own.at[1 + j, :, :, cols], local.at[j]) for j in range(3)]
+    locals_.append(pltpu.make_async_copy(wograd, own.at[0], local.at[3]))
+    for copy in locals_:
+        copy.start()
+    for j in range(3):
+        for m, dev in enumerate(peers):
+            column_copy(m, j, dev).start()
+    each(seqs, normed_sum.start)
+    each(seqs, result_sum.start)
     ggrad[...] = jnp.zeros_like(ggrad)
 
-    def rows(s):
-        tg, back = attn_back_rows(reduce.total(s), tok[s], mgrad[s], gains[0:1])
+    def piece(ref, c):
+        return ref.at[c // pieces, lax.rem(c, pieces)]
+
+    def line_push(src, dst, send, recv, dev):
+        return pltpu.make_async_remote_copy(
+            src_ref=src, dst_ref=dst, send_sem=send, recv_sem=recv, device_id=(dev, me), device_id_type=MESH
+        )
+
+    def inward(c):
+        return line_push(piece(own, c), piece(held, c), os.at[c], or_.at[c], outer_end)
+
+    def across(c):
+        return line_push(piece(held, c), met.at[c // 2], ps.at[c], pr.at[c], partner)
+
+    def share(c):
+        return line_push(piece(out, c), piece(out, c), qs.at[c], qr.at[c], partner)
+
+    def outward(c):
+        return line_push(piece(out, c), piece(out, c), fs.at[c], fr.at[c], outer)
+
+    def mine(c):
+        return 1 + lax.rem(c, 2) == z
+
+    def ready(part):
+        for j in range(parts):
+
+            @pl.when(part == j)
+            def _():
+                locals_[(3, 0, 1, 2)[j]].wait()
+                if j > 0:
+                    for m, dev in enumerate(peers):
+                        column_copy(m, j - 1, dev).wait_recv()
+
+    def step(c):
+        @pl.when(lax.rem(c, pieces) == 0)
+        def _():
+            ready(c // pieces)
+
+        @pl.when(jnp.logical_not(inner))
+        def _():
+            inward(c).start()
+
+        @pl.when(inner)
+        def _():
+            inward(c).wait_recv()
+            here = piece(held, c)
+            here[...] = (here[...].astype(F32) + piece(own, c)[...].astype(F32)).astype(BF16)
+
+            @pl.when(jnp.logical_not(mine(c)))
+            def _():
+                across(c).start()
+
+    def settle(c):
+        @pl.when(jnp.logical_and(inner, mine(c)))
+        def _():
+            across(c).wait_recv()
+            piece(out, c)[...] = (piece(held, c)[...].astype(F32) + met[c // 2].astype(F32)).astype(BF16)
+            share(c).start()
+            outward(c).start()
+
+    def forward(c):
+        @pl.when(jnp.logical_and(inner, jnp.logical_not(mine(c))))
+        def _():
+            share(c).wait_recv()
+            outward(c).start()
+
+    def token_rows(s):
+        tg, back = attn_back_rows(normed_sum.total(s), tok[s], mgrad[s], gains[0:1])
         tgrad[s] = tg
         ggrad[...] += jnp.sum(back, axis=0, keepdims=True)
 
-    each(seqs, rows)
+    def out_rows(s):
+        result[s] = (middle[s] + result_sum.total(s)).astype(BF16)
+
+    jobs = (
+        (step, 0, chunks), (settle, 1, chunks), (forward, 2, chunks),
+        (normed_sum.hop1, 2, seqs), (normed_sum.hop2, 6, seqs), (token_rows, 10, seqs),
+        (result_sum.hop1, 6, seqs), (result_sum.hop2, 10, seqs), (out_rows, 14, seqs),
+    )
+
+    def tick(i, _):
+        for job, lag, count in jobs:
+
+            @pl.when(jnp.logical_and(i >= lag, i < lag + count))
+            def _():
+                job(i - lag)
+
+        return 0
+
+    lax.fori_loop(0, max(lag + count for _, lag, count in jobs), tick, 0)
 
     parcel[...] = jnp.zeros_like(parcel)
     devices = parcel.shape[0]
@@ -578,203 +691,99 @@
     def parcel_copy(m, dev):
         return at.push(parcel.at[dev], landed.at[m], gsend.at[m], grecv.at[m], dev)
 
-    for m, dev in enumerate(at.peers()):
+    for m, dev in enumerate(peers):
         parcel_copy(m, dev).start()
-    total = parcel[at.me]
-    for m, dev in enumerate(at.peers()):
+    total = parcel[me]
+    for m, dev in enumerate(peers):
         parcel_copy(m, dev).wait_recv()
         total = total + landed[m]
-    small[...] = total
-    each(seqs, reduce.finish)
-    for m, dev in enumerate(at.peers()):
-        weight_copy(m, dev).wait()
+    spare[0] = total
+
+    def small_copy(k):
+        return line_push(spare.at[0], spare.at[1 + k], ss.at[k], sr.at[k], line[k])
+
+    for k in range(3):
+        small_copy(k).start()
+
+    @pl.when(jnp.logical_not(inner))
+    def _():
+        each(chunks, lambda c: outward(c).wait_recv())
+        each(chunks, lambda c: inward(c).wait_send())
+
+    @pl.when(inner)
+    def _():
+        def sent(c):
+            outward(c).wait_send()
+
+            @pl.when(mine(c))
+            def _():
+                share(c).wait_send()
+
+            @pl.when(jnp.logical_not(mine(c)))
+            def _():
+                across(c).wait_send()
+
+        each(chunks, sent)
+
+    each(seqs, normed_sum.finish, result_sum.finish)
+    for m, dev in enumerate(peers):
         parcel_copy(m, dev).wait_send()
-    own.wait()
-
-
-def final(part, wgrad, tokens, mgrad, gains, ffn_back, qk_back):
+        for j in range(3):
+            column_copy(m, j, dev).wait_send()
+    total = spare[0]
+    for k in range(3):
+        small_copy(k).wait()
+        total = total + spare[1 + k]
+    small_out[...] = total
+
+
+def finish(wgrad, wograd, npart, opart, tokens, middle, mgrad, gains, ffn_back, qk_back):
     seqs, rows, width = tokens.shape
     ep = lax.axis_size("ep")
-    if ep != 8:
-        normed_grad = lax.psum_scatter(part, "ep", scatter_dimension=1, tiled=True).astype(F32)
+    if ep != 8 or lax.axis_size("rep") != 4:
+        normed_grad = lax.psum_scatter(npart, "ep", scatter_dimension=1, tiled=True).astype(F32)
+        moe = lax.psum_scatter(opart, "ep", scatter_dimension=1, tiled=True).astype(F32)
         tg, backs = attn_back_rows(normed_grad, tokens, mgrad, gains[0])
         wrows = lax.all_to_all(wgrad, "ep", split_axis=1, concat_axis=2, tiled=True)
         share = width // ep
         small = jnp.concatenate([jnp.sum(backs, axis=(0, 1)), ffn_back[0], qk_back[0], qk_back[1]])
-        small = lax.psum(small, "ep")
+        small = lax.psum(small, ("ep", "rep"))
         mine = lax.axis_index("ep") * share
         cut = [lax.dynamic_slice_in_dim(small, k * width + mine, share).reshape(-1, 128) for k in range(2)]
         small = jnp.concatenate(cut + [small[2 * width :].reshape(2, HEAD_DIM)], axis=0)
-        return tg, jnp.pad(small, ((0, 8 - small.shape[0]), (0, 0))), wrows
+        big = lax.psum(jnp.concatenate([wograd[None], wrows], axis=0), "rep")
+        return big, jnp.pad(small, ((0, 8 - small.shape[0]), (0, 0))), (middle + moe).astype(BF16), tg
     others = jnp.concatenate([ffn_back, jnp.pad(qk_back[:2], ((0, 0), (0, width - HEAD_DIM)))], axis=0)
-    part = part.reshape(seqs, ep, rows, width)
+    npart, opart = (p.reshape(seqs, ep, rows, width) for p in (npart, opart))
+    pieces = 4
+    block = wograd.shape[0] // pieces
+    wgrad = wgrad.reshape(3, wgrad.shape[1] // block, block, wgrad.shape[2])
+    wograd = wograd.reshape(pieces, block, width)
+    whole = (4, pieces, block, width)
     dma = pltpu.SemaphoreType.DMA
-    return pl.pallas_call(
-        final_kernel,
-        out_shape=(
-            sds(tokens.shape, BF16),
-            sds((8, 128), F32),
-            sds((3, wgrad.shape[1] // ep, wgrad.shape[2] * ep), BF16),
-        ),
-        in_specs=[VM] * 6,
-        out_specs=(VM, VM, AN),
-        scratch_shapes=[pltpu.VMEM((1, width), F32), pltpu.VMEM((ep, 8, 128), F32), pltpu.VMEM((7, 8, 128), F32)]
-        + Reduce.scratch(part)
-        + [dma((7,)), dma((7,)), dma, dma((7,)), dma((7,))],
-        compiler_params=pltpu.CompilerParams(collective_id=4, **COMM),
-        name="final",
-    )(part, wgrad, tokens, mgrad, gains, others)
-
-
-def line_kernel(
-    own, small, opart, mid_rows, out, small_out, result, held, met, landed, os, or_, ps, pr, qs, qr, fs, fr, ss, sr, *scratch
-):
-    at = Place()
-    reduce = Reduce(at, opart, *scratch)
-    seqs = opart.shape[0]
-    z = lax.axis_index("rep")
-    ep = lax.axis_index("ep")
-    chunks = own.shape[0]
-
-    def push(src, dst, send, recv, dev):
-        return pltpu.make_async_remote_copy(
-            src_ref=src, dst_ref=dst, send_sem=send, recv_sem=recv, device_id=(dev, ep), device_id_type=MESH
-        )
-
-    barrier = pltpu.get_barrier_semaphore()
-    others = [lax.rem(z + k, 4) for k in range(1, 4)]
-    for dev in others:
-        pl.semaphore_signal(barrier, inc=1, device_id=(dev, ep), device_id_type=MESH)
-    for dev in (at.xn, at.yn, at.sb):
-        pl.semaphore_signal(barrier, inc=1, device_id=(z, dev), device_id_type=MESH)
-    pl.semaphore_wait(barrier, 6)
-    inner = jnp.logical_and(z > 0, z < 3)
-    middle, partner, outer = 1 + z // 3, 3 - z, 3 * (z - 1)
-
-    def inward(c):
-        return push(own.at[c], held.at[c], os.at[c], or_.at[c], middle)
-
-    def across(c):
-        return push(held.at[c], met.at[c], ps.at[c], pr.at[c], partner)
-
-    def share(c):
-        return push(out.at[c], out.at[c], qs.at[c], qr.at[c], partner)
-
-    def outward(c):
-        return push(out.at[c], out.at[c], fs.at[c], fr.at[c], outer)
-
-    def small_copy(k):
-        return push(small, landed.at[k], ss.at[k], sr.at[k], others[k])
-
-    def out_rows(s):
-        result[s] = (mid_rows[s] + reduce.total(s)).astype(BF16)
-
-    for k in range(3):
-        small_copy(k).start()
-
-    @pl.when(jnp.logical_not(inner))
-    def _():
-        each(chunks, lambda c: inward(c).start())
-        each(seqs, reduce.start)
-        each(seqs, reduce.hop1)
-        each(seqs, reduce.hop2)
-        each(seqs, out_rows)
-        each(chunks, lambda c: outward(c).wait_recv())
-        each(chunks, lambda c: inward(c).wait_send())
-
-    def mine(c):
-        return 1 + lax.rem(c, 2) == z
-
-    @pl.when(inner)
-    def _():
-        each(seqs, reduce.start)
-        half = seqs // 2
-
-        def run(c, _):
-            for step, lag in ((reduce.hop1, 0), (reduce.hop2, half), (out_rows, 2 * half)):
-
-                @pl.when(jnp.logical_and(c >= lag, c < seqs + lag))
-                def _():
-                    step(c - lag)
-
-            @pl.when(c < chunks)
-            def _():
-                inward(c).wait_recv()
-                held[c] = (held[c].astype(F32) + own[c].astype(F32)).astype(BF16)
-
-                @pl.when(jnp.logical_not(mine(c)))
-                def _():
-                    across(c).start()
-
-            b = c - 1
-
-            @pl.when(jnp.logical_and(jnp.logical_and(c >= 1, c < chunks + 1), mine(c + 1)))
-            def _():
-                across(b).wait_recv()
-                out[b] = (held[b].astype(F32) + met[b].astype(F32)).astype(BF16)
-                share(b).start()
-                outward(b).start()
-
-            a = c - 2
-
-            @pl.when(jnp.logical_and(c >= 2, jnp.logical_not(mine(c))))
-            def _():
-                share(a).wait_recv()
-                outward(a).start()
-
-            return 0
-
-        lax.fori_loop(0, chunks + 2, run, 0)
-
-        def finish(c):
-            outward(c).wait_send()
-
-            @pl.when(mine(c))
-            def _():
-                share(c).wait_send()
-
-            @pl.when(jnp.logical_not(mine(c)))
-            def _():
-                across(c).wait_send()
-
-        each(chunks, finish)
-
-    each(seqs, reduce.finish)
-    total = small[...]
-    for k in range(3):
-        small_copy(k).wait()
-        total = total + landed[k]
-    small_out[...] = total
-
-
-def line_sum(big, small, opart, middle):
-    if lax.axis_size("rep") != 4 or lax.axis_size("ep") != 8:
-        moe = lax.psum_scatter(opart, "ep", scatter_dimension=1, tiled=True).astype(F32)
-        return lax.psum(big, "rep"), lax.psum(small, "rep"), (middle + moe).astype(BF16)
-    seqs, tokens, width = middle.shape
-    opart = opart.reshape(seqs, 8, tokens, width)
-    assert 2 * seqs <= 18
-    count, rows, cols = big.shape
-    chunks = 16
-    own = big.reshape(chunks, count * rows // chunks, cols)
-    dma = pltpu.SemaphoreType.DMA
-    out, small, result = pl.pallas_call(
-        line_kernel,
-        out_shape=(sds(own.shape, BF16), sds(small.shape, F32), sds(middle.shape, BF16)),
-        in_specs=[VM] * 4,
-        out_specs=(VM, VM, VM),
+    chunks = 4 * pieces
+    out, small, result, tgrad = pl.pallas_call(
+        finish_kernel,
+        out_shape=(sds(whole, BF16), sds((8, 128), F32), sds(tokens.shape, BF16), sds(tokens.shape, BF16)),
+        in_specs=[VM, VM, AN, AN] + [VM] * 5,
+        out_specs=(VM, VM, VM, VM),
         scratch_shapes=[
-            pltpu.VMEM(own.shape, BF16),
-            pltpu.VMEM(own.shape, BF16),
-            pltpu.VMEM((3,) + small.shape, F32),
+            pltpu.VMEM(whole, BF16),
+            pltpu.VMEM(whole, BF16),
+            pltpu.VMEM((chunks // 2, block, width), BF16),
+            pltpu.VMEM((1, width), F32),
+            pltpu.VMEM((ep, 8, 128), F32),
+            pltpu.VMEM((7, 8, 128), F32),
+            pltpu.VMEM((4, 8, 128), F32),
         ]
+        + [dma((7, 3)), dma((7, 3)), dma((4,)), dma((7,)), dma((7,))]
         + [dma((chunks,))] * 8
         + [dma((3,))] * 2
-        + Reduce.scratch(opart),
-        compiler_params=pltpu.CompilerParams(collective_id=5, **COMM),
-        name="line_sum",
-    )(own, small, opart, middle)
-    return out.reshape(big.shape), small, result
+        + 2 * Reduce.scratch(npart),
+        compiler_params=pltpu.CompilerParams(collective_id=4, has_side_effects=True, vmem_limit_bytes=61 << 20),
+        name="finish",
+    )(wgrad, wograd, npart, opart, tokens, middle, mgrad, gains, others)
+    return out.reshape(4, pieces * block, width), small, result, tgrad
 
 
 def dot(a, b, ca, cb):
@@ -1419,16 +1428,16 @@
     npart, wgrad, wograd, qk_back = attend_back(
         agrad, normed, pre, low, ctx, weights, output_weight, small_in, cos, sin
     )
-    token_grad, small, wrows = final(npart, wgrad, tokens, mgrad, gains, ffn_back, qk_back)
-    big = jnp.concatenate([wrows, wograd[None]], axis=0)
 
     def widen(into, value, j):
         return lax.dynamic_update_slice(into, value.astype(F32)[None], (j, 0, 0))
 
     in_all = widen(jnp.zeros((local,) + in0.shape, F32), in0, 0)
     out_all = widen(jnp.zeros((local,) + out0.shape, F32), out0, 0)
-    big, in_all, out_all = lax.optimization_barrier((big, in_all, out_all))
-    sums, small, result = line_sum(big, small, out_part, middle)
+    npart, in_all, out_all = lax.optimization_barrier((npart, in_all, out_all))
+    sums, small, result, token_grad = finish(
+        wgrad, wograd, npart, out_part, tokens, middle, mgrad, gains, ffn_back, qk_back
+    )
 
     def head_share(vector):
         return lax.dynamic_slice_in_dim(vector, me * (HEAD_DIM // ep), HEAD_DIM // ep)
@@ -1436,10 +1445,10 @@
     return (
         result,
         token_grad,
-        sums[0].astype(F32),
         sums[1].astype(F32),
         sums[2].astype(F32),
         sums[3].astype(F32),
+        sums[0].astype(F32),
         small[:share].reshape(-1),
         small[share : 2 * share].reshape(-1),
         head_share(small[2 * share]),

time: 846 us -> 834 us (0.986)
    pallas_call x2 -> x1, Pallas kernels: 313 us -> 307 us  [finish(): pl.pallas_call(finish_kernel, out_shape=(sds(whole, BF16), sds((8, 128),...]
  transfers between devices with their start and end apart: 5 -> 5, of which waited for: 0 -> 0; matrix products, arithmetic and copies ran while one was open for 4% -> 3% of each run, Pallas kernels for 81% -> 82%
where the time goes in v6:
time: 834 us; the launch traced here: 826 us
  Pallas kernels  775 us (93%)
  other arithmetic  26.1 us (3%)
  between operations  14.8 us (2%)
  local copies, waits for them, and re-layouts  8.62 us (1%)
    pallas_call x1, Pallas kernels, finish(): pl.pallas_call(finish_kernel, out_shape=(sds(whole, BF16), sds((8, 128),...  307 us
    pallas_call x1, Pallas kernels, mix(): pl.pallas_call(mix_kernel, out_shape=(sds(tokens.shape, F32), sds((seqs,...  102 us
    pallas_call x1, Pallas kernels, back(): pl.pallas_call(back_kernel, out_shape=(sds(cot.shape, F32), sds((1, width...  79.4 us
    pallas_call x1, Pallas kernels, front(): pl.pallas_call(front_kernel, out_shape=(sds((seqs, rows * ep, width), BF1...  63.7 us
    pallas_call x1, Pallas kernels, attend_back(): pl.pallas_call(attend_back_kernel, out_shape=(sds(agrad.shape, BF16), sds...  45.4 us
    pallas_call x1, Pallas kernels, expert_second(): pl.pallas_call(second_kernel, out_shape=(sds((rows, hidden), BF16), sds((...  40.7 us
    pallas_call x1, Pallas kernels, expert_first(): pl.pallas_call(functools.partial(first_kernel, capacity, top), out_shape=...  37.8 us
    pallas_call x2, Pallas kernels, expert_tail(): pl.pallas_call(functools.partial(tail_kernel, j), out_shape=(sds((rows, w...  35.6 us
  transfers between devices with their start and end apart: 5, of which 0 were waited for; matrix products, arithmetic and copies ran while one was open for 3% of the time, Pallas kernels for 82%

profile of v6, /device:TPU:0, one launch (start us, length us, event | category | flops | bytes accessed | tf_op | source)
XLA Modules:
  0.0 825.7 jit_solution(7264799973589476114)
XLA Ops:
  7.2 0.0 all-gather.2.cloned.1.call-start
  7.9 0.7 bitcast_convert_fusion.4
  8.6 0.7 maximum_convert_fusion
  9.2 0.6 select_maximum_fusion.1.pk
  9.8 63.7 %front.1 = (bf16[8,256,2048]{2,1,0:T(8,128)(2,1)}, bf16[3,2048,256]{2,1,0:T(8,128)(2,1)}, bf16[8,32,2176]{2,1,0:T(8,128)(2,1)}, f32[8,2048]{1,0:T(8,128)}, f32[8,128]{1,0:T(8,128)}) custom-call(bf16[8,32,2048]{2,1,0:T(8,128)(2,1)} %tok.5, bf16[8,32,2048]{2,1,0:T(8,128)(2,1)} %cot.3, s32[8,8,32]{2,1,0:T(8,128)} %bitcast.55, bf16[8,8,32]{2,1,0:T(8,128)(2,1)} %bitcast.56, ...), custom_call_target="tpu_custom_call" | custom-call | tf_op jit(solution)/shard_map/front/pallas_call | solution.py:431
  73.5 0.0 all-gather.2.cloned.1.call-update
  73.5 0.0 reduce-scatter.7.cloned.1.call-start
  73.6 24.9 %attend.1 = (bf16[8,256,2048]{2,1,0:T(8,128)(2,1)}, f32[2,8,256,256]{3,2,1,0:T(8,128)}, bf16[3,8,256,256]{3,2,1,0:T(8,128)(2,1)}, bf16[8,256,256]{2,1,0:T(8,128)(2,1)}, bf16[8,256,2048]{2,1,0:T(8,128)(2,1)}) custom-call(bf16[8,256,2048]{2,1,0:T(8,128)(2,1)} %get-tuple-element.57.tok, bf16[3,2048,256]{2,1,0:T(8,128)(2,1)} %get-tuple-element.58.w, ...), custom_call_target="tpu_custom_call" | custom-call | flops 10000000000 | bytes 40000000 | tf_op jit(solution)/shard_map/attend/pallas_call | solution.py:831
  98.5 102.0 %mix.1 = (f32[8,32,2048]{2,1,0:T(8,128)}, bf16[8,256,2048]{2,1,0:T(8,128)(2,1)}) custom-call(bf16[8,8,32,2048]{3,2,1,0:T(8,128)(2,1)} %bitcast.50, bf16[8,32,2048]{2,1,0:T(8,128)(2,1)} %tok.5, f32[8,128]{1,0:T(8,128)} %get-tuple-element.60.small, f32[8,2048]{1,0:T(8,128)} %get-tuple-element.59.gains), custom_call_target="tpu_custom_call" | custom-call | tf_op jit(solution)/shard_map/mix/pallas_call | solution.py:487
  200.4 0.0 all-gather.2.cloned.1.call-done.cot.table
  200.5 37.8 %expert_first.1 = (f32[8,16,256]{2,1,0:T(8,128)}, f32[8,16,256]{2,1,0:T(8,128)}, s32[2,9]{1,0:T(2,128)}, bf16[1280,1024]{1,0:T(8,128)(2,1)}, bf16[1280,2048]{1,0...) custom-call(s32[1]{0:T(128)} %bitcast.number, ...), custom_call_target="tpu_custom_call" | custom-call | flops 20000000000 | bytes 60000000 | tf_op jit(solution)/shard_map/expert_first/pallas_call | solution.py:1133
  238.2 0.0 reduce-scatter.7.cloned.1.call-update
  238.3 0.0 reduce-scatter.5.cloned.1.call-start
  238.3 19.5 %first_in_grad.1 = bf16[2048,2048]{1,0:T(8,128)(2,1)} custom-call(s32[2,9]{1,0:T(2,128)} %get-tuple-element.64.starts.refs_0_, bf16[2,1280,2048]{2,1,0:T(8,128)(2,1)} %get-tuple-element.71.x_all, bf16[1280,2048]{1,0:T(8,128)(2,1)} %get-tuple-element.68.dgu), custom_call_target="tpu_custom_call" | custom-call | flops 10000000000 | bytes 20000000 | tf_op jit(solution)/shard_map/first_in_grad/pallas_call | solution.py:1201
  257.8 0.0 reduce-scatter.5.cloned.1.call-update
  257.8 0.0 reduce-scatter.11.cloned.1.call-start
  257.9 40.7 %expert_second.1 = (bf16[1280,1024]{1,0:T(8,128)(2,1)}, bf16[1280,2048]{1,0:T(8,128)(2,1)}, bf16[1024,2048]{1,0:T(8,128)(2,1)}, bf16[2048,2048]{1,0:T(8,128)(2,1)}) custom-call(s32[2,9]{1,0:T(2,128)} %get-tuple-element.64.starts.refs_0_, bf16[2,1280,2048]{2,1,0:T(8,128)(2,1)} %get-tuple-element.71.x_all, bf16[1280,2048]{1,0:T(8,128)(2,1)} %get-tuple-element.72.dy_all, ...), custom_call_target="tpu_custom_call" | custom-call | flops 24999999488 | bytes 60000000 | tf_op jit(solution)/shard_map/expert_second/pallas_call | solution.py:1261
  298.6 0.0 reduce-scatter.11.cloned.1.call-update
  298.6 0.2 reduce-scatter.9.cloned.1.call-start
  298.8 0.4 reduce-scatter.9.cloned.1.call-update
  299.2 17.9 %expert_tail.2 = (bf16[1280,2048]{1,0:T(8,128)(2,1)}, bf16[1280,2048]{1,0:T(8,128)(2,1)}) custom-call(s32[2,9]{1,0:T(2,128)} %get-tuple-element.64.starts.refs_0_, bf16[1280,1024]{1,0:T(8,128)(2,1)} %get-tuple-element.67.act, bf16[1280,2048]{1,0:T(8,128)(2,1)} %get-tuple-element.68.dgu, bf16[2,2048,2048]{2,1,0:T(8,128)(2,1)} %w_in.7, ...), custom_call_target="tpu_custom_call" | custom-call | flops 12000000000 | bytes 30000000 | tf_op jit(solution)/shard_map/expert_tail/pallas_call | solution.py:1307
  317.0 17.8 %expert_tail.3 = (bf16[1280,2048]{1,0:T(8,128)(2,1)}, bf16[1280,2048]{1,0:T(8,128)(2,1)}) custom-call(s32[2,9]{1,0:T(2,128)} %get-tuple-element.64.starts.refs_0_, bf16[1280,1024]{1,0:T(8,128)(2,1)} %get-tuple-element.73.act, bf16[1280,2048]{1,0:T(8,128)(2,1)} %get-tuple-element.74.dgu, bf16[2,2048,2048]{2,1,0:T(8,128)(2,1)} %w_in.7, ...), custom_call_target="tpu_custom_call" | custom-call | flops 12000000000 | bytes 30000000 | tf_op jit(solution)/shard_map/expert_tail/pallas_call | solution.py:1307
  334.8 19.6 %combine.1 = (bf16[8,256,2048]{2,1,0:T(8,128)(2,1)}, bf16[8,256,2048]{2,1,0:T(8,128)(2,1)}) custom-call(s32[2,9]{1,0:T(2,128)} %get-tuple-element.64.starts.refs_0_, f32[8,16,256]{2,1,0:T(8,128)} %get-tuple-element.65.refs_1_, f32[8,16,256]{2,1,0:T(8,128)} %get-tuple-element.66.refs_2_, bf16[1280,2048]{1,0:T(8,128)(2,1)} %get-tuple-element.69.refs_3_, ...), custom_call_target="tpu_custom_call" | custom-call | flops 3000000000 | bytes 40000000 | tf_op jit(solution)/shard_map/combine/pallas_call | solution.py:1358
  354.4 79.4 %back.1 = (f32[8,32,2048]{2,1,0:T(8,128)}, f32[1,2048]{1,0:T(1,128)}, bf16[8,256,2048]{2,1,0:T(8,128)(2,1)}) custom-call(bf16[8,8,32,2048]{3,2,1,0:T(8,128)(2,1)} %bitcast.49, f32[8,32,2048]{2,1,0:T(8,128)} %get-tuple-element.79.middle, bf16[8,32,2048]{2,1,0:T(8,128)(2,1)} %cot.3, f32[8,128]{1,0:T(8,128)} %get-tuple-element.60.small, ...), custom_call_target="tpu_custom_call" | custom-call | tf_op jit(solution)/shard_map/back/pallas_call | solution.py:532
  433.8 0.0 copy-start.2
  433.8 45.4 %attend_back.1 = (bf16[8,256,2048]{2,1,0:T(8,128)(2,1)}, bf16[3,2048,256]{2,1,0:T(8,128)(2,1)}, bf16[256,2048]{1,0:T(8,128)(2,1)}, f32[8,128]{1,0:T(8,128)}) custom-call(bf16[8,256,2048]{2,1,0:T(8,128)(2,1)} %get-tuple-element.80.agrad, bf16[8,256,2048]{2,1,0:T(8,128)(2,1)} %get-tuple-element.81.normed, f32[2,8,256,256]{3,2,1,0:T(8,128)} %get-tuple-element.82.pre, ...), custom_call_target="tpu_custom_call" | custom-call | flops 20000000000 | bytes 40000000 | tf_op jit(solution)/shard_map/attend_back/pallas_call | solution.py:919
  479.2 0.7 slice.31
  479.9 0.0 copy-done.2
  479.9 0.6 select_maximum_fusion.others
  480.5 0.0 reduce-scatter.7.cloned.1.call-done
  480.5 3.7 pad_convert_fusion.1
  484.3 0.0 reduce-scatter.5.cloned.1.call-done
  484.3 6.1 pad_convert_fusion
  490.4 306.9 %finish.1 = (bf16[4,4,64,2048]{3,2,1,0:T(8,128)(2,1)}, f32[8,128]{1,0:T(8,128)}, bf16[8,32,2048]{2,1,0:T(8,128)(2,1)}, bf16[8,32,2048]{2,1,0:T(8,128)(2,1)}) custom-call(bf16[3,32,64,256]{3,2,1,0:T(8,128)(2,1)} %bitcast.51, bf16[4,64,2048]{2,1,0:T(8,128)(2,1)} %bitcast.54, bf16[8,8,32,2048]{3,2,1,0:T(8,128)(2,1)} %bitcast.48, ...), custom_call_target="tpu_custom_call" | custom-call | tf_op jit(solution)/shard_map/finish/pallas_call | solution.py:765
  797.3 0.8 fusion.3
  798.1 0.6 fusion.1
  798.7 0.6 fusion
  799.3 1.3 slice_bitcast_fusion
  800.6 2.7 fusion.2
  803.3 1.6 bitcast_convert_fusion
  805.0 1.6 bitcast_convert_fusion.1
  806.6 1.6 bitcast_convert_fusion.2
  808.2 1.6 bitcast_convert_fusion.3
  809.9 0.0 copy-start.1
  809.9 0.0 reduce-scatter.11.cloned.1.call-done
  809.9 2.9 convert_dynamic-update-slice_fusion.1
  812.7 0.0 copy-start
  812.7 0.0 reduce-scatter.9.cloned.1.call-done
  812.7 4.2 convert_dynamic-update-slice_fusion
  817.0 0.0 copy-done.1
  817.0 1.0 copy.34
  817.9 0.0 copy-done
  817.9 1.0 copy.35
  (1 shorter events, 0.0 us)
Async XLA Ops:
  7.2 193.3 %all-gather.2.cloned.1.call-start = ((), (), s32[]{:S(2)}) async-start(), calls=%async_computation.4 | async-start | bytes 10027008 | tf_op jit(solution)/shard_map/all_gather | solution.py:1397
  73.5 407.0 %reduce-scatter.7.cloned.1.call-start = ((), (), s32[]{:S(2)}) async-start(), calls=%async_computation.6 | async-start | bytes 5242880 | tf_op jit(solution)/shard_map/reduce_scatter | solution.py:1414
  238.3 246.0 %reduce-scatter.5.cloned.1.call-start = ((), (), s32[]{:S(2)}) async-start(), calls=%async_computation.5 | async-start | bytes 10485760 | tf_op jit(solution)/shard_map/reduce_scatter | solution.py:1414
  257.8 552.0 %reduce-scatter.11.cloned.1.call-start = ((), (), s32[]{:S(2)}) async-start(), calls=%async_computation.8 | async-start | bytes 5242880 | tf_op jit(solution)/shard_map/reduce_scatter | solution.py:1414
  298.6 514.2 %reduce-scatter.9.cloned.1.call-start = ((), (), s32[]{:S(2)}) async-start(), calls=%async_computation.7 | async-start | bytes 10485760 | tf_op jit(solution)/shard_map/reduce_scatter | solution.py:1414
  433.8 46.1 %copy-start.2 = (f32[1,2048]{1,0:T(1,128)S(1)}, f32[1,2048]{1,0:T(1,128)}, u32[]{:S(2)}) copy-start(f32[1,2048]{1,0:T(1,128)} %get-tuple-element.92) | copy-start | bytes 24580
  809.9 7.1 copy-start.1
  812.7 5.2 copy-start
Sparse Core Ops, SparseCore 0:
  73.7 79.4 all-gather.1
  238.4 80.9 reduce-scatter.6
  321.8 145.1 reduce-scatter.4
  469.1 92.8 reduce-scatter.10
  564.2 226.3 reduce-scatter.8

commit v7 on v6

--- a/solution.py
+++ b/solution.py
@@ -139,23 +139,15 @@
         pltpu.make_async_copy(self.own.at[s], self.block(s, at.me), self.lsem.at[s]).wait()
 
 
-def gather_tail(seqs, gather):
+def gather_tail(gather, low, high):
     def relay(i, _):
-        gather.relay(2 * i, True)
-        gather.relay(2 * i + 1, False)
+        gather.relay(low + 2 * i, True)
+        gather.relay(low + 2 * i + 1, False)
         return 0
 
-    def far(s, _):
-        gather.relay_far(s)
-        return 0
-
-    def finish(s, _):
-        gather.finish(s)
-        return 0
-
-    lax.fori_loop(0, seqs // 2, relay, 0)
-    lax.fori_loop(0, seqs, far, 0)
-    lax.fori_loop(0, seqs, finish, 0)
+    lax.fori_loop(0, (high - low) // 2, relay, 0)
+    each(high, gather.relay_far, low=low)
+    each(high, gather.finish, low=low)
 
 
 class Reduce:
@@ -253,25 +245,27 @@
             self.second(s, k).wait_send()
 
 
-def each(n, *steps):
+def each(n, *steps, low=0):
     def run(s, _):
         for step in steps:
             step(s)
         return 0
 
-    lax.fori_loop(0, n, run, 0)
+    lax.fori_loop(low, n, run, 0)
 
 
 COMM = dict(has_side_effects=True, vmem_limit_bytes=60 << 20)
 
 
 def front_kernel(
-    tok, cot, ids, gates, wq, wk, wv, pk, full, weights, routed, gains, small,
-    packets, gsend, grecv, glocal, wsend, wrecv, psend, precv, rsend, rrecv, lsend, lrecv, local,
+    tok, cot, ids, gates, wq, wk, wv, pk, full, weights, cot_full, gains, small,
+    packets, own, gsend, grecv, glocal, csend, crecv, clocal,
+    wsend, wrecv, psend, precv, rsend, rrecv, lsend, lrecv, local,
 ):
     at = Place()
     z = at.rep
-    gather = Gather(at, tok, full, gsend, grecv, glocal)
+    gather = Gather(at, own, full, gsend, grecv, glocal)
+    cot_gather = Gather(at, cot, cot_full, csend, crecv, clocal)
     seqs, _, width = tok.shape
     top = ids.shape[1]
     block, cols = wq.shape[0], weights.shape[2]
@@ -310,12 +304,6 @@
         packet_copy(m, dev).start()
         for j in range(3):
             weight_copy(m, j, dev).start()
-    each(seqs, gather.start)
-    own_cols = pl.ds(pl.multiple_of(at.me * cols, cols), cols)
-    mine = pl.ds(pl.multiple_of(at.me * block, block), block)
-    own = [pltpu.make_async_copy(w.at[:, own_cols], weights.at[j, mine], local.at[j]) for j, w in enumerate((wq, wk, wv))]
-    for copy in own:
-        copy.start()
 
     place = lax.broadcasted_iota(jnp.int32, (top, 128), 0)
     lane = lax.broadcasted_iota(jnp.int32, (top, 128), 1)
@@ -323,11 +311,21 @@
     second = jnp.where(lane == place + top, 1.0, 0.0).astype(BF16)
 
     def join(s):
-        routed[s, :, 0:width] = cot[s]
+        own[s, :, 0:width] = tok[s]
         table = dot(ids[s].astype(F32).astype(BF16), first, 0, 0) + dot(gates[s], second, 0, 0)
-        routed[s, :, width : width + 128] = table.astype(BF16)
+        own[s, :, width : width + 128] = table.astype(BF16)
 
     each(seqs, join)
+    each(seqs, gather.start)
+    own_cols = pl.ds(pl.multiple_of(at.me * cols, cols), cols)
+    mine = pl.ds(pl.multiple_of(at.me * block, block), block)
+    own_weights = [
+        pltpu.make_async_copy(w.at[:, own_cols], weights.at[j, mine], local.at[j]) for j, w in enumerate((wq, wk, wv))
+    ]
+    for copy in own_weights:
+        copy.start()
+    early = seqs // 2
+    each(early, cot_gather.start)
 
     for m, dev in enumerate(peers):
         for j in range(3):
@@ -365,12 +363,19 @@
         gather.relay(2 * i + 1, False)
         return 0
 
+    def cot_relay(i, _):
+        cot_gather.relay(2 * i, True)
+        cot_gather.relay(2 * i + 1, False)
+        return 0
+
     pairs = seqs // 2
     lax.fori_loop(0, pairs // 2, relay, 0)
     pass_on(1)
     lax.fori_loop(pairs // 2, pairs, relay, 0)
     pass_on(2)
+    lax.fori_loop(0, early // 2, cot_relay, 0)
     each(seqs, gather.relay_far)
+    each(early, cot_gather.relay_far)
     for m, dev in enumerate(peers):
         packet_copy(m, dev).wait_recv()
     packets[at.me] = pk[...]
@@ -389,6 +394,7 @@
         small[1:2] += pltpu.roll(packets[o, base + 1 : base + 2], o * heads, 1)
         small[2:3] += pltpu.roll(packets[o, base + 2 : base + 3], o, 1)
     each(seqs, gather.finish)
+    each(early, cot_gather.finish)
     pass_on(3)
 
     def sent(q, going, right):
@@ -404,7 +410,7 @@
         packet_copy(m, dev).wait_send()
         for j in range(3):
             weight_copy(m, j, dev).wait_send()
-    for copy in own:
+    for copy in own_weights:
         copy.wait()
 
 
@@ -414,32 +420,33 @@
     cols = wq.shape[1] // ep
     top = ids.shape[1]
     if ep != 8 or lax.axis_size("rep") != 4:
-        full = lax.all_gather(tokens, "ep", axis=1, tiled=True)
-        weights = [lax.all_to_all(w, "ep", split_axis=1, concat_axis=0, tiled=True) for w in (wq, wk, wv)]
         routes = jnp.concatenate([ids.astype(BF16), gates], axis=1).transpose(0, 2, 1)
         routes = jnp.pad(routes, ((0, 0), (0, 0), (0, 128 - 2 * top)))
+        full = lax.all_gather(jnp.concatenate([tokens, routes], axis=-1), "ep", axis=1, tiled=True)
+        weights = [lax.all_to_all(w, "ep", split_axis=1, concat_axis=0, tiled=True) for w in (wq, wk, wv)]
         packets = lax.all_gather(packet, "ep", axis=0)
         share, heads = width // (128 * ep), HEAD_DIM // ep
         gains = jnp.stack([packets[:, :share].reshape(width), packets[:, share : 2 * share].reshape(width)])
         lens = jnp.pad(packets[:, 2 * share + 2, 0], (0, 128 - ep))
         few = [packets[:, 2 * share + k, :heads].reshape(HEAD_DIM) for k in range(2)] + [lens]
         return (
-            full, jnp.stack(weights), jnp.concatenate([cotangent, routes], axis=-1),
+            full, jnp.stack(weights), lax.all_gather(cotangent, "ep", axis=1, tiled=True),
             jnp.pad(gains, ((0, 6), (0, 0))), jnp.pad(jnp.stack(few), ((0, 5), (0, 0))),
         )
     dma = pltpu.SemaphoreType.DMA
     return pl.pallas_call(
         front_kernel,
         out_shape=(
+            sds((seqs, rows * ep, width + 128), BF16),
+            sds((3, wq.shape[0] * ep, cols), BF16),
             sds((seqs, rows * ep, width), BF16),
-            sds((3, wq.shape[0] * ep, cols), BF16),
-            sds((seqs, rows, width + 128), BF16),
             sds((8, width), F32),
             sds((8, 128), F32),
         ),
         in_specs=[VM] * 8,
-        out_specs=(AN, AN, VM, VM, VM),
-        scratch_shapes=[pltpu.VMEM((ep,) + packet.shape, F32)]
+        out_specs=(AN, AN, AN, VM, VM),
+        scratch_shapes=[pltpu.VMEM((ep,) + packet.shape, F32), pltpu.VMEM((seqs, rows, width + 128), BF16)]
+        + Gather.scratch(seqs)
         + Gather.scratch(seqs)
         + [dma((7, 3)), dma((7, 3)), dma((7,)), dma((7,))]
         + [dma((7, 4))] * 4
@@ -454,45 +461,11 @@
     return (place[None] < small[2, :seqs, None]).astype(F32)[..., None]
 
 
-def mix_kernel(part, tok, small, gains, middle, full, own, *scratch):
-    at = Place()
-    seqs = tok.shape[0]
-    reduce = Reduce(at, part, *scratch[: Reduce.sems])
-    gather = Gather(at, own, full, *scratch[Reduce.sems :])
-    at.greet((at.xn, at.yn, at.sb))
-    each(seqs, reduce.start)
-    each(seqs, reduce.hop1)
-    each(seqs, reduce.hop2)
-
-    def rows(s):
-        living = live_rows(small, s, at.me, tok.shape[1])
-        mid, mixed = mix_rows(reduce.total(s), tok[s], living, gains[1:2])
-        middle[s] = mid
-        own[s] = mixed
-        gather.start(s)
-
-    each(seqs, rows)
-    gather_tail(seqs, gather)
-    each(seqs, reduce.finish)
-
-
 def mix(part, tokens, small, gains):
-    seqs, rows, width = tokens.shape
-    ep = lax.axis_size("ep")
-    if ep != 8:
-        total = lax.psum_scatter(part, "ep", scatter_dimension=1, tiled=True).astype(F32)
-        middle, mixed = mix_rows(total, tokens, plain_living(small, seqs, rows), gains[1])
-        return middle, lax.all_gather(mixed, "ep", axis=1, tiled=True)
-    part = part.reshape(seqs, ep, rows, width)
-    return pl.pallas_call(
-        mix_kernel,
-        out_shape=(sds(tokens.shape, F32), sds((seqs, rows * ep, width), BF16)),
-        in_specs=[AN] + [VM] * 3,
-        out_specs=(VM, AN),
-        scratch_shapes=[pltpu.VMEM(tokens.shape, BF16)] + Reduce.scratch(part) + Gather.scratch(seqs),
-        compiler_params=pltpu.CompilerParams(collective_id=2, **COMM),
-        name="mix",
-    )(part, tokens, small, gains)
+    seqs, rows, _ = tokens.shape
+    total = lax.psum_scatter(part, "ep", scatter_dimension=1, tiled=True).astype(F32)
+    middle, mixed = mix_rows(total, tokens, plain_living(small, seqs, rows), gains[1])
+    return middle, lax.all_gather(mixed, "ep", axis=1, tiled=True)
 
 
 def back_kernel(gpart, middle, cot, small, gains, mgrad, ggrad, full, own, *scratch):
@@ -516,7 +489,7 @@
         gather.start(s)
 
     each(seqs, rows)
-    gather_tail(seqs, gather)
+    gather_tail(gather, 0, seqs)
     each(seqs, rg.finish)
 
 
@@ -802,46 +775,91 @@
     return p * (1.0 / jnp.sum(p, axis=-1, keepdims=True))
 
 
-def attend_kernel(tok, w, wo, gains, small, cos, sin, normed, pre, low, ctx, part):
-    length = seq_len(small, pl.program_id(0))
-    v = tok[0].astype(F32)
+def packed_slots(number, table, length_live, top):
+    tab = table.astype(F32)
+    length = tab.shape[0]
+    lane = lax.broadcasted_iota(jnp.int32, tab.shape, 1)
+    row = lax.broadcasted_iota(jnp.int32, (length, 1), 0).astype(F32)
+    chosen = jnp.logical_and(jnp.logical_and(tab == number, lane < top), row < length_live)
+    gates = jnp.where(chosen, pltpu.roll(tab, 128 - top, 1), 0.0).astype(BF16)
+    chosen = jnp.where(chosen, 1.0, 0.0).astype(BF16)
+    ones = jnp.ones((8, 128), BF16)
+    hit = dot(ones, chosen, 1, 1)
+    weight = dot(ones, gates, 1, 1)
+    earlier = lax.broadcasted_iota(jnp.int32, (length, length), 0)
+    later = lax.broadcasted_iota(jnp.int32, (length, length), 1)
+    rank = dot(hit.astype(BF16), jnp.where(earlier < later, 1.0, 0.0).astype(BF16), 1, 0)
+    return jnp.where(hit > 0.5, rank, -1.0), weight, jnp.sum(hit[0:1], axis=1, keepdims=True)
+
+
+def attend_rows(top, number, s, block, w, wo, gains, small, cos, sin, normed, pre, low, ctx, part, slots, starts):
+    width = normed.shape[1]
+    length = seq_len(small, s)
+    v = block[:, 0:width].astype(F32)
     x = (v * inverse_rms(v) * gains[0:1]).astype(BF16)
-    normed[0] = x
+    normed[...] = x
     q_pre, k_pre = dot(x, w[0], 1, 0), dot(x, w[1], 1, 0)
     value = dot(x, w[2], 1, 0).astype(BF16)
-    pre[0, 0], pre[1, 0] = q_pre, k_pre
-    low[2, 0] = value
+    pre[0], pre[1] = q_pre, k_pre
+    low[2] = value
     for h in range(q_pre.shape[1] // HEAD_DIM):
         cols = slice(h * HEAD_DIM, (h + 1) * HEAD_DIM)
         rot = []
         for i, (u, g) in enumerate(((q_pre[:, cols], small[0:1]), (k_pre[:, cols], small[1:2]))):
             rot.append(rope(u * inverse_rms(u) * g, cos[...], sin[...]).astype(BF16))
-            low[i, 0, :, cols] = rot[i]
+            low[i, :, cols] = rot[i]
         attention = probabilities(rot[0], rot[1], length).astype(BF16)
-        ctx[0, :, cols] = dot(attention, value[:, cols], 1, 0).astype(BF16)
-    part[0] = dot(ctx[0], wo[...], 1, 0).astype(BF16)
-
-
-def attend(full, weights, wo, gains, small, cos, sin):
-    seqs, length, width = full.shape
+        ctx[:, cols] = dot(attention, value[:, cols], 1, 0).astype(BF16)
+    part[...] = dot(ctx[...], wo[...], 1, 0).astype(BF16).reshape(part.shape)
+    table = block[:, width : width + 128]
+    lane = lax.broadcasted_iota(jnp.int32, (1, 128), 1)
+    for j, ref in enumerate(slots):
+        slot, weight, count = packed_slots(number + j, table, length, top)
+        ref[0:8] = slot
+        ref[8:16] = weight
+        row = starts[j : j + 1]
+        after = jnp.sum(jnp.where(lane == s, row, 0.0), axis=1, keepdims=True) + 16.0 * jnp.floor((count + 15.0) * 0.0625)
+        starts[j : j + 1] = jnp.where(lane == s + 1, after, row)
+
+
+def attend_kernel(top, number, full, w, wo, gains, small, cos, sin, normed, pre, low, ctx, part, slots0, slots1, starts):
+    s = pl.program_id(0)
+
+    @pl.when(s == 0)
+    def _():
+        starts[...] = jnp.zeros_like(starts)
+
+    attend_rows(
+        top, number[0].astype(F32), s, full.at[0], w, wo, gains, small, cos, sin,
+        normed.at[0], pre.at[:, 0], low.at[:, 0], ctx.at[0], part.at[0], (slots0.at[0], slots1.at[0]), starts,
+    )
+
+
+def attend(top, number, full, weights, wo, gains, small, cos, sin):
+    seqs, length, wide = full.shape
+    width = wide - 128
     cols = weights.shape[2]
     row = lambda i, *_: (i, 0, 0)
     row2 = lambda i, *_: (0, i, 0, 0)
     two = lambda i, *_: (0, 0)
+    slot = pl.BlockSpec((1, 16, length), row)
     return pl.pallas_call(
-        attend_kernel,
+        functools.partial(attend_kernel, top),
         out_shape=(
-            sds(full.shape, BF16),
+            sds((seqs, length, width), BF16),
             sds((2, seqs, length, cols), F32),
             sds((3, seqs, length, cols), BF16),
             sds((seqs, length, cols), BF16),
-            sds(full.shape, BF16),
+            sds((seqs, length, width), BF16),
+            sds((seqs, 16, length), F32),
+            sds((seqs, 16, length), F32),
+            sds((8, 128), F32),
         ),
         grid_spec=pltpu.PrefetchScalarGridSpec(
-            num_scalar_prefetch=0,
+            num_scalar_prefetch=1,
             grid=(seqs,),
             in_specs=[
-                pl.BlockSpec((1, length, width), row),
+                pl.BlockSpec((1, length, wide), row),
                 pl.BlockSpec(weights.shape, lambda i, *_: (0, 0, 0)),
                 pl.BlockSpec(wo.shape, two),
                 pl.BlockSpec((8, width), two),
@@ -855,12 +873,143 @@
                 pl.BlockSpec((3, 1, length, cols), row2),
                 pl.BlockSpec((1, length, cols), row),
                 pl.BlockSpec((1, length, width), row),
+                slot,
+                slot,
+                pl.BlockSpec((8, 128), two),
             ),
         ),
         compiler_params=pltpu.CompilerParams(dimension_semantics=("arbitrary",), vmem_limit_bytes=60 << 20),
         cost_estimate=pl.CostEstimate(flops=10**10, bytes_accessed=4 * 10**7, transcendentals=10**6),
         name="attend",
-    )(full, weights, wo, gains, small, cos, sin)
+    )(number, full, weights, wo, gains, small, cos, sin)
+
+
+def attend_mix_kernel(
+    top, local, full, w, wo, gains, small, cos, sin, tok, cot, _cot_early,
+    normed, pre, low, ctx, middle, mixed, cot_full, slots0, slots1, starts,
+    own, blocks, nbuf, pbuf, lbuf, cbuf, part, begins, tsem, ssem, *scratch,
+):
+    at = Place()
+    seqs = tok.shape[0]
+    n = Reduce.sems
+    reduce = Reduce(at, part, *scratch[:n])
+    gather = Gather(at, own, mixed, *scratch[n : n + 3])
+    cot_gather = Gather(at, cot, cot_full, *scratch[n + 3 :])
+    number = (at.me * local).astype(F32)
+    early = seqs // 2
+    at.greet((at.xn, at.yn, at.sb))
+    each(seqs, cot_gather.start, low=early)
+    begins[...] = jnp.zeros_like(begins)
+
+    def load(s):
+        return pltpu.make_async_copy(full.at[s], blocks.at[lax.rem(s, 2)], tsem.at[lax.rem(s, 2)])
+
+    def stores(s):
+        k = lax.rem(s, 2)
+        pairs = ((nbuf.at[k], normed.at[s]), (pbuf.at[k], pre.at[:, s]), (lbuf.at[k], low.at[:, s]), (cbuf.at[k], ctx.at[s]))
+        return [pltpu.make_async_copy(src, dst, ssem.at[i, k]) for i, (src, dst) in enumerate(pairs)]
+
+    load(0).start()
+
+    def sequence(s):
+        k = lax.rem(s, 2)
+        load(s).wait()
+
+        @pl.when(s + 1 < seqs)
+        def _():
+            load(s + 1).start()
+
+        @pl.when(s >= 2)
+        def _():
+            for copy in stores(s - 2):
+                copy.wait()
+
+        attend_rows(
+            top, number, s, blocks.at[k], w, wo, gains, small, cos, sin,
+            nbuf.at[k], pbuf.at[k], lbuf.at[k], cbuf.at[k], part.at[s], (slots0.at[s], slots1.at[s]), begins,
+        )
+        for copy in stores(s):
+            copy.start()
+        reduce.start(s)
+
+    def rows(s):
+        living = live_rows(small, s, at.me, tok.shape[1])
+        mid, out = mix_rows(reduce.total(s), tok[s], living, gains[1:2])
+        middle[s] = mid
+        own[s] = out
+        gather.start(s)
+
+    def cot_pair(p):
+        @pl.when(lax.rem(p, 2) == 0)
+        def _():
+            cot_gather.relay(early + p, True)
+            cot_gather.relay(early + p + 1, False)
+
+    jobs = (
+        (sequence, 0, seqs), (reduce.hop1, 1, seqs), (cot_pair, 3, early), (reduce.hop2, 3, seqs),
+        (lambda s: cot_gather.relay_far(early + s), 7, early), (rows, 5, seqs),
+    )
+
+    def tick(i, _):
+        for job, lag, count in jobs:
+
+            @pl.when(jnp.logical_and(i >= lag, i < lag + count))
+            def _():
+                job(i - lag)
+
+        return 0
+
+    lax.fori_loop(0, max(lag + count for _, lag, count in jobs), tick, 0)
+    starts[...] = begins[...].astype(jnp.int32)
+    each(seqs, cot_gather.finish, low=early)
+    gather_tail(gather, 0, seqs)
+    for s in (seqs - 2, seqs - 1):
+        for copy in stores(s):
+            copy.wait()
+    each(seqs, reduce.finish)
+
+
+def attend_mix(top, local, full, weights, wo, gains, small, cos, sin, tokens, cotangent, cot_early):
+    seqs, rows, width = tokens.shape
+    length = full.shape[1]
+    cols = weights.shape[2]
+    part = sds((seqs, 8, rows, width), BF16)
+    dma = pltpu.SemaphoreType.DMA
+    return pl.pallas_call(
+        functools.partial(attend_mix_kernel, top, local),
+        out_shape=(
+            sds((seqs, length, width), BF16),
+            sds((2, seqs, length, cols), F32),
+            sds((3, seqs, length, cols), BF16),
+            sds((seqs, length, cols), BF16),
+            sds(tokens.shape, F32),
+            sds((seqs, length, width), BF16),
+            sds((seqs, length, width), BF16),
+            sds((seqs, 16, length), F32),
+            sds((seqs, 16, length), F32),
+            sds((8, 128), jnp.int32),
+        ),
+        in_specs=[AN] + [VM] * 8 + [AN],
+        out_specs=(AN, AN, AN, AN, VM, AN, AN, VM, VM, VM),
+        input_output_aliases={9: 6},
+        scratch_shapes=[
+            pltpu.VMEM(tokens.shape, BF16),
+            pltpu.VMEM((2,) + full.shape[1:], BF16),
+            pltpu.VMEM((2, length, width), BF16),
+            pltpu.VMEM((2, 2, length, cols), F32),
+            pltpu.VMEM((2, 3, length, cols), BF16),
+            pltpu.VMEM((2, length, cols), BF16),
+            pltpu.VMEM(part.shape, BF16),
+            pltpu.VMEM((8, 128), F32),
+            dma((2,)),
+            dma((4, 2)),
+        ]
+        + Reduce.scratch(part)
+        + Gather.scratch(seqs)
+        + Gather.scratch(seqs),
+        compiler_params=pltpu.CompilerParams(collective_id=2, **COMM),
+        name="attend_mix",
+    )(full, weights, wo, gains, small, cos, sin, tokens, cotangent, cot_early)
 
 
 def attend_back_kernel(
@@ -960,23 +1109,6 @@
     return -(-seqs * capacity // BLOCK) * BLOCK
 
 
-def packed_slots(number, table, length_live, top):
-    tab = table.astype(F32)
-    length = tab.shape[0]
-    lane = lax.broadcasted_iota(jnp.int32, tab.shape, 1)
-    row = lax.broadcasted_iota(jnp.int32, (length, 1), 0).astype(F32)
-    chosen = jnp.logical_and(jnp.logical_and(tab == number, lane < top), row < length_live)
-    gates = jnp.where(chosen, pltpu.roll(tab, 128 - top, 1), 0.0).astype(BF16)
-    chosen = jnp.where(chosen, 1.0, 0.0).astype(BF16)
-    ones = jnp.ones((8, 128), BF16)
-    hit = dot(ones, chosen, 1, 1)
-    weight = dot(ones, gates, 1, 1)
-    earlier = lax.broadcasted_iota(jnp.int32, (length, length), 0)
-    later = lax.broadcasted_iota(jnp.int32, (length, length), 1)
-    rank = dot(hit.astype(BF16), jnp.where(earlier < later, 1.0, 0.0).astype(BF16), 1, 0)
-    return jnp.where(hit > 0.5, rank, -1.0), weight, jnp.sum(hit[0:1]).astype(jnp.int32)
-
-
 def forward_blocks(blocks, x, dy, wi, wo, acts, dgus):
     hidden = wo.shape[0]
     part = min(hidden, 512)
@@ -1047,8 +1179,8 @@
 
 
 def first_kernel(
-    capacity, top, number, mixed, cot, table, small, w_in, w_out,
-    slots0, slots1, starts, act, dgu, x_all, dy_all, out_grad,
+    capacity, starts, mixed, cot, slots0, slots1, w_in, w_out,
+    act, dgu, x_all, dy_all, out_grad,
     x, dy, wi, wo, acts, dgus, acc, stage, wsem, ssem, rsem,
 ):
     step = pl.program_id(0)
@@ -1062,36 +1194,27 @@
     def _():
         for copy in loads:
             copy.start()
-        starts[0, 0] = 0
-        starts[1, 0] = 0
 
     packed = []
     for k in range(together):
-        spread, gate_spread, counts = [], [], []
-        for j, slots in enumerate((slots0, slots1)):
-            slot, weight, count = packed_slots(
-                (number[0] + j).astype(F32), table[k], seq_len(small, step * together + k), top
-            )
-            slots[k, 0:8] = slot
-            slots[k, 8:16] = weight
-            place = lax.broadcasted_iota(jnp.int32, (capacity, slot.shape[1]), 0).astype(F32) == slot[0:1]
+        spread, gate_spread = [], []
+        for slots in (slots0, slots1):
+            column = lax.broadcasted_iota(jnp.int32, (capacity, slots.shape[2]), 0).astype(F32)
+            place = column == slots[k, 0:1]
             spread.append(jnp.where(place, 1.0, 0.0).astype(BF16))
-            gate_spread.append(jnp.where(place, weight[0:1], 0.0).astype(BF16))
-            counts.append(count)
+            gate_spread.append(jnp.where(place, slots[k, 8:9], 0.0).astype(BF16))
         packed.append(
             (
-                counts,
                 dot(jnp.concatenate(spread, axis=0), mixed[k], 1, 0).astype(BF16),
                 dot(jnp.concatenate(gate_spread, axis=0), cot[k], 1, 0).astype(BF16),
             )
         )
-    for k, (counts, x_rows, dy_rows) in enumerate(packed):
+    for k, (x_rows, dy_rows) in enumerate(packed):
         s = step * together + k
         for j in range(2):
             start = pl.multiple_of(starts[j, s], 16)
             x[j, pl.ds(start, capacity)] = x_rows[j * capacity : (j + 1) * capacity]
             dy[j, pl.ds(start, capacity)] = dy_rows[j * capacity : (j + 1) * capacity]
-            starts[j, s + 1] = start + (counts[j] + 15) // 16 * 16
 
     @pl.when(step == steps - 1)
     def _():
@@ -1122,7 +1245,7 @@
             copy.wait()
 
 
-def expert_first(number, mixed, cot, small, w_in, w_out, capacity, top):
+def expert_first(starts, mixed, cot, slots, w_in, w_out, capacity):
     seqs, length, width = mixed.shape
     hidden = w_out.shape[1]
     rows = pack_rows(seqs, capacity)
@@ -1131,11 +1254,8 @@
     together = 2
     slot_spec = pl.BlockSpec((together, 16, length), seq)
     return pl.pallas_call(
-        functools.partial(first_kernel, capacity, top),
+        functools.partial(first_kernel, capacity),
         out_shape=(
-            sds((seqs, 16, length), F32),
-            sds((seqs, 16, length), F32),
-            sds((2, seqs + 1), jnp.int32),
             sds((rows, hidden), BF16),
             sds((rows, 2 * hidden), BF16),
             sds((2, rows, width), BF16),
@@ -1148,12 +1268,12 @@
             in_specs=[
                 pl.BlockSpec((together, length, width), seq),
                 pl.BlockSpec((together, length, width), seq),
-                pl.BlockSpec((together, length, 128), lambda i, *_: (i, 0, width // 128)),
-                pl.BlockSpec((8, 128), lambda i, *_: (0, 0)),
+                slot_spec,
+                slot_spec,
                 AN,
                 AN,
             ],
-            out_specs=(slot_spec, slot_spec, pl.BlockSpec(memory_space=pltpu.SMEM), AN, AN, AN, AN, AN),
+            out_specs=(AN, AN, AN, AN, AN),
             scratch_shapes=[
                 pltpu.VMEM((2, rows, width), BF16),
                 pltpu.VMEM((2, rows, width), BF16),
@@ -1171,11 +1291,11 @@
         compiler_params=pltpu.CompilerParams(dimension_semantics=("arbitrary",), vmem_limit_bytes=63 << 20),
         cost_estimate=pl.CostEstimate(flops=2 * 10**10, bytes_accessed=6 * 10**7, transcendentals=10**6),
         name="expert_first",
-    )(number, mixed, cot, cot, small, w_in, w_out)
-
-
-def in_grad_kernel(starts, x_all, dgu, in_grad, x, dgus, acc, stage, lsem, ssem):
-    blocks = (starts[0, starts.shape[1] - 1] + BLOCK - 1) // BLOCK
+    )(starts, mixed, cot, *slots, w_in, w_out)
+
+
+def in_grad_kernel(seqs, starts, x_all, dgu, in_grad, x, dgus, acc, stage, lsem, ssem):
+    blocks = (starts[0, seqs] + BLOCK - 1) // BLOCK
 
     def load(b):
         rows = pl.ds(pl.multiple_of(b * BLOCK, BLOCK), BLOCK)
@@ -1195,11 +1315,11 @@
     drain_tiles(in_grad, acc, stage, ssem)
 
 
-def first_in_grad(starts, x_all, dgu):
+def first_in_grad(seqs, starts, x_all, dgu):
     rows, width = x_all.shape[1:]
     dma = pltpu.SemaphoreType.DMA
     return pl.pallas_call(
-        in_grad_kernel,
+        functools.partial(in_grad_kernel, seqs),
         out_shape=sds((width, dgu.shape[1]), BF16),
         grid_spec=pltpu.PrefetchScalarGridSpec(
             num_scalar_prefetch=1,
@@ -1222,10 +1342,10 @@
 
 
 def second_kernel(
-    starts, x_all, dy_all, w_in, w_out, act, dgu, out_grad, in_grad,
+    seqs, starts, x_all, dy_all, w_in, w_out, act, dgu, out_grad, in_grad,
     x, dy, wi, wo, acts, dgus, acc, stage, wsem, lsem, ssem, rsem,
 ):
-    blocks = (starts[1, starts.shape[1] - 1] + BLOCK - 1) // BLOCK
+    blocks = (starts[1, seqs] + BLOCK - 1) // BLOCK
     loads = [pltpu.make_async_copy(w_in.at[1], wi, wsem.at[0]), pltpu.make_async_copy(w_out.at[1], wo, wsem.at[1])]
 
     def load(b, action):
@@ -1254,12 +1374,12 @@
         copy.wait()
 
 
-def expert_second(starts, x_all, dy_all, w_in, w_out):
+def expert_second(seqs, starts, x_all, dy_all, w_in, w_out):
     rows, width = dy_all.shape
     hidden = w_out.shape[1]
     dma = pltpu.SemaphoreType.DMA
     return pl.pallas_call(
-        second_kernel,
+        functools.partial(second_kernel, seqs),
         out_shape=(
             sds((rows, hidden), BF16),
             sds((rows, 2 * hidden), BF16),
@@ -1292,20 +1412,19 @@
     )(starts, x_all, dy_all, w_in, w_out)
 
 
-def tail_kernel(j, starts, act, dgu, w_in, w_out, produced, dx):
-    @pl.when(pl.program_id(0) * BLOCK < starts[j, starts.shape[1] - 1])
+def tail_kernel(j, seqs, starts, act, dgu, w_in, w_out, produced, dx):
+    @pl.when(pl.program_id(0) * BLOCK < starts[j, seqs])
     def _():
         produced[...] = dot(act[...], w_out[...], 1, 0).astype(BF16)
         dx[...] = dot(dgu[...], w_in[...], 1, 1).astype(BF16)
 
 
-def expert_tail(j, starts, act, dgu, w_in, w_out):
+def expert_tail(j, seqs, starts, act, dgu, w_in, w_out):
     rows, hidden = act.shape
     width = w_in.shape[1]
-    last = starts.shape[1] - 1
-    block = lambda i, st: (jnp.maximum(jnp.minimum(i, (st[j, last] + BLOCK - 1) // BLOCK - 1), 0), 0)
+    block = lambda i, st: (jnp.maximum(jnp.minimum(i, (st[j, seqs] + BLOCK - 1) // BLOCK - 1), 0), 0)
     return pl.pallas_call(
-        functools.partial(tail_kernel, j),
+        functools.partial(tail_kernel, j, seqs),
         out_shape=(sds((rows, width), BF16), sds((rows, width), BF16)),
         grid_spec=pltpu.PrefetchScalarGridSpec(
             num_scalar_prefetch=1,
@@ -1376,7 +1495,7 @@
 ):
     ep = lax.axis_size("ep")
     me = lax.axis_index("ep")
-    _, rows, _ = tokens.shape
+    seqs, rows, _ = tokens.shape
     length = rows * ep
     top = gate_weights.shape[2]
     local = expert_in.shape[0]
@@ -1390,11 +1509,10 @@
     packet = jnp.pad(packet, ((0, -packet.shape[0] % 8), (0, 0)))
     share = gains.shape[0] // 2
 
-    full, weights, routed, gains, small_in = front(
+    full, weights, cot_full, gains, small_in = front(
         tokens, cotangent, expert_ids.transpose(0, 2, 1), gate_weights.transpose(0, 2, 1),
         query_weight, key_weight, value_weight, packet,
     )
-    cot_full = lax.all_gather(routed, "ep", axis=1, tiled=True)
 
     half = HEAD_DIM // 2
     frequency = ROPE_BASE ** (-(np.arange(half, dtype=np.float32) * np.float32(2.0 / HEAD_DIM)))
@@ -1402,26 +1520,34 @@
     cos = jnp.asarray(np.concatenate([np.cos(angles)] * 2, axis=-1), F32)
     sin = jnp.asarray(np.concatenate([-np.sin(angles), np.sin(angles)], axis=-1), F32)
 
-    normed, pre, low, ctx, part = attend(full, weights, output_weight, gains, small_in, cos, sin)
-    middle, mixed = mix(part, tokens, small_in, gains)
-
-    number = (me * local).astype(jnp.int32)[None]
-    slots0, slots1, starts, act0, dgu0, x_all, dy_all, out_grad0 = expert_first(
-        number, mixed, cot_full, small_in, expert_in, expert_out, capacity, top
+    if ep == 8 and lax.axis_size("rep") == 4:
+        normed, pre, low, ctx, middle, mixed, cot_full, slots0, slots1, starts = attend_mix(
+            top, local, full, weights, output_weight, gains, small_in, cos, sin, tokens, cotangent, cot_full
+        )
+    else:
+        number = (me * local).astype(jnp.int32)[None]
+        normed, pre, low, ctx, part, slots0, slots1, starts = attend(
+            top, number, full, weights, output_weight, gains, small_in, cos, sin
+        )
+        starts = starts.astype(jnp.int32)
+        middle, mixed = mix(part, tokens, small_in, gains)
+
+    act0, dgu0, x_all, dy_all, out_grad0 = expert_first(
+        starts, mixed, cot_full, (slots0, slots1), expert_in, expert_out, capacity
     )
 
     def over_rep(value):
         return lax.psum_scatter(value, "rep", scatter_dimension=0, tiled=True)
 
     out0 = over_rep(out_grad0)
-    in_grad0 = first_in_grad(starts, x_all, dgu0)
+    in_grad0 = first_in_grad(seqs, starts, x_all, dgu0)
     in0 = over_rep(in_grad0)
     x_all, _ = lax.optimization_barrier((x_all, in_grad0))
-    act1, dgu1, out_grad1, in_grad1 = expert_second(starts, x_all, dy_all, expert_in, expert_out)
+    act1, dgu1, out_grad1, in_grad1 = expert_second(seqs, starts, x_all, dy_all, expert_in, expert_out)
     in1 = over_rep(in_grad1)
     out1 = over_rep(out_grad1)
-    produced0, dx0 = expert_tail(0, starts, act0, dgu0, expert_in, expert_out)
-    produced1, dx1 = expert_tail(1, starts, act1, dgu1, expert_in, expert_out)
+    produced0, dx0 = expert_tail(0, seqs, starts, act0, dgu0, expert_in, expert_out)
+    produced1, dx1 = expert_tail(1, seqs, starts, act1, dgu1, expert_in, expert_out)
     out_part, grad_part = combine(starts, (slots0, slots1), (produced0, produced1), (dx0, dx1), capacity)
 
     mgrad, ffn_back, agrad = back(grad_part, middle, cotangent, small_in, gains)

time: 834 us -> 817 us (0.980)
  Pallas kernels: 775 us -> 759 us
    pallas_call x8 -> x7, Pallas kernels: 324 us -> 307 us  [the longest x1 98.5 us: attend_mix(): pl.pallas_call(functools.partial(attend_mix_kernel, top, local), out_shap...]
  transfers between devices with their start and end apart: 5 -> 4, of which waited for: 0 -> 0; matrix products, arithmetic and copies ran while one was open for 3% -> 3% of each run, Pallas kernels for 82% -> 68%
where the time goes in v7:
time: 817 us; the launch traced here: 809 us
  Pallas kernels  759 us (93%)
  other arithmetic  26 us (3%)
  between operations  14.7 us (2%)
  local copies, waits for them, and re-layouts  8.63 us (1%)
    pallas_call x1, Pallas kernels, finish(): pl.pallas_call(finish_kernel, out_shape=(sds(whole, BF16), sds((8, 128),...  307 us
    pallas_call x1, Pallas kernels, attend_mix(): pl.pallas_call(functools.partial(attend_mix_kernel, top, local), out_shap...  98.5 us
    pallas_call x1, Pallas kernels, back(): pl.pallas_call(back_kernel, out_shape=(sds(cot.shape, F32), sds((1, width...  79.4 us
    pallas_call x1, Pallas kernels, front(): pl.pallas_call(front_kernel, out_shape=(sds((seqs, rows * ep, width + 128...  77.2 us
    pallas_call x1, Pallas kernels, attend_back(): pl.pallas_call(attend_back_kernel, out_shape=(sds(agrad.shape, BF16), sds...  45.3 us
    pallas_call x1, Pallas kernels, expert_second(): pl.pallas_call(functools.partial(second_kernel, seqs), out_shape=(sds((ro...  40.7 us
    pallas_call x2, Pallas kernels, expert_tail(): pl.pallas_call(functools.partial(tail_kernel, j, seqs), out_shape=(sds((r...  35.7 us
    pallas_call x1, Pallas kernels, expert_first(): pl.pallas_call(functools.partial(first_kernel, capacity), out_shape=(sds(...  35.5 us
  transfers between devices with their start and end apart: 4, of which 0 were waited for; matrix products, arithmetic and copies ran while one was open for 3% of the time, Pallas kernels for 68%

profile of v7, /device:TPU:0, one launch (start us, length us, event | category | flops | bytes accessed | tf_op | source)
XLA Modules:
  0.0 808.8 jit_solution(13022516192911367497)
XLA Ops:
  7.2 0.0 reduce-scatter.7.cloned.1.call-start
  7.9 0.7 bitcast_convert_fusion.4
  8.6 0.7 maximum_convert_fusion
  9.2 0.6 select_maximum_fusion.1.pk
  9.8 77.2 %front.1 = (bf16[8,256,2176]{2,1,0:T(8,128)(2,1)}, bf16[3,2048,256]{2,1,0:T(8,128)(2,1)}, bf16[8,256,2048]{2,1,0:T(8,128)(2,1)}, f32[8,2048]{1,0:T(8,128)}, f32[8,128]{1,0:T(8,128)}) custom-call(bf16[8,32,2048]{2,1,0:T(8,128)(2,1)} %tok.5, bf16[8,32,2048]{2,1,0:T(8,128)(2,1)} %cot.5, s32[8,8,32]{2,1,0:T(8,128)} %bitcast.52, bf16[8,8,32]{2,1,0:T(8,128)(2,1)} %bitcast.53, ...), custom_call_target="tpu_custom_call" | custom-call | tf_op jit(solution)/shard_map/front/pallas_call | solution.py:437
  87.0 98.5 %attend_mix.1 = (bf16[8,256,2048]{2,1,0:T(8,128)(2,1)}, f32[2,8,256,256]{3,2,1,0:T(8,128)}, bf16[3,8,256,256]{3,2,1,0:T(8,128)(2,1)}, bf16[8,256,256]{2,1,0:T(8,...) custom-call(bf16[8,256,2176]{2,1,0:T(8,128)(2,1)} %get-tuple-element, ...), custom_call_target="tpu_custom_call", output_to_operand_aliasing={{6}: (9, {})} | custom-call | tf_op jit(solution)/shard_map/attend_mix/pallas_call | solution.py:978
  185.5 35.5 %expert_first.1 = (bf16[1280,1024]{1,0:T(8,128)(2,1)}, bf16[1280,2048]{1,0:T(8,128)(2,1)}, bf16[2,1280,2048]{2,1,0:T(8,128)(2,1)}, bf16[1280,2048]{1,0:T(8,128)(2,1)}, bf16[1024,2048]{1,0:T(8,128)(2,1)}) custom-call(s32[8,128]{1,0:T(8,128)} %get-tuple-element.62.starts.refs_0_, bf16[8,256,2048]{2,1,0:T(8,128)(2,1)} %get-tuple-element.65.mixed, ...), custom_call_target="tpu_custom_call" | custom-call | flops 20000000000 | bytes 60000000 | tf_op jit(solution)/shard_map/expert_first/pallas_call | solution.py:1256
  221.0 0.0 reduce-scatter.7.cloned.1.call-update
  221.1 0.0 reduce-scatter.5.cloned.1.call-start
  221.1 19.5 %first_in_grad.1 = bf16[2048,2048]{1,0:T(8,128)(2,1)} custom-call(s32[8,128]{1,0:T(8,128)} %get-tuple-element.62.starts.refs_0_, bf16[2,1280,2048]{2,1,0:T(8,128)(2,1)} %get-tuple-element.71.x_all, bf16[1280,2048]{1,0:T(8,128)(2,1)} %get-tuple-element.68.dgu), custom_call_target="tpu_custom_call" | custom-call | flops 10000000000 | bytes 20000000 | tf_op jit(solution)/shard_map/first_in_grad/pallas_call | solution.py:1321
  240.7 0.0 reduce-scatter.5.cloned.1.call-update
  240.7 0.0 reduce-scatter.11.cloned.1.call-start
  240.7 40.7 %expert_second.1 = (bf16[1280,1024]{1,0:T(8,128)(2,1)}, bf16[1280,2048]{1,0:T(8,128)(2,1)}, bf16[1024,2048]{1,0:T(8,128)(2,1)}, bf16[2048,2048]{1,0:T(8,128)(2,1)}) custom-call(s32[8,128]{1,0:T(8,128)} %get-tuple-element.62.starts.refs_0_, bf16[2,1280,2048]{2,1,0:T(8,128)(2,1)} %get-tuple-element.71.x_all, bf16[1280,2048]{1,0:T(8,128)(2,1)} %get-tuple-element.72.dy_all, ...), custom_call_target="tpu_custom_call" | custom-call | flops 24999999488 | bytes 60000000 | tf_op jit(solution)/shard_map/expert_second/pallas_call | solution.py:1381
  281.4 0.0 reduce-scatter.11.cloned.1.call-update
  281.4 0.2 reduce-scatter.9.cloned.1.call-start
  281.7 0.3 reduce-scatter.9.cloned.1.call-update
  282.0 17.8 %expert_tail.2 = (bf16[1280,2048]{1,0:T(8,128)(2,1)}, bf16[1280,2048]{1,0:T(8,128)(2,1)}) custom-call(s32[8,128]{1,0:T(8,128)} %get-tuple-element.62.starts.refs_0_, bf16[1280,1024]{1,0:T(8,128)(2,1)} %get-tuple-element.67.act, bf16[1280,2048]{1,0:T(8,128)(2,1)} %get-tuple-element.68.dgu, bf16[2,2048,2048]{2,1,0:T(8,128)(2,1)} %w_in.7, ...), custom_call_target="tpu_custom_call" | custom-call | flops 12000000000 | bytes 30000000 | tf_op jit(solution)/shard_map/expert_tail/pallas_call | solution.py:1426
  299.9 17.8 %expert_tail.3 = (bf16[1280,2048]{1,0:T(8,128)(2,1)}, bf16[1280,2048]{1,0:T(8,128)(2,1)}) custom-call(s32[8,128]{1,0:T(8,128)} %get-tuple-element.62.starts.refs_0_, bf16[1280,1024]{1,0:T(8,128)(2,1)} %get-tuple-element.73.act, bf16[1280,2048]{1,0:T(8,128)(2,1)} %get-tuple-element.74.dgu, bf16[2,2048,2048]{2,1,0:T(8,128)(2,1)} %w_in.7, ...), custom_call_target="tpu_custom_call" | custom-call | flops 12000000000 | bytes 30000000 | tf_op jit(solution)/shard_map/expert_tail/pallas_call | solution.py:1426
  317.7 19.6 %combine.1 = (bf16[8,256,2048]{2,1,0:T(8,128)(2,1)}, bf16[8,256,2048]{2,1,0:T(8,128)(2,1)}) custom-call(s32[8,128]{1,0:T(8,128)} %get-tuple-element.62.starts.refs_0_, f32[8,16,256]{2,1,0:T(8,128)} %get-tuple-element.63.slots0.refs_1_, f32[8,16,256]{2,1,0:T(8,128)} %get-tuple-element.64.slots1.refs_2_, bf16[1280,2048]{1,0:T(8,128)(2,1)} %get-tuple-element.69.refs_3_, ...), custom_call_target="tpu_custom_call" | custom-call | flops 3000000000 | bytes 40000000 | tf_op jit(solution)/shard_map/combine/pallas_call | solution.py:1477
  337.3 79.4 %back.1 = (f32[8,32,2048]{2,1,0:T(8,128)}, f32[1,2048]{1,0:T(1,128)}, bf16[8,256,2048]{2,1,0:T(8,128)(2,1)}) custom-call(bf16[8,8,32,2048]{3,2,1,0:T(8,128)(2,1)} %bitcast.47, f32[8,32,2048]{2,1,0:T(8,128)} %get-tuple-element.79.middle, bf16[8,32,2048]{2,1,0:T(8,128)(2,1)} %cot.5, f32[8,128]{1,0:T(8,128)} %get-tuple-element.60.small, ...), custom_call_target="tpu_custom_call" | custom-call | tf_op jit(solution)/shard_map/back/pallas_call | solution.py:505
  416.7 0.0 copy-start.2
  416.8 45.3 %attend_back.1 = (bf16[8,256,2048]{2,1,0:T(8,128)(2,1)}, bf16[3,2048,256]{2,1,0:T(8,128)(2,1)}, bf16[256,2048]{1,0:T(8,128)(2,1)}, f32[8,128]{1,0:T(8,128)}) custom-call(bf16[8,256,2048]{2,1,0:T(8,128)(2,1)} %get-tuple-element.80.agrad, bf16[8,256,2048]{2,1,0:T(8,128)(2,1)} %get-tuple-element.81.normed, f32[2,8,256,256]{3,2,1,0:T(8,128)} %get-tuple-element.82.pre, ...), custom_call_target="tpu_custom_call" | custom-call | flops 20000000000 | bytes 40000000 | tf_op jit(solution)/shard_map/attend_back/pallas_call | solution.py:1068
  462.1 0.7 slice.31
  462.8 0.0 copy-done.2
  462.8 0.6 select_maximum_fusion.others
  463.4 0.0 reduce-scatter.7.cloned.1.call-done
  463.4 3.7 pad_convert_fusion.1
  467.1 0.0 reduce-scatter.5.cloned.1.call-done
  467.1 6.1 pad_convert_fusion
  473.2 307.2 %finish.1 = (bf16[4,4,64,2048]{3,2,1,0:T(8,128)(2,1)}, f32[8,128]{1,0:T(8,128)}, bf16[8,32,2048]{2,1,0:T(8,128)(2,1)}, bf16[8,32,2048]{2,1,0:T(8,128)(2,1)}) custom-call(bf16[3,32,64,256]{3,2,1,0:T(8,128)(2,1)} %bitcast.48, bf16[4,64,2048]{2,1,0:T(8,128)(2,1)} %bitcast.51, bf16[8,8,32,2048]{3,2,1,0:T(8,128)(2,1)} %bitcast.46, ...), custom_call_target="tpu_custom_call" | custom-call | tf_op jit(solution)/shard_map/finish/pallas_call | solution.py:738
  780.5 0.8 fusion.3
  781.2 0.6 fusion.1
  781.8 0.6 fusion
  782.4 1.3 slice_bitcast_fusion
  783.7 2.7 fusion.2
  786.5 1.6 bitcast_convert_fusion
  788.1 1.6 bitcast_convert_fusion.1
  789.7 1.6 bitcast_convert_fusion.2
  791.4 1.6 bitcast_convert_fusion.3
  793.0 0.0 copy-start.1
  793.0 0.0 reduce-scatter.11.cloned.1.call-done
  793.0 2.9 convert_dynamic-update-slice_fusion.1
  795.9 0.0 copy-start
  795.9 0.0 reduce-scatter.9.cloned.1.call-done
  795.9 4.2 convert_dynamic-update-slice_fusion
  800.1 0.0 copy-done.1
  800.1 1.0 copy.36
  801.1 0.0 copy-done
  801.1 1.0 copy.37
  (1 shorter events, 0.0 us)
Async XLA Ops:
  7.2 456.2 %reduce-scatter.7.cloned.1.call-start = ((), (), s32[]{:S(2)}) async-start(), calls=%async_computation.5 | async-start | bytes 5242880 | tf_op jit(solution)/shard_map/reduce_scatter | solution.py:1540
  221.1 246.1 %reduce-scatter.5.cloned.1.call-start = ((), (), s32[]{:S(2)}) async-start(), calls=%async_computation.4 | async-start | bytes 10485760 | tf_op jit(solution)/shard_map/reduce_scatter | solution.py:1540
  240.7 552.3 %reduce-scatter.11.cloned.1.call-start = ((), (), s32[]{:S(2)}) async-start(), calls=%async_computation.7 | async-start | bytes 5242880 | tf_op jit(solution)/shard_map/reduce_scatter | solution.py:1540
  281.4 514.4 %reduce-scatter.9.cloned.1.call-start = ((), (), s32[]{:S(2)}) async-start(), calls=%async_computation.6 | async-start | bytes 10485760 | tf_op jit(solution)/shard_map/reduce_scatter | solution.py:1540
  416.7 46.0 %copy-start.2 = (f32[1,2048]{1,0:T(1,128)S(1)}, f32[1,2048]{1,0:T(1,128)}, u32[]{:S(2)}) copy-start(f32[1,2048]{1,0:T(1,128)} %get-tuple-element.92) | copy-start | bytes 24580
  793.0 7.1 copy-start.1
  795.9 5.2 copy-start
Sparse Core Ops, SparseCore 0:
  221.2 81.2 reduce-scatter.6
  304.9 145.1 reduce-scatter.4
  452.3 92.8 reduce-scatter.10
  547.5 226.3 reduce-scatter.8

commit v8 on v7

--- a/solution.py
+++ b/solution.py
@@ -763,6 +763,14 @@
     return lax.dot_general(a, b, (((ca,), (cb,)), ((), ())), preferred_element_type=F32)
 
 
+def rope_tables(table):
+    half = HEAD_DIM // 2
+    values = table[...]
+    turned = pltpu.roll(values, half, 1)
+    first = lax.broadcasted_iota(jnp.int32, values.shape, 1) < half
+    return jnp.where(first, values, turned), jnp.where(first, -turned, values)
+
+
 def rope(v, cos, sin_turn):
     return v * cos + pltpu.roll(v, HEAD_DIM // 2, 1) * sin_turn
 
@@ -792,9 +800,10 @@
     return jnp.where(hit > 0.5, rank, -1.0), weight, jnp.sum(hit[0:1], axis=1, keepdims=True)
 
 
-def attend_rows(top, number, s, block, w, wo, gains, small, cos, sin, normed, pre, low, ctx, part, slots, starts):
+def attend_rows(top, number, s, block, w, wo, gains, small, table, normed, pre, low, ctx, part, slots, starts):
     width = normed.shape[1]
     length = seq_len(small, s)
+    cos, sin = rope_tables(table)
     v = block[:, 0:width].astype(F32)
     x = (v * inverse_rms(v) * gains[0:1]).astype(BF16)
     normed[...] = x
@@ -806,15 +815,15 @@
         cols = slice(h * HEAD_DIM, (h + 1) * HEAD_DIM)
         rot = []
         for i, (u, g) in enumerate(((q_pre[:, cols], small[0:1]), (k_pre[:, cols], small[1:2]))):
-            rot.append(rope(u * inverse_rms(u) * g, cos[...], sin[...]).astype(BF16))
+            rot.append(rope(u * inverse_rms(u) * g, cos, sin).astype(BF16))
             low[i, :, cols] = rot[i]
         attention = probabilities(rot[0], rot[1], length).astype(BF16)
         ctx[:, cols] = dot(attention, value[:, cols], 1, 0).astype(BF16)
     part[...] = dot(ctx[...], wo[...], 1, 0).astype(BF16).reshape(part.shape)
-    table = block[:, width : width + 128]
+    routes = block[:, width : width + 128]
     lane = lax.broadcasted_iota(jnp.int32, (1, 128), 1)
     for j, ref in enumerate(slots):
-        slot, weight, count = packed_slots(number + j, table, length, top)
+        slot, weight, count = packed_slots(number + j, routes, length, top)
         ref[0:8] = slot
         ref[8:16] = weight
         row = starts[j : j + 1]
@@ -822,7 +831,7 @@
         starts[j : j + 1] = jnp.where(lane == s + 1, after, row)
 
 
-def attend_kernel(top, number, full, w, wo, gains, small, cos, sin, normed, pre, low, ctx, part, slots0, slots1, starts):
+def attend_kernel(top, number, full, w, wo, gains, small, table, normed, pre, low, ctx, part, slots0, slots1, starts):
     s = pl.program_id(0)
 
     @pl.when(s == 0)
@@ -830,12 +839,12 @@
         starts[...] = jnp.zeros_like(starts)
 
     attend_rows(
-        top, number[0].astype(F32), s, full.at[0], w, wo, gains, small, cos, sin,
+        top, number[0].astype(F32), s, full.at[0], w, wo, gains, small, table,
         normed.at[0], pre.at[:, 0], low.at[:, 0], ctx.at[0], part.at[0], (slots0.at[0], slots1.at[0]), starts,
     )
 
 
-def attend(top, number, full, weights, wo, gains, small, cos, sin):
+def attend(top, number, full, weights, wo, gains, small, table):
     seqs, length, wide = full.shape
     width = wide - 128
     cols = weights.shape[2]
@@ -865,7 +874,6 @@
                 pl.BlockSpec((8, width), two),
                 pl.BlockSpec((8, 128), two),
                 pl.BlockSpec((length, HEAD_DIM), two),
-                pl.BlockSpec((length, HEAD_DIM), two),
             ],
             out_specs=(
                 pl.BlockSpec((1, length, width), row),
@@ -881,11 +889,11 @@
         compiler_params=pltpu.CompilerParams(dimension_semantics=("arbitrary",), vmem_limit_bytes=60 << 20),
         cost_estimate=pl.CostEstimate(flops=10**10, bytes_accessed=4 * 10**7, transcendentals=10**6),
         name="attend",
-    )(number, full, weights, wo, gains, small, cos, sin)
+    )(number, full, weights, wo, gains, small, table)
 
 
 def attend_mix_kernel(
-    top, local, full, w, wo, gains, small, cos, sin, tok, cot, _cot_early,
+    top, local, full, w, wo, gains, small, table, tok, cot, _cot_early,
     normed, pre, low, ctx, middle, mixed, cot_full, slots0, slots1, starts,
     own, blocks, nbuf, pbuf, lbuf, cbuf, part, begins, tsem, ssem, *scratch,
 ):
@@ -925,7 +933,7 @@
                 copy.wait()
 
         attend_rows(
-            top, number, s, blocks.at[k], w, wo, gains, small, cos, sin,
+            top, number, s, blocks.at[k], w, wo, gains, small, table,
             nbuf.at[k], pbuf.at[k], lbuf.at[k], cbuf.at[k], part.at[s], (slots0.at[s], slots1.at[s]), begins,
         )
         for copy in stores(s):
@@ -969,7 +977,7 @@
     each(seqs, reduce.finish)
 
 
-def attend_mix(top, local, full, weights, wo, gains, small, cos, sin, tokens, cotangent, cot_early):
+def attend_mix(top, local, full, weights, wo, gains, small, table, tokens, cotangent, cot_early):
     seqs, rows, width = tokens.shape
     length = full.shape[1]
     cols = weights.shape[2]
@@ -989,9 +997,9 @@
             sds((seqs, 16, length), F32),
             sds((8, 128), jnp.int32),
         ),
-        in_specs=[AN] + [VM] * 8 + [AN],
+        in_specs=[AN] + [VM] * 7 + [AN],
         out_specs=(AN, AN, AN, AN, VM, AN, AN, VM, VM, VM),
-        input_output_aliases={9: 6},
+        input_output_aliases={8: 6},
         scratch_shapes=[
             pltpu.VMEM(tokens.shape, BF16),
             pltpu.VMEM((2,) + full.shape[1:], BF16),
@@ -1009,14 +1017,16 @@
         + Gather.scratch(seqs),
         compiler_params=pltpu.CompilerParams(collective_id=2, **COMM),
         name="attend_mix",
-    )(full, weights, wo, gains, small, cos, sin, tokens, cotangent, cot_early)
+    )(full, weights, wo, gains, small, table, tokens, cotangent, cot_early)
 
 
 def attend_back_kernel(
-    agrad, normed, pre, low, ctx, w, wo, small, cos, sin, part, wgrad, wograd, gains, wacc, woacc
+    agrad, normed, pre, low, ctx, w, wo, small, table, part, wgrad, wograd, gains, wacc, woacc,
+    gbuf, total,
 ):
     s = pl.program_id(0)
     length = seq_len(small, s)
+    cos, sin = rope_tables(table)
 
     @pl.when(s == 0)
     def _():
@@ -1039,18 +1049,32 @@
         sg = (attention * (pg - jnp.sum(attention * pg, axis=-1, keepdims=True))).astype(BF16)
         for i, (rot_grad, g) in enumerate(((dot(sg, k, 1, 0), small[0:1]), (dot(sg, q, 0, 0), small[1:2]))):
             wgt = rot_grad * scale
-            u = wgt * cos[...] + pltpu.roll(wgt * sin[...], half, 1)
+            u = wgt * cos + pltpu.roll(wgt * sin, half, 1)
             v = pre[i, 0, :, cols]
             r = inverse_rms(v)
             grads[i].append(rms_back(v, r, u * g).astype(BF16))
             gains[i : i + 1] += jnp.sum(u * v * r, axis=0, keepdims=True)
-    total = None
     for i in range(3):
-        g = grads[i][0] if len(grads[i]) == 1 else jnp.concatenate(grads[i], axis=1)
+        for h, g in enumerate(grads[i]):
+            gbuf[i, :, h * HEAD_DIM : (h + 1) * HEAD_DIM] = g
+
+    def project(i, _):
+        g = gbuf[i]
         wacc[i] += dot(normed[0], g, 0, 0)
         piece = dot(g, w[i], 1, 1)
-        total = piece if total is None else total + piece
-    part[0] = total.astype(BF16)
+
+        @pl.when(i == 0)
+        def _():
+            total[...] = piece
+
+        @pl.when(i > 0)
+        def _():
+            total[...] += piece
+
+        return 0
+
+    lax.fori_loop(0, 3, project, 0)
+    part[0] = total[...].astype(BF16)
 
     @pl.when(s == pl.num_programs(0) - 1)
     def _():
@@ -1058,7 +1082,7 @@
         wograd[...] = woacc[...].astype(BF16)
 
 
-def attend_back(agrad, normed, pre, low, ctx, weights, wo, small, cos, sin):
+def attend_back(agrad, normed, pre, low, ctx, weights, wo, small, table):
     seqs, length, width = agrad.shape
     cols = weights.shape[2]
     row = lambda i, *_: (i, 0, 0)
@@ -1086,7 +1110,6 @@
                 pl.BlockSpec(wo.shape, two),
                 pl.BlockSpec((8, 128), two),
                 pl.BlockSpec((length, HEAD_DIM), two),
-                pl.BlockSpec((length, HEAD_DIM), two),
             ],
             out_specs=(
                 pl.BlockSpec((1, length, width), row),
@@ -1094,12 +1117,17 @@
                 pl.BlockSpec(wo.shape, two),
                 pl.BlockSpec((8, HEAD_DIM), two),
             ),
-            scratch_shapes=[pltpu.VMEM(weights.shape, F32), pltpu.VMEM(wo.shape, F32)],
+            scratch_shapes=[
+                pltpu.VMEM(weights.shape, F32),
+                pltpu.VMEM(wo.shape, F32),
+                pltpu.VMEM((3, length, cols), BF16),
+                pltpu.VMEM((length, width), F32),
+            ],
         ),
         compiler_params=pltpu.CompilerParams(dimension_semantics=("arbitrary",), vmem_limit_bytes=60 << 20),
         cost_estimate=pl.CostEstimate(flops=2 * 10**10, bytes_accessed=4 * 10**7, transcendentals=10**6),
         name="attend_back",
-    )(agrad, normed, pre, low, ctx, weights, wo, small, cos, sin)
+    )(agrad, normed, pre, low, ctx, weights, wo, small, table)
 
 
 BLOCK = 256
@@ -1109,25 +1137,23 @@
     return -(-seqs * capacity // BLOCK) * BLOCK
 
 
-def forward_blocks(blocks, x, dy, wi, wo, acts, dgus):
-    hidden = wo.shape[0]
+def each_block(blocks, hidden, job):
     part = min(hidden, 512)
-
-    def forward(b, _):
+    parts = hidden // part
+
+    def run(i, _):
+        b, h = i // parts, lax.rem(i, parts)
         rows = pl.ds(pl.multiple_of(b * BLOCK, BLOCK), BLOCK)
-        for h in range(hidden // part):
-            gcols, ucols = pl.ds(h * part, part), pl.ds(hidden + h * part, part)
-            gate = dot(x[rows], wi[:, gcols], 1, 0)
-            up = dot(x[rows], wi[:, ucols], 1, 0)
-            dact = dot(dy[rows], wo[gcols], 1, 1)
-            sig = 1.0 / (1.0 + jnp.exp(-gate))
-            silu = gate * sig
-            acts[rows, gcols] = (silu * up).astype(BF16)
-            dgus[rows, gcols] = (dact * up * sig * (1.0 + gate * (1.0 - sig))).astype(BF16)
-            dgus[rows, ucols] = (dact * silu).astype(BF16)
+        low = pl.multiple_of(h * part, part)
+        job(rows, pl.ds(low, part), pl.ds(pl.multiple_of(hidden + low, part), part))
         return 0
 
-    lax.fori_loop(0, blocks, forward, 0)
+    lax.fori_loop(0, blocks * parts, run, 0)
+
+
+def swiglu_back(gate, up, dact):
+    sig = 1.0 / (1.0 + jnp.exp(-gate))
+    return dact * up * sig * (1.0 + gate * (1.0 - sig)), dact * (gate * sig)
 
 
 def gradient_tiles(blocks, left, right, result, acc, stage, ssem, busy):
@@ -1179,21 +1205,21 @@
 
 
 def first_kernel(
-    capacity, starts, mixed, cot, slots0, slots1, w_in, w_out,
-    act, dgu, x_all, dy_all, out_grad,
-    x, dy, wi, wo, acts, dgus, acc, stage, wsem, ssem, rsem,
+    capacity, starts, mixed, cot, slots0, slots1, w_in,
+    act, pair, x_all, dy_all, out_grad,
+    x, dy, wi, acts, pairs, acc, stage, wsem, ssem, rsem,
 ):
     step = pl.program_id(0)
     steps = pl.num_programs(0)
     together = mixed.shape[0]
     seqs = steps * together
     width = mixed.shape[2]
-    loads = [pltpu.make_async_copy(w_in.at[0], wi, wsem.at[0]), pltpu.make_async_copy(w_out.at[0], wo, wsem.at[1])]
+    hidden = acts.shape[1]
+    load = pltpu.make_async_copy(w_in.at[0], wi, wsem)
 
     @pl.when(step == 0)
     def _():
-        for copy in loads:
-            copy.start()
+        load.start()
 
     packed = []
     for k in range(together):
@@ -1229,14 +1255,21 @@
                 return 0
 
             lax.fori_loop(past, end, clear, 0)
-        saves = [pltpu.make_async_copy(x, x_all, rsem.at[0]), pltpu.make_async_copy(dy.at[1], dy_all, rsem.at[1])]
+        saves = [pltpu.make_async_copy(x, x_all, rsem.at[0]), pltpu.make_async_copy(dy, dy_all, rsem.at[1])]
         for copy in saves:
             copy.start()
         blocks = (starts[0, seqs] + BLOCK - 1) // BLOCK
-        for copy in loads:
-            copy.wait()
-        forward_blocks(blocks, x.at[0], dy.at[0], wi, wo, acts, dgus)
-        saves += [pltpu.make_async_copy(acts, act, rsem.at[2]), pltpu.make_async_copy(dgus, dgu, rsem.at[3])]
+        load.wait()
+
+        def forward(rows, gcols, ucols):
+            gate = dot(x[0, rows], wi[:, gcols], 1, 0)
+            up = dot(x[0, rows], wi[:, ucols], 1, 0)
+            acts[rows, gcols] = (gate * (1.0 / (1.0 + jnp.exp(-gate))) * up).astype(BF16)
+            pairs[rows, gcols] = gate.astype(BF16)
+            pairs[rows, ucols] = up.astype(BF16)
+
+        each_block(blocks, hidden, forward)
+        saves += [pltpu.make_async_copy(acts, act.at[0], rsem.at[2]), pltpu.make_async_copy(pairs, pair, rsem.at[3])]
         for copy in saves[2:]:
             copy.start()
         gradient_tiles(blocks, acts, dy.at[0], out_grad, acc, stage, ssem, False)
@@ -1245,9 +1278,8 @@
             copy.wait()
 
 
-def expert_first(starts, mixed, cot, slots, w_in, w_out, capacity):
+def expert_first(starts, mixed, cot, slots, w_in, hidden, capacity):
     seqs, length, width = mixed.shape
-    hidden = w_out.shape[1]
     rows = pack_rows(seqs, capacity)
     dma = pltpu.SemaphoreType.DMA
     seq = lambda i, *_: (i, 0, 0)
@@ -1256,10 +1288,10 @@
     return pl.pallas_call(
         functools.partial(first_kernel, capacity),
         out_shape=(
-            sds((rows, hidden), BF16),
+            sds((2, rows, hidden), BF16),
             sds((rows, 2 * hidden), BF16),
             sds((2, rows, width), BF16),
-            sds((rows, width), BF16),
+            sds((2, rows, width), BF16),
             sds((hidden, width), BF16),
         ),
         grid_spec=pltpu.PrefetchScalarGridSpec(
@@ -1271,88 +1303,108 @@
                 slot_spec,
                 slot_spec,
                 AN,
-                AN,
             ],
             out_specs=(AN, AN, AN, AN, AN),
             scratch_shapes=[
                 pltpu.VMEM((2, rows, width), BF16),
                 pltpu.VMEM((2, rows, width), BF16),
                 pltpu.VMEM(w_in.shape[1:], BF16),
-                pltpu.VMEM(w_out.shape[1:], BF16),
                 pltpu.VMEM((rows, hidden), BF16),
                 pltpu.VMEM((rows, 2 * hidden), BF16),
-                pltpu.VMEM((256, 1024), F32),
-                pltpu.VMEM((2, 256, 1024), BF16),
-                dma((2,)),
+                pltpu.VMEM((512, 1024), F32),
+                pltpu.VMEM((2, 512, 1024), BF16),
+                dma,
                 dma((2,)),
                 dma((4,)),
             ],
         ),
-        compiler_params=pltpu.CompilerParams(dimension_semantics=("arbitrary",), vmem_limit_bytes=63 << 20),
+        compiler_params=pltpu.CompilerParams(dimension_semantics=("arbitrary",), vmem_limit_bytes=62 << 20),
         cost_estimate=pl.CostEstimate(flops=2 * 10**10, bytes_accessed=6 * 10**7, transcendentals=10**6),
         name="expert_first",
-    )(starts, mixed, cot, *slots, w_in, w_out)
-
-
-def in_grad_kernel(seqs, starts, x_all, dgu, in_grad, x, dgus, acc, stage, lsem, ssem):
+    )(starts, mixed, cot, *slots, w_in)
+
+
+def in_grad_kernel(
+    seqs, starts, x_all, dy_all, pair, w_out, dgu, in_grad, x, dy, wo, pairs, dgus, acc, stage, lsem, wsem, ssem, rsem
+):
     blocks = (starts[0, seqs] + BLOCK - 1) // BLOCK
-
-    def load(b):
+    hidden = wo.shape[0]
+    weights = pltpu.make_async_copy(w_out.at[0], wo, wsem)
+    weights.start()
+
+    def run(b, action):
         rows = pl.ds(pl.multiple_of(b * BLOCK, BLOCK), BLOCK)
-        return (
-            pltpu.make_async_copy(x_all.at[0, rows], x.at[rows], lsem.at[0, b]),
-            pltpu.make_async_copy(dgu.at[rows], dgus.at[rows], lsem.at[1, b]),
-        )
-
-    def run(b, action):
-        for copy in load(b):
+        for copy in (
+            pltpu.make_async_copy(dy_all.at[0, rows], dy.at[rows], lsem.at[0, b]),
+            pltpu.make_async_copy(pair.at[rows], pairs.at[rows], lsem.at[1, b]),
+            pltpu.make_async_copy(x_all.at[0, rows], x.at[rows], lsem.at[2, b]),
+        ):
             getattr(copy, action)()
         return 0
 
     lax.fori_loop(0, blocks, lambda b, _: run(b, "start"), 0)
+    weights.wait()
     lax.fori_loop(0, blocks, lambda b, _: run(b, "wait"), 0)
-    gradient_tiles(blocks, x, dgus, in_grad, acc, stage, ssem, False)
-    drain_tiles(in_grad, acc, stage, ssem)
-
-
-def first_in_grad(seqs, starts, x_all, dgu):
+
+    def backward(rows, gcols, ucols):
+        dact = dot(dy[rows], wo[gcols], 1, 1)
+        dgate, dup = swiglu_back(pairs[rows, gcols].astype(F32), pairs[rows, ucols].astype(F32), dact)
+        dgus[rows, gcols] = dgate.astype(BF16)
+        dgus[rows, ucols] = dup.astype(BF16)
+
+    each_block(blocks, hidden, backward)
+    save = pltpu.make_async_copy(dgus, dgu.at[0], rsem)
+    save.start()
+    gradient_tiles(blocks, x, dgus, in_grad.at[0], acc, stage, ssem, False)
+    drain_tiles(in_grad.at[0], acc, stage, ssem)
+    save.wait()
+
+
+def first_in_grad(seqs, starts, x_all, dy_all, pair, w_out):
     rows, width = x_all.shape[1:]
+    hidden = w_out.shape[1]
     dma = pltpu.SemaphoreType.DMA
     return pl.pallas_call(
         functools.partial(in_grad_kernel, seqs),
-        out_shape=sds((width, dgu.shape[1]), BF16),
+        out_shape=(sds((2, rows, 2 * hidden), BF16), sds((2, width, 2 * hidden), BF16)),
         grid_spec=pltpu.PrefetchScalarGridSpec(
             num_scalar_prefetch=1,
             grid=(1,),
-            in_specs=[AN, AN],
-            out_specs=AN,
+            in_specs=[AN] * 4,
+            out_specs=(AN, AN),
             scratch_shapes=[
                 pltpu.VMEM((rows, width), BF16),
-                pltpu.VMEM(dgu.shape, BF16),
+                pltpu.VMEM((rows, width), BF16),
+                pltpu.VMEM(w_out.shape[1:], BF16),
+                pltpu.VMEM((rows, 2 * hidden), BF16),
+                pltpu.VMEM((rows, 2 * hidden), BF16),
                 pltpu.VMEM((512, 2048), F32),
                 pltpu.VMEM((2, 512, 2048), BF16),
-                dma((2, rows // BLOCK)),
+                dma((3, rows // BLOCK)),
+                dma,
                 dma((2,)),
+                dma,
             ],
         ),
         compiler_params=pltpu.CompilerParams(dimension_semantics=("arbitrary",), vmem_limit_bytes=60 << 20),
         cost_estimate=pl.CostEstimate(flops=10**10, bytes_accessed=2 * 10**7, transcendentals=0),
         name="first_in_grad",
-    )(starts, x_all, dgu)
+    )(starts, x_all, dy_all, pair, w_out)
 
 
 def second_kernel(
-    seqs, starts, x_all, dy_all, w_in, w_out, act, dgu, out_grad, in_grad,
+    seqs, starts, x_all, dy_all, w_in, w_out, _act, _dgu, _in_grad, act, dgu, in_grad, out_grad,
     x, dy, wi, wo, acts, dgus, acc, stage, wsem, lsem, ssem, rsem,
 ):
     blocks = (starts[1, seqs] + BLOCK - 1) // BLOCK
+    hidden = wo.shape[0]
     loads = [pltpu.make_async_copy(w_in.at[1], wi, wsem.at[0]), pltpu.make_async_copy(w_out.at[1], wo, wsem.at[1])]
 
     def load(b, action):
         rows = pl.ds(pl.multiple_of(b * BLOCK, BLOCK), BLOCK)
         for copy in (
             pltpu.make_async_copy(x_all.at[1, rows], x.at[rows], lsem.at[0, b]),
-            pltpu.make_async_copy(dy_all.at[rows], dy.at[rows], lsem.at[1, b]),
+            pltpu.make_async_copy(dy_all.at[1, rows], dy.at[rows], lsem.at[1, b]),
         ):
             getattr(copy, action)()
         return 0
@@ -1363,33 +1415,39 @@
     for copy in loads:
         copy.wait()
     lax.fori_loop(0, blocks, lambda b, _: load(b, "wait"), 0)
-    forward_blocks(blocks, x, dy, wi, wo, acts, dgus)
-    saves = [pltpu.make_async_copy(acts, act, rsem.at[0]), pltpu.make_async_copy(dgus, dgu, rsem.at[1])]
+
+    def both(rows, gcols, ucols):
+        gate = dot(x[rows], wi[:, gcols], 1, 0)
+        up = dot(x[rows], wi[:, ucols], 1, 0)
+        dact = dot(dy[rows], wo[gcols], 1, 1)
+        acts[rows, gcols] = (gate * (1.0 / (1.0 + jnp.exp(-gate))) * up).astype(BF16)
+        dgate, dup = swiglu_back(gate, up, dact)
+        dgus[rows, gcols] = dgate.astype(BF16)
+        dgus[rows, ucols] = dup.astype(BF16)
+
+    each_block(blocks, hidden, both)
+    saves = [pltpu.make_async_copy(acts, act.at[1], rsem.at[0]), pltpu.make_async_copy(dgus, dgu.at[1], rsem.at[1])]
     for copy in saves:
         copy.start()
-    gradient_tiles(blocks, x, dgus, in_grad, acc, stage, ssem, False)
+    gradient_tiles(blocks, x, dgus, in_grad.at[1], acc, stage, ssem, False)
     gradient_tiles(blocks, acts, dy, out_grad, acc, stage, ssem, True)
     drain_tiles(out_grad, acc, stage, ssem)
     for copy in saves:
         copy.wait()
 
 
-def expert_second(seqs, starts, x_all, dy_all, w_in, w_out):
-    rows, width = dy_all.shape
+def expert_second(seqs, starts, x_all, dy_all, w_in, w_out, act, dgu, in_grad):
+    rows, width = dy_all.shape[1:]
     hidden = w_out.shape[1]
     dma = pltpu.SemaphoreType.DMA
     return pl.pallas_call(
         functools.partial(second_kernel, seqs),
-        out_shape=(
-            sds((rows, hidden), BF16),
-            sds((rows, 2 * hidden), BF16),
-            sds((hidden, width), BF16),
-            sds((width, 2 * hidden), BF16),
-        ),
+        out_shape=(sds(act.shape, BF16), sds(dgu.shape, BF16), sds(in_grad.shape, BF16), sds((hidden, width), BF16)),
+        input_output_aliases={5: 0, 6: 1, 7: 2},
         grid_spec=pltpu.PrefetchScalarGridSpec(
             num_scalar_prefetch=1,
             grid=(1,),
-            in_specs=[AN] * 4,
+            in_specs=[AN] * 7,
             out_specs=(AN, AN, AN, AN),
             scratch_shapes=[
                 pltpu.VMEM((rows, width), BF16),
@@ -1409,37 +1467,48 @@
         compiler_params=pltpu.CompilerParams(dimension_semantics=("arbitrary",), vmem_limit_bytes=60 << 20),
         cost_estimate=pl.CostEstimate(flops=25 * 10**9, bytes_accessed=6 * 10**7, transcendentals=10**6),
         name="expert_second",
-    )(starts, x_all, dy_all, w_in, w_out)
-
-
-def tail_kernel(j, seqs, starts, act, dgu, w_in, w_out, produced, dx):
-    @pl.when(pl.program_id(0) * BLOCK < starts[j, seqs])
+    )(starts, x_all, dy_all, w_in, w_out, act, dgu, in_grad)
+
+
+def tail_kernel(seqs, starts, act, dgu, w_in, w_out, produced, dx):
+    @pl.when(pl.program_id(1) * BLOCK < starts[pl.program_id(0), seqs])
     def _():
-        produced[...] = dot(act[...], w_out[...], 1, 0).astype(BF16)
-        dx[...] = dot(dgu[...], w_in[...], 1, 1).astype(BF16)
-
-
-def expert_tail(j, seqs, starts, act, dgu, w_in, w_out):
-    rows, hidden = act.shape
+        part = min(produced.shape[1], 256)
+
+        def run(i, _):
+            cols = pl.ds(pl.multiple_of(i * part, part), part)
+            produced[:, cols] = dot(act[...], w_out[:, cols], 1, 0).astype(BF16)
+            dx[:, cols] = dot(dgu[...], w_in[cols], 1, 1).astype(BF16)
+            return 0
+
+        lax.fori_loop(0, produced.shape[1] // part, run, 0)
+
+
+def expert_tails(seqs, starts, act, dgu, w_in, w_out):
+    _, rows, hidden = act.shape
     width = w_in.shape[1]
-    block = lambda i, st: (jnp.maximum(jnp.minimum(i, (st[j, seqs] + BLOCK - 1) // BLOCK - 1), 0), 0)
+
+    def block(j, i, st):
+        return j, jnp.maximum(jnp.minimum(i, (st[j, seqs] + BLOCK - 1) // BLOCK - 1), 0), 0
+
+    out = pl.BlockSpec((None, BLOCK, width), block)
     return pl.pallas_call(
-        functools.partial(tail_kernel, j, seqs),
-        out_shape=(sds((rows, width), BF16), sds((rows, width), BF16)),
+        functools.partial(tail_kernel, seqs),
+        out_shape=(sds((2, rows, width), BF16), sds((2, rows, width), BF16)),
         grid_spec=pltpu.PrefetchScalarGridSpec(
             num_scalar_prefetch=1,
-            grid=(rows // BLOCK,),
+            grid=(2, rows // BLOCK),
             in_specs=[
-                pl.BlockSpec((BLOCK, hidden), block),
-                pl.BlockSpec((BLOCK, 2 * hidden), block),
-                pl.BlockSpec((None,) + w_in.shape[1:], lambda i, *_: (j, 0, 0)),
-                pl.BlockSpec((None,) + w_out.shape[1:], lambda i, *_: (j, 0, 0)),
+                pl.BlockSpec((None, BLOCK, hidden), block),
+                pl.BlockSpec((None, BLOCK, 2 * hidden), block),
+                pl.BlockSpec((None,) + w_in.shape[1:], lambda j, i, *_: (j, 0, 0)),
+                pl.BlockSpec((None,) + w_out.shape[1:], lambda j, i, *_: (j, 0, 0)),
             ],
-            out_specs=(pl.BlockSpec((BLOCK, width), block), pl.BlockSpec((BLOCK, width), block)),
+            out_specs=(out, out),
         ),
-        compiler_params=pltpu.CompilerParams(dimension_semantics=("arbitrary",), vmem_limit_bytes=60 << 20),
-        cost_estimate=pl.CostEstimate(flops=12 * 10**9, bytes_accessed=3 * 10**7, transcendentals=0),
-        name="expert_tail",
+        compiler_params=pltpu.CompilerParams(dimension_semantics=("arbitrary", "arbitrary"), vmem_limit_bytes=60 << 20),
+        cost_estimate=pl.CostEstimate(flops=24 * 10**9, bytes_accessed=6 * 10**7, transcendentals=0),
+        name="expert_tails",
     )(starts, act, dgu, w_in, w_out)
 
 
@@ -1447,9 +1516,7 @@
     s = pl.program_id(0)
     starts = refs[0]
     slots = refs[1 : 1 + local]
-    produced = refs[1 + local : 1 + 2 * local]
-    dx = refs[1 + 2 * local : 1 + 3 * local]
-    out_part, grad_part = refs[1 + 3 * local :]
+    produced, dx, out_part, grad_part = refs[1 + local :]
     out_sum, grad_sum = None, None
     for j in range(local):
         length = slots[j].shape[2]
@@ -1457,8 +1524,8 @@
         place = column == slots[j][0, 0:1]
         span = pl.ds(pl.multiple_of(starts[j, s], 16), capacity)
         held = lax.broadcasted_iota(jnp.int32, (capacity, 1), 0) < starts[j, s + 1] - starts[j, s]
-        rows = jnp.where(held, produced[j][span], 0.0).astype(BF16)
-        grads = jnp.where(held, dx[j][span], 0.0).astype(BF16)
+        rows = jnp.where(held, produced[j, span], 0.0).astype(BF16)
+        grads = jnp.where(held, dx[j, span], 0.0).astype(BF16)
         out = dot(jnp.where(place, slots[j][0, 8:9], 0.0).astype(BF16), rows, 0, 0)
         grad = dot(jnp.where(place, 1.0, 0.0).astype(BF16), grads, 0, 0)
         out_sum = out if out_sum is None else out_sum + out
@@ -1470,23 +1537,22 @@
 def combine(starts, slots, produced, dx, capacity):
     local = len(slots)
     seqs, _, length = slots[0].shape
-    width = produced[0].shape[1]
+    width = produced.shape[2]
     seq = lambda i, *_: (i, 0, 0)
-    two = lambda i, *_: (0, 0)
-    rows = pl.BlockSpec(produced[0].shape, two)
+    rows = pl.BlockSpec(produced.shape, lambda i, *_: (0, 0, 0))
     return pl.pallas_call(
         functools.partial(combine_kernel, capacity, local),
         out_shape=(sds((seqs, length, width), BF16), sds((seqs, length, width), BF16)),
         grid_spec=pltpu.PrefetchScalarGridSpec(
             num_scalar_prefetch=1,
             grid=(seqs,),
-            in_specs=[pl.BlockSpec((1, 16, length), seq)] * local + [rows] * (2 * local),
+            in_specs=[pl.BlockSpec((1, 16, length), seq)] * local + [rows] * 2,
             out_specs=(pl.BlockSpec((1, length, width), seq), pl.BlockSpec((1, length, width), seq)),
         ),
         compiler_params=pltpu.CompilerParams(dimension_semantics=("arbitrary",), vmem_limit_bytes=60 << 20),
         cost_estimate=pl.CostEstimate(flops=3 * 10**9, bytes_accessed=4 * 10**7, transcendentals=0),
         name="combine",
-    )(starts, *slots, *produced, *dx)
+    )(starts, *slots, produced, dx)
 
 
 def shards(
@@ -1499,6 +1565,7 @@
     length = rows * ep
     top = gate_weights.shape[2]
     local = expert_in.shape[0]
+    hidden = expert_out.shape[1]
     experts = local * ep
     capacity = -(-(length * top * 9 // (8 * experts)) // 16) * 16
 
@@ -1517,50 +1584,47 @@
     half = HEAD_DIM // 2
     frequency = ROPE_BASE ** (-(np.arange(half, dtype=np.float32) * np.float32(2.0 / HEAD_DIM)))
     angles = np.arange(length, dtype=np.float32)[:, None] * frequency.astype(np.float32)[None, :]
-    cos = jnp.asarray(np.concatenate([np.cos(angles)] * 2, axis=-1), F32)
-    sin = jnp.asarray(np.concatenate([-np.sin(angles), np.sin(angles)], axis=-1), F32)
+    table = jnp.asarray(np.concatenate([np.cos(angles), np.sin(angles)], axis=-1), F32)
 
     if ep == 8 and lax.axis_size("rep") == 4:
         normed, pre, low, ctx, middle, mixed, cot_full, slots0, slots1, starts = attend_mix(
-            top, local, full, weights, output_weight, gains, small_in, cos, sin, tokens, cotangent, cot_full
+            top, local, full, weights, output_weight, gains, small_in, table, tokens, cotangent, cot_full
         )
     else:
         number = (me * local).astype(jnp.int32)[None]
         normed, pre, low, ctx, part, slots0, slots1, starts = attend(
-            top, number, full, weights, output_weight, gains, small_in, cos, sin
+            top, number, full, weights, output_weight, gains, small_in, table
         )
         starts = starts.astype(jnp.int32)
         middle, mixed = mix(part, tokens, small_in, gains)
 
-    act0, dgu0, x_all, dy_all, out_grad0 = expert_first(
-        starts, mixed, cot_full, (slots0, slots1), expert_in, expert_out, capacity
+    act, pair, x_all, dy_all, out_grad0 = expert_first(
+        starts, mixed, cot_full, (slots0, slots1), expert_in, hidden, capacity
     )
 
-    def over_rep(value):
-        return lax.psum_scatter(value, "rep", scatter_dimension=0, tiled=True)
-
-    out0 = over_rep(out_grad0)
-    in_grad0 = first_in_grad(seqs, starts, x_all, dgu0)
-    in0 = over_rep(in_grad0)
-    x_all, _ = lax.optimization_barrier((x_all, in_grad0))
-    act1, dgu1, out_grad1, in_grad1 = expert_second(seqs, starts, x_all, dy_all, expert_in, expert_out)
-    in1 = over_rep(in_grad1)
-    out1 = over_rep(out_grad1)
-    produced0, dx0 = expert_tail(0, seqs, starts, act0, dgu0, expert_in, expert_out)
-    produced1, dx1 = expert_tail(1, seqs, starts, act1, dgu1, expert_in, expert_out)
-    out_part, grad_part = combine(starts, (slots0, slots1), (produced0, produced1), (dx0, dx1), capacity)
+    def over_rep(value, axis):
+        return lax.psum_scatter(value, "rep", scatter_dimension=axis, tiled=True)
+
+    out0 = over_rep(out_grad0, 0)
+    dgu, in_grad = first_in_grad(seqs, starts, x_all, dy_all, pair, expert_out)
+    act, dgu, in_grad, out_grad1 = expert_second(
+        seqs, starts, x_all, dy_all, expert_in, expert_out, act, dgu, in_grad
+    )
+    in_both = over_rep(in_grad, 1)
+    out1 = over_rep(out_grad1, 0)
+    produced, dx = expert_tails(seqs, starts, act, dgu, expert_in, expert_out)
+    out_part, grad_part = combine(starts, (slots0, slots1), produced, dx, capacity)
 
     mgrad, ffn_back, agrad = back(grad_part, middle, cotangent, small_in, gains)
     npart, wgrad, wograd, qk_back = attend_back(
-        agrad, normed, pre, low, ctx, weights, output_weight, small_in, cos, sin
+        agrad, normed, pre, low, ctx, weights, output_weight, small_in, table
     )
 
     def widen(into, value, j):
         return lax.dynamic_update_slice(into, value.astype(F32)[None], (j, 0, 0))
 
-    in_all = widen(jnp.zeros((local,) + in0.shape, F32), in0, 0)
     out_all = widen(jnp.zeros((local,) + out0.shape, F32), out0, 0)
-    npart, in_all, out_all = lax.optimization_barrier((npart, in_all, out_all))
+    npart, out_all = lax.optimization_barrier((npart, out_all))
     sums, small, result, token_grad = finish(
         wgrad, wograd, npart, out_part, tokens, middle, mgrad, gains, ffn_back, qk_back
     )
@@ -1579,7 +1643,7 @@
         small[share : 2 * share].reshape(-1),
         head_share(small[2 * share]),
         head_share(small[2 * share + 1]),
-        widen(in_all, in1, 1),
+        in_both.astype(F32),
         widen(out_all, out1, 1),
     )
 

time: 817 us -> 806 us (0.987)
    pallas_call x1, Pallas kernels: 307 us -> 291 us  [finish(): pl.pallas_call(finish_kernel, out_shape=(sds(whole, BF16), sds((8, 128),...]
    pallas_call x4 -> x3, Pallas kernels: 95.9 us -> 111 us  [the longest x1 42.7 us: expert_tails(): pl.pallas_call(functools.partial(tail_kernel, seqs), out_shape=(sds((2, r...]
    dynamic_update_slice x4 -> x2, other arithmetic: 16.9 us -> 6.51 us  [widen(): return lax.dynamic_update_slice(into, value.astype(F32)[None], (j, 0, 0))]
    pallas_call x1, Pallas kernels: 45.3 us -> 53.8 us  [attend_back(): pl.pallas_call(attend_back_kernel, out_shape=(sds(agrad.shape, BF16), sds...]
  transfers between devices with their start and end apart: 4 -> 3, of which waited for: 0 -> 0; matrix products, arithmetic and copies ran while one was open for 3% -> 3% of each run, Pallas kernels for 68% -> 69%
where the time goes in v8:
time: 806 us
  Pallas kernels  759 us (94%)
  other arithmetic  22.4 us (3%)
  between operations  14.5 us (2%)
  local copies, waits for them, and re-layouts  8.64 us (1%)
    pallas_call x1, Pallas kernels, finish(): pl.pallas_call(finish_kernel, out_shape=(sds(whole, BF16), sds((8, 128),...  291 us
    pallas_call x1, Pallas kernels, attend_mix(): pl.pallas_call(functools.partial(attend_mix_kernel, top, local), out_shap...  98.5 us
    pallas_call x1, Pallas kernels, back(): pl.pallas_call(back_kernel, out_shape=(sds(cot.shape, F32), sds((1, width...  79.4 us
    pallas_call x1, Pallas kernels, front(): pl.pallas_call(front_kernel, out_shape=(sds((seqs, rows * ep, width + 128...  77.2 us
    pallas_call x1, Pallas kernels, attend_back(): pl.pallas_call(attend_back_kernel, out_shape=(sds(agrad.shape, BF16), sds...  53.8 us
    pallas_call x1, Pallas kernels, expert_tails(): pl.pallas_call(functools.partial(tail_kernel, seqs), out_shape=(sds((2, r...  42.7 us
    pallas_call x1, Pallas kernels, expert_second(): pl.pallas_call(functools.partial(second_kernel, seqs), out_shape=(sds(act...  41.4 us
    pallas_call x1, Pallas kernels, expert_first(): pl.pallas_call(functools.partial(first_kernel, capacity), out_shape=(sds(...  29.1 us
  transfers between devices with their start and end apart: 3, of which 0 were waited for; matrix products, arithmetic and copies ran while one was open for 3% of the time, Pallas kernels for 69%

profile of v8, /device:TPU:0, one launch (start us, length us, event | category | flops | bytes accessed | tf_op | source)
XLA Modules:
  0.0 805.6 jit_solution(726395384444548711)
XLA Ops:
  7.2 0.0 reduce-scatter.4.cloned.1.call-start
  7.9 0.7 bitcast_convert_fusion.4
  8.6 0.7 maximum_convert_fusion
  9.2 0.6 select_maximum_fusion.1.pk
  9.8 77.2 %front.1 = (bf16[8,256,2176]{2,1,0:T(8,128)(2,1)}, bf16[3,2048,256]{2,1,0:T(8,128)(2,1)}, bf16[8,256,2048]{2,1,0:T(8,128)(2,1)}, f32[8,2048]{1,0:T(8,128)}, f32[8,128]{1,0:T(8,128)}) custom-call(bf16[8,32,2048]{2,1,0:T(8,128)(2,1)} %tok.5, bf16[8,32,2048]{2,1,0:T(8,128)(2,1)} %cot.5, s32[8,8,32]{2,1,0:T(8,128)} %bitcast.47, bf16[8,8,32]{2,1,0:T(8,128)(2,1)} %bitcast.48, ...), custom_call_target="tpu_custom_call" | custom-call | tf_op jit(solution)/shard_map/front/pallas_call | solution.py:437
  87.0 98.5 %attend_mix.1 = (bf16[8,256,2048]{2,1,0:T(8,128)(2,1)}, f32[2,8,256,256]{3,2,1,0:T(8,128)}, bf16[3,8,256,256]{3,2,1,0:T(8,128)(2,1)}, bf16[8,256,256]{2,1,0:T(8,...) custom-call(bf16[8,256,2176]{2,1,0:T(8,128)(2,1)} %get-tuple-element, ...), custom_call_target="tpu_custom_call", output_to_operand_aliasing={{6}: (8, {})} | custom-call | tf_op jit(solution)/shard_map/attend_mix/pallas_call | solution.py:986
  185.5 29.1 %expert_first.1 = (bf16[2,1280,1024]{2,1,0:T(8,128)(2,1)}, bf16[1280,2048]{1,0:T(8,128)(2,1)}, bf16[2,1280,2048]{2,1,0:T(8,128)(2,1)}, bf16[2,1280,2048]{2,1,0:T(8,128)(2,1)}, bf16[1024,2048]{1,0:T(8,128)(2,1)}) custom-call(s32[8,128]{1,0:T(8,128)} %get-tuple-element.60.starts.refs_0_, bf16[8,256,2048]{2,1,0:T(8,128)(2,1)} %get-tuple-element.63.mixed, ...), custom_call_target="tpu_custom_call" | custom-call | flops 20000000000 | bytes 60000000 | tf_op jit(solution)/shard_map/expert_first/pallas_call | solution.py:1288
  214.6 0.0 reduce-scatter.4.cloned.1.call-update
  214.7 0.0 reduce-scatter.8.cloned.1.call-start
  214.7 26.9 %first_in_grad.1 = (bf16[2,1280,2048]{2,1,0:T(8,128)(2,1)}, bf16[2,2048,2048]{2,1,0:T(8,128)(2,1)}) custom-call(s32[8,128]{1,0:T(8,128)} %get-tuple-element.60.starts.refs_0_, bf16[2,1280,2048]{2,1,0:T(8,128)(2,1)} %get-tuple-element.65.x_all, bf16[2,1280,2048]{2,1,0:T(8,128)(2,1)} %get-tuple-element.66.dy_all, bf16[1280,2048]{1,0:T(8,128)(2,1)} %get-tuple-element.68.pair, ...), custom_call_target="tpu_custom_call" | custom-call | flops 10000000000 | bytes 20000000 | tf_op jit(solution)/shard_map/first_in_grad/pallas_call | solution.py:1367
  241.6 41.4 %expert_second.1 = (bf16[2,1280,1024]{2,1,0:T(8,128)(2,1)}, bf16[2,1280,2048]{2,1,0:T(8,128)(2,1)}, bf16[2,2048,2048]{2,1,0:T(8,128)(2,1)}, bf16[1024,2048]{1,0:T(8,128)(2,1)}) custom-call(s32[8,128]{1,0:T(8,128)} %get-tuple-element.60.starts.refs_0_, ...), custom_call_target="tpu_custom_call", output_to_operand_aliasing={{0}: (5, {}), {1}: (6, {}), {2}: (7, {})} | custom-call | flops 24999999488 | bytes 60000000 | tf_op jit(solution)/shard_map/expert_second/pallas_call | solution.py:1443
  283.0 0.0 reduce-scatter.8.cloned.1.call-update
  283.0 0.3 reduce-scatter.6.cloned.1.call-start
  283.3 0.5 reduce-scatter.6.cloned.1.call-update
  283.8 42.7 %expert_tails.1 = (bf16[2,1280,2048]{2,1,0:T(8,128)(2,1)}, bf16[2,1280,2048]{2,1,0:T(8,128)(2,1)}) custom-call(s32[8,128]{1,0:T(8,128)} %get-tuple-element.60.starts.refs_0_, bf16[2,1280,1024]{2,1,0:T(8,128)(2,1)} %get-tuple-element.71.act, bf16[2,1280,2048]{2,1,0:T(8,128)(2,1)} %get-tuple-element.72.dgu, bf16[2,2048,2048]{2,1,0:T(8,128)(2,1)} %w_in.5, ...), custom_call_target="tpu_custom_call" | custom-call | flops 24000000000 | bytes 60000000 | tf_op jit(solution)/shard_map/expert_tails/pallas_call | solution.py:1495
  326.4 19.5 %combine.1 = (bf16[8,256,2048]{2,1,0:T(8,128)(2,1)}, bf16[8,256,2048]{2,1,0:T(8,128)(2,1)}) custom-call(s32[8,128]{1,0:T(8,128)} %get-tuple-element.60.starts.refs_0_, f32[8,16,256]{2,1,0:T(8,128)} %get-tuple-element.61.slots0.refs_1_, f32[8,16,256]{2,1,0:T(8,128)} %get-tuple-element.62.slots1.refs_2_, bf16[2,1280,2048]{2,1,0:T(8,128)(2,1)} %get-tuple-element.73.refs_3_, ...), custom_call_target="tpu_custom_call" | custom-call | flops 3000000000 | bytes 40000000 | tf_op jit(solution)/shard_map/combine/pallas_call | solution.py:1543
  345.9 79.4 %back.1 = (f32[8,32,2048]{2,1,0:T(8,128)}, f32[1,2048]{1,0:T(1,128)}, bf16[8,256,2048]{2,1,0:T(8,128)(2,1)}) custom-call(bf16[8,8,32,2048]{3,2,1,0:T(8,128)(2,1)} %bitcast.43, f32[8,32,2048]{2,1,0:T(8,128)} %get-tuple-element.76.middle, bf16[8,32,2048]{2,1,0:T(8,128)(2,1)} %cot.5, f32[8,128]{1,0:T(8,128)} %get-tuple-element.58.small, ...), custom_call_target="tpu_custom_call" | custom-call | tf_op jit(solution)/shard_map/back/pallas_call | solution.py:505
  425.3 0.0 copy-start.2
  425.3 53.8 %attend_back.1 = (bf16[8,256,2048]{2,1,0:T(8,128)(2,1)}, bf16[3,2048,256]{2,1,0:T(8,128)(2,1)}, bf16[256,2048]{1,0:T(8,128)(2,1)}, f32[8,128]{1,0:T(8,128)}) custom-call(bf16[8,256,2048]{2,1,0:T(8,128)(2,1)} %get-tuple-element.77.agrad, bf16[8,256,2048]{2,1,0:T(8,128)(2,1)} %get-tuple-element.78.normed, f32[2,8,256,256]{3,2,1,0:T(8,128)} %get-tuple-element.79.pre, ...), custom_call_target="tpu_custom_call" | custom-call | flops 20000000000 | bytes 40000000 | tf_op jit(solution)/shard_map/attend_back/pallas_call | solution.py:1092
  479.1 0.7 slice.31
  479.8 0.0 copy-done.2
  479.8 0.6 select_maximum_fusion.others
  480.4 0.0 reduce-scatter.4.cloned.1.call-done
  480.4 3.7 pad_convert_fusion
  484.2 290.9 %finish.1 = (bf16[4,4,64,2048]{3,2,1,0:T(8,128)(2,1)}, f32[8,128]{1,0:T(8,128)}, bf16[8,32,2048]{2,1,0:T(8,128)(2,1)}, bf16[8,32,2048]{2,1,0:T(8,128)(2,1)}) custom-call(bf16[3,32,64,256]{3,2,1,0:T(8,128)(2,1)} %bitcast.44, bf16[4,64,2048]{2,1,0:T(8,128)(2,1)} %bitcast.46, bf16[8,8,32,2048]{3,2,1,0:T(8,128)(2,1)} %bitcast.42, ...), custom_call_target="tpu_custom_call" | custom-call | tf_op jit(solution)/shard_map/finish/pallas_call | solution.py:738
  775.0 0.8 fusion.3
  775.8 0.6 fusion
  776.4 0.6 fusion.1
  776.9 1.3 slice_bitcast_fusion
  778.3 2.7 fusion.2
  781.0 1.6 bitcast_convert_fusion
  782.7 1.6 bitcast_convert_fusion.1
  784.3 1.6 bitcast_convert_fusion.2
  785.9 1.6 bitcast_convert_fusion.3
  787.6 0.0 reduce-scatter.8.cloned.1.call-done
  787.6 2.8 convert_dynamic-update-slice_fusion
  790.4 0.0 copy-start.1
  790.4 0.0 copy-start
  790.4 0.0 reduce-scatter.6.cloned.1.call-done
  790.4 6.8 convert_element_type.57
  797.2 0.0 copy-done.1
  797.2 1.0 copy.40
  798.1 0.0 copy-done
  798.1 1.0 copy.41
  (1 shorter events, 0.0 us)
Async XLA Ops:
  7.2 473.3 %reduce-scatter.4.cloned.1.call-start = ((), (), s32[]{:S(2)}) async-start(), calls=%async_computation.3 | async-start | bytes 5242880 | tf_op jit(solution)/shard_map/reduce_scatter | solution.py:1606
  214.7 572.9 %reduce-scatter.8.cloned.1.call-start = ((), (), s32[]{:S(2)}) async-start(), calls=%async_computation.5 | async-start | bytes 5242880 | tf_op jit(solution)/shard_map/reduce_scatter | solution.py:1606
  283.0 507.3 %reduce-scatter.6.cloned.1.call-start = ((), (), s32[]{:S(2)}) async-start(), calls=%async_computation.4 | async-start | bytes 20971520 | tf_op jit(solution)/shard_map/reduce_scatter | solution.py:1606
  425.3 54.5 %copy-start.2 = (f32[1,2048]{1,0:T(1,128)S(1)}, f32[1,2048]{1,0:T(1,128)}, u32[]{:S(2)}) copy-start(f32[1,2048]{1,0:T(1,128)} %get-tuple-element.89) | copy-start | bytes 24580
  790.4 6.8 copy-start.1
  790.4 7.8 copy-start
Sparse Core Ops, SparseCore 0:
  214.8 79.4 reduce-scatter.3
  296.6 85.4 reduce-scatter.7
  384.5 372.0 reduce-scatter.5

commit v9 on v8

--- a/solution.py
+++ b/solution.py
@@ -1022,7 +1022,6 @@
 
 def attend_back_kernel(
     agrad, normed, pre, low, ctx, w, wo, small, table, part, wgrad, wograd, gains, wacc, woacc,
-    gbuf, total,
 ):
     s = pl.program_id(0)
     length = seq_len(small, s)
@@ -1054,27 +1053,13 @@
             r = inverse_rms(v)
             grads[i].append(rms_back(v, r, u * g).astype(BF16))
             gains[i : i + 1] += jnp.sum(u * v * r, axis=0, keepdims=True)
+    total = None
     for i in range(3):
-        for h, g in enumerate(grads[i]):
-            gbuf[i, :, h * HEAD_DIM : (h + 1) * HEAD_DIM] = g
-
-    def project(i, _):
-        g = gbuf[i]
+        g = grads[i][0] if len(grads[i]) == 1 else jnp.concatenate(grads[i], axis=1)
         wacc[i] += dot(normed[0], g, 0, 0)
         piece = dot(g, w[i], 1, 1)
-
-        @pl.when(i == 0)
-        def _():
-            total[...] = piece
-
-        @pl.when(i > 0)
-        def _():
-            total[...] += piece
-
-        return 0
-
-    lax.fori_loop(0, 3, project, 0)
-    part[0] = total[...].astype(BF16)
+        total = piece if total is None else total + piece
+    part[0] = total.astype(BF16)
 
     @pl.when(s == pl.num_programs(0) - 1)
     def _():
@@ -1120,8 +1105,6 @@
             scratch_shapes=[
                 pltpu.VMEM(weights.shape, F32),
                 pltpu.VMEM(wo.shape, F32),
-                pltpu.VMEM((3, length, cols), BF16),
-                pltpu.VMEM((length, width), F32),
             ],
         ),
         compiler_params=pltpu.CompilerParams(dimension_semantics=("arbitrary",), vmem_limit_bytes=60 << 20),
@@ -1151,9 +1134,18 @@
     lax.fori_loop(0, blocks * parts, run, 0)
 
 
-def swiglu_back(gate, up, dact):
-    sig = 1.0 / (1.0 + jnp.exp(-gate))
-    return dact * up * sig * (1.0 + gate * (1.0 - sig)), dact * (gate * sig)
+def forward_blocks(blocks, x, dy, wi, wo, acts, dgus):
+    def job(rows, gcols, ucols):
+        gate = dot(x[rows], wi[:, gcols], 1, 0)
+        up = dot(x[rows], wi[:, ucols], 1, 0)
+        dact = dot(dy[rows], wo[gcols], 1, 1)
+        sig = 1.0 / (1.0 + jnp.exp(-gate))
+        silu = gate * sig
+        acts[rows, gcols] = (silu * up).astype(BF16)
+        dgus[rows, gcols] = (dact * up * sig * (1.0 + gate * (1.0 - sig))).astype(BF16)
+        dgus[rows, ucols] = (dact * silu).astype(BF16)
+
+    each_block(blocks, wo.shape[0], job)
 
 
 def gradient_tiles(blocks, left, right, result, acc, stage, ssem, busy):
@@ -1205,21 +1197,21 @@
 
 
 def first_kernel(
-    capacity, starts, mixed, cot, slots0, slots1, w_in,
-    act, pair, x_all, dy_all, out_grad,
-    x, dy, wi, acts, pairs, acc, stage, wsem, ssem, rsem,
+    capacity, starts, mixed, cot, slots0, slots1, w_in, w_out,
+    act, dgu, x_all, dy_all, out_grad,
+    x, dy, wi, wo, acts, dgus, acc, stage, wsem, ssem, rsem,
 ):
     step = pl.program_id(0)
     steps = pl.num_programs(0)
     together = mixed.shape[0]
     seqs = steps * together
     width = mixed.shape[2]
-    hidden = acts.shape[1]
-    load = pltpu.make_async_copy(w_in.at[0], wi, wsem)
+    loads = [pltpu.make_async_copy(w_in.at[0], wi, wsem.at[0]), pltpu.make_async_copy(w_out.at[0], wo, wsem.at[1])]
 
     @pl.when(step == 0)
     def _():
-        load.start()
+        for copy in loads:
+            copy.start()
 
     packed = []
     for k in range(together):
@@ -1255,21 +1247,14 @@
                 return 0
 
             lax.fori_loop(past, end, clear, 0)
-        saves = [pltpu.make_async_copy(x, x_all, rsem.at[0]), pltpu.make_async_copy(dy, dy_all, rsem.at[1])]
+        saves = [pltpu.make_async_copy(x, x_all, rsem.at[0]), pltpu.make_async_copy(dy.at[1], dy_all, rsem.at[1])]
         for copy in saves:
             copy.start()
         blocks = (starts[0, seqs] + BLOCK - 1) // BLOCK
-        load.wait()
-
-        def forward(rows, gcols, ucols):
-            gate = dot(x[0, rows], wi[:, gcols], 1, 0)
-            up = dot(x[0, rows], wi[:, ucols], 1, 0)
-            acts[rows, gcols] = (gate * (1.0 / (1.0 + jnp.exp(-gate))) * up).astype(BF16)
-            pairs[rows, gcols] = gate.astype(BF16)
-            pairs[rows, ucols] = up.astype(BF16)
-
-        each_block(blocks, hidden, forward)
-        saves += [pltpu.make_async_copy(acts, act.at[0], rsem.at[2]), pltpu.make_async_copy(pairs, pair, rsem.at[3])]
+        for copy in loads:
+            copy.wait()
+        forward_blocks(blocks, x.at[0], dy.at[0], wi, wo, acts, dgus)
+        saves += [pltpu.make_async_copy(acts, act.at[0], rsem.at[2]), pltpu.make_async_copy(dgus, dgu.at[0], rsem.at[3])]
         for copy in saves[2:]:
             copy.start()
         gradient_tiles(blocks, acts, dy.at[0], out_grad, acc, stage, ssem, False)
@@ -1278,8 +1263,9 @@
             copy.wait()
 
 
-def expert_first(starts, mixed, cot, slots, w_in, hidden, capacity):
+def expert_first(starts, mixed, cot, slots, w_in, w_out, capacity):
     seqs, length, width = mixed.shape
+    hidden = w_out.shape[1]
     rows = pack_rows(seqs, capacity)
     dma = pltpu.SemaphoreType.DMA
     seq = lambda i, *_: (i, 0, 0)
@@ -1289,9 +1275,9 @@
         functools.partial(first_kernel, capacity),
         out_shape=(
             sds((2, rows, hidden), BF16),
-            sds((rows, 2 * hidden), BF16),
+            sds((2, rows, 2 * hidden), BF16),
             sds((2, rows, width), BF16),
-            sds((2, rows, width), BF16),
+            sds((rows, width), BF16),
             sds((hidden, width), BF16),
         ),
         grid_spec=pltpu.PrefetchScalarGridSpec(
@@ -1303,108 +1289,88 @@
                 slot_spec,
                 slot_spec,
                 AN,
+                AN,
             ],
             out_specs=(AN, AN, AN, AN, AN),
             scratch_shapes=[
                 pltpu.VMEM((2, rows, width), BF16),
                 pltpu.VMEM((2, rows, width), BF16),
                 pltpu.VMEM(w_in.shape[1:], BF16),
+                pltpu.VMEM(w_out.shape[1:], BF16),
                 pltpu.VMEM((rows, hidden), BF16),
                 pltpu.VMEM((rows, 2 * hidden), BF16),
-                pltpu.VMEM((512, 1024), F32),
-                pltpu.VMEM((2, 512, 1024), BF16),
-                dma,
+                pltpu.VMEM((256, 1024), F32),
+                pltpu.VMEM((2, 256, 1024), BF16),
+                dma((2,)),
                 dma((2,)),
                 dma((4,)),
             ],
         ),
-        compiler_params=pltpu.CompilerParams(dimension_semantics=("arbitrary",), vmem_limit_bytes=62 << 20),
+        compiler_params=pltpu.CompilerParams(dimension_semantics=("arbitrary",), vmem_limit_bytes=63 << 20),
         cost_estimate=pl.CostEstimate(flops=2 * 10**10, bytes_accessed=6 * 10**7, transcendentals=10**6),
         name="expert_first",
-    )(starts, mixed, cot, *slots, w_in)
-
-
-def in_grad_kernel(
-    seqs, starts, x_all, dy_all, pair, w_out, dgu, in_grad, x, dy, wo, pairs, dgus, acc, stage, lsem, wsem, ssem, rsem
-):
+    )(starts, mixed, cot, *slots, w_in, w_out)
+
+
+def in_grad_kernel(seqs, starts, x_all, dgu, in_grad, x, dgus, acc, stage, lsem, ssem):
     blocks = (starts[0, seqs] + BLOCK - 1) // BLOCK
-    hidden = wo.shape[0]
-    weights = pltpu.make_async_copy(w_out.at[0], wo, wsem)
-    weights.start()
+
+    def load(b):
+        rows = pl.ds(pl.multiple_of(b * BLOCK, BLOCK), BLOCK)
+        return (
+            pltpu.make_async_copy(x_all.at[0, rows], x.at[rows], lsem.at[0, b]),
+            pltpu.make_async_copy(dgu.at[0, rows], dgus.at[rows], lsem.at[1, b]),
+        )
 
     def run(b, action):
-        rows = pl.ds(pl.multiple_of(b * BLOCK, BLOCK), BLOCK)
-        for copy in (
-            pltpu.make_async_copy(dy_all.at[0, rows], dy.at[rows], lsem.at[0, b]),
-            pltpu.make_async_copy(pair.at[rows], pairs.at[rows], lsem.at[1, b]),
-            pltpu.make_async_copy(x_all.at[0, rows], x.at[rows], lsem.at[2, b]),
-        ):
+        for copy in load(b):
             getattr(copy, action)()
         return 0
 
     lax.fori_loop(0, blocks, lambda b, _: run(b, "start"), 0)
-    weights.wait()
     lax.fori_loop(0, blocks, lambda b, _: run(b, "wait"), 0)
-
-    def backward(rows, gcols, ucols):
-        dact = dot(dy[rows], wo[gcols], 1, 1)
-        dgate, dup = swiglu_back(pairs[rows, gcols].astype(F32), pairs[rows, ucols].astype(F32), dact)
-        dgus[rows, gcols] = dgate.astype(BF16)
-        dgus[rows, ucols] = dup.astype(BF16)
-
-    each_block(blocks, hidden, backward)
-    save = pltpu.make_async_copy(dgus, dgu.at[0], rsem)
-    save.start()
-    gradient_tiles(blocks, x, dgus, in_grad.at[0], acc, stage, ssem, False)
-    drain_tiles(in_grad.at[0], acc, stage, ssem)
-    save.wait()
-
-
-def first_in_grad(seqs, starts, x_all, dy_all, pair, w_out):
+    gradient_tiles(blocks, x, dgus, in_grad, acc, stage, ssem, False)
+    drain_tiles(in_grad, acc, stage, ssem)
+
+
+def first_in_grad(seqs, starts, x_all, dgu):
     rows, width = x_all.shape[1:]
-    hidden = w_out.shape[1]
     dma = pltpu.SemaphoreType.DMA
     return pl.pallas_call(
         functools.partial(in_grad_kernel, seqs),
-        out_shape=(sds((2, rows, 2 * hidden), BF16), sds((2, width, 2 * hidden), BF16)),
+        out_shape=sds((width, dgu.shape[2]), BF16),
         grid_spec=pltpu.PrefetchScalarGridSpec(
             num_scalar_prefetch=1,
             grid=(1,),
-            in_specs=[AN] * 4,
-            out_specs=(AN, AN),
+            in_specs=[AN, AN],
+            out_specs=AN,
             scratch_shapes=[
                 pltpu.VMEM((rows, width), BF16),
-                pltpu.VMEM((rows, width), BF16),
-                pltpu.VMEM(w_out.shape[1:], BF16),
-                pltpu.VMEM((rows, 2 * hidden), BF16),
-                pltpu.VMEM((rows, 2 * hidden), BF16),
+                pltpu.VMEM(dgu.shape[1:], BF16),
                 pltpu.VMEM((512, 2048), F32),
                 pltpu.VMEM((2, 512, 2048), BF16),
-                dma((3, rows // BLOCK)),
-                dma,
+                dma((2, rows // BLOCK)),
                 dma((2,)),
-                dma,
             ],
         ),
         compiler_params=pltpu.CompilerParams(dimension_semantics=("arbitrary",), vmem_limit_bytes=60 << 20),
         cost_estimate=pl.CostEstimate(flops=10**10, bytes_accessed=2 * 10**7, transcendentals=0),
         name="first_in_grad",
-    )(starts, x_all, dy_all, pair, w_out)
+    )(starts, x_all, dgu)
 
 
 def second_kernel(
-    seqs, starts, x_all, dy_all, w_in, w_out, _act, _dgu, _in_grad, act, dgu, in_grad, out_grad,
+    seqs, starts, x_all, dy_all, w_in, w_out, _act, _dgu, act, dgu, in_grad, out_grad,
     x, dy, wi, wo, acts, dgus, acc, stage, wsem, lsem, ssem, rsem,
 ):
     blocks = (starts[1, seqs] + BLOCK - 1) // BLOCK
-    hidden = wo.shape[0]
     loads = [pltpu.make_async_copy(w_in.at[1], wi, wsem.at[0]), pltpu.make_async_copy(w_out.at[1], wo, wsem.at[1])]
 
     def load(b, action):
         rows = pl.ds(pl.multiple_of(b * BLOCK, BLOCK), BLOCK)
         for copy in (
             pltpu.make_async_copy(x_all.at[1, rows], x.at[rows], lsem.at[0, b]),
-            pltpu.make_async_copy(dy_all.at[1, rows], dy.at[rows], lsem.at[1, b]),
+            pltpu.make_async_copy(dy_all.at[rows], dy.at[rows], lsem.at[1, b]),
         ):
             getattr(copy, action)()
         return 0
@@ -1416,38 +1382,31 @@
         copy.wait()
     lax.fori_loop(0, blocks, lambda b, _: load(b, "wait"), 0)
 
-    def both(rows, gcols, ucols):
-        gate = dot(x[rows], wi[:, gcols], 1, 0)
-        up = dot(x[rows], wi[:, ucols], 1, 0)
-        dact = dot(dy[rows], wo[gcols], 1, 1)
-        acts[rows, gcols] = (gate * (1.0 / (1.0 + jnp.exp(-gate))) * up).astype(BF16)
-        dgate, dup = swiglu_back(gate, up, dact)
-        dgus[rows, gcols] = dgate.astype(BF16)
-        dgus[rows, ucols] = dup.astype(BF16)
-
-    each_block(blocks, hidden, both)
+    forward_blocks(blocks, x, dy, wi, wo, acts, dgus)
     saves = [pltpu.make_async_copy(acts, act.at[1], rsem.at[0]), pltpu.make_async_copy(dgus, dgu.at[1], rsem.at[1])]
     for copy in saves:
         copy.start()
-    gradient_tiles(blocks, x, dgus, in_grad.at[1], acc, stage, ssem, False)
+    gradient_tiles(blocks, x, dgus, in_grad, acc, stage, ssem, False)
     gradient_tiles(blocks, acts, dy, out_grad, acc, stage, ssem, True)
     drain_tiles(out_grad, acc, stage, ssem)
     for copy in saves:
         copy.wait()
 
 
-def expert_second(seqs, starts, x_all, dy_all, w_in, w_out, act, dgu, in_grad):
-    rows, width = dy_all.shape[1:]
+def expert_second(seqs, starts, x_all, dy_all, w_in, w_out, act, dgu):
+    rows, width = dy_all.shape
     hidden = w_out.shape[1]
     dma = pltpu.SemaphoreType.DMA
     return pl.pallas_call(
         functools.partial(second_kernel, seqs),
-        out_shape=(sds(act.shape, BF16), sds(dgu.shape, BF16), sds(in_grad.shape, BF16), sds((hidden, width), BF16)),
-        input_output_aliases={5: 0, 6: 1, 7: 2},
+        out_shape=(
+            sds(act.shape, BF16), sds(dgu.shape, BF16), sds((width, 2 * hidden), BF16), sds((hidden, width), BF16)
+        ),
+        input_output_aliases={5: 0, 6: 1},
         grid_spec=pltpu.PrefetchScalarGridSpec(
             num_scalar_prefetch=1,
             grid=(1,),
-            in_specs=[AN] * 7,
+            in_specs=[AN] * 6,
             out_specs=(AN, AN, AN, AN),
             scratch_shapes=[
                 pltpu.VMEM((rows, width), BF16),
@@ -1467,13 +1426,13 @@
         compiler_params=pltpu.CompilerParams(dimension_semantics=("arbitrary",), vmem_limit_bytes=60 << 20),
         cost_estimate=pl.CostEstimate(flops=25 * 10**9, bytes_accessed=6 * 10**7, transcendentals=10**6),
         name="expert_second",
-    )(starts, x_all, dy_all, w_in, w_out, act, dgu, in_grad)
+    )(starts, x_all, dy_all, w_in, w_out, act, dgu)
 
 
 def tail_kernel(seqs, starts, act, dgu, w_in, w_out, produced, dx):
     @pl.when(pl.program_id(1) * BLOCK < starts[pl.program_id(0), seqs])
     def _():
-        part = min(produced.shape[1], 256)
+        part = min(produced.shape[1], 512)
 
         def run(i, _):
             cols = pl.ds(pl.multiple_of(i * part, part), part)
@@ -1565,7 +1524,6 @@
     length = rows * ep
     top = gate_weights.shape[2]
     local = expert_in.shape[0]
-    hidden = expert_out.shape[1]
     experts = local * ep
     capacity = -(-(length * top * 9 // (8 * experts)) // 16) * 16
 
@@ -1598,20 +1556,20 @@
         starts = starts.astype(jnp.int32)
         middle, mixed = mix(part, tokens, small_in, gains)
 
-    act, pair, x_all, dy_all, out_grad0 = expert_first(
-        starts, mixed, cot_full, (slots0, slots1), expert_in, hidden, capacity
+    act, dgu, x_all, dy_all, out_grad0 = expert_first(
+        starts, mixed, cot_full, (slots0, slots1), expert_in, expert_out, capacity
     )
 
-    def over_rep(value, axis):
-        return lax.psum_scatter(value, "rep", scatter_dimension=axis, tiled=True)
-
-    out0 = over_rep(out_grad0, 0)
-    dgu, in_grad = first_in_grad(seqs, starts, x_all, dy_all, pair, expert_out)
-    act, dgu, in_grad, out_grad1 = expert_second(
-        seqs, starts, x_all, dy_all, expert_in, expert_out, act, dgu, in_grad
-    )
-    in_both = over_rep(in_grad, 1)
-    out1 = over_rep(out_grad1, 0)
+    def over_rep(value):
+        return lax.psum_scatter(value, "rep", scatter_dimension=0, tiled=True)
+
+    out0 = over_rep(out_grad0)
+    in_grad0 = first_in_grad(seqs, starts, x_all, dgu)
+    in0 = over_rep(in_grad0)
+    x_all, _ = lax.optimization_barrier((x_all, in_grad0))
+    act, dgu, in_grad1, out_grad1 = expert_second(seqs, starts, x_all, dy_all, expert_in, expert_out, act, dgu)
+    in1 = over_rep(in_grad1)
+    out1 = over_rep(out_grad1)
     produced, dx = expert_tails(seqs, starts, act, dgu, expert_in, expert_out)
     out_part, grad_part = combine(starts, (slots0, slots1), produced, dx, capacity)
 
@@ -1619,12 +1577,6 @@
     npart, wgrad, wograd, qk_back = attend_back(
         agrad, normed, pre, low, ctx, weights, output_weight, small_in, table
     )
-
-    def widen(into, value, j):
-        return lax.dynamic_update_slice(into, value.astype(F32)[None], (j, 0, 0))
-
-    out_all = widen(jnp.zeros((local,) + out0.shape, F32), out0, 0)
-    npart, out_all = lax.optimization_barrier((npart, out_all))
     sums, small, result, token_grad = finish(
         wgrad, wograd, npart, out_part, tokens, middle, mgrad, gains, ffn_back, qk_back
     )
@@ -1643,8 +1595,8 @@
         small[share : 2 * share].reshape(-1),
         head_share(small[2 * share]),
         head_share(small[2 * share + 1]),
-        in_both.astype(F32),
-        widen(out_all, out1, 1),
+        jnp.stack([in0, in1]).astype(F32),
+        jnp.stack([out0, out1]).astype(F32),
     )
 
 

time: 806 us -> 813 us (level)
  Pallas kernels: 759 us -> 769 us
    pallas_call x1, Pallas kernels: 291 us -> 314 us  [finish(): pl.pallas_call(finish_kernel, out_shape=(sds(whole, BF16), sds((8, 128),...]
    pallas_call x1, Pallas kernels: 53.8 us -> 45.5 us  [attend_back(): pl.pallas_call(attend_back_kernel, out_shape=(sds(agrad.shape, BF16), sds...]
  transfers between devices with their start and end apart: 3 -> 4, of which waited for: 0 -> 0; matrix products, arithmetic and copies ran while one was open for 3% -> 2% of each run, Pallas kernels for 69% -> 69%
where the time goes in v9:
time: 813 us
  Pallas kernels  769 us (95%)
  other arithmetic  19.3 us (2%)
  between operations  14.5 us (2%)
  local copies, waits for them, and re-layouts  8.64 us (1%)
    pallas_call x1, Pallas kernels, finish(): pl.pallas_call(finish_kernel, out_shape=(sds(whole, BF16), sds((8, 128),...  314 us
    pallas_call x1, Pallas kernels, attend_mix(): pl.pallas_call(functools.partial(attend_mix_kernel, top, local), out_shap...  98.4 us
    pallas_call x1, Pallas kernels, back(): pl.pallas_call(back_kernel, out_shape=(sds(cot.shape, F32), sds((1, width...  79.7 us
    pallas_call x1, Pallas kernels, front(): pl.pallas_call(front_kernel, out_shape=(sds((seqs, rows * ep, width + 128...  77.1 us
    pallas_call x1, Pallas kernels, attend_back(): pl.pallas_call(attend_back_kernel, out_shape=(sds(agrad.shape, BF16), sds...  45.5 us
    pallas_call x1, Pallas kernels, expert_second(): pl.pallas_call(functools.partial(second_kernel, seqs), out_shape=(sds(act...  41.3 us
    pallas_call x1, Pallas kernels, expert_tails(): pl.pallas_call(functools.partial(tail_kernel, seqs), out_shape=(sds((2, r...  38 us
    pallas_call x1, Pallas kernels, expert_first(): pl.pallas_call(functools.partial(first_kernel, capacity), out_shape=(sds(...  36.2 us
  transfers between devices with their start and end apart: 4, of which 0 were waited for; matrix products, arithmetic and copies ran while one was open for 2% of the time, Pallas kernels for 69%

profile of v9, /device:TPU:0, one launch (start us, length us, event | category | flops | bytes accessed | tf_op | source)
XLA Modules:
  0.0 812.8 jit_solution(14237295045340555954)
XLA Ops:
  7.2 0.0 reduce-scatter.9.cloned.1.call-start
  7.9 0.7 bitcast_convert_fusion.4
  8.6 0.7 maximum_convert_fusion.2
  9.2 0.6 select_maximum_fusion.1.pk
  9.8 77.1 %front.1 = (bf16[8,256,2176]{2,1,0:T(8,128)(2,1)}, bf16[3,2048,256]{2,1,0:T(8,128)(2,1)}, bf16[8,256,2048]{2,1,0:T(8,128)(2,1)}, f32[8,2048]{1,0:T(8,128)}, f32[8,128]{1,0:T(8,128)}) custom-call(bf16[8,32,2048]{2,1,0:T(8,128)(2,1)} %tok.5, bf16[8,32,2048]{2,1,0:T(8,128)(2,1)} %cot.5, s32[8,8,32]{2,1,0:T(8,128)} %bitcast.50, bf16[8,8,32]{2,1,0:T(8,128)(2,1)} %bitcast.51, ...), custom_call_target="tpu_custom_call" | custom-call | tf_op jit(solution)/shard_map/front/pallas_call | solution.py:437
  87.0 98.4 %attend_mix.1 = (bf16[8,256,2048]{2,1,0:T(8,128)(2,1)}, f32[2,8,256,256]{3,2,1,0:T(8,128)}, bf16[3,8,256,256]{3,2,1,0:T(8,128)(2,1)}, bf16[8,256,256]{2,1,0:T(8,...) custom-call(bf16[8,256,2176]{2,1,0:T(8,128)(2,1)} %get-tuple-element, ...), custom_call_target="tpu_custom_call", output_to_operand_aliasing={{6}: (8, {})} | custom-call | tf_op jit(solution)/shard_map/attend_mix/pallas_call | solution.py:986
  185.4 36.2 %expert_first.1 = (bf16[2,1280,1024]{2,1,0:T(8,128)(2,1)}, bf16[2,1280,2048]{2,1,0:T(8,128)(2,1)}, bf16[2,1280,2048]{2,1,0:T(8,128)(2,1)}, bf16[1280,2048]{1,0:T(8,128)(2,1)}, bf16[1024,2048]{1,0:T(8,128)(2,1)}) custom-call(s32[8,128]{1,0:T(8,128)} %get-tuple-element.57.starts.refs_0_, bf16[8,256,2048]{2,1,0:T(8,128)(2,1)} %get-tuple-element.60.mixed, ...), custom_call_target="tpu_custom_call" | custom-call | flops 20000000000 | bytes 60000000 | tf_op jit(solution)/shard_map/expert_first/pallas_call | solution.py:1274
  221.6 0.0 reduce-scatter.9.cloned.1.call-update
  221.6 0.0 reduce-scatter.11.cloned.1.call-start
  221.7 19.1 %first_in_grad.1 = bf16[2048,2048]{1,0:T(8,128)(2,1)} custom-call(s32[8,128]{1,0:T(8,128)} %get-tuple-element.57.starts.refs_0_, bf16[2,1280,2048]{2,1,0:T(8,128)(2,1)} %get-tuple-element.64.x_all, bf16[2,1280,2048]{2,1,0:T(8,128)(2,1)} %get-tuple-element.63.dgu._dgu), custom_call_target="tpu_custom_call" | custom-call | flops 10000000000 | bytes 20000000 | tf_op jit(solution)/shard_map/first_in_grad/pallas_call | solution.py:1339
  240.8 41.3 %expert_second.1 = (bf16[2,1280,1024]{2,1,0:T(8,128)(2,1)}, bf16[2,1280,2048]{2,1,0:T(8,128)(2,1)}, bf16[2048,2048]{1,0:T(8,128)(2,1)}, bf16[1024,2048]{1,0:T(8,128)(2,1)}) custom-call(s32[8,128]{1,0:T(8,128)} %get-tuple-element.57.starts.refs_0_, bf16[2,1280,2048]{2,1,0:T(8,128)(2,1)} %get-tuple-element.64.x_all, ...), custom_call_target="tpu_custom_call", output_to_operand_aliasing={{0}: (5, {}), {1}: (6, {})} | custom-call | flops 24999999488 | bytes 60000000 | tf_op jit(solution)/shard_map/expert_second/pallas_call | solution.py:1400
  282.1 0.0 reduce-scatter.11.cloned.1.call-update
  282.1 0.0 reduce-scatter.7.cloned.1.call-start
  282.2 0.7 reduce-scatter.7.cloned.1.call-update
  282.8 0.0 reduce-scatter.5.cloned.1.call-start
  282.9 0.5 reduce-scatter.5.cloned.1.call-update
  283.4 38.0 %expert_tails.1 = (bf16[2,1280,2048]{2,1,0:T(8,128)(2,1)}, bf16[2,1280,2048]{2,1,0:T(8,128)(2,1)}) custom-call(s32[8,128]{1,0:T(8,128)} %get-tuple-element.57.starts.refs_0_, bf16[2,1280,1024]{2,1,0:T(8,128)(2,1)} %get-tuple-element.67.act, bf16[2,1280,2048]{2,1,0:T(8,128)(2,1)} %get-tuple-element.68.dgu, bf16[2,2048,2048]{2,1,0:T(8,128)(2,1)} %w_in.5, ...), custom_call_target="tpu_custom_call" | custom-call | flops 24000000000 | bytes 60000000 | tf_op jit(solution)/shard_map/expert_tails/pallas_call | solution.py:1454
  321.4 19.5 %combine.1 = (bf16[8,256,2048]{2,1,0:T(8,128)(2,1)}, bf16[8,256,2048]{2,1,0:T(8,128)(2,1)}) custom-call(s32[8,128]{1,0:T(8,128)} %get-tuple-element.57.starts.refs_0_, f32[8,16,256]{2,1,0:T(8,128)} %get-tuple-element.58.slots0.refs_1_, f32[8,16,256]{2,1,0:T(8,128)} %get-tuple-element.59.slots1.refs_2_, bf16[2,1280,2048]{2,1,0:T(8,128)(2,1)} %get-tuple-element.69.refs_3_, ...), custom_call_target="tpu_custom_call" | custom-call | flops 3000000000 | bytes 40000000 | tf_op jit(solution)/shard_map/combine/pallas_call | solution.py:1502
  340.9 79.7 %back.1 = (f32[8,32,2048]{2,1,0:T(8,128)}, f32[1,2048]{1,0:T(1,128)}, bf16[8,256,2048]{2,1,0:T(8,128)(2,1)}) custom-call(bf16[8,8,32,2048]{3,2,1,0:T(8,128)(2,1)} %bitcast.43, f32[8,32,2048]{2,1,0:T(8,128)} %get-tuple-element.72.middle, bf16[8,32,2048]{2,1,0:T(8,128)(2,1)} %cot.5, f32[8,128]{1,0:T(8,128)} %get-tuple-element.55.small, ...), custom_call_target="tpu_custom_call" | custom-call | tf_op jit(solution)/shard_map/back/pallas_call | solution.py:505
  420.6 0.0 copy-start.2
  420.6 45.5 %attend_back.1 = (bf16[8,256,2048]{2,1,0:T(8,128)(2,1)}, bf16[3,2048,256]{2,1,0:T(8,128)(2,1)}, bf16[256,2048]{1,0:T(8,128)(2,1)}, f32[8,128]{1,0:T(8,128)}) custom-call(bf16[8,256,2048]{2,1,0:T(8,128)(2,1)} %get-tuple-element.73.agrad, bf16[8,256,2048]{2,1,0:T(8,128)(2,1)} %get-tuple-element.74.normed, f32[2,8,256,256]{3,2,1,0:T(8,128)} %get-tuple-element.75.pre, ...), custom_call_target="tpu_custom_call" | custom-call | flops 20000000000 | bytes 40000000 | tf_op jit(solution)/shard_map/attend_back/pallas_call | solution.py:1077
  466.1 0.7 slice.31
  466.8 0.0 copy-done.2
  466.8 0.6 select_maximum_fusion.others
  467.4 314.2 %finish.1 = (bf16[4,4,64,2048]{3,2,1,0:T(8,128)(2,1)}, f32[8,128]{1,0:T(8,128)}, bf16[8,32,2048]{2,1,0:T(8,128)(2,1)}, bf16[8,32,2048]{2,1,0:T(8,128)(2,1)}) custom-call(bf16[3,32,64,256]{3,2,1,0:T(8,128)(2,1)} %bitcast.44, bf16[4,64,2048]{2,1,0:T(8,128)(2,1)} %bitcast.47, bf16[8,8,32,2048]{3,2,1,0:T(8,128)(2,1)} %bitcast.42, ...), custom_call_target="tpu_custom_call" | custom-call | tf_op jit(solution)/shard_map/finish/pallas_call | solution.py:738
  781.6 0.8 fusion.1
  782.4 0.6 dynamic-slice_bitcast_fusion
  783.0 0.6 dynamic-slice_bitcast_fusion.1
  783.5 1.3 slice_bitcast_fusion
  784.9 2.7 fusion
  787.6 1.6 bitcast_convert_fusion
  789.3 1.6 bitcast_convert_fusion.1
  790.9 1.6 bitcast_convert_fusion.2
  792.5 1.6 bitcast_convert_fusion.3
  794.2 0.0 reduce-scatter.9.cloned.1.call-done
  794.2 0.0 reduce-scatter.11.cloned.1.call-done
  794.2 3.8 maximum_convert_fusion.1
  798.0 0.0 reduce-scatter.7.cloned.1.call-done
  798.0 0.0 reduce-scatter.5.cloned.1.call-done
  798.0 0.0 copy-start.1
  798.0 0.0 copy-start
  798.0 6.3 maximum_convert_fusion
  804.3 0.0 copy-done.1
  804.3 1.0 copy.37
  805.3 0.0 copy-done
  805.3 1.0 copy.38
  (1 shorter events, 0.0 us)
Async XLA Ops:
  7.2 787.0 %reduce-scatter.9.cloned.1.call-start = ((), (), s32[]{:S(2)}) async-start(), calls=%async_computation.6 | async-start | bytes 5242880 | tf_op jit(solution)/shard_map/reduce_scatter | solution.py:1564
  221.6 572.5 %reduce-scatter.11.cloned.1.call-start = ((), (), s32[]{:S(2)}) async-start(), calls=%async_computation.7 | async-start | bytes 5242880 | tf_op jit(solution)/shard_map/reduce_scatter | solution.py:1564
  282.1 515.9 %reduce-scatter.7.cloned.1.call-start = ((), (), s32[]{:S(2)}) async-start(), calls=%async_computation.5 | async-start | bytes 10485760 | tf_op jit(solution)/shard_map/reduce_scatter | solution.py:1564
  282.8 515.1 %reduce-scatter.5.cloned.1.call-start = ((), (), s32[]{:S(2)}) async-start(), calls=%async_computation.4 | async-start | bytes 10485760 | tf_op jit(solution)/shard_map/reduce_scatter | solution.py:1564
  420.6 46.2 %copy-start.2 = (f32[1,2048]{1,0:T(1,128)S(1)}, f32[1,2048]{1,0:T(1,128)}, u32[]{:S(2)}) copy-start(f32[1,2048]{1,0:T(1,128)} %get-tuple-element.83) | copy-start | bytes 24580
  798.0 6.3 copy-start.1
  798.0 7.3 copy-start
Sparse Core Ops, SparseCore 0:
  221.8 81.5 reduce-scatter.8
  305.6 77.2 reduce-scatter.10
  385.9 166.3 reduce-scatter.6
  554.5 221.6 reduce-scatter.4

commit v10 on v8

--- a/solution.py
+++ b/solution.py
@@ -78,9 +78,9 @@
             src_ref=src, dst_ref=dst, send_sem=send, recv_sem=recv, device_id=(self.rep, dev), device_id_type=MESH
         )
 
-    def peers(self):
-        sb, dx, dy = self.sb, self.dx, self.dy
-        return (self.xn, self.yn, self.dg, sb, sb + dx, sb + dy, sb + dx + dy)
+    def peer(self, m):
+        k = m + 1
+        return self.me + (k % 2) * (self.sb - self.me) + (k // 2 % 2) * self.dx + (k // 4) * self.dy
 
     def greet(self, peers):
         barrier = pltpu.get_barrier_semaphore()
@@ -270,40 +270,42 @@
     top = ids.shape[1]
     block, cols = wq.shape[0], weights.shape[2]
     quarter = block // 4
-    peers = at.peers()
     barrier = pltpu.get_barrier_semaphore()
     line = [lax.rem(z + k, 4) for k in range(1, 4)]
     for dev in line:
         pl.semaphore_signal(barrier, inc=1, device_id=(dev, at.me), device_id_type=MESH)
-    for dev in peers:
-        pl.semaphore_signal(barrier, inc=1, device_id=(z, dev), device_id_type=MESH)
+    each(7, lambda m: pl.semaphore_signal(barrier, inc=1, device_id=(z, at.peer(m)), device_id_type=MESH))
     pl.semaphore_wait(barrier, 10)
 
-    def packet_copy(m, dev):
-        return at.push(pk, packets.at[at.me], psend.at[m], precv.at[m], dev)
-
-    def weight_copy(m, j, dev):
+    def packet_copy(m):
+        return at.push(pk, packets.at[at.me], psend.at[m], precv.at[m], at.peer(m))
+
+    def weight_copy(m, j):
+        dev = at.peer(m)
         theirs = pl.ds(pl.multiple_of(dev * cols, cols), cols)
         src = (wq, wk, wv)[j].at[pl.ds(pl.multiple_of(z * quarter, quarter), quarter), theirs]
         dst = weights.at[j, pl.ds(pl.multiple_of(at.me * block + z * quarter, quarter), quarter)]
         return at.push(src, dst, wsend.at[m, j], wrecv.at[m, j], dev)
 
-    def weight_landed(m, j, dev):
+    def weight_landed(m, j):
+        dev = at.peer(m)
         dst = weights.at[j, pl.ds(pl.multiple_of(dev * block + z * quarter, quarter), quarter)]
         return at.push(dst, dst, wsend.at[m, j], wrecv.at[m, j], dev)
 
     def walk(m, q, right):
-        part = weights.at[:, pl.ds(pl.multiple_of(peers[m] * block + q * quarter, quarter), quarter)]
+        part = weights.at[:, pl.ds(pl.multiple_of(at.peer(m) * block + q * quarter, quarter), quarter)]
         send, recv, dev = (rsend, rrecv, z + 1) if right else (lsend, lrecv, z - 1)
         return pltpu.make_async_remote_copy(
             src_ref=part, dst_ref=part, send_sem=send.at[m, q], recv_sem=recv.at[m, q],
             device_id=(dev, at.me), device_id_type=MESH,
         )
 
-    for m, dev in enumerate(peers):
-        packet_copy(m, dev).start()
+    def send_weights(m):
+        packet_copy(m).start()
         for j in range(3):
-            weight_copy(m, j, dev).start()
+            weight_copy(m, j).start()
+
+    each(7, send_weights)
 
     place = lax.broadcasted_iota(jnp.int32, (top, 128), 0)
     lane = lax.broadcasted_iota(jnp.int32, (top, 128), 1)
@@ -327,9 +329,9 @@
     early = seqs // 2
     each(early, cot_gather.start)
 
-    for m, dev in enumerate(peers):
+    def set_out(m):
         for j in range(3):
-            weight_landed(m, j, dev).wait_recv()
+            weight_landed(m, j).wait_recv()
 
         @pl.when(z < 3)
         def _():
@@ -339,24 +341,27 @@
         def _():
             walk(m, z, False).start()
 
+    each(7, set_out)
+
     def pass_on(d):
-        @pl.when(z - d >= 0)
-        def _():
-            for m in range(7):
+        def step(m):
+            @pl.when(z - d >= 0)
+            def _():
                 walk(m, z - d, True).wait_recv()
 
                 @pl.when(z < 3)
                 def _():
                     walk(m, z - d, True).start()
 
-        @pl.when(z + d <= 3)
-        def _():
-            for m in range(7):
+            @pl.when(z + d <= 3)
+            def _():
                 walk(m, z + d, False).wait_recv()
 
                 @pl.when(z > 0)
                 def _():
                     walk(m, z + d, False).start()
+
+        each(7, step)
 
     def relay(i, _):
         gather.relay(2 * i, True)
@@ -376,8 +381,7 @@
     lax.fori_loop(0, early // 2, cot_relay, 0)
     each(seqs, gather.relay_far)
     each(early, cot_gather.relay_far)
-    for m, dev in enumerate(peers):
-        packet_copy(m, dev).wait_recv()
+    each(7, lambda m: packet_copy(m).wait_recv())
     packets[at.me] = pk[...]
     devices = packets.shape[0]
     share = width // (128 * devices)
@@ -397,19 +401,22 @@
     each(early, cot_gather.finish)
     pass_on(3)
 
-    def sent(q, going, right):
-        @pl.when(going)
-        def _():
-            for m in range(7):
-                walk(m, q, right).wait_send()
-
-    for q in range(4):
-        sent(q, jnp.logical_and(q <= z, z < 3), True)
-        sent(q, jnp.logical_and(q >= z, z > 0), False)
-    for m, dev in enumerate(peers):
-        packet_copy(m, dev).wait_send()
+    def sent(m):
+        for q in range(4):
+
+            @pl.when(jnp.logical_and(q <= z, z < 3))
+            def _():
+                walk(m, q, True).wait_send()
+
+            @pl.when(jnp.logical_and(q >= z, z > 0))
+            def _():
+                walk(m, q, False).wait_send()
+
+        packet_copy(m).wait_send()
         for j in range(3):
-            weight_copy(m, j, dev).wait_send()
+            weight_copy(m, j).wait_send()
+
+    each(7, sent)
     for copy in own_weights:
         copy.wait()
 
@@ -532,19 +539,18 @@
     parts, pieces = own.shape[:2]
     chunks = parts * pieces
     width = wgrad.shape[3]
-    peers = at.peers()
     barrier = pltpu.get_barrier_semaphore()
     line = [lax.rem(z + k, 4) for k in range(1, 4)]
     for dev in line:
         pl.semaphore_signal(barrier, inc=1, device_id=(dev, me), device_id_type=MESH)
-    for dev in peers:
-        pl.semaphore_signal(barrier, inc=1, device_id=(z, dev), device_id_type=MESH)
+    each(7, lambda m: pl.semaphore_signal(barrier, inc=1, device_id=(z, at.peer(m)), device_id_type=MESH))
     pl.semaphore_wait(barrier, 10)
     inner = jnp.logical_and(z > 0, z < 3)
     outer_end, partner, outer = 1 + z // 3, 3 - z, 3 * (z - 1)
     cols = pl.ds(pl.multiple_of(me * width, width), width)
 
-    def column_copy(m, j, dev):
+    def column_copy(m, j):
+        dev = at.peer(m)
         rows = pl.ds(pl.multiple_of(dev * pieces, pieces), pieces)
         return at.push(wgrad.at[j, rows], own.at[1 + j, :, :, cols], wsend.at[m, j], wrecv.at[m, j], dev)
 
@@ -554,8 +560,7 @@
     for copy in locals_:
         copy.start()
     for j in range(3):
-        for m, dev in enumerate(peers):
-            column_copy(m, j, dev).start()
+        each(7, lambda m, j=j: column_copy(m, j).start())
     each(seqs, normed_sum.start)
     each(seqs, result_sum.start)
     ggrad[...] = jnp.zeros_like(ggrad)
@@ -590,8 +595,7 @@
             def _():
                 locals_[(3, 0, 1, 2)[j]].wait()
                 if j > 0:
-                    for m, dev in enumerate(peers):
-                        column_copy(m, j - 1, dev).wait_recv()
+                    each(7, lambda m: column_copy(m, j - 1).wait_recv())
 
     def step(c):
         @pl.when(lax.rem(c, pieces) == 0)
@@ -661,16 +665,18 @@
             parcel[dev, rows_of + k : rows_of + k + 1] = others[0:1, lanes]
         parcel[dev, 2 * rows_of : 2 * rows_of + 2] = others[1:3, 0:128]
 
-    def parcel_copy(m, dev):
+    def parcel_copy(m):
+        dev = at.peer(m)
         return at.push(parcel.at[dev], landed.at[m], gsend.at[m], grecv.at[m], dev)
 
-    for m, dev in enumerate(peers):
-        parcel_copy(m, dev).start()
-    total = parcel[me]
-    for m, dev in enumerate(peers):
-        parcel_copy(m, dev).wait_recv()
-        total = total + landed[m]
-    spare[0] = total
+    each(7, lambda m: parcel_copy(m).start())
+    spare[0] = parcel[me]
+
+    def add_parcel(m):
+        parcel_copy(m).wait_recv()
+        spare[0] += landed[m]
+
+    each(7, add_parcel)
 
     def small_copy(k):
         return line_push(spare.at[0], spare.at[1 + k], ss.at[k], sr.at[k], line[k])
@@ -699,10 +705,13 @@
         each(chunks, sent)
 
     each(seqs, normed_sum.finish, result_sum.finish)
-    for m, dev in enumerate(peers):
-        parcel_copy(m, dev).wait_send()
+
+    def all_sent(m):
+        parcel_copy(m).wait_send()
         for j in range(3):
-            column_copy(m, j, dev).wait_send()
+            column_copy(m, j).wait_send()
+
+    each(7, all_sent)
     total = spare[0]
     for k in range(3):
         small_copy(k).wait()
@@ -1022,7 +1031,6 @@
 
 def attend_back_kernel(
     agrad, normed, pre, low, ctx, w, wo, small, table, part, wgrad, wograd, gains, wacc, woacc,
-    gbuf, total,
 ):
     s = pl.program_id(0)
     length = seq_len(small, s)
@@ -1054,27 +1062,13 @@
             r = inverse_rms(v)
             grads[i].append(rms_back(v, r, u * g).astype(BF16))
             gains[i : i + 1] += jnp.sum(u * v * r, axis=0, keepdims=True)
+    total = None
     for i in range(3):
-        for h, g in enumerate(grads[i]):
-            gbuf[i, :, h * HEAD_DIM : (h + 1) * HEAD_DIM] = g
-
-    def project(i, _):
-        g = gbuf[i]
+        g = grads[i][0] if len(grads[i]) == 1 else jnp.concatenate(grads[i], axis=1)
         wacc[i] += dot(normed[0], g, 0, 0)
         piece = dot(g, w[i], 1, 1)
-
-        @pl.when(i == 0)
-        def _():
-            total[...] = piece
-
-        @pl.when(i > 0)
-        def _():
-            total[...] += piece
-
-        return 0
-
-    lax.fori_loop(0, 3, project, 0)
-    part[0] = total[...].astype(BF16)
+        total = piece if total is None else total + piece
+    part[0] = total.astype(BF16)
 
     @pl.when(s == pl.num_programs(0) - 1)
     def _():
@@ -1120,8 +1114,6 @@
             scratch_shapes=[
                 pltpu.VMEM(weights.shape, F32),
                 pltpu.VMEM(wo.shape, F32),
-                pltpu.VMEM((3, length, cols), BF16),
-                pltpu.VMEM((length, width), F32),
             ],
         ),
         compiler_params=pltpu.CompilerParams(dimension_semantics=("arbitrary",), vmem_limit_bytes=60 << 20),
@@ -1131,6 +1123,7 @@
 
 
 BLOCK = 256
+FIRST_TILE = (256, 1024)
 
 
 def pack_rows(seqs, capacity):
@@ -1154,6 +1147,19 @@
 def swiglu_back(gate, up, dact):
     sig = 1.0 / (1.0 + jnp.exp(-gate))
     return dact * up * sig * (1.0 + gate * (1.0 - sig)), dact * (gate * sig)
+
+
+def forward_blocks(blocks, x, dy, wi, wo, acts, dgus):
+    def job(rows, gcols, ucols):
+        gate = dot(x[rows], wi[:, gcols], 1, 0)
+        up = dot(x[rows], wi[:, ucols], 1, 0)
+        dact = dot(dy[rows], wo[gcols], 1, 1)
+        acts[rows, gcols] = (gate * (1.0 / (1.0 + jnp.exp(-gate))) * up).astype(BF16)
+        dgate, dup = swiglu_back(gate, up, dact)
+        dgus[rows, gcols] = dgate.astype(BF16)
+        dgus[rows, ucols] = dup.astype(BF16)
+
+    each_block(blocks, wo.shape[0], job)
 
 
 def gradient_tiles(blocks, left, right, result, acc, stage, ssem, busy):
@@ -1311,8 +1317,8 @@
                 pltpu.VMEM(w_in.shape[1:], BF16),
                 pltpu.VMEM((rows, hidden), BF16),
                 pltpu.VMEM((rows, 2 * hidden), BF16),
-                pltpu.VMEM((512, 1024), F32),
-                pltpu.VMEM((2, 512, 1024), BF16),
+                pltpu.VMEM(FIRST_TILE, F32),
+                pltpu.VMEM((2,) + FIRST_TILE, BF16),
                 dma,
                 dma((2,)),
                 dma((4,)),
@@ -1355,8 +1361,8 @@
     each_block(blocks, hidden, backward)
     save = pltpu.make_async_copy(dgus, dgu.at[0], rsem)
     save.start()
-    gradient_tiles(blocks, x, dgus, in_grad.at[0], acc, stage, ssem, False)
-    drain_tiles(in_grad.at[0], acc, stage, ssem)
+    gradient_tiles(blocks, x, dgus, in_grad, acc, stage, ssem, False)
+    drain_tiles(in_grad, acc, stage, ssem)
     save.wait()
 
 
@@ -1366,7 +1372,7 @@
     dma = pltpu.SemaphoreType.DMA
     return pl.pallas_call(
         functools.partial(in_grad_kernel, seqs),
-        out_shape=(sds((2, rows, 2 * hidden), BF16), sds((2, width, 2 * hidden), BF16)),
+        out_shape=(sds((2, rows, 2 * hidden), BF16), sds((width, 2 * hidden), BF16)),
         grid_spec=pltpu.PrefetchScalarGridSpec(
             num_scalar_prefetch=1,
             grid=(1,),
@@ -1393,11 +1399,10 @@
 
 
 def second_kernel(
-    seqs, starts, x_all, dy_all, w_in, w_out, _act, _dgu, _in_grad, act, dgu, in_grad, out_grad,
+    seqs, starts, x_all, dy_all, w_in, w_out, _act, _dgu, act, dgu, in_grad, out_grad,
     x, dy, wi, wo, acts, dgus, acc, stage, wsem, lsem, ssem, rsem,
 ):
     blocks = (starts[1, seqs] + BLOCK - 1) // BLOCK
-    hidden = wo.shape[0]
     loads = [pltpu.make_async_copy(w_in.at[1], wi, wsem.at[0]), pltpu.make_async_copy(w_out.at[1], wo, wsem.at[1])]
 
     def load(b, action):
@@ -1416,38 +1421,31 @@
         copy.wait()
     lax.fori_loop(0, blocks, lambda b, _: load(b, "wait"), 0)
 
-    def both(rows, gcols, ucols):
-        gate = dot(x[rows], wi[:, gcols], 1, 0)
-        up = dot(x[rows], wi[:, ucols], 1, 0)
-        dact = dot(dy[rows], wo[gcols], 1, 1)
-        acts[rows, gcols] = (gate * (1.0 / (1.0 + jnp.exp(-gate))) * up).astype(BF16)
-        dgate, dup = swiglu_back(gate, up, dact)
-        dgus[rows, gcols] = dgate.astype(BF16)
-        dgus[rows, ucols] = dup.astype(BF16)
-
-    each_block(blocks, hidden, both)
+    forward_blocks(blocks, x, dy, wi, wo, acts, dgus)
     saves = [pltpu.make_async_copy(acts, act.at[1], rsem.at[0]), pltpu.make_async_copy(dgus, dgu.at[1], rsem.at[1])]
     for copy in saves:
         copy.start()
-    gradient_tiles(blocks, x, dgus, in_grad.at[1], acc, stage, ssem, False)
+    gradient_tiles(blocks, x, dgus, in_grad, acc, stage, ssem, False)
     gradient_tiles(blocks, acts, dy, out_grad, acc, stage, ssem, True)
     drain_tiles(out_grad, acc, stage, ssem)
     for copy in saves:
         copy.wait()
 
 
-def expert_second(seqs, starts, x_all, dy_all, w_in, w_out, act, dgu, in_grad):
+def expert_second(seqs, starts, x_all, dy_all, w_in, w_out, act, dgu):
     rows, width = dy_all.shape[1:]
     hidden = w_out.shape[1]
     dma = pltpu.SemaphoreType.DMA
     return pl.pallas_call(
         functools.partial(second_kernel, seqs),
-        out_shape=(sds(act.shape, BF16), sds(dgu.shape, BF16), sds(in_grad.shape, BF16), sds((hidden, width), BF16)),
-        input_output_aliases={5: 0, 6: 1, 7: 2},
+        out_shape=(
+            sds(act.shape, BF16), sds(dgu.shape, BF16), sds((width, 2 * hidden), BF16), sds((hidden, width), BF16)
+        ),
+        input_output_aliases={5: 0, 6: 1},
         grid_spec=pltpu.PrefetchScalarGridSpec(
             num_scalar_prefetch=1,
             grid=(1,),
-            in_specs=[AN] * 7,
+            in_specs=[AN] * 6,
             out_specs=(AN, AN, AN, AN),
             scratch_shapes=[
                 pltpu.VMEM((rows, width), BF16),
@@ -1467,13 +1465,13 @@
         compiler_params=pltpu.CompilerParams(dimension_semantics=("arbitrary",), vmem_limit_bytes=60 << 20),
         cost_estimate=pl.CostEstimate(flops=25 * 10**9, bytes_accessed=6 * 10**7, transcendentals=10**6),
         name="expert_second",
-    )(starts, x_all, dy_all, w_in, w_out, act, dgu, in_grad)
+    )(starts, x_all, dy_all, w_in, w_out, act, dgu)
 
 
 def tail_kernel(seqs, starts, act, dgu, w_in, w_out, produced, dx):
     @pl.when(pl.program_id(1) * BLOCK < starts[pl.program_id(0), seqs])
     def _():
-        part = min(produced.shape[1], 256)
+        part = min(produced.shape[1], 512)
 
         def run(i, _):
             cols = pl.ds(pl.multiple_of(i * part, part), part)
@@ -1602,16 +1600,16 @@
         starts, mixed, cot_full, (slots0, slots1), expert_in, hidden, capacity
     )
 
-    def over_rep(value, axis):
-        return lax.psum_scatter(value, "rep", scatter_dimension=axis, tiled=True)
-
-    out0 = over_rep(out_grad0, 0)
-    dgu, in_grad = first_in_grad(seqs, starts, x_all, dy_all, pair, expert_out)
-    act, dgu, in_grad, out_grad1 = expert_second(
-        seqs, starts, x_all, dy_all, expert_in, expert_out, act, dgu, in_grad
-    )
-    in_both = over_rep(in_grad, 1)
-    out1 = over_rep(out_grad1, 0)
+    def over_rep(value):
+        return lax.psum_scatter(value, "rep", scatter_dimension=0, tiled=True)
+
+    out0 = over_rep(out_grad0)
+    dgu, in_grad0 = first_in_grad(seqs, starts, x_all, dy_all, pair, expert_out)
+    in0 = over_rep(in_grad0)
+    x_all, _ = lax.optimization_barrier((x_all, in_grad0))
+    act, dgu, in_grad1, out_grad1 = expert_second(seqs, starts, x_all, dy_all, expert_in, expert_out, act, dgu)
+    in1 = over_rep(in_grad1)
+    out1 = over_rep(out_grad1)
     produced, dx = expert_tails(seqs, starts, act, dgu, expert_in, expert_out)
     out_part, grad_part = combine(starts, (slots0, slots1), produced, dx, capacity)
 
@@ -1619,15 +1617,16 @@
     npart, wgrad, wograd, qk_back = attend_back(
         agrad, normed, pre, low, ctx, weights, output_weight, small_in, table
     )
-
-    def widen(into, value, j):
-        return lax.dynamic_update_slice(into, value.astype(F32)[None], (j, 0, 0))
-
-    out_all = widen(jnp.zeros((local,) + out0.shape, F32), out0, 0)
-    npart, out_all = lax.optimization_barrier((npart, out_all))
     sums, small, result, token_grad = finish(
         wgrad, wograd, npart, out_part, tokens, middle, mgrad, gains, ffn_back, qk_back
     )
+
+    def widen(into, value, j):
+        return lax.dynamic_update_slice(into, value.astype(F32)[None], (j, 0, 0))
+
+    small, out0 = lax.optimization_barrier((small, out0))
+    out_all = widen(jnp.zeros((local,) + out0.shape, F32), out0, 0)
+    small, out_all = lax.optimization_barrier((small, out_all))
 
     def head_share(vector):
         return lax.dynamic_slice_in_dim(vector, me * (HEAD_DIM // ep), HEAD_DIM // ep)
@@ -1643,7 +1642,7 @@
         small[share : 2 * share].reshape(-1),
         head_share(small[2 * share]),
         head_share(small[2 * share + 1]),
-        in_both.astype(F32),
+        jnp.stack([in0, in1]).astype(F32),
         widen(out_all, out1, 1),
     )
 

time: 806 us -> 815 us (1.011)
  Pallas kernels: 759 us -> 769 us
    pallas_call x1, Pallas kernels: 291 us -> 312 us  [finish(): pl.pallas_call(finish_kernel, out_shape=(sds(whole, BF16), sds((8, 128),...]
    pallas_call x1, Pallas kernels: 53.8 us -> 45.3 us  [attend_back(): pl.pallas_call(attend_back_kernel, out_shape=(sds(agrad.shape, BF16), sds...]
  transfers between devices with their start and end apart: 3 -> 4, of which waited for: 0 -> 0; matrix products, arithmetic and copies ran while one was open for 3% -> 2% of each run, Pallas kernels for 69% -> 69%
where the time goes in v10:
time: 815 us; the launch traced here: 814 us
  Pallas kernels  769 us (94%)
  other arithmetic  21.9 us (3%)
  between operations  14.5 us (2%)
    pallas_call x1, Pallas kernels, finish(): pl.pallas_call(finish_kernel, out_shape=(sds(whole, BF16), sds((8, 128),...  312 us
    pallas_call x1, Pallas kernels, attend_mix(): pl.pallas_call(functools.partial(attend_mix_kernel, top, local), out_shap...  98.5 us
    pallas_call x1, Pallas kernels, back(): pl.pallas_call(back_kernel, out_shape=(sds(cot.shape, F32), sds((1, width...  79.4 us
    pallas_call x1, Pallas kernels, front(): pl.pallas_call(front_kernel, out_shape=(sds((seqs, rows * ep, width + 128...  77.3 us
    pallas_call x1, Pallas kernels, attend_back(): pl.pallas_call(attend_back_kernel, out_shape=(sds(agrad.shape, BF16), sds...  45.3 us
    pallas_call x1, Pallas kernels, expert_second(): pl.pallas_call(functools.partial(second_kernel, seqs), out_shape=(sds(act...  41.4 us
    pallas_call x1, Pallas kernels, expert_tails(): pl.pallas_call(functools.partial(tail_kernel, seqs), out_shape=(sds((2, r...  38 us
    pallas_call x1, Pallas kernels, expert_first(): pl.pallas_call(functools.partial(first_kernel, capacity), out_shape=(sds(...  31.1 us
  transfers between devices with their start and end apart: 4, of which 0 were waited for; matrix products, arithmetic and copies ran while one was open for 2% of the time, Pallas kernels for 69%

profile of v10, /device:TPU:0, one launch (start us, length us, event | category | flops | bytes accessed | tf_op | source)
XLA Modules:
  0.0 814.5 jit_solution(8149678930464469988)
XLA Ops:
  7.2 0.0 reduce-scatter.5.cloned.1.call-start
  7.9 0.7 bitcast_convert_fusion.4
  8.6 0.7 maximum_convert_fusion.1
  9.2 0.6 select_maximum_fusion.1.pk
  9.8 77.3 %front.1 = (bf16[8,256,2176]{2,1,0:T(8,128)(2,1)}, bf16[3,2048,256]{2,1,0:T(8,128)(2,1)}, bf16[8,256,2048]{2,1,0:T(8,128)(2,1)}, f32[8,2048]{1,0:T(8,128)}, f32[8,128]{1,0:T(8,128)}) custom-call(bf16[8,32,2048]{2,1,0:T(8,128)(2,1)} %tok.5, bf16[8,32,2048]{2,1,0:T(8,128)(2,1)} %cot.5, s32[8,8,32]{2,1,0:T(8,128)} %bitcast.51, bf16[8,8,32]{2,1,0:T(8,128)(2,1)} %bitcast.52, ...), custom_call_target="tpu_custom_call" | custom-call | tf_op jit(solution)/shard_map/front/pallas_call | solution.py:444
  87.2 98.5 %attend_mix.1 = (bf16[8,256,2048]{2,1,0:T(8,128)(2,1)}, f32[2,8,256,256]{3,2,1,0:T(8,128)}, bf16[3,8,256,256]{3,2,1,0:T(8,128)(2,1)}, bf16[8,256,256]{2,1,0:T(8,...) custom-call(bf16[8,256,2176]{2,1,0:T(8,128)(2,1)} %get-tuple-element, ...), custom_call_target="tpu_custom_call", output_to_operand_aliasing={{6}: (8, {})} | custom-call | tf_op jit(solution)/shard_map/attend_mix/pallas_call | solution.py:995
  185.7 31.1 %expert_first.1 = (bf16[2,1280,1024]{2,1,0:T(8,128)(2,1)}, bf16[1280,2048]{1,0:T(8,128)(2,1)}, bf16[2,1280,2048]{2,1,0:T(8,128)(2,1)}, bf16[2,1280,2048]{2,1,0:T(8,128)(2,1)}, bf16[1024,2048]{1,0:T(8,128)(2,1)}) custom-call(s32[8,128]{1,0:T(8,128)} %get-tuple-element.63.starts.refs_0_, bf16[8,256,2048]{2,1,0:T(8,128)(2,1)} %get-tuple-element.66.mixed, ...), custom_call_target="tpu_custom_call" | custom-call | flops 20000000000 | bytes 60000000 | tf_op jit(solution)/shard_map/expert_first/pallas_call | solution.py:1294
  216.8 0.0 reduce-scatter.5.cloned.1.call-update
  216.8 0.0 reduce-scatter.11.cloned.1.call-start
  216.9 26.6 %first_in_grad.1 = (bf16[2,1280,2048]{2,1,0:T(8,128)(2,1)}, bf16[2048,2048]{1,0:T(8,128)(2,1)}) custom-call(s32[8,128]{1,0:T(8,128)} %get-tuple-element.63.starts.refs_0_, bf16[2,1280,2048]{2,1,0:T(8,128)(2,1)} %get-tuple-element.72.x_all, bf16[2,1280,2048]{2,1,0:T(8,128)(2,1)} %get-tuple-element.69.dy_all, bf16[1280,2048]{1,0:T(8,128)(2,1)} %get-tuple-element.70.pair, ...), custom_call_target="tpu_custom_call" | custom-call | flops 10000000000 | bytes 20000000 | tf_op jit(solution)/shard_map/first_in_grad/pallas_call | solution.py:1373
  243.5 41.4 %expert_second.1 = (bf16[2,1280,1024]{2,1,0:T(8,128)(2,1)}, bf16[2,1280,2048]{2,1,0:T(8,128)(2,1)}, bf16[2048,2048]{1,0:T(8,128)(2,1)}, bf16[1024,2048]{1,0:T(8,128)(2,1)}) custom-call(s32[8,128]{1,0:T(8,128)} %get-tuple-element.63.starts.refs_0_, bf16[2,1280,2048]{2,1,0:T(8,128)(2,1)} %get-tuple-element.72.x_all, ...), custom_call_target="tpu_custom_call", output_to_operand_aliasing={{0}: (5, {}), {1}: (6, {})} | custom-call | flops 24999999488 | bytes 60000000 | tf_op jit(solution)/shard_map/expert_second/pallas_call | solution.py:1439
  284.9 0.0 reduce-scatter.11.cloned.1.call-update
  284.9 0.0 reduce-scatter.9.cloned.1.call-start
  284.9 0.7 reduce-scatter.9.cloned.1.call-update
  285.6 0.0 reduce-scatter.7.cloned.1.call-start
  285.7 0.5 reduce-scatter.7.cloned.1.call-update
  286.2 38.0 %expert_tails.1 = (bf16[2,1280,2048]{2,1,0:T(8,128)(2,1)}, bf16[2,1280,2048]{2,1,0:T(8,128)(2,1)}) custom-call(s32[8,128]{1,0:T(8,128)} %get-tuple-element.63.starts.refs_0_, bf16[2,1280,1024]{2,1,0:T(8,128)(2,1)} %get-tuple-element.75.act, bf16[2,1280,2048]{2,1,0:T(8,128)(2,1)} %get-tuple-element.76.dgu, bf16[2,2048,2048]{2,1,0:T(8,128)(2,1)} %w_in.5, ...), custom_call_target="tpu_custom_call" | custom-call | flops 24000000000 | bytes 60000000 | tf_op jit(solution)/shard_map/expert_tails/pallas_call | solution.py:1493
  324.2 19.5 %combine.1 = (bf16[8,256,2048]{2,1,0:T(8,128)(2,1)}, bf16[8,256,2048]{2,1,0:T(8,128)(2,1)}) custom-call(s32[8,128]{1,0:T(8,128)} %get-tuple-element.63.starts.refs_0_, f32[8,16,256]{2,1,0:T(8,128)} %get-tuple-element.64.slots0.refs_1_, f32[8,16,256]{2,1,0:T(8,128)} %get-tuple-element.65.slots1.refs_2_, bf16[2,1280,2048]{2,1,0:T(8,128)(2,1)} %get-tuple-element.77.refs_3_, ...), custom_call_target="tpu_custom_call" | custom-call | flops 3000000000 | bytes 40000000 | tf_op jit(solution)/shard_map/combine/pallas_call | solution.py:1541
  343.7 79.4 %back.1 = (f32[8,32,2048]{2,1,0:T(8,128)}, f32[1,2048]{1,0:T(1,128)}, bf16[8,256,2048]{2,1,0:T(8,128)(2,1)}) custom-call(bf16[8,8,32,2048]{3,2,1,0:T(8,128)(2,1)} %bitcast.45, f32[8,32,2048]{2,1,0:T(8,128)} %get-tuple-element.80.middle, bf16[8,32,2048]{2,1,0:T(8,128)(2,1)} %cot.5, f32[8,128]{1,0:T(8,128)} %get-tuple-element.61.small, ...), custom_call_target="tpu_custom_call" | custom-call | tf_op jit(solution)/shard_map/back/pallas_call | solution.py:512
  423.1 0.0 copy-start.2
  423.1 45.3 %attend_back.1 = (bf16[8,256,2048]{2,1,0:T(8,128)(2,1)}, bf16[3,2048,256]{2,1,0:T(8,128)(2,1)}, bf16[256,2048]{1,0:T(8,128)(2,1)}, f32[8,128]{1,0:T(8,128)}) custom-call(bf16[8,256,2048]{2,1,0:T(8,128)(2,1)} %get-tuple-element.81.agrad, bf16[8,256,2048]{2,1,0:T(8,128)(2,1)} %get-tuple-element.82.normed, f32[2,8,256,256]{3,2,1,0:T(8,128)} %get-tuple-element.83.pre, ...), custom_call_target="tpu_custom_call" | custom-call | flops 20000000000 | bytes 40000000 | tf_op jit(solution)/shard_map/attend_back/pallas_call | solution.py:1086
  468.5 0.7 slice.31
  469.1 0.0 copy-done.2
  469.1 0.6 select_maximum_fusion.others
  469.8 312.3 %finish.1 = (bf16[4,4,64,2048]{3,2,1,0:T(8,128)(2,1)}, f32[8,128]{1,0:T(8,128)}, bf16[8,32,2048]{2,1,0:T(8,128)(2,1)}, bf16[8,32,2048]{2,1,0:T(8,128)(2,1)}) custom-call(bf16[3,32,64,256]{3,2,1,0:T(8,128)(2,1)} %bitcast.46, bf16[4,64,2048]{2,1,0:T(8,128)(2,1)} %bitcast.50, bf16[8,8,32,2048]{3,2,1,0:T(8,128)(2,1)} %bitcast.44, ...), custom_call_target="tpu_custom_call" | custom-call | tf_op jit(solution)/shard_map/finish/pallas_call | solution.py:747
  782.1 2.8 fusion.2
  784.9 1.6 bitcast_convert_fusion
  786.5 1.6 bitcast_convert_fusion.1
  788.1 1.6 bitcast_convert_fusion.2
  789.8 0.0 copy-start.3
  789.8 1.6 bitcast_convert_fusion.3
  791.4 0.0 reduce-scatter.5.cloned.1.call-done
  791.4 3.7 pad_convert_fusion
  795.1 0.0 copy-done.3
  795.1 0.6 fusion.1
  795.7 0.6 fusion
  796.3 0.6 slice_bitcast_fusion
  796.9 0.0 reduce-scatter.11.cloned.1.call-done
  796.9 2.8 convert_dynamic-update-slice_fusion
  799.7 0.0 reduce-scatter.9.cloned.1.call-done
  799.7 0.0 reduce-scatter.7.cloned.1.call-done
  799.7 0.0 copy-start.1
  799.7 0.0 copy-start
  799.7 6.3 maximum_convert_fusion
  806.0 0.0 copy-done.1
  806.0 1.0 copy.38
  807.0 0.0 copy-done
  807.0 1.0 copy.39
  (2 shorter events, 0.0 us)
Async XLA Ops:
  7.2 784.2 %reduce-scatter.5.cloned.1.call-start = ((), (), s32[]{:S(2)}) async-start(), calls=%async_computation.4 | async-start | bytes 5242880 | tf_op jit(solution)/shard_map/reduce_scatter | solution.py:1604
  216.8 580.1 %reduce-scatter.11.cloned.1.call-start = ((), (), s32[]{:S(2)}) async-start(), calls=%async_computation.7 | async-start | bytes 5242880 | tf_op jit(solution)/shard_map/reduce_scatter | solution.py:1604
  284.9 514.8 %reduce-scatter.9.cloned.1.call-start = ((), (), s32[]{:S(2)}) async-start(), calls=%async_computation.6 | async-start | bytes 10485760 | tf_op jit(solution)/shard_map/reduce_scatter | solution.py:1604
  285.6 514.0 %reduce-scatter.7.cloned.1.call-start = ((), (), s32[]{:S(2)}) async-start(), calls=%async_computation.5 | async-start | bytes 10485760 | tf_op jit(solution)/shard_map/reduce_scatter | solution.py:1604
  423.1 46.0 %copy-start.2 = (f32[1,2048]{1,0:T(1,128)S(1)}, f32[1,2048]{1,0:T(1,128)}, u32[]{:S(2)}) copy-start(f32[1,2048]{1,0:T(1,128)} %get-tuple-element.91) | copy-start | bytes 24580
  789.8 5.4 copy-start.3
  799.7 6.3 copy-start.1
  799.7 7.3 copy-start
Sparse Core Ops, SparseCore 0:
  216.9 80.0 reduce-scatter.4
  299.3 85.2 reduce-scatter.10
  386.9 162.4 reduce-scatter.8
  552.2 222.6 reduce-scatter.6

commit v11 on v10

--- a/solution.py
+++ b/solution.py
@@ -717,6 +717,12 @@
         small_copy(k).wait()
         total = total + spare[1 + k]
     small_out[...] = total
+    few = total[2 * rows_of : 2 * rows_of + 2]
+    heads = HEAD_DIM // devices
+    moved = jnp.zeros_like(few)
+    for k in range(devices):
+        moved += jnp.where(me == k, pltpu.roll(few, (128 - k * heads) % 128, 1), 0.0)
+    small_out[2 * rows_of : 2 * rows_of + 2] = moved
 
 
 def finish(wgrad, wograd, npart, opart, tokens, middle, mgrad, gains, ffn_back, qk_back):
@@ -732,7 +738,9 @@
         small = lax.psum(small, ("ep", "rep"))
         mine = lax.axis_index("ep") * share
         cut = [lax.dynamic_slice_in_dim(small, k * width + mine, share).reshape(-1, 128) for k in range(2)]
-        small = jnp.concatenate(cut + [small[2 * width :].reshape(2, HEAD_DIM)], axis=0)
+        few = small[2 * width :].reshape(2, HEAD_DIM)
+        few = jnp.roll(few, -lax.axis_index("ep") * (HEAD_DIM // ep), axis=1)
+        small = jnp.concatenate(cut + [few], axis=0)
         big = lax.psum(jnp.concatenate([wograd[None], wrows], axis=0), "rep")
         return big, jnp.pad(small, ((0, 8 - small.shape[0]), (0, 0))), (middle + moe).astype(BF16), tg
     others = jnp.concatenate([ffn_back, jnp.pad(qk_back[:2], ((0, 0), (0, width - HEAD_DIM)))], axis=0)
@@ -1062,17 +1070,19 @@
             r = inverse_rms(v)
             grads[i].append(rms_back(v, r, u * g).astype(BF16))
             gains[i : i + 1] += jnp.sum(u * v * r, axis=0, keepdims=True)
+    width = w.shape[2]
+    joined = jnp.concatenate([g for kind in grads for g in kind], axis=1)
+    wacc[...] += dot(normed[0], joined, 0, 0)
     total = None
     for i in range(3):
-        g = grads[i][0] if len(grads[i]) == 1 else jnp.concatenate(grads[i], axis=1)
-        wacc[i] += dot(normed[0], g, 0, 0)
-        piece = dot(g, w[i], 1, 1)
+        piece = dot(joined[:, i * width : (i + 1) * width], w[i], 1, 1)
         total = piece if total is None else total + piece
     part[0] = total.astype(BF16)
 
     @pl.when(s == pl.num_programs(0) - 1)
     def _():
-        wgrad[...] = wacc[...].astype(BF16)
+        for i in range(3):
+            wgrad[i] = wacc[:, i * width : (i + 1) * width].astype(BF16)
         wograd[...] = woacc[...].astype(BF16)
 
 
@@ -1112,7 +1122,7 @@
                 pl.BlockSpec((8, HEAD_DIM), two),
             ),
             scratch_shapes=[
-                pltpu.VMEM(weights.shape, F32),
+                pltpu.VMEM((weights.shape[1], 3 * cols), F32),
                 pltpu.VMEM(wo.shape, F32),
             ],
         ),
@@ -1123,7 +1133,7 @@
 
 
 BLOCK = 256
-FIRST_TILE = (256, 1024)
+FIRST_TILE = (512, 1024)
 
 
 def pack_rows(seqs, capacity):
@@ -1454,8 +1464,8 @@
                 pltpu.VMEM(w_out.shape[1:], BF16),
                 pltpu.VMEM((rows, hidden), BF16),
                 pltpu.VMEM((rows, 2 * hidden), BF16),
-                pltpu.VMEM((512, 2048), F32),
-                pltpu.VMEM((2, 512, 2048), BF16),
+                pltpu.VMEM((256, 2048), F32),
+                pltpu.VMEM((2, 256, 2048), BF16),
                 dma((2,)),
                 dma((2, rows // BLOCK)),
                 dma((2,)),
@@ -1514,16 +1524,39 @@
     s = pl.program_id(0)
     starts = refs[0]
     slots = refs[1 : 1 + local]
-    produced, dx, out_part, grad_part = refs[1 + local :]
+    produced, dx, out_part, grad_part, held_out, held_grad, sems = refs[1 + local :]
+    seqs = pl.num_programs(0)
+
+    def loads(s):
+        k = lax.rem(s, 2)
+        copies = []
+        for j in range(local):
+            span = pl.ds(pl.multiple_of(starts[j, s], 16), capacity)
+            copies.append(pltpu.make_async_copy(produced.at[j, span], held_out.at[k, j], sems.at[k, 0, j]))
+            copies.append(pltpu.make_async_copy(dx.at[j, span], held_grad.at[k, j], sems.at[k, 1, j]))
+        return copies
+
+    @pl.when(s == 0)
+    def _():
+        for copy in loads(s):
+            copy.start()
+
+    @pl.when(s + 1 < seqs)
+    def _():
+        for copy in loads(s + 1):
+            copy.start()
+
+    for copy in loads(s):
+        copy.wait()
+    slot = lax.rem(s, 2)
     out_sum, grad_sum = None, None
     for j in range(local):
         length = slots[j].shape[2]
         column = lax.broadcasted_iota(jnp.int32, (capacity, length), 0).astype(F32)
         place = column == slots[j][0, 0:1]
-        span = pl.ds(pl.multiple_of(starts[j, s], 16), capacity)
         held = lax.broadcasted_iota(jnp.int32, (capacity, 1), 0) < starts[j, s + 1] - starts[j, s]
-        rows = jnp.where(held, produced[j, span], 0.0).astype(BF16)
-        grads = jnp.where(held, dx[j, span], 0.0).astype(BF16)
+        rows = jnp.where(held, held_out[slot, j], 0.0).astype(BF16)
+        grads = jnp.where(held, held_grad[slot, j], 0.0).astype(BF16)
         out = dot(jnp.where(place, slots[j][0, 8:9], 0.0).astype(BF16), rows, 0, 0)
         grad = dot(jnp.where(place, 1.0, 0.0).astype(BF16), grads, 0, 0)
         out_sum = out if out_sum is None else out_sum + out
@@ -1537,15 +1570,16 @@
     seqs, _, length = slots[0].shape
     width = produced.shape[2]
     seq = lambda i, *_: (i, 0, 0)
-    rows = pl.BlockSpec(produced.shape, lambda i, *_: (0, 0, 0))
+    held = pltpu.VMEM((2, local, capacity, width), BF16)
     return pl.pallas_call(
         functools.partial(combine_kernel, capacity, local),
         out_shape=(sds((seqs, length, width), BF16), sds((seqs, length, width), BF16)),
         grid_spec=pltpu.PrefetchScalarGridSpec(
             num_scalar_prefetch=1,
             grid=(seqs,),
-            in_specs=[pl.BlockSpec((1, 16, length), seq)] * local + [rows] * 2,
+            in_specs=[pl.BlockSpec((1, 16, length), seq)] * local + [AN] * 2,
             out_specs=(pl.BlockSpec((1, length, width), seq), pl.BlockSpec((1, length, width), seq)),
+            scratch_shapes=[held, held, pltpu.SemaphoreType.DMA((2, 2, local))],
         ),
         compiler_params=pltpu.CompilerParams(dimension_semantics=("arbitrary",), vmem_limit_bytes=60 << 20),
         cost_estimate=pl.CostEstimate(flops=3 * 10**9, bytes_accessed=4 * 10**7, transcendentals=0),
@@ -1628,9 +1662,7 @@
     out_all = widen(jnp.zeros((local,) + out0.shape, F32), out0, 0)
     small, out_all = lax.optimization_barrier((small, out_all))
 
-    def head_share(vector):
-        return lax.dynamic_slice_in_dim(vector, me * (HEAD_DIM // ep), HEAD_DIM // ep)
-
+    heads = HEAD_DIM // ep
     return (
         result,
         token_grad,
@@ -1640,8 +1672,8 @@
         sums[0].astype(F32),
         small[:share].reshape(-1),
         small[share : 2 * share].reshape(-1),
-        head_share(small[2 * share]),
-        head_share(small[2 * share + 1]),
+        small[2 * share, :heads],
+        small[2 * share + 1, :heads],
         jnp.stack([in0, in1]).astype(F32),
         widen(out_all, out1, 1),
     )

time: 815 us -> 816 us (level)
  no operation moved by 1% of the time
where the time goes in v11:
time: 816 us; the launch traced here: 815 us
  Pallas kernels  771 us (94%)
  other arithmetic  21.9 us (3%)
  between operations  14.5 us (2%)
    pallas_call x1, Pallas kernels, finish(): pl.pallas_call(finish_kernel, out_shape=(sds(whole, BF16), sds((8, 128),...  313 us
    pallas_call x1, Pallas kernels, attend_mix(): pl.pallas_call(functools.partial(attend_mix_kernel, top, local), out_shap...  98.5 us
    pallas_call x1, Pallas kernels, back(): pl.pallas_call(back_kernel, out_shape=(sds(cot.shape, F32), sds((1, width...  79.5 us
    pallas_call x1, Pallas kernels, front(): pl.pallas_call(front_kernel, out_shape=(sds((seqs, rows * ep, width + 128...  77.3 us
    pallas_call x1, Pallas kernels, attend_back(): pl.pallas_call(attend_back_kernel, out_shape=(sds(agrad.shape, BF16), sds...  46.6 us
    pallas_call x1, Pallas kernels, expert_second(): pl.pallas_call(functools.partial(second_kernel, seqs), out_shape=(sds(act...  44.1 us
    pallas_call x1, Pallas kernels, expert_tails(): pl.pallas_call(functools.partial(tail_kernel, seqs), out_shape=(sds((2, r...  38 us
    pallas_call x1, Pallas kernels, expert_first(): pl.pallas_call(functools.partial(first_kernel, capacity), out_shape=(sds(...  29.1 us
  transfers between devices with their start and end apart: 4, of which 0 were waited for; matrix products, arithmetic and copies ran while one was open for 2% of the time, Pallas kernels for 69%

profile of v11, /device:TPU:0, one launch (start us, length us, event | category | flops | bytes accessed | tf_op | source)
XLA Modules:
  0.0 815.0 jit_solution(7247579028515314692)
XLA Ops:
  7.2 0.0 reduce-scatter.5.cloned.1.call-start
  7.9 0.7 bitcast_convert_fusion.4
  8.6 0.7 maximum_convert_fusion.1
  9.2 0.6 select_maximum_fusion.1.pk
  9.8 77.3 %front.1 = (bf16[8,256,2176]{2,1,0:T(8,128)(2,1)}, bf16[3,2048,256]{2,1,0:T(8,128)(2,1)}, bf16[8,256,2048]{2,1,0:T(8,128)(2,1)}, f32[8,2048]{1,0:T(8,128)}, f32[8,128]{1,0:T(8,128)}) custom-call(bf16[8,32,2048]{2,1,0:T(8,128)(2,1)} %tok.5, bf16[8,32,2048]{2,1,0:T(8,128)(2,1)} %cot.5, s32[8,8,32]{2,1,0:T(8,128)} %bitcast.51, bf16[8,8,32]{2,1,0:T(8,128)(2,1)} %bitcast.52, ...), custom_call_target="tpu_custom_call" | custom-call | tf_op jit(solution)/shard_map/front/pallas_call | solution.py:444
  87.2 98.5 %attend_mix.1 = (bf16[8,256,2048]{2,1,0:T(8,128)(2,1)}, f32[2,8,256,256]{3,2,1,0:T(8,128)}, bf16[3,8,256,256]{3,2,1,0:T(8,128)(2,1)}, bf16[8,256,256]{2,1,0:T(8,...) custom-call(bf16[8,256,2176]{2,1,0:T(8,128)(2,1)} %get-tuple-element, ...), custom_call_target="tpu_custom_call", output_to_operand_aliasing={{6}: (8, {})} | custom-call | tf_op jit(solution)/shard_map/attend_mix/pallas_call | solution.py:1003
  185.7 29.1 %expert_first.1 = (bf16[2,1280,1024]{2,1,0:T(8,128)(2,1)}, bf16[1280,2048]{1,0:T(8,128)(2,1)}, bf16[2,1280,2048]{2,1,0:T(8,128)(2,1)}, bf16[2,1280,2048]{2,1,0:T(8,128)(2,1)}, bf16[1024,2048]{1,0:T(8,128)(2,1)}) custom-call(s32[8,128]{1,0:T(8,128)} %get-tuple-element.63.starts.refs_0_, bf16[8,256,2048]{2,1,0:T(8,128)(2,1)} %get-tuple-element.66.mixed, ...), custom_call_target="tpu_custom_call" | custom-call | flops 20000000000 | bytes 60000000 | tf_op jit(solution)/shard_map/expert_first/pallas_call | solution.py:1304
  214.9 0.0 reduce-scatter.5.cloned.1.call-update
  214.9 0.0 reduce-scatter.11.cloned.1.call-start
  214.9 26.6 %first_in_grad.1 = (bf16[2,1280,2048]{2,1,0:T(8,128)(2,1)}, bf16[2048,2048]{1,0:T(8,128)(2,1)}) custom-call(s32[8,128]{1,0:T(8,128)} %get-tuple-element.63.starts.refs_0_, bf16[2,1280,2048]{2,1,0:T(8,128)(2,1)} %get-tuple-element.72.x_all, bf16[2,1280,2048]{2,1,0:T(8,128)(2,1)} %get-tuple-element.69.dy_all, bf16[1280,2048]{1,0:T(8,128)(2,1)} %get-tuple-element.70.pair, ...), custom_call_target="tpu_custom_call" | custom-call | flops 10000000000 | bytes 20000000 | tf_op jit(solution)/shard_map/first_in_grad/pallas_call | solution.py:1383
  241.5 44.1 %expert_second.1 = (bf16[2,1280,1024]{2,1,0:T(8,128)(2,1)}, bf16[2,1280,2048]{2,1,0:T(8,128)(2,1)}, bf16[2048,2048]{1,0:T(8,128)(2,1)}, bf16[1024,2048]{1,0:T(8,128)(2,1)}) custom-call(s32[8,128]{1,0:T(8,128)} %get-tuple-element.63.starts.refs_0_, bf16[2,1280,2048]{2,1,0:T(8,128)(2,1)} %get-tuple-element.72.x_all, ...), custom_call_target="tpu_custom_call", output_to_operand_aliasing={{0}: (5, {}), {1}: (6, {})} | custom-call | flops 24999999488 | bytes 60000000 | tf_op jit(solution)/shard_map/expert_second/pallas_call | solution.py:1449
  285.7 0.0 reduce-scatter.11.cloned.1.call-update
  285.7 0.0 reduce-scatter.9.cloned.1.call-start
  285.7 0.7 reduce-scatter.9.cloned.1.call-update
  286.4 0.0 reduce-scatter.7.cloned.1.call-start
  286.5 0.5 reduce-scatter.7.cloned.1.call-update
  287.0 38.0 %expert_tails.1 = (bf16[2,1280,2048]{2,1,0:T(8,128)(2,1)}, bf16[2,1280,2048]{2,1,0:T(8,128)(2,1)}) custom-call(s32[8,128]{1,0:T(8,128)} %get-tuple-element.63.starts.refs_0_, bf16[2,1280,1024]{2,1,0:T(8,128)(2,1)} %get-tuple-element.75.act, bf16[2,1280,2048]{2,1,0:T(8,128)(2,1)} %get-tuple-element.76.dgu, bf16[2,2048,2048]{2,1,0:T(8,128)(2,1)} %w_in.5, ...), custom_call_target="tpu_custom_call" | custom-call | flops 24000000000 | bytes 60000000 | tf_op jit(solution)/shard_map/expert_tails/pallas_call | solution.py:1503
  325.0 18.0 %combine.1 = (bf16[8,256,2048]{2,1,0:T(8,128)(2,1)}, bf16[8,256,2048]{2,1,0:T(8,128)(2,1)}) custom-call(s32[8,128]{1,0:T(8,128)} %get-tuple-element.63.starts.refs_0_, f32[8,16,256]{2,1,0:T(8,128)} %get-tuple-element.64.slots0.refs_1_, f32[8,16,256]{2,1,0:T(8,128)} %get-tuple-element.65.slots1.refs_2_, bf16[2,1280,2048]{2,1,0:T(8,128)(2,1)} %get-tuple-element.77.refs_3_, ...), custom_call_target="tpu_custom_call" | custom-call | flops 3000000000 | bytes 40000000 | tf_op jit(solution)/shard_map/combine/pallas_call | solution.py:1574
  343.1 79.5 %back.1 = (f32[8,32,2048]{2,1,0:T(8,128)}, f32[1,2048]{1,0:T(1,128)}, bf16[8,256,2048]{2,1,0:T(8,128)(2,1)}) custom-call(bf16[8,8,32,2048]{3,2,1,0:T(8,128)(2,1)} %bitcast.45, f32[8,32,2048]{2,1,0:T(8,128)} %get-tuple-element.80.middle, bf16[8,32,2048]{2,1,0:T(8,128)(2,1)} %cot.5, f32[8,128]{1,0:T(8,128)} %get-tuple-element.61.small, ...), custom_call_target="tpu_custom_call" | custom-call | tf_op jit(solution)/shard_map/back/pallas_call | solution.py:512
  422.6 0.0 copy-start.2
  422.6 46.6 %attend_back.1 = (bf16[8,256,2048]{2,1,0:T(8,128)(2,1)}, bf16[3,2048,256]{2,1,0:T(8,128)(2,1)}, bf16[256,2048]{1,0:T(8,128)(2,1)}, f32[8,128]{1,0:T(8,128)}) custom-call(bf16[8,256,2048]{2,1,0:T(8,128)(2,1)} %get-tuple-element.81.agrad, bf16[8,256,2048]{2,1,0:T(8,128)(2,1)} %get-tuple-element.82.normed, f32[2,8,256,256]{3,2,1,0:T(8,128)} %get-tuple-element.83.pre, ...), custom_call_target="tpu_custom_call" | custom-call | flops 20000000000 | bytes 40000000 | tf_op jit(solution)/shard_map/attend_back/pallas_call | solution.py:1096
  469.2 0.7 slice.31
  469.9 0.0 copy-done.2
  469.9 0.6 select_maximum_fusion.others
  470.5 312.8 %finish.1 = (bf16[4,4,64,2048]{3,2,1,0:T(8,128)(2,1)}, f32[8,128]{1,0:T(8,128)}, bf16[8,32,2048]{2,1,0:T(8,128)(2,1)}, bf16[8,32,2048]{2,1,0:T(8,128)(2,1)}) custom-call(bf16[3,32,64,256]{3,2,1,0:T(8,128)(2,1)} %bitcast.46, bf16[4,64,2048]{2,1,0:T(8,128)(2,1)} %bitcast.50, bf16[8,8,32,2048]{3,2,1,0:T(8,128)(2,1)} %bitcast.44, ...), custom_call_target="tpu_custom_call" | custom-call | tf_op jit(solution)/shard_map/finish/pallas_call | solution.py:755
  783.3 2.8 fusion
  786.1 1.6 bitcast_convert_fusion
  787.7 1.6 bitcast_convert_fusion.1
  789.3 1.6 bitcast_convert_fusion.2
  791.0 0.0 copy-start.3
  791.0 1.6 bitcast_convert_fusion.3
  792.6 0.0 reduce-scatter.5.cloned.1.call-done
  792.6 3.7 pad_convert_fusion
  796.3 0.0 copy-done.3
  796.3 0.5 slice_bitcast_fusion.2
  796.9 0.6 slice_bitcast_fusion
  797.4 0.0 reduce-scatter.11.cloned.1.call-done
  797.4 2.8 convert_dynamic-update-slice_fusion
  800.2 0.0 reduce-scatter.9.cloned.1.call-done
  800.2 0.0 reduce-scatter.7.cloned.1.call-done
  800.2 0.0 copy-start.1
  800.2 0.0 copy-start
  800.2 6.3 maximum_convert_fusion
  806.5 0.0 copy-done.1
  806.5 1.0 copy.38
  807.5 0.0 copy-done
  807.5 1.0 copy.39
  (1 shorter events, 0.0 us)
Async XLA Ops:
  7.2 785.4 %reduce-scatter.5.cloned.1.call-start = ((), (), s32[]{:S(2)}) async-start(), calls=%async_computation.4 | async-start | bytes 5242880 | tf_op jit(solution)/shard_map/reduce_scatter | solution.py:1638
  214.9 582.5 %reduce-scatter.11.cloned.1.call-start = ((), (), s32[]{:S(2)}) async-start(), calls=%async_computation.7 | async-start | bytes 5242880 | tf_op jit(solution)/shard_map/reduce_scatter | solution.py:1638
  285.7 514.5 %reduce-scatter.9.cloned.1.call-start = ((), (), s32[]{:S(2)}) async-start(), calls=%async_computation.6 | async-start | bytes 10485760 | tf_op jit(solution)/shard_map/reduce_scatter | solution.py:1638
  286.4 513.8 %reduce-scatter.7.cloned.1.call-start = ((), (), s32[]{:S(2)}) async-start(), calls=%async_computation.5 | async-start | bytes 10485760 | tf_op jit(solution)/shard_map/reduce_scatter | solution.py:1638
  422.6 47.3 %copy-start.2 = (f32[1,2048]{1,0:T(1,128)S(1)}, f32[1,2048]{1,0:T(1,128)}, u32[]{:S(2)}) copy-start(f32[1,2048]{1,0:T(1,128)} %get-tuple-element.91) | copy-start | bytes 24580
  791.0 5.4 copy-start.3
  800.2 6.3 copy-start.1
  800.2 7.3 copy-start
Sparse Core Ops, SparseCore 0:
  215.0 79.3 reduce-scatter.4
  296.6 89.0 reduce-scatter.10
  388.1 162.9 reduce-scatter.8
  553.9 222.6 reduce-scatter.6

commit v12 on v11

--- a/solution.py
+++ b/solution.py
@@ -257,210 +257,23 @@
 COMM = dict(has_side_effects=True, vmem_limit_bytes=60 << 20)
 
 
-def front_kernel(
-    tok, cot, ids, gates, wq, wk, wv, pk, full, weights, cot_full, gains, small,
-    packets, own, gsend, grecv, glocal, csend, crecv, clocal,
-    wsend, wrecv, psend, precv, rsend, rrecv, lsend, lrecv, local,
-):
-    at = Place()
-    z = at.rep
-    gather = Gather(at, own, full, gsend, grecv, glocal)
-    cot_gather = Gather(at, cot, cot_full, csend, crecv, clocal)
-    seqs, _, width = tok.shape
+def front(tokens, cotangent, ids, gates, wq, wk, wv, packet):
+    _, _, width = tokens.shape
+    ep = lax.axis_size("ep")
     top = ids.shape[1]
-    block, cols = wq.shape[0], weights.shape[2]
-    quarter = block // 4
-    barrier = pltpu.get_barrier_semaphore()
-    line = [lax.rem(z + k, 4) for k in range(1, 4)]
-    for dev in line:
-        pl.semaphore_signal(barrier, inc=1, device_id=(dev, at.me), device_id_type=MESH)
-    each(7, lambda m: pl.semaphore_signal(barrier, inc=1, device_id=(z, at.peer(m)), device_id_type=MESH))
-    pl.semaphore_wait(barrier, 10)
-
-    def packet_copy(m):
-        return at.push(pk, packets.at[at.me], psend.at[m], precv.at[m], at.peer(m))
-
-    def weight_copy(m, j):
-        dev = at.peer(m)
-        theirs = pl.ds(pl.multiple_of(dev * cols, cols), cols)
-        src = (wq, wk, wv)[j].at[pl.ds(pl.multiple_of(z * quarter, quarter), quarter), theirs]
-        dst = weights.at[j, pl.ds(pl.multiple_of(at.me * block + z * quarter, quarter), quarter)]
-        return at.push(src, dst, wsend.at[m, j], wrecv.at[m, j], dev)
-
-    def weight_landed(m, j):
-        dev = at.peer(m)
-        dst = weights.at[j, pl.ds(pl.multiple_of(dev * block + z * quarter, quarter), quarter)]
-        return at.push(dst, dst, wsend.at[m, j], wrecv.at[m, j], dev)
-
-    def walk(m, q, right):
-        part = weights.at[:, pl.ds(pl.multiple_of(at.peer(m) * block + q * quarter, quarter), quarter)]
-        send, recv, dev = (rsend, rrecv, z + 1) if right else (lsend, lrecv, z - 1)
-        return pltpu.make_async_remote_copy(
-            src_ref=part, dst_ref=part, send_sem=send.at[m, q], recv_sem=recv.at[m, q],
-            device_id=(dev, at.me), device_id_type=MESH,
-        )
-
-    def send_weights(m):
-        packet_copy(m).start()
-        for j in range(3):
-            weight_copy(m, j).start()
-
-    each(7, send_weights)
-
-    place = lax.broadcasted_iota(jnp.int32, (top, 128), 0)
-    lane = lax.broadcasted_iota(jnp.int32, (top, 128), 1)
-    first = jnp.where(lane == place, 1.0, 0.0).astype(BF16)
-    second = jnp.where(lane == place + top, 1.0, 0.0).astype(BF16)
-
-    def join(s):
-        own[s, :, 0:width] = tok[s]
-        table = dot(ids[s].astype(F32).astype(BF16), first, 0, 0) + dot(gates[s], second, 0, 0)
-        own[s, :, width : width + 128] = table.astype(BF16)
-
-    each(seqs, join)
-    each(seqs, gather.start)
-    own_cols = pl.ds(pl.multiple_of(at.me * cols, cols), cols)
-    mine = pl.ds(pl.multiple_of(at.me * block, block), block)
-    own_weights = [
-        pltpu.make_async_copy(w.at[:, own_cols], weights.at[j, mine], local.at[j]) for j, w in enumerate((wq, wk, wv))
-    ]
-    for copy in own_weights:
-        copy.start()
-    early = seqs // 2
-    each(early, cot_gather.start)
-
-    def set_out(m):
-        for j in range(3):
-            weight_landed(m, j).wait_recv()
-
-        @pl.when(z < 3)
-        def _():
-            walk(m, z, True).start()
-
-        @pl.when(z > 0)
-        def _():
-            walk(m, z, False).start()
-
-    each(7, set_out)
-
-    def pass_on(d):
-        def step(m):
-            @pl.when(z - d >= 0)
-            def _():
-                walk(m, z - d, True).wait_recv()
-
-                @pl.when(z < 3)
-                def _():
-                    walk(m, z - d, True).start()
-
-            @pl.when(z + d <= 3)
-            def _():
-                walk(m, z + d, False).wait_recv()
-
-                @pl.when(z > 0)
-                def _():
-                    walk(m, z + d, False).start()
-
-        each(7, step)
-
-    def relay(i, _):
-        gather.relay(2 * i, True)
-        gather.relay(2 * i + 1, False)
-        return 0
-
-    def cot_relay(i, _):
-        cot_gather.relay(2 * i, True)
-        cot_gather.relay(2 * i + 1, False)
-        return 0
-
-    pairs = seqs // 2
-    lax.fori_loop(0, pairs // 2, relay, 0)
-    pass_on(1)
-    lax.fori_loop(pairs // 2, pairs, relay, 0)
-    pass_on(2)
-    lax.fori_loop(0, early // 2, cot_relay, 0)
-    each(seqs, gather.relay_far)
-    each(early, cot_gather.relay_far)
-    each(7, lambda m: packet_copy(m).wait_recv())
-    packets[at.me] = pk[...]
-    devices = packets.shape[0]
-    share = width // (128 * devices)
-    heads = HEAD_DIM // devices
-    gains[...] = jnp.zeros_like(gains)
-    small[...] = jnp.zeros_like(small)
-    for o in range(devices):
-        for k in range(share):
-            lanes = pl.ds((o * share + k) * 128, 128)
-            gains[0:1, lanes] = packets[o, k : k + 1]
-            gains[1:2, lanes] = packets[o, share + k : share + k + 1]
-        base = 2 * share
-        small[0:1] += pltpu.roll(packets[o, base : base + 1], o * heads, 1)
-        small[1:2] += pltpu.roll(packets[o, base + 1 : base + 2], o * heads, 1)
-        small[2:3] += pltpu.roll(packets[o, base + 2 : base + 3], o, 1)
-    each(seqs, gather.finish)
-    each(early, cot_gather.finish)
-    pass_on(3)
-
-    def sent(m):
-        for q in range(4):
-
-            @pl.when(jnp.logical_and(q <= z, z < 3))
-            def _():
-                walk(m, q, True).wait_send()
-
-            @pl.when(jnp.logical_and(q >= z, z > 0))
-            def _():
-                walk(m, q, False).wait_send()
-
-        packet_copy(m).wait_send()
-        for j in range(3):
-            weight_copy(m, j).wait_send()
-
-    each(7, sent)
-    for copy in own_weights:
-        copy.wait()
-
-
-def front(tokens, cotangent, ids, gates, wq, wk, wv, packet):
-    seqs, rows, width = tokens.shape
-    ep = lax.axis_size("ep")
-    cols = wq.shape[1] // ep
-    top = ids.shape[1]
-    if ep != 8 or lax.axis_size("rep") != 4:
-        routes = jnp.concatenate([ids.astype(BF16), gates], axis=1).transpose(0, 2, 1)
-        routes = jnp.pad(routes, ((0, 0), (0, 0), (0, 128 - 2 * top)))
-        full = lax.all_gather(jnp.concatenate([tokens, routes], axis=-1), "ep", axis=1, tiled=True)
-        weights = [lax.all_to_all(w, "ep", split_axis=1, concat_axis=0, tiled=True) for w in (wq, wk, wv)]
-        packets = lax.all_gather(packet, "ep", axis=0)
-        share, heads = width // (128 * ep), HEAD_DIM // ep
-        gains = jnp.stack([packets[:, :share].reshape(width), packets[:, share : 2 * share].reshape(width)])
-        lens = jnp.pad(packets[:, 2 * share + 2, 0], (0, 128 - ep))
-        few = [packets[:, 2 * share + k, :heads].reshape(HEAD_DIM) for k in range(2)] + [lens]
-        return (
-            full, jnp.stack(weights), lax.all_gather(cotangent, "ep", axis=1, tiled=True),
-            jnp.pad(gains, ((0, 6), (0, 0))), jnp.pad(jnp.stack(few), ((0, 5), (0, 0))),
-        )
-    dma = pltpu.SemaphoreType.DMA
-    return pl.pallas_call(
-        front_kernel,
-        out_shape=(
-            sds((seqs, rows * ep, width + 128), BF16),
-            sds((3, wq.shape[0] * ep, cols), BF16),
-            sds((seqs, rows * ep, width), BF16),
-            sds((8, width), F32),
-            sds((8, 128), F32),
-        ),
-        in_specs=[VM] * 8,
-        out_specs=(AN, AN, AN, VM, VM),
-        scratch_shapes=[pltpu.VMEM((ep,) + packet.shape, F32), pltpu.VMEM((seqs, rows, width + 128), BF16)]
-        + Gather.scratch(seqs)
-        + Gather.scratch(seqs)
-        + [dma((7, 3)), dma((7, 3)), dma((7,)), dma((7,))]
-        + [dma((7, 4))] * 4
-        + [dma((3,))],
-        compiler_params=pltpu.CompilerParams(collective_id=1, **COMM),
-        name="front",
-    )(tokens, cotangent, ids, gates, wq, wk, wv, packet)
+    routes = jnp.concatenate([ids.astype(BF16), gates], axis=1).transpose(0, 2, 1)
+    routes = jnp.pad(routes, ((0, 0), (0, 0), (0, 128 - 2 * top)))
+    full = lax.all_gather(jnp.concatenate([tokens, routes], axis=-1), "ep", axis=1, tiled=True)
+    weights = [lax.all_to_all(w, "ep", split_axis=1, concat_axis=0, tiled=True) for w in (wq, wk, wv)]
+    packets = lax.all_gather(packet, "ep", axis=0)
+    share, heads = width // (128 * ep), HEAD_DIM // ep
+    gains = jnp.stack([packets[:, :share].reshape(width), packets[:, share : 2 * share].reshape(width)])
+    lens = jnp.pad(packets[:, 2 * share + 2, 0], (0, 128 - ep))
+    few = [packets[:, 2 * share + k, :heads].reshape(HEAD_DIM) for k in range(2)] + [lens]
+    return (
+        full, jnp.stack(weights), lax.all_gather(cotangent, "ep", axis=1, tiled=True),
+        jnp.pad(gains, ((0, 6), (0, 0))), jnp.pad(jnp.stack(few), ((0, 5), (0, 0))),
+    )
 
 
 def plain_living(small, seqs, rows):
@@ -909,40 +722,176 @@
     )(number, full, weights, wo, gains, small, table)
 
 
-def attend_mix_kernel(
-    top, local, full, w, wo, gains, small, table, tok, cot, _cot_early,
-    normed, pre, low, ctx, middle, mixed, cot_full, slots0, slots1, starts,
-    own, blocks, nbuf, pbuf, lbuf, cbuf, part, begins, tsem, ssem, *scratch,
+def forward_kernel(
+    top, experts, tok, cot, ids, gates, wq, wk, wv, pk, wo, table,
+    weights_out, gains, small, normed, pre, low, ctx, middle, mixed, cot_full, slots0, slots1, starts,
+    weights, full, packets, own, mixed_own, nbuf, pbuf, lbuf, cbuf, part, begins, ssem,
+    wsend, wrecv, psend, precv, rsend, rrecv, lsend, lrecv, local, *scratch,
 ):
     at = Place()
-    seqs = tok.shape[0]
+    z = at.rep
     n = Reduce.sems
     reduce = Reduce(at, part, *scratch[:n])
-    gather = Gather(at, own, mixed, *scratch[n : n + 3])
-    cot_gather = Gather(at, cot, cot_full, *scratch[n + 3 :])
-    number = (at.me * local).astype(F32)
+    gather = Gather(at, own, full, *scratch[n : n + 3])
+    cot_gather = Gather(at, cot, cot_full, *scratch[n + 3 : n + 6])
+    mixed_gather = Gather(at, mixed_own, mixed, *scratch[n + 6 :])
+    seqs, rows, width = tok.shape
+    top = ids.shape[1]
+    block, cols = wq.shape[0], weights.shape[2]
+    quarter = block // 4
+    barrier = pltpu.get_barrier_semaphore()
+    line = [lax.rem(z + k, 4) for k in range(1, 4)]
+    for dev in line:
+        pl.semaphore_signal(barrier, inc=1, device_id=(dev, at.me), device_id_type=MESH)
+    each(7, lambda m: pl.semaphore_signal(barrier, inc=1, device_id=(z, at.peer(m)), device_id_type=MESH))
+    pl.semaphore_wait(barrier, 10)
+
+    def packet_copy(m):
+        return at.push(pk, packets.at[at.me], psend.at[m], precv.at[m], at.peer(m))
+
+    def weight_copy(m, j):
+        dev = at.peer(m)
+        theirs = pl.ds(pl.multiple_of(dev * cols, cols), cols)
+        src = (wq, wk, wv)[j].at[pl.ds(pl.multiple_of(z * quarter, quarter), quarter), theirs]
+        dst = weights.at[j, pl.ds(pl.multiple_of(at.me * block + z * quarter, quarter), quarter)]
+        return at.push(src, dst, wsend.at[m, j], wrecv.at[m, j], dev)
+
+    def weight_landed(m, j):
+        dev = at.peer(m)
+        dst = weights.at[j, pl.ds(pl.multiple_of(dev * block + z * quarter, quarter), quarter)]
+        return at.push(dst, dst, wsend.at[m, j], wrecv.at[m, j], dev)
+
+    def walk(m, q, right):
+        part = weights.at[:, pl.ds(pl.multiple_of(at.peer(m) * block + q * quarter, quarter), quarter)]
+        send, recv, dev = (rsend, rrecv, z + 1) if right else (lsend, lrecv, z - 1)
+        return pltpu.make_async_remote_copy(
+            src_ref=part, dst_ref=part, send_sem=send.at[m, q], recv_sem=recv.at[m, q],
+            device_id=(dev, at.me), device_id_type=MESH,
+        )
+
+    def send_weights(m):
+        packet_copy(m).start()
+        for j in range(3):
+            weight_copy(m, j).start()
+
+    each(7, send_weights)
+
+    place = lax.broadcasted_iota(jnp.int32, (top, 128), 0)
+    lane = lax.broadcasted_iota(jnp.int32, (top, 128), 1)
+    first = jnp.where(lane == place, 1.0, 0.0).astype(BF16)
+    second = jnp.where(lane == place + top, 1.0, 0.0).astype(BF16)
+
+    def join(s):
+        own[s, :, 0:width] = tok[s]
+        table = dot(ids[s].astype(F32).astype(BF16), first, 0, 0) + dot(gates[s], second, 0, 0)
+        own[s, :, width : width + 128] = table.astype(BF16)
+
+    each(seqs, join)
+    each(seqs, gather.start)
+    own_cols = pl.ds(pl.multiple_of(at.me * cols, cols), cols)
+    mine = pl.ds(pl.multiple_of(at.me * block, block), block)
+    own_weights = [
+        pltpu.make_async_copy(w.at[:, own_cols], weights.at[j, mine], local.at[j]) for j, w in enumerate((wq, wk, wv))
+    ]
+    for copy in own_weights:
+        copy.start()
     early = seqs // 2
-    at.greet((at.xn, at.yn, at.sb))
+    each(early, cot_gather.start)
+
+    def set_out(m):
+        for j in range(3):
+            weight_landed(m, j).wait_recv()
+
+        @pl.when(z < 3)
+        def _():
+            walk(m, z, True).start()
+
+        @pl.when(z > 0)
+        def _():
+            walk(m, z, False).start()
+
+    each(7, set_out)
+
+    def pass_on(d):
+        def step(m):
+            @pl.when(z - d >= 0)
+            def _():
+                walk(m, z - d, True).wait_recv()
+
+                @pl.when(z < 3)
+                def _():
+                    walk(m, z - d, True).start()
+
+            @pl.when(z + d <= 3)
+            def _():
+                walk(m, z + d, False).wait_recv()
+
+                @pl.when(z > 0)
+                def _():
+                    walk(m, z + d, False).start()
+
+        each(7, step)
+
+    def relay(i, _):
+        gather.relay(2 * i, True)
+        gather.relay(2 * i + 1, False)
+        return 0
+
+    pairs = seqs // 2
+    lax.fori_loop(0, pairs // 2, relay, 0)
+    pass_on(1)
+    lax.fori_loop(pairs // 2, pairs, relay, 0)
+    pass_on(2)
+    each(seqs, gather.relay_far)
+    each(7, lambda m: packet_copy(m).wait_recv())
+    packets[at.me] = pk[...]
+    devices = packets.shape[0]
+    share = width // (128 * devices)
+    heads = HEAD_DIM // devices
+    gains[...] = jnp.zeros_like(gains)
+    small[...] = jnp.zeros_like(small)
+    for o in range(devices):
+        for k in range(share):
+            lanes = pl.ds((o * share + k) * 128, 128)
+            gains[0:1, lanes] = packets[o, k : k + 1]
+            gains[1:2, lanes] = packets[o, share + k : share + k + 1]
+        base = 2 * share
+        small[0:1] += pltpu.roll(packets[o, base : base + 1], o * heads, 1)
+        small[1:2] += pltpu.roll(packets[o, base + 1 : base + 2], o * heads, 1)
+        small[2:3] += pltpu.roll(packets[o, base + 2 : base + 3], o, 1)
+    each(seqs, gather.finish)
+    pass_on(3)
+
+    def sent(m):
+        for q in range(4):
+
+            @pl.when(jnp.logical_and(q <= z, z < 3))
+            def _():
+                walk(m, q, True).wait_send()
+
+            @pl.when(jnp.logical_and(q >= z, z > 0))
+            def _():
+                walk(m, q, False).wait_send()
+
+        packet_copy(m).wait_send()
+        for j in range(3):
+            weight_copy(m, j).wait_send()
+
+    for copy in own_weights:
+        copy.wait()
+    keep = pltpu.make_async_copy(weights, weights_out, local.at[3])
+    keep.start()
     each(seqs, cot_gather.start, low=early)
+    number = (at.me * experts).astype(F32)
     begins[...] = jnp.zeros_like(begins)
-
-    def load(s):
-        return pltpu.make_async_copy(full.at[s], blocks.at[lax.rem(s, 2)], tsem.at[lax.rem(s, 2)])
 
     def stores(s):
         k = lax.rem(s, 2)
         pairs = ((nbuf.at[k], normed.at[s]), (pbuf.at[k], pre.at[:, s]), (lbuf.at[k], low.at[:, s]), (cbuf.at[k], ctx.at[s]))
         return [pltpu.make_async_copy(src, dst, ssem.at[i, k]) for i, (src, dst) in enumerate(pairs)]
 
-    load(0).start()
-
     def sequence(s):
         k = lax.rem(s, 2)
-        load(s).wait()
-
-        @pl.when(s + 1 < seqs)
-        def _():
-            load(s + 1).start()
 
         @pl.when(s >= 2)
         def _():
@@ -950,7 +899,7 @@
                 copy.wait()
 
         attend_rows(
-            top, number, s, blocks.at[k], w, wo, gains, small, table,
+            top, number, s, full.at[s], weights, wo, gains, small, table,
             nbuf.at[k], pbuf.at[k], lbuf.at[k], cbuf.at[k], part.at[s], (slots0.at[s], slots1.at[s]), begins,
         )
         for copy in stores(s):
@@ -961,18 +910,18 @@
         living = live_rows(small, s, at.me, tok.shape[1])
         mid, out = mix_rows(reduce.total(s), tok[s], living, gains[1:2])
         middle[s] = mid
-        own[s] = out
-        gather.start(s)
+        mixed_own[s] = out
+        mixed_gather.start(s)
 
     def cot_pair(p):
         @pl.when(lax.rem(p, 2) == 0)
         def _():
-            cot_gather.relay(early + p, True)
-            cot_gather.relay(early + p + 1, False)
+            cot_gather.relay(p, True)
+            cot_gather.relay(p + 1, False)
 
     jobs = (
-        (sequence, 0, seqs), (reduce.hop1, 1, seqs), (cot_pair, 3, early), (reduce.hop2, 3, seqs),
-        (lambda s: cot_gather.relay_far(early + s), 7, early), (rows, 5, seqs),
+        (sequence, 0, seqs), (reduce.hop1, 1, seqs), (cot_pair, 0, seqs), (reduce.hop2, 3, seqs),
+        (cot_gather.relay_far, 4, seqs), (rows, 5, seqs),
     )
 
     def tick(i, _):
@@ -986,23 +935,28 @@
 
     lax.fori_loop(0, max(lag + count for _, lag, count in jobs), tick, 0)
     starts[...] = begins[...].astype(jnp.int32)
-    each(seqs, cot_gather.finish, low=early)
-    gather_tail(gather, 0, seqs)
+    each(seqs, cot_gather.finish)
+    gather_tail(mixed_gather, 0, seqs)
     for s in (seqs - 2, seqs - 1):
         for copy in stores(s):
             copy.wait()
     each(seqs, reduce.finish)
-
-
-def attend_mix(top, local, full, weights, wo, gains, small, table, tokens, cotangent, cot_early):
+    each(7, sent)
+    keep.wait()
+
+
+def forward(top, experts, tokens, cotangent, ids, gates, wq, wk, wv, packet, wo, table):
     seqs, rows, width = tokens.shape
-    length = full.shape[1]
-    cols = weights.shape[2]
+    length, cols = rows * 8, wq.shape[1] // 8
     part = sds((seqs, 8, rows, width), BF16)
+    weights = (3, wq.shape[0] * 8, cols)
     dma = pltpu.SemaphoreType.DMA
     return pl.pallas_call(
-        functools.partial(attend_mix_kernel, top, local),
+        functools.partial(forward_kernel, top, experts),
         out_shape=(
+            sds(weights, BF16),
+            sds((8, width), F32),
+            sds((8, 128), F32),
             sds((seqs, length, width), BF16),
             sds((2, seqs, length, cols), F32),
             sds((3, seqs, length, cols), BF16),
@@ -1014,27 +968,30 @@
             sds((seqs, 16, length), F32),
             sds((8, 128), jnp.int32),
         ),
-        in_specs=[AN] + [VM] * 7 + [AN],
-        out_specs=(AN, AN, AN, AN, VM, AN, AN, VM, VM, VM),
-        input_output_aliases={8: 6},
+        in_specs=[VM] * 10,
+        out_specs=(AN, VM, VM, AN, AN, AN, AN, VM, AN, AN, VM, VM, VM),
         scratch_shapes=[
+            pltpu.VMEM(weights, BF16),
+            pltpu.VMEM((seqs, length, width + 128), BF16),
+            pltpu.VMEM((8,) + packet.shape, F32),
+            pltpu.VMEM((seqs, rows, width + 128), BF16),
             pltpu.VMEM(tokens.shape, BF16),
-            pltpu.VMEM((2,) + full.shape[1:], BF16),
             pltpu.VMEM((2, length, width), BF16),
             pltpu.VMEM((2, 2, length, cols), F32),
             pltpu.VMEM((2, 3, length, cols), BF16),
             pltpu.VMEM((2, length, cols), BF16),
             pltpu.VMEM(part.shape, BF16),
             pltpu.VMEM((8, 128), F32),
-            dma((2,)),
             dma((4, 2)),
         ]
+        + [dma((7, 3)), dma((7, 3)), dma((7,)), dma((7,))]
+        + [dma((7, 4))] * 4
+        + [dma((4,))]
         + Reduce.scratch(part)
-        + Gather.scratch(seqs)
-        + Gather.scratch(seqs),
-        compiler_params=pltpu.CompilerParams(collective_id=2, **COMM),
-        name="attend_mix",
-    )(full, weights, wo, gains, small, table, tokens, cotangent, cot_early)
+        + 3 * Gather.scratch(seqs),
+        compiler_params=pltpu.CompilerParams(collective_id=1, **COMM),
+        name="forward",
+    )(tokens, cotangent, ids, gates, wq, wk, wv, packet, wo, table)
 
 
 def attend_back_kernel(
@@ -1464,8 +1421,8 @@
                 pltpu.VMEM(w_out.shape[1:], BF16),
                 pltpu.VMEM((rows, hidden), BF16),
                 pltpu.VMEM((rows, 2 * hidden), BF16),
-                pltpu.VMEM((256, 2048), F32),
-                pltpu.VMEM((2, 256, 2048), BF16),
+                pltpu.VMEM((512, 2048), F32),
+                pltpu.VMEM((2, 512, 2048), BF16),
                 dma((2,)),
                 dma((2, rows // BLOCK)),
                 dma((2,)),
@@ -1608,21 +1565,21 @@
     packet = jnp.pad(packet, ((0, -packet.shape[0] % 8), (0, 0)))
     share = gains.shape[0] // 2
 
-    full, weights, cot_full, gains, small_in = front(
-        tokens, cotangent, expert_ids.transpose(0, 2, 1), gate_weights.transpose(0, 2, 1),
-        query_weight, key_weight, value_weight, packet,
-    )
-
     half = HEAD_DIM // 2
     frequency = ROPE_BASE ** (-(np.arange(half, dtype=np.float32) * np.float32(2.0 / HEAD_DIM)))
     angles = np.arange(length, dtype=np.float32)[:, None] * frequency.astype(np.float32)[None, :]
     table = jnp.asarray(np.concatenate([np.cos(angles), np.sin(angles)], axis=-1), F32)
 
+    arrays = (
+        tokens, cotangent, expert_ids.transpose(0, 2, 1), gate_weights.transpose(0, 2, 1),
+        query_weight, key_weight, value_weight, packet,
+    )
     if ep == 8 and lax.axis_size("rep") == 4:
-        normed, pre, low, ctx, middle, mixed, cot_full, slots0, slots1, starts = attend_mix(
-            top, local, full, weights, output_weight, gains, small_in, table, tokens, cotangent, cot_full
-        )
+        (
+            weights, gains, small_in, normed, pre, low, ctx, middle, mixed, cot_full, slots0, slots1, starts,
+        ) = forward(top, local, *arrays, output_weight, table)
     else:
+        full, weights, cot_full, gains, small_in = front(*arrays)
         number = (me * local).astype(jnp.int32)[None]
         normed, pre, low, ctx, part, slots0, slots1, starts = attend(
             top, number, full, weights, output_weight, gains, small_in, table
@@ -1663,13 +1620,14 @@
     small, out_all = lax.optimization_barrier((small, out_all))
 
     heads = HEAD_DIM // ep
+    wide = sums.astype(F32)
     return (
         result,
         token_grad,
-        sums[1].astype(F32),
-        sums[2].astype(F32),
-        sums[3].astype(F32),
-        sums[0].astype(F32),
+        wide[1],
+        wide[2],
+        wide[3],
+        wide[0],
         small[:share].reshape(-1),
         small[share : 2 * share].reshape(-1),
         small[2 * share, :heads],

time: 816 us -> 802 us (0.983)
  Pallas kernels: 771 us -> 761 us
    pallas_call x2 -> x1, Pallas kernels: 176 us -> 169 us  [forward(): pl.pallas_call(functools.partial(forward_kernel, top, experts), out_shape...]
  transfers between devices with their start and end apart: 4 -> 4, of which waited for: 0 -> 0; matrix products, arithmetic and copies ran while one was open for 2% -> 2% of each run, Pallas kernels for 69% -> 70%
where the time goes in v12:
time: 802 us
  Pallas kernels  761 us (95%)
  other arithmetic  15.4 us (2%)
  between operations  14.5 us (2%)
  local copies, waits for them, and re-layouts  9.69 us (1%)
    pallas_call x1, Pallas kernels, finish(): pl.pallas_call(finish_kernel, out_shape=(sds(whole, BF16), sds((8, 128),...  312 us
    pallas_call x1, Pallas kernels, forward(): pl.pallas_call(functools.partial(forward_kernel, top, experts), out_shape...  169 us
    pallas_call x1, Pallas kernels, back(): pl.pallas_call(back_kernel, out_shape=(sds(cot.shape, F32), sds((1, width...  79.6 us
    pallas_call x1, Pallas kernels, attend_back(): pl.pallas_call(attend_back_kernel, out_shape=(sds(agrad.shape, BF16), sds...  46.5 us
    pallas_call x1, Pallas kernels, expert_second(): pl.pallas_call(functools.partial(second_kernel, seqs), out_shape=(sds(act...  41.4 us
    pallas_call x1, Pallas kernels, expert_tails(): pl.pallas_call(functools.partial(tail_kernel, seqs), out_shape=(sds((2, r...  38 us
    pallas_call x1, Pallas kernels, expert_first(): pl.pallas_call(functools.partial(first_kernel, capacity), out_shape=(sds(...  29.1 us
    pallas_call x1, Pallas kernels, first_in_grad(): pl.pallas_call(functools.partial(in_grad_kernel, seqs), out_shape=(sds((2...  26.6 us
  transfers between devices with their start and end apart: 4, of which 0 were waited for; matrix products, arithmetic and copies ran while one was open for 2% of the time, Pallas kernels for 70%

profile of v12, /device:TPU:0, one launch (start us, length us, event | category | flops | bytes accessed | tf_op | source)
XLA Modules:
  0.0 801.5 jit_solution(4771996211999161617)
XLA Ops:
  7.2 0.0 reduce-scatter.5.cloned.1.call-start
  7.9 0.7 bitcast_convert_fusion
  8.6 0.7 maximum_convert_fusion.1
  9.2 0.6 select_maximum_fusion.1.pk
  9.8 169.4 %forward.1 = (bf16[3,2048,256]{2,1,0:T(8,128)(2,1)}, f32[8,2048]{1,0:T(8,128)}, f32[8,128]{1,0:T(8,128)}, bf16[8,256,2048]{2,1,0:T(8,128)(2,1)}, f32[2,8,256,256...) custom-call(bf16[8,32,2048]{2,1,0:T(8,128)(2,1)} %tok.3, ...), custom_call_target="tpu_custom_call" | custom-call | tf_op jit(solution)/shard_map/forward/pallas_call | solution.py:954
  179.3 29.1 %expert_first.1 = (bf16[2,1280,1024]{2,1,0:T(8,128)(2,1)}, bf16[1280,2048]{1,0:T(8,128)(2,1)}, bf16[2,1280,2048]{2,1,0:T(8,128)(2,1)}, bf16[2,1280,2048]{2,1,0:T(8,128)(2,1)}, bf16[1024,2048]{1,0:T(8,128)(2,1)}) custom-call(s32[8,128]{1,0:T(8,128)} %get-tuple-element.56.starts.refs_0_, bf16[8,256,2048]{2,1,0:T(8,128)(2,1)} %get-tuple-element.59.mixed, ...), custom_call_target="tpu_custom_call" | custom-call | flops 20000000000 | bytes 60000000 | tf_op jit(solution)/shard_map/expert_first/pallas_call | solution.py:1261
  208.4 0.0 reduce-scatter.5.cloned.1.call-update
  208.4 0.0 reduce-scatter.11.cloned.1.call-start
  208.5 26.6 %first_in_grad.1 = (bf16[2,1280,2048]{2,1,0:T(8,128)(2,1)}, bf16[2048,2048]{1,0:T(8,128)(2,1)}) custom-call(s32[8,128]{1,0:T(8,128)} %get-tuple-element.56.starts.refs_0_, bf16[2,1280,2048]{2,1,0:T(8,128)(2,1)} %get-tuple-element.65.x_all, bf16[2,1280,2048]{2,1,0:T(8,128)(2,1)} %get-tuple-element.62.dy_all, bf16[1280,2048]{1,0:T(8,128)(2,1)} %get-tuple-element.63.pair, ...), custom_call_target="tpu_custom_call" | custom-call | flops 10000000000 | bytes 20000000 | tf_op jit(solution)/shard_map/first_in_grad/pallas_call | solution.py:1340
  235.1 41.4 %expert_second.1 = (bf16[2,1280,1024]{2,1,0:T(8,128)(2,1)}, bf16[2,1280,2048]{2,1,0:T(8,128)(2,1)}, bf16[2048,2048]{1,0:T(8,128)(2,1)}, bf16[1024,2048]{1,0:T(8,128)(2,1)}) custom-call(s32[8,128]{1,0:T(8,128)} %get-tuple-element.56.starts.refs_0_, bf16[2,1280,2048]{2,1,0:T(8,128)(2,1)} %get-tuple-element.65.x_all, ...), custom_call_target="tpu_custom_call", output_to_operand_aliasing={{0}: (5, {}), {1}: (6, {})} | custom-call | flops 24999999488 | bytes 60000000 | tf_op jit(solution)/shard_map/expert_second/pallas_call | solution.py:1406
  276.5 0.0 reduce-scatter.11.cloned.1.call-update
  276.5 0.0 reduce-scatter.9.cloned.1.call-start
  276.6 0.7 reduce-scatter.9.cloned.1.call-update
  277.3 0.0 reduce-scatter.7.cloned.1.call-start
  277.3 0.5 reduce-scatter.7.cloned.1.call-update
  277.8 38.0 %expert_tails.1 = (bf16[2,1280,2048]{2,1,0:T(8,128)(2,1)}, bf16[2,1280,2048]{2,1,0:T(8,128)(2,1)}) custom-call(s32[8,128]{1,0:T(8,128)} %get-tuple-element.56.starts.refs_0_, bf16[2,1280,1024]{2,1,0:T(8,128)(2,1)} %get-tuple-element.68.act, bf16[2,1280,2048]{2,1,0:T(8,128)(2,1)} %get-tuple-element.69.dgu, bf16[2,2048,2048]{2,1,0:T(8,128)(2,1)} %w_in.5, ...), custom_call_target="tpu_custom_call" | custom-call | flops 24000000000 | bytes 60000000 | tf_op jit(solution)/shard_map/expert_tails/pallas_call | solution.py:1460
  315.9 18.0 %combine.1 = (bf16[8,256,2048]{2,1,0:T(8,128)(2,1)}, bf16[8,256,2048]{2,1,0:T(8,128)(2,1)}) custom-call(s32[8,128]{1,0:T(8,128)} %get-tuple-element.56.starts.refs_0_, f32[8,16,256]{2,1,0:T(8,128)} %get-tuple-element.57.slots0.refs_1_, f32[8,16,256]{2,1,0:T(8,128)} %get-tuple-element.58.slots1.refs_2_, bf16[2,1280,2048]{2,1,0:T(8,128)(2,1)} %get-tuple-element.70.refs_3_, ...), custom_call_target="tpu_custom_call" | custom-call | flops 3000000000 | bytes 40000000 | tf_op jit(solution)/shard_map/combine/pallas_call | solution.py:1531
  333.9 79.6 %back.1 = (f32[8,32,2048]{2,1,0:T(8,128)}, f32[1,2048]{1,0:T(1,128)}, bf16[8,256,2048]{2,1,0:T(8,128)(2,1)}) custom-call(bf16[8,8,32,2048]{3,2,1,0:T(8,128)(2,1)} %bitcast.37, f32[8,32,2048]{2,1,0:T(8,128)} %get-tuple-element.73.middle, bf16[8,32,2048]{2,1,0:T(8,128)(2,1)} %cot.3, f32[8,128]{1,0:T(8,128)} %get-tuple-element.74.small, ...), custom_call_target="tpu_custom_call" | custom-call | tf_op jit(solution)/shard_map/back/pallas_call | solution.py:325
  413.5 0.0 copy-start.2
  413.5 46.5 %attend_back.1 = (bf16[8,256,2048]{2,1,0:T(8,128)(2,1)}, bf16[3,2048,256]{2,1,0:T(8,128)(2,1)}, bf16[256,2048]{1,0:T(8,128)(2,1)}, f32[8,128]{1,0:T(8,128)}) custom-call(bf16[8,256,2048]{2,1,0:T(8,128)(2,1)} %get-tuple-element.76.agrad, bf16[8,256,2048]{2,1,0:T(8,128)(2,1)} %get-tuple-element.77.normed, f32[2,8,256,256]{3,2,1,0:T(8,128)} %get-tuple-element.78.pre, ...), custom_call_target="tpu_custom_call" | custom-call | flops 20000000000 | bytes 40000000 | tf_op jit(solution)/shard_map/attend_back/pallas_call | solution.py:1053
  460.0 0.7 slice.31
  460.7 0.0 copy-done.2
  460.7 0.6 select_maximum_fusion.others
  461.3 311.8 %finish.1 = (bf16[4,4,64,2048]{3,2,1,0:T(8,128)(2,1)}, f32[8,128]{1,0:T(8,128)}, bf16[8,32,2048]{2,1,0:T(8,128)(2,1)}, bf16[8,32,2048]{2,1,0:T(8,128)(2,1)}) custom-call(bf16[3,32,64,256]{3,2,1,0:T(8,128)(2,1)} %bitcast.38, bf16[4,64,2048]{2,1,0:T(8,128)(2,1)} %bitcast.46, bf16[8,8,32,2048]{3,2,1,0:T(8,128)(2,1)} %bitcast.36, ...), custom_call_target="tpu_custom_call" | custom-call | tf_op jit(solution)/shard_map/finish/pallas_call | solution.py:568
  773.2 6.0 fusion
  779.1 0.0 copy-start.3
  779.1 0.0 reduce-scatter.5.cloned.1.call-done
  779.1 3.7 pad_convert_fusion
  782.8 0.0 copy-done.3
  782.8 0.5 slice_bitcast_fusion.2
  783.4 0.6 slice_bitcast_fusion
  783.9 0.0 reduce-scatter.11.cloned.1.call-done
  783.9 2.8 convert_dynamic-update-slice_fusion
  786.7 0.0 reduce-scatter.9.cloned.1.call-done
  786.7 0.0 reduce-scatter.7.cloned.1.call-done
  786.7 0.0 copy-start.1
  786.7 0.0 copy-start
  786.7 6.3 maximum_convert_fusion
  793.0 0.0 copy-done.1
  793.0 1.0 copy.36
  794.0 0.0 copy-done
  794.0 1.0 copy.37
  (1 shorter events, 0.0 us)
Async XLA Ops:
  7.2 771.9 %reduce-scatter.5.cloned.1.call-start = ((), (), s32[]{:S(2)}) async-start(), calls=%async_computation.4 | async-start | bytes 5242880 | tf_op jit(solution)/shard_map/reduce_scatter | solution.py:1595
  208.4 575.5 %reduce-scatter.11.cloned.1.call-start = ((), (), s32[]{:S(2)}) async-start(), calls=%async_computation.7 | async-start | bytes 5242880 | tf_op jit(solution)/shard_map/reduce_scatter | solution.py:1595
  276.5 510.2 %reduce-scatter.9.cloned.1.call-start = ((), (), s32[]{:S(2)}) async-start(), calls=%async_computation.6 | async-start | bytes 10485760 | tf_op jit(solution)/shard_map/reduce_scatter | solution.py:1595
  277.3 509.4 %reduce-scatter.7.cloned.1.call-start = ((), (), s32[]{:S(2)}) async-start(), calls=%async_computation.5 | async-start | bytes 10485760 | tf_op jit(solution)/shard_map/reduce_scatter | solution.py:1595
  413.5 47.2 %copy-start.2 = (f32[1,2048]{1,0:T(1,128)S(1)}, f32[1,2048]{1,0:T(1,128)}, u32[]{:S(2)}) copy-start(f32[1,2048]{1,0:T(1,128)} %get-tuple-element.87) | copy-start | bytes 24580
  779.1 3.7 copy-start.3
  786.7 6.3 copy-start.1
  786.7 7.3 copy-start
Sparse Core Ops, SparseCore 0:
  208.6 79.4 reduce-scatter.4
  290.3 85.2 reduce-scatter.10
  378.0 162.8 reduce-scatter.8
  543.7 222.7 reduce-scatter.6

commit v13 on v12

--- a/solution.py
+++ b/solution.py
@@ -723,9 +723,9 @@
 
 
 def forward_kernel(
-    top, experts, tok, cot, ids, gates, wq, wk, wv, pk, wo, table,
-    weights_out, gains, small, normed, pre, low, ctx, middle, mixed, cot_full, slots0, slots1, starts,
-    weights, full, packets, own, mixed_own, nbuf, pbuf, lbuf, cbuf, part, begins, ssem,
+    top, experts, capacity, tok, cot, ids, gates, wq, wk, wv, pk, wo, table,
+    weights_out, gains, small, normed, pre, low, ctx, middle, mixed, cot_full, slots0, slots1, starts, packed,
+    weights, full, packets, cot_rows, packed_rows, csem, dsem, own, mixed_own, nbuf, pbuf, lbuf, cbuf, part, begins, ssem,
     wsend, wrecv, psend, precv, rsend, rrecv, lsend, lrecv, local, *scratch,
 ):
     at = Place()
@@ -936,7 +936,49 @@
     lax.fori_loop(0, max(lag + count for _, lag, count in jobs), tick, 0)
     starts[...] = begins[...].astype(jnp.int32)
     each(seqs, cot_gather.finish)
-    gather_tail(mixed_gather, 0, seqs)
+
+    def cot_load(s):
+        k = lax.rem(s, 2)
+        return pltpu.make_async_copy(cot_full.at[s], cot_rows.at[k], csem.at[k])
+
+    def pack_store(s):
+        k = lax.rem(s, 2)
+        return pltpu.make_async_copy(packed_rows.at[k], packed.at[s], dsem.at[k])
+
+    def pack(s):
+        k = lax.rem(s, 2)
+        cot_load(s).wait()
+
+        @pl.when(s + 1 < seqs)
+        def _():
+            cot_load(s + 1).start()
+
+        @pl.when(s >= 2)
+        def _():
+            pack_store(s - 2).wait()
+
+        spread = []
+        for slots in (slots0, slots1):
+            place = lax.broadcasted_iota(jnp.int32, (capacity, length), 0).astype(F32) == slots[s, 0:1]
+            spread.append(jnp.where(place, slots[s, 8:9], 0.0).astype(BF16))
+        packed_rows[k] = dot(jnp.concatenate(spread, axis=0), cot_rows[k], 1, 0).astype(BF16)
+        pack_store(s).start()
+
+    length = cot_full.shape[1]
+    cot_load(0).start()
+
+    def relay_and_pack(i, _):
+        mixed_gather.relay(2 * i, True)
+        mixed_gather.relay(2 * i + 1, False)
+        pack(2 * i)
+        pack(2 * i + 1)
+        return 0
+
+    lax.fori_loop(0, seqs // 2, relay_and_pack, 0)
+    each(seqs, mixed_gather.relay_far)
+    each(seqs, mixed_gather.finish)
+    pack_store(seqs - 2).wait()
+    pack_store(seqs - 1).wait()
     for s in (seqs - 2, seqs - 1):
         for copy in stores(s):
             copy.wait()
@@ -945,14 +987,14 @@
     keep.wait()
 
 
-def forward(top, experts, tokens, cotangent, ids, gates, wq, wk, wv, packet, wo, table):
+def forward(top, experts, capacity, tokens, cotangent, ids, gates, wq, wk, wv, packet, wo, table):
     seqs, rows, width = tokens.shape
     length, cols = rows * 8, wq.shape[1] // 8
     part = sds((seqs, 8, rows, width), BF16)
     weights = (3, wq.shape[0] * 8, cols)
     dma = pltpu.SemaphoreType.DMA
     return pl.pallas_call(
-        functools.partial(forward_kernel, top, experts),
+        functools.partial(forward_kernel, top, experts, capacity),
         out_shape=(
             sds(weights, BF16),
             sds((8, width), F32),
@@ -967,13 +1009,18 @@
             sds((seqs, 16, length), F32),
             sds((seqs, 16, length), F32),
             sds((8, 128), jnp.int32),
+            sds((seqs, 2 * capacity, width), BF16),
         ),
         in_specs=[VM] * 10,
-        out_specs=(AN, VM, VM, AN, AN, AN, AN, VM, AN, AN, VM, VM, VM),
+        out_specs=(AN, VM, VM, AN, AN, AN, AN, VM, AN, AN, VM, VM, VM, AN),
         scratch_shapes=[
             pltpu.VMEM(weights, BF16),
             pltpu.VMEM((seqs, length, width + 128), BF16),
             pltpu.VMEM((8,) + packet.shape, F32),
+            pltpu.VMEM((2, length, width), BF16),
+            pltpu.VMEM((2, 2 * capacity, width), BF16),
+            dma((2,)),
+            dma((2,)),
             pltpu.VMEM((seqs, rows, width + 128), BF16),
             pltpu.VMEM(tokens.shape, BF16),
             pltpu.VMEM((2, length, width), BF16),
@@ -1178,7 +1225,7 @@
 
 
 def first_kernel(
-    capacity, starts, mixed, cot, slots0, slots1, w_in,
+    capacity, starts, mixed, weighted, slots0, slots1, w_in,
     act, pair, x_all, dy_all, out_grad,
     x, dy, wi, acts, pairs, acc, stage, wsem, ssem, rsem,
 ):
@@ -1194,26 +1241,19 @@
     def _():
         load.start()
 
-    packed = []
+    rows_of = []
     for k in range(together):
-        spread, gate_spread = [], []
+        spread = []
         for slots in (slots0, slots1):
-            column = lax.broadcasted_iota(jnp.int32, (capacity, slots.shape[2]), 0).astype(F32)
-            place = column == slots[k, 0:1]
+            place = lax.broadcasted_iota(jnp.int32, (capacity, slots.shape[2]), 0).astype(F32) == slots[k, 0:1]
             spread.append(jnp.where(place, 1.0, 0.0).astype(BF16))
-            gate_spread.append(jnp.where(place, slots[k, 8:9], 0.0).astype(BF16))
-        packed.append(
-            (
-                dot(jnp.concatenate(spread, axis=0), mixed[k], 1, 0).astype(BF16),
-                dot(jnp.concatenate(gate_spread, axis=0), cot[k], 1, 0).astype(BF16),
-            )
-        )
-    for k, (x_rows, dy_rows) in enumerate(packed):
+        rows_of.append(dot(jnp.concatenate(spread, axis=0), mixed[k], 1, 0).astype(BF16))
+    for k, x_rows in enumerate(rows_of):
         s = step * together + k
         for j in range(2):
             start = pl.multiple_of(starts[j, s], 16)
             x[j, pl.ds(start, capacity)] = x_rows[j * capacity : (j + 1) * capacity]
-            dy[j, pl.ds(start, capacity)] = dy_rows[j * capacity : (j + 1) * capacity]
+            dy[j, pl.ds(start, capacity)] = weighted[k, j * capacity : (j + 1) * capacity]
 
     @pl.when(step == steps - 1)
     def _():
@@ -1251,7 +1291,7 @@
             copy.wait()
 
 
-def expert_first(starts, mixed, cot, slots, w_in, hidden, capacity):
+def expert_first(starts, mixed, weighted, slots, w_in, hidden, capacity):
     seqs, length, width = mixed.shape
     rows = pack_rows(seqs, capacity)
     dma = pltpu.SemaphoreType.DMA
@@ -1272,7 +1312,7 @@
             grid=(seqs // together,),
             in_specs=[
                 pl.BlockSpec((together, length, width), seq),
-                pl.BlockSpec((together, length, width), seq),
+                pl.BlockSpec((together, 2 * capacity, width), seq),
                 slot_spec,
                 slot_spec,
                 AN,
@@ -1294,7 +1334,7 @@
         compiler_params=pltpu.CompilerParams(dimension_semantics=("arbitrary",), vmem_limit_bytes=62 << 20),
         cost_estimate=pl.CostEstimate(flops=2 * 10**10, bytes_accessed=6 * 10**7, transcendentals=10**6),
         name="expert_first",
-    )(starts, mixed, cot, *slots, w_in)
+    )(starts, mixed, weighted, *slots, w_in)
 
 
 def in_grad_kernel(
@@ -1576,8 +1616,8 @@
     )
     if ep == 8 and lax.axis_size("rep") == 4:
         (
-            weights, gains, small_in, normed, pre, low, ctx, middle, mixed, cot_full, slots0, slots1, starts,
-        ) = forward(top, local, *arrays, output_weight, table)
+            weights, gains, small_in, normed, pre, low, ctx, middle, mixed, cot_full, slots0, slots1, starts, weighted,
+        ) = forward(top, local, capacity, *arrays, output_weight, table)
     else:
         full, weights, cot_full, gains, small_in = front(*arrays)
         number = (me * local).astype(jnp.int32)[None]
@@ -1586,9 +1626,14 @@
         )
         starts = starts.astype(jnp.int32)
         middle, mixed = mix(part, tokens, small_in, gains)
+        column = jnp.arange(capacity, dtype=F32)[None, :, None]
+        spread = [jnp.where(column == t[:, 0:1], t[:, 8:9], 0.0).astype(BF16) for t in (slots0, slots1)]
+        weighted = jnp.einsum(
+            "srt,std->srd", jnp.concatenate(spread, axis=1), cot_full, preferred_element_type=F32
+        ).astype(BF16)
 
     act, pair, x_all, dy_all, out_grad0 = expert_first(
-        starts, mixed, cot_full, (slots0, slots1), expert_in, hidden, capacity
+        starts, mixed, weighted, (slots0, slots1), expert_in, hidden, capacity
     )
 
     def over_rep(value):
@@ -1611,13 +1656,6 @@
     sums, small, result, token_grad = finish(
         wgrad, wograd, npart, out_part, tokens, middle, mgrad, gains, ffn_back, qk_back
     )
-
-    def widen(into, value, j):
-        return lax.dynamic_update_slice(into, value.astype(F32)[None], (j, 0, 0))
-
-    small, out0 = lax.optimization_barrier((small, out0))
-    out_all = widen(jnp.zeros((local,) + out0.shape, F32), out0, 0)
-    small, out_all = lax.optimization_barrier((small, out_all))
 
     heads = HEAD_DIM // ep
     wide = sums.astype(F32)
@@ -1633,7 +1671,7 @@
         small[2 * share, :heads],
         small[2 * share + 1, :heads],
         jnp.stack([in0, in1]).astype(F32),
-        widen(out_all, out1, 1),
+        jnp.stack([out0, out1]).astype(F32),
     )
 
 

time: 802 us -> 800 us (level)
  no operation moved by 1% of the time
where the time goes in v13:
time: 800 us; the launch traced here: 799 us
  Pallas kernels  760 us (95%)
  between operations  14.5 us (2%)
  other arithmetic  12.7 us (2%)
  local copies, waits for them, and re-layouts  11.2 us (1%)
    pallas_call x1, Pallas kernels, finish(): pl.pallas_call(finish_kernel, out_shape=(sds(whole, BF16), sds((8, 128),...  312 us
    pallas_call x1, Pallas kernels, forward(): pl.pallas_call(functools.partial(forward_kernel, top, experts, capacity),...  169 us
    pallas_call x1, Pallas kernels, back(): pl.pallas_call(back_kernel, out_shape=(sds(cot.shape, F32), sds((1, width...  79.6 us
    pallas_call x1, Pallas kernels, attend_back(): pl.pallas_call(attend_back_kernel, out_shape=(sds(agrad.shape, BF16), sds...  46.5 us
    pallas_call x1, Pallas kernels, expert_second(): pl.pallas_call(functools.partial(second_kernel, seqs), out_shape=(sds(act...  41.3 us
    pallas_call x1, Pallas kernels, expert_tails(): pl.pallas_call(functools.partial(tail_kernel, seqs), out_shape=(sds((2, r...  38 us
    pallas_call x1, Pallas kernels, expert_first(): pl.pallas_call(functools.partial(first_kernel, capacity), out_shape=(sds(...  28.2 us
    pallas_call x1, Pallas kernels, first_in_grad(): pl.pallas_call(functools.partial(in_grad_kernel, seqs), out_shape=(sds((2...  26.6 us
  transfers between devices with their start and end apart: 4, of which 0 were waited for; matrix products, arithmetic and copies ran while one was open for 2% of the time, Pallas kernels for 70%

profile of v13, /device:TPU:0, one launch (start us, length us, event | category | flops | bytes accessed | tf_op | source)
XLA Modules:
  0.0 799.3 jit_solution(4095480413188561343)
XLA Ops:
  7.2 0.0 reduce-scatter.9.cloned.1.call-start
  7.9 0.7 bitcast_convert_fusion
  8.6 0.7 maximum_convert_fusion.2
  9.2 0.6 select_maximum_fusion.1.pk
  9.8 169.5 %forward.1 = (bf16[3,2048,256]{2,1,0:T(8,128)(2,1)}, f32[8,2048]{1,0:T(8,128)}, f32[8,128]{1,0:T(8,128)}, bf16[8,256,2048]{2,1,0:T(8,128)(2,1)}, f32[2,8,256,256...) custom-call(bf16[8,32,2048]{2,1,0:T(8,128)(2,1)} %tok.3, ...), custom_call_target="tpu_custom_call" | custom-call | tf_op jit(solution)/shard_map/forward/pallas_call | solution.py:996
  179.3 28.2 %expert_first.1 = (bf16[2,1280,1024]{2,1,0:T(8,128)(2,1)}, bf16[1280,2048]{1,0:T(8,128)(2,1)}, bf16[2,1280,2048]{2,1,0:T(8,128)(2,1)}, bf16[2,1280,2048]{2,1,0:T(8,128)(2,1)}, bf16[1024,2048]{1,0:T(8,128)(2,1)}) custom-call(s32[8,128]{1,0:T(8,128)} %get-tuple-element.52.starts.refs_0_, bf16[8,256,2048]{2,1,0:T(8,128)(2,1)} %get-tuple-element.55.mixed, ...), custom_call_target="tpu_custom_call" | custom-call | flops 20000000000 | bytes 60000000 | tf_op jit(solution)/shard_map/expert_first/pallas_call | solution.py:1301
  207.5 0.0 reduce-scatter.9.cloned.1.call-update
  207.5 0.0 reduce-scatter.11.cloned.1.call-start
  207.5 26.6 %first_in_grad.1 = (bf16[2,1280,2048]{2,1,0:T(8,128)(2,1)}, bf16[2048,2048]{1,0:T(8,128)(2,1)}) custom-call(s32[8,128]{1,0:T(8,128)} %get-tuple-element.52.starts.refs_0_, bf16[2,1280,2048]{2,1,0:T(8,128)(2,1)} %get-tuple-element.61.x_all, bf16[2,1280,2048]{2,1,0:T(8,128)(2,1)} %get-tuple-element.58.dy_all, bf16[1280,2048]{1,0:T(8,128)(2,1)} %get-tuple-element.59.pair, ...), custom_call_target="tpu_custom_call" | custom-call | flops 10000000000 | bytes 20000000 | tf_op jit(solution)/shard_map/first_in_grad/pallas_call | solution.py:1380
  234.2 41.3 %expert_second.1 = (bf16[2,1280,1024]{2,1,0:T(8,128)(2,1)}, bf16[2,1280,2048]{2,1,0:T(8,128)(2,1)}, bf16[2048,2048]{1,0:T(8,128)(2,1)}, bf16[1024,2048]{1,0:T(8,128)(2,1)}) custom-call(s32[8,128]{1,0:T(8,128)} %get-tuple-element.52.starts.refs_0_, bf16[2,1280,2048]{2,1,0:T(8,128)(2,1)} %get-tuple-element.61.x_all, ...), custom_call_target="tpu_custom_call", output_to_operand_aliasing={{0}: (5, {}), {1}: (6, {})} | custom-call | flops 24999999488 | bytes 60000000 | tf_op jit(solution)/shard_map/expert_second/pallas_call | solution.py:1446
  275.5 0.0 reduce-scatter.11.cloned.1.call-update
  275.5 0.0 reduce-scatter.7.cloned.1.call-start
  275.6 0.7 reduce-scatter.7.cloned.1.call-update
  276.3 0.0 reduce-scatter.5.cloned.1.call-start
  276.3 0.5 reduce-scatter.5.cloned.1.call-update
  276.8 38.0 %expert_tails.1 = (bf16[2,1280,2048]{2,1,0:T(8,128)(2,1)}, bf16[2,1280,2048]{2,1,0:T(8,128)(2,1)}) custom-call(s32[8,128]{1,0:T(8,128)} %get-tuple-element.52.starts.refs_0_, bf16[2,1280,1024]{2,1,0:T(8,128)(2,1)} %get-tuple-element.64.act, bf16[2,1280,2048]{2,1,0:T(8,128)(2,1)} %get-tuple-element.65.dgu, bf16[2,2048,2048]{2,1,0:T(8,128)(2,1)} %w_in.5, ...), custom_call_target="tpu_custom_call" | custom-call | flops 24000000000 | bytes 60000000 | tf_op jit(solution)/shard_map/expert_tails/pallas_call | solution.py:1500
  314.8 18.0 %combine.1 = (bf16[8,256,2048]{2,1,0:T(8,128)(2,1)}, bf16[8,256,2048]{2,1,0:T(8,128)(2,1)}) custom-call(s32[8,128]{1,0:T(8,128)} %get-tuple-element.52.starts.refs_0_, f32[8,16,256]{2,1,0:T(8,128)} %get-tuple-element.53.slots0.refs_1_, f32[8,16,256]{2,1,0:T(8,128)} %get-tuple-element.54.slots1.refs_2_, bf16[2,1280,2048]{2,1,0:T(8,128)(2,1)} %get-tuple-element.66.refs_3_, ...), custom_call_target="tpu_custom_call" | custom-call | flops 3000000000 | bytes 40000000 | tf_op jit(solution)/shard_map/combine/pallas_call | solution.py:1571
  332.9 79.6 %back.1 = (f32[8,32,2048]{2,1,0:T(8,128)}, f32[1,2048]{1,0:T(1,128)}, bf16[8,256,2048]{2,1,0:T(8,128)(2,1)}) custom-call(bf16[8,8,32,2048]{3,2,1,0:T(8,128)(2,1)} %bitcast.35, f32[8,32,2048]{2,1,0:T(8,128)} %get-tuple-element.69.middle, bf16[8,32,2048]{2,1,0:T(8,128)(2,1)} %cot.3, f32[8,128]{1,0:T(8,128)} %get-tuple-element.70.small, ...), custom_call_target="tpu_custom_call" | custom-call | tf_op jit(solution)/shard_map/back/pallas_call | solution.py:325
  412.5 0.0 copy-start.2
  412.5 46.5 %attend_back.1 = (bf16[8,256,2048]{2,1,0:T(8,128)(2,1)}, bf16[3,2048,256]{2,1,0:T(8,128)(2,1)}, bf16[256,2048]{1,0:T(8,128)(2,1)}, f32[8,128]{1,0:T(8,128)}) custom-call(bf16[8,256,2048]{2,1,0:T(8,128)(2,1)} %get-tuple-element.72.agrad, bf16[8,256,2048]{2,1,0:T(8,128)(2,1)} %get-tuple-element.73.normed, f32[2,8,256,256]{3,2,1,0:T(8,128)} %get-tuple-element.74.pre, ...), custom_call_target="tpu_custom_call" | custom-call | flops 20000000000 | bytes 40000000 | tf_op jit(solution)/shard_map/attend_back/pallas_call | solution.py:1100
  459.0 0.7 slice.31
  459.7 0.0 copy-done.2
  459.7 0.6 select_maximum_fusion.others
  460.3 311.8 %finish.1 = (bf16[4,4,64,2048]{3,2,1,0:T(8,128)(2,1)}, f32[8,128]{1,0:T(8,128)}, bf16[8,32,2048]{2,1,0:T(8,128)(2,1)}, bf16[8,32,2048]{2,1,0:T(8,128)(2,1)}) custom-call(bf16[3,32,64,256]{3,2,1,0:T(8,128)(2,1)} %bitcast.36, bf16[4,64,2048]{2,1,0:T(8,128)(2,1)} %bitcast.43, bf16[8,8,32,2048]{3,2,1,0:T(8,128)(2,1)} %bitcast.34, ...), custom_call_target="tpu_custom_call" | custom-call | tf_op jit(solution)/shard_map/finish/pallas_call | solution.py:568
  772.2 1.3 slice_bitcast_fusion.2
  773.4 1.3 slice_bitcast_fusion
  774.8 5.9 fusion
  780.7 0.0 reduce-scatter.9.cloned.1.call-done
  780.7 0.0 reduce-scatter.11.cloned.1.call-done
  780.7 3.8 maximum_convert_fusion.1
  784.5 0.0 reduce-scatter.7.cloned.1.call-done
  784.5 0.0 reduce-scatter.5.cloned.1.call-done
  784.5 0.0 copy-start.1
  784.5 0.0 copy-start
  784.6 6.3 maximum_convert_fusion
  790.9 0.0 copy-done.1
  790.9 1.0 copy.35
  791.8 0.0 copy-done
  791.8 1.0 copy.36
  (1 shorter events, 0.0 us)
Async XLA Ops:
  7.2 773.5 %reduce-scatter.9.cloned.1.call-start = ((), (), s32[]{:S(2)}) async-start(), calls=%async_computation.6 | async-start | bytes 5242880 | tf_op jit(solution)/shard_map/reduce_scatter | solution.py:1640
  207.5 573.2 %reduce-scatter.11.cloned.1.call-start = ((), (), s32[]{:S(2)}) async-start(), calls=%async_computation.7 | async-start | bytes 5242880 | tf_op jit(solution)/shard_map/reduce_scatter | solution.py:1640
  275.5 509.0 %reduce-scatter.7.cloned.1.call-start = ((), (), s32[]{:S(2)}) async-start(), calls=%async_computation.5 | async-start | bytes 10485760 | tf_op jit(solution)/shard_map/reduce_scatter | solution.py:1640
  276.3 508.3 %reduce-scatter.5.cloned.1.call-start = ((), (), s32[]{:S(2)}) async-start(), calls=%async_computation.4 | async-start | bytes 10485760 | tf_op jit(solution)/shard_map/reduce_scatter | solution.py:1640
  412.5 47.2 %copy-start.2 = (f32[1,2048]{1,0:T(1,128)S(1)}, f32[1,2048]{1,0:T(1,128)}, u32[]{:S(2)}) copy-start(f32[1,2048]{1,0:T(1,128)} %get-tuple-element.83) | copy-start | bytes 24580
  784.5 6.3 copy-start.1
  784.5 7.3 copy-start
Sparse Core Ops, SparseCore 0:
  207.6 79.5 reduce-scatter.8
  289.5 85.1 reduce-scatter.10
  377.1 162.8 reduce-scatter.6
  542.7 222.7 reduce-scatter.4
